TPU v7x, 256 devices: a whole 4x4x8 slice. The times are simulated.
256 devices in a mesh: seq: 128 (over z, x, y), tp: 2 (over core).
Axes of the slice: x: 4, y: 4, z: 8, core: 2. Of those that a mesh axis runs over, the one named last changes fastest.
Arguments:
- img_qkv: bfloat16 [1, 4096, 3, 2048], P(None, 'seq', None, 'tp'), may hold values from -7 to 7
- txt_qkv: bfloat16 [1, 256, 3, 2048], P(None, None, None, 'tp'), may hold values from -7 to 7
- frame_index: int32 [1, 4096], P(None, 'seq'), may hold values from 0 to 32
- row_index: int32 [1, 4096], P(None, 'seq'), may hold values from 0 to 44
- column_index: int32 [1, 4096], P(None, 'seq'), may hold values from 0 to 79
- txt_len: int32 [1], replicated, may hold values from 64 to 256
- residual: bfloat16 [1, 4096, 3072], P(None, ('seq', 'tp')), may hold values from -6 to 6
- w_proj: bfloat16 [2048, 3072], P('tp'), may hold values from -0.125 to 0.125
- proj_bias: float32 [3072], replicated, may hold values from -3 to 3
- gate: float32 [3072], replicated, may hold values from -4 to 4
Outputs:
- img_out: bfloat16 [1, 4096, 3072], P(None, ('seq', 'tp'))
- txt_out: bfloat16 [1, 256, 2048], P(None, None, 'tp')
All inputs are finite; a program needn't handle non-finite values.
Results may differ from a plain program's by a relative error of at most 0.0082.
Values may be sent and summed in bfloat16 or wider, within the bound.
No kernel may reach another device: no remote copies, remote signals or barrier semaphores. Data moves between devices by JAX's collectives and lax.ppermute only.
A program may use at most 64 MiB of HBM per device.

v0:
```python
import math

import jax
import jax.numpy as jnp
from jax import lax
from jax.sharding import Mesh
from jax.sharding import PartitionSpec as P

HD = 128
SEQ = ("seq_0", "seq_1", "seq_2")
SEQ_TP = ("seq_0", "seq_1", "seq_2", "tp")


rope_base = 256.0
neg_large = -1e30


def gathered_by_axis(x, axes, dim):
    for axis in reversed(axes):
        x = lax.all_gather(x, axis, axis=dim, tiled=True)
    return x


def copy_for_each(x, axis):
    size = lax.axis_size(axis)
    return lax.all_to_all(jnp.broadcast_to(x[None], (size, *x.shape)), axis, 0, 0, tiled=True)


def over_copies(x, axis):
    everything = copy_for_each(x, axis)
    return jnp.sum(everything.astype(jnp.float32), axis=0)


def rope_tables(frame_index, row_index, column_index, head_dim):
    frame_part = head_dim // 8
    second = (head_dim - frame_part) // 2
    pieces = []
    for places, part_width in (
        (frame_index, frame_part),
        (row_index, second),
        (column_index, second),
    ):
        pair_ids = jnp.arange(part_width // 2).astype(jnp.float32)
        pair_rates = rope_base ** (-2.0 * pair_ids / part_width)
        pieces.append(places.astype(jnp.float32)[:, None] * pair_rates[None, :])
    angles = jnp.repeat(jnp.concatenate(pieces, axis=1), 2, axis=1)
    parity = jnp.arange(head_dim) % 2
    signed = jnp.where(parity == 0, -1.0, 1.0).astype(jnp.float32)
    return (jnp.cos(angles), jnp.sin(angles) * signed[None, :])


def rotate(block_in, cosine, sine_table):
    values = block_in.astype(jnp.float32)
    parity = jnp.arange(values.shape[-1]) % 2
    partner = jnp.where(parity == 0, jnp.roll(values, -1, axis=-1), jnp.roll(values, 1, axis=-1))
    return (values * cosine[:, None, :] + partner * sine_table[:, None, :]).astype(jnp.bfloat16)


def absorb(carry_state, queries, block_keys, block_values, live_keys, score_scale):
    peak, weight_sum, blended = carry_state
    scores = (
        jnp.einsum("cqd,ckd->cqk", queries, block_keys, preferred_element_type=jnp.float32)
        * score_scale
    )
    if live_keys is not None:
        scores = jnp.where(live_keys[:, None, :], scores, neg_large)
    new_peak = jnp.maximum(peak, jnp.max(scores, axis=2))
    weights = jnp.exp(scores - new_peak[:, :, None])
    if live_keys is not None:
        weights = jnp.where(live_keys[:, None, :], weights, 0.0)
    shrink = jnp.exp(peak - new_peak)
    weight_sum = weight_sum * shrink + jnp.sum(weights, axis=2)
    blended = blended * shrink[:, :, None] + jnp.einsum(
        "cqk,ckd->cqd",
        weights.astype(jnp.bfloat16),
        block_values,
        preferred_element_type=jnp.float32,
    )
    return (new_peak, weight_sum, blended)


def shards(
    img_qkv,
    txt_qkv,
    frame_index,
    row_index,
    column_index,
    txt_len,
    residual,
    w_proj,
    proj_bias,
    gate,
):
    clips = img_qkv.shape[0]
    clip_tok = img_qkv.shape[1]
    head_dim = HD
    heads_tp = img_qkv.shape[3] // head_dim
    seq_count = lax.axis_size(SEQ)
    tp_count = lax.axis_size("tp")
    groups = seq_count // heads_tp
    per_group = clip_tok // groups
    txt_total = txt_qkv.shape[1]
    txt_share = txt_total // groups
    position = lax.axis_index(SEQ)
    my_head = position % heads_tp
    my_group = position // heads_tp
    score_scale = 1.0 / math.sqrt(head_dim)
    cosine, sine_table = rope_tables(
        frame_index.reshape(-1), row_index.reshape(-1), column_index.reshape(-1), head_dim
    )
    img_query = rotate(
        img_qkv[:, :, 0].reshape(clips * clip_tok, heads_tp, head_dim), cosine, sine_table
    ).reshape(clips, clip_tok, heads_tp, head_dim)
    img_key = rotate(
        img_qkv[:, :, 1].reshape(clips * clip_tok, heads_tp, head_dim), cosine, sine_table
    ).reshape(clips, clip_tok, heads_tp, head_dim)
    img_value = img_qkv[:, :, 2].reshape(clips, clip_tok, heads_tp, head_dim)
    query_send = (
        img_query.reshape(clips, groups, per_group, heads_tp, head_dim)
        .transpose(1, 3, 0, 2, 4)
        .reshape(seq_count, clips * per_group, head_dim)
    )
    key_value = jnp.stack([img_key, img_value], axis=2)
    txt_head = lax.dynamic_slice_in_dim(txt_qkv, my_head * head_dim, head_dim, 3)
    txt_query = lax.dynamic_slice_in_dim(txt_head[:, :, 0], my_group * txt_share, txt_share, 1)
    img_rows_count = seq_count * per_group
    query_rows = img_rows_count + txt_share
    start_state = (
        jnp.full((clips, query_rows), neg_large, jnp.float32),
        jnp.zeros((clips, query_rows), jnp.float32),
        jnp.zeros((clips, query_rows, head_dim), jnp.float32),
    )
    copies = jnp.broadcast_to(
        key_value.transpose(3, 0, 1, 2, 4)[None], (groups, heads_tp, clips, clip_tok, 2, head_dim)
    ).reshape(seq_count, clips, clip_tok, 2, head_dim)
    query_recv, pair_recv = (
        lax.all_to_all(query_send, SEQ, split_axis=0, concat_axis=0, tiled=True),
        lax.all_to_all(copies, SEQ, split_axis=0, concat_axis=0, tiled=True),
    )
    ordered = (
        query_recv.reshape(seq_count, clips, per_group, head_dim)
        .transpose(1, 0, 2, 3)
        .reshape(clips, img_rows_count, head_dim)
    )
    queries = jnp.concatenate([ordered, txt_query], axis=1)
    sources = max(1, min(seq_count, 2048 // clip_tok))
    while seq_count % sources:
        sources -= 1
    all_pairs = pair_recv.transpose(1, 0, 2, 3, 4).reshape(
        clips, seq_count // sources, sources * clip_tok, 2, head_dim
    )
    key_blocks = all_pairs.transpose(1, 0, 2, 3, 4)

    def sweep_block(carry_state, key_block):
        return (
            absorb(carry_state, queries, key_block[:, :, 0], key_block[:, :, 1], None, score_scale),
            None,
        )

    carry_state, unused = lax.scan(sweep_block, start_state, key_blocks)
    txt_live = jnp.arange(txt_total)[None, :] < txt_len[:, None]
    peak, weight_sum, blended = absorb(
        carry_state, queries, txt_head[:, :, 1], txt_head[:, :, 2], txt_live, score_scale
    )
    attended = (blended / weight_sum[:, :, None]).astype(jnp.bfloat16)
    img_part = (
        attended[:, :img_rows_count]
        .reshape(clips, seq_count, per_group, head_dim)
        .transpose(1, 0, 2, 3)
    )
    txt_part = attended[:, img_rows_count:]
    returned = lax.all_to_all(img_part, SEQ, split_axis=0, concat_axis=0, tiled=True)
    home_rows = (
        returned.reshape(groups, heads_tp, clips, per_group, head_dim)
        .transpose(2, 0, 3, 1, 4)
        .reshape(clips, clip_tok, heads_tp * head_dim)
    )
    txt_index = my_group * txt_share + jnp.arange(txt_share)
    txt_keep = (txt_index[None, :] < txt_len[:, None])[:, :, None]
    txt_part = jnp.where(txt_keep, txt_part, jnp.zeros_like(txt_part))
    gathered = gathered_by_axis(txt_part[None], SEQ, 0)
    txt_out = (
        gathered.reshape(groups, heads_tp, clips, txt_share, head_dim)
        .transpose(2, 0, 3, 1, 4)
        .reshape(clips, txt_total, heads_tp * head_dim)
    )
    row_share = clip_tok // tp_count
    share_rows = clips * row_share
    ordered_rows = (
        home_rows.reshape(clips, tp_count, row_share, heads_tp * head_dim)
        .transpose(1, 0, 2, 3)
        .reshape(tp_count * share_rows, heads_tp * head_dim)
    )
    full_sum = over_copies(
        jnp.dot(ordered_rows, w_proj, preferred_element_type=jnp.float32).astype(jnp.bfloat16), "tp"
    ).astype(jnp.float32)
    projected = lax.dynamic_slice_in_dim(full_sum, lax.axis_index("tp") * share_rows, share_rows, 0)
    projected = projected.reshape(clips, row_share, projected.shape[1])
    img_out = (
        residual.astype(jnp.float32) + gate[None, None, :] * (projected + proj_bias[None, None, :])
    ).astype(jnp.bfloat16)
    return (img_out, txt_out)


def solution(mesh):
    split = Mesh(mesh.devices.reshape(8, 4, 4, mesh.shape["tp"]), ("seq_0", "seq_1", "seq_2", "tp"))
    placed = (
        P(None, SEQ, None, "tp"),
        P(None, None, None, "tp"),
        P(None, SEQ),
        P(None, SEQ),
        P(None, SEQ),
        P(),
        P(None, SEQ_TP, None),
        P("tp", None),
        P(),
        P(),
    )
    return jax.shard_map(
        shards,
        mesh=split,
        in_specs=placed,
        out_specs=(P(None, SEQ_TP, None), P(None, None, "tp")),
        check_vma=False,
    )
```

profile of v0, /device:TPU:1, one launch (start us, length us, event | category | flops | bytes accessed | tf_op | source)
XLA Modules:
  0.0 180.9 jit_solution(878013164419484406)
XLA Ops:
  0.7 1.0 convert_bitcast_fusion.1
  1.9 0.1 fusion.40
  2.0 0.7 convert_bitcast_fusion.4
  2.6 0.7 convert_bitcast_fusion.2
  3.5 0.2 fusion.37
  3.6 0.3 broadcast_in_dim.107
  3.9 0.6 sin.18
  4.5 0.3 broadcast_in_dim.105
  4.9 0.6 cos.18
  5.5 0.2 copy.90
  5.7 0.3 copy.80
  6.0 0.2 copy.91
  6.2 0.3 copy.82
  6.5 0.1 fusion.29
  6.7 0.7 copy.83
  7.4 16.3 %all-to-all-start.1 = ((bf16[128,2,128]{2,1,0:T(2,128)(2,1)}), bf16[128,2,128]{2,1,0:T(2,128)(2,1)S(1)}, u32[]{:S(2)}, u32[]{:S(2)}) async-start(bf16[128,2,128]{2,1,0:T(2,128)(2,1)} %bitcast.19), calls=%async_computation.1 | async-start | bytes 131072 | tf_op jit(solution)/shard_map/all_to_all | solution.py:137
  24.4 0.1 copy.70
  24.5 0.2 copy.71
  24.7 0.1 copy.72
  24.8 0.1 copy.73
  25.0 0.1 fusion.22
  25.2 9.2 %all-to-all-done.1 = bf16[128,2,128]{2,1,0:T(2,128)(2,1)S(1)} async-done(((bf16[128,2,128]{2,1,0:T(2,128)(2,1)}), bf16[128,2,128]{2,1,0:T(2,128)(2,1)S(1)}, u32[]{:S(2)}, u32[]{:S(2)}) %all-to-all-start.1) | async-done | bytes 65568 | tf_op jit(solution)/shard_map/all_to_all | solution.py:137
  34.4 1.8 %broadcast_in_dim.111 = bf16[16,8,32,2,128]{4,2,3,1,0:T(8,128)(2,1)} broadcast(bf16[8,32,2,128]{3,1,2,0:T(8,128)(2,1)S(1)} %copy.77), dimensions={1,2,3,4} | broadcast | bytes 2228224 | tf_op jit(solution)/shard_map/broadcast_in_dim | solution.py:133
  36.2 7.3 %all-to-all-start = ((bf16[128,1,32,2,128]{4,2,3,1,0:T(8,128)(2,1)}), bf16[128,1,32,2,128]{4,2,3,1,0:T(8,128)(2,1)}, u32[]{:S(2)}, u32[]{:S(2)}) async-start(bf16[128,1,32,2,128]{4,2,3,1,0:T(8,128)(2,1)} %bitcast.143), calls=%async_computation | async-start | bytes 4194304 | tf_op jit(solution)/shard_map/all_to_all | solution.py:138
  44.4 0.3 fusion.42
  44.7 46.9 %all-to-all-done = bf16[128,1,32,2,128]{4,2,3,1,0:T(8,128)(2,1)} async-done(((bf16[128,1,32,2,128]{4,2,3,1,0:T(8,128)(2,1)}), bf16[128,1,32,2,128]{4,2,3,1,0:T(8,128)(2,1)}, u32[]{:S(2)}, u32[]{:S(2)}) %all-to-all-start) | async-done | bytes 2097184 | tf_op jit(solution)/shard_map/all_to_all | solution.py:138
  91.6 3.3 %copy.78 = bf16[128,1,32,2,128]{4,2,0,3,1:T(8,128)(2,1)} copy(bf16[128,1,32,2,128]{4,2,3,1,0:T(8,128)(2,1)} %all-to-all-done) | data formatting | bytes 4194304 | tf_op jit(solution)/shard_map/all_to_all | solution.py:138
  94.9 12.0 %while.15 = (s32[]{:T(128)}, f32[1,272]{1,0:T(1,128)S(1)}, f32[1,272]{1,0:T(1,128)S(1)}, f32[1,272,128]{2,1,0:T(8,128)S(1)}, bf16[2,1,2048,2,128]{4,2,0,3,1:T(8,...) while((s32[]{:T(128)}, f32[1,272]{1,0:T(1,128)S(1)}, ...), condition=%wide.region_3.4_spmd.clone, body=%wide.region_0.3_spmd.clone.sunk | while | flops 288661088 | bytes 19112000 | solution.py:160
  94.9 1.3 dynamic-slice_bitcast_fusion.7
  96.2 1.9 %fusion.51 = (f32[272]{0:T(512)S(1)}, f32[2048,272]{0,1:T(8,128)}) fusion(bf16[1,272,128]{2,1,0:T(8,128)(2,1)S(1)} %get-tuple-element.184, bf16[1,2048,2,128]{3,1,2,0:T(8,128)(2,1)S(1)} %dynamic-slice_bitcast_fusion.7), kind=kOutput, calls=%fused_computation.85.clone.1 | convolution fusion | flops 143720176 | bytes 2823232 | tf_op jit(solution)/shard_map/while/body/eval_jaxpr/cqd,ckd->cqk/dot_general | solution.py:62
  98.0 2.3 %fusion.55 = f32[1,272,128]{2,1,0:T(8,128)S(1)} fusion(f32[2048,272]{0,1:T(8,128)} %get-tuple-element.160, f32[272]{0:T(512)S(1)} %get-tuple-element.161, bf16[1,2048,2,128]{3,1,2,0:T(8,128)(2,1)S(1)} %dynamic-slice_bitcast_fusion.7, f32[1,272,128]{2,1,0:T(8,128)S(1)} %get-tuple-element.174, f32[272]{0:T(512)S(1)} %get-tuple-element.162, pred[]{:T(512)S(6)} %compare.8), kind=kOutput, calls=%fused_computation.5.clone.1 | convolution fusion | flops 143824896 | bytes 3035137 | tf_op jit(solution)/shard_map/while/body/eval_jaxpr/cqk,ckd->cqd/dot_general | solution.py:73
  100.3 0.5 fusion.53
  100.9 1.3 dynamic-slice_bitcast_fusion.7
  102.2 1.9 %fusion.51 = (f32[272]{0:T(512)S(1)}, f32[2048,272]{0,1:T(8,128)}) fusion(bf16[1,272,128]{2,1,0:T(8,128)(2,1)S(1)} %get-tuple-element.184, bf16[1,2048,2,128]{3,1,2,0:T(8,128)(2,1)S(1)} %dynamic-slice_bitcast_fusion.7), kind=kOutput, calls=%fused_computation.85.clone.1 | convolution fusion | flops 143720176 | bytes 2823232 | tf_op jit(solution)/shard_map/while/body/eval_jaxpr/cqd,ckd->cqk/dot_general | solution.py:62
  104.1 2.3 %fusion.55 = f32[1,272,128]{2,1,0:T(8,128)S(1)} fusion(f32[2048,272]{0,1:T(8,128)} %get-tuple-element.160, f32[272]{0:T(512)S(1)} %get-tuple-element.161, bf16[1,2048,2,128]{3,1,2,0:T(8,128)(2,1)S(1)} %dynamic-slice_bitcast_fusion.7, f32[1,272,128]{2,1,0:T(8,128)S(1)} %get-tuple-element.174, f32[272]{0:T(512)S(1)} %get-tuple-element.162, pred[]{:T(512)S(6)} %compare.8), kind=kOutput, calls=%fused_computation.5.clone.1 | convolution fusion | flops 143824896 | bytes 3035137 | tf_op jit(solution)/shard_map/while/body/eval_jaxpr/cqk,ckd->cqd/dot_general | solution.py:73
  106.4 0.5 fusion.53
  106.9 0.2 fusion.13
  107.2 0.2 fusion.12
  107.4 0.6 slice.86
  108.1 9.1 %all-gather = bf16[4,16,128]{2,1,0:T(8,128)(2,1)S(1)} all-gather(bf16[1,16,128]{2,1,0:T(8,128)(2,1)S(1)} %slice_select_fusion), channel_id=2, replica_groups=mesh['seq_0'=8,'seq_1'=4,'seq_2'=4,'tp'=2] {'seq_2'}, dimensions={0}, use_global_device_ids=true | all-gather | bytes 20480 | tf_op jit(solution)/shard_map/all_gather | solution.py:20
  117.2 9.0 %all-gather.1 = bf16[16,16,128]{2,1,0:T(8,128)(2,1)S(1)} all-gather(bf16[4,16,128]{2,1,0:T(8,128)(2,1)S(1)} %all-gather), channel_id=3, replica_groups=mesh['seq_0'=8,'seq_1'=4,'seq_2'=4,'tp'=2] {'seq_1'}, dimensions={0}, use_global_device_ids=true | all-gather | bytes 81920 | tf_op jit(solution)/shard_map/all_gather | solution.py:20
  126.2 11.2 %all-to-all-start.2 = ((bf16[128,1,2,128]{3,2,1,0:T(2,128)(2,1)}), bf16[128,1,2,128]{3,2,1,0:T(2,128)(2,1)S(1)}, u32[]{:S(2)}, u32[]{:S(2)}) async-start(bf16[128,1,2,128]{3,2,1,0:T(2,128)(2,1)} %bitcast.28), calls=%async_computation.2 | async-start | bytes 131072 | tf_op jit(solution)/shard_map/all_to_all | solution.py:172
  137.4 20.6 %all-gather.2 = bf16[128,16,128]{2,1,0:T(8,128)(2,1)S(1)} all-gather(bf16[16,16,128]{2,1,0:T(8,128)(2,1)S(1)} %all-gather.1), channel_id=4, replica_groups=mesh['seq_0'=8,'seq_1'=4,'seq_2'=4,'tp'=2] {'seq_0'}, dimensions={0}, use_global_device_ids=true | all-gather | bytes 589824 | tf_op jit(solution)/shard_map/all_gather | solution.py:20
  158.1 0.1 copy.88
  158.2 1.0 reshape.362
  159.3 4.0 %convolution_convert_fusion = bf16[32,3072]{1,0:T(8,128)(2,1)S(1)} fusion(bf16[1024,3072]{1,0:T(8,128)(2,1)} %param.19, bf16[4,8,8,128]{3,2,1,0:T(8,128)(2,1)S(1)} %bitcast.155), kind=kOutput, calls=%fused_computation.19 | convolution fusion | flops 201424896 | bytes 6553600 | tf_op jit(solution)/shard_map/dot_general | solution.py:195
  163.3 16.8 %all_to_all.20 = bf16[2,32,3072]{2,1,0:T(8,128)(2,1)S(1)} all-to-all(bf16[2,32,3072]{2,1,0:T(8,128)(2,1)S(1)} %broadcast_in_dim.117), channel_id=1, replica_groups=mesh['seq_0'=8,'seq_1'=4,'seq_2'=4,'tp'=2] {'tp'}, dimensions={0} | all-to-all | bytes 786432 | tf_op jit(solution)/shard_map/all_to_all | solution.py:26
  180.2 0.7 fusion.15
  (55 shorter events, 1.4 us)
Async XLA Ops:
  0.6 43.7 %copy-start = (bf16[1,256,3,1024]{3,1,2,0:T(8,128)(2,1)S(1)}, bf16[1,256,3,1024]{3,1,2,0:T(8,128)(2,1)}, u32[]{:S(2)}) copy-start(bf16[1,256,3,1024]{3,1,2,0:T(8,128)(2,1)} %param.13) | copy-start | bytes 4718596
  7.4 27.0 %all-to-all-start.1 = ((bf16[128,2,128]{2,1,0:T(2,128)(2,1)}), bf16[128,2,128]{2,1,0:T(2,128)(2,1)S(1)}, u32[]{:S(2)}, u32[]{:S(2)}) async-start(bf16[128,2,128]{2,1,0:T(2,128)(2,1)} %bitcast.19), calls=%async_computation.1 | async-start | bytes 131072 | tf_op jit(solution)/shard_map/all_to_all | solution.py:137
  36.2 55.4 %all-to-all-start = ((bf16[128,1,32,2,128]{4,2,3,1,0:T(8,128)(2,1)}), bf16[128,1,32,2,128]{4,2,3,1,0:T(8,128)(2,1)}, u32[]{:S(2)}, u32[]{:S(2)}) async-start(bf16[128,1,32,2,128]{4,2,3,1,0:T(8,128)(2,1)} %bitcast.143), calls=%async_computation | async-start | bytes 4194304 | tf_op jit(solution)/shard_map/all_to_all | solution.py:138
  98.0 2.3 %copy-start.1 = (f32[2048,272]{0,1:T(8,128)S(1)}, f32[2048,272]{0,1:T(8,128)}, u32[]{:S(2)}) copy-start(f32[2048,272]{0,1:T(8,128)} %get-tuple-element.160) | copy-start | bytes 6684676 | tf_op jit(solution)/shard_map/while
  104.0 2.3 %copy-start.1 = (f32[2048,272]{0,1:T(8,128)S(1)}, f32[2048,272]{0,1:T(8,128)}, u32[]{:S(2)}) copy-start(f32[2048,272]{0,1:T(8,128)} %get-tuple-element.160) | copy-start | bytes 6684676 | tf_op jit(solution)/shard_map/while
  126.2 33.0 %all-to-all-start.2 = ((bf16[128,1,2,128]{3,2,1,0:T(2,128)(2,1)}), bf16[128,1,2,128]{3,2,1,0:T(2,128)(2,1)S(1)}, u32[]{:S(2)}, u32[]{:S(2)}) async-start(bf16[128,1,2,128]{3,2,1,0:T(2,128)(2,1)} %bitcast.28), calls=%async_computation.2 | async-start | bytes 131072 | tf_op jit(solution)/shard_map/all_to_all | solution.py:172
  159.3 20.9 %copy-start.3 = (f32[3072]{0:T(1024)S(1)}, f32[3072]{0:T(1024)}, u32[]{:S(2)}) copy-start(f32[3072]{0:T(1024)} %param.20) | copy-start | bytes 36868
  159.3 20.9 %copy-start.4 = (f32[3072]{0:T(1024)S(1)}, f32[3072]{0:T(1024)}, u32[]{:S(2)}) copy-start(f32[3072]{0:T(1024)} %param.21) | copy-start | bytes 36868
  163.3 16.9 %copy-start.2 = (bf16[1,16,3072]{2,1,0:T(8,128)(2,1)S(1)}, bf16[1,16,3072]{2,1,0:T(8,128)(2,1)}, u32[]{:S(2)}) copy-start(bf16[1,16,3072]{2,1,0:T(8,128)(2,1)} %param.18) | copy-start | bytes 294916
where the time goes:
time: 181 us
  waiting for transfers between devices  56.1 us (31%)
  blocking collectives  55.5 us (31%)
  starting transfers between devices  34.9 us (19%)
  local copies, waits for them, and re-layouts  14.5 us (8%)
  matrix products  12.8 us (7%)
  other arithmetic  5.25 us (3%)
    all_to_all x1, waiting for transfers between devices, shards(): lax.all_to_all(copies, SEQ, split_axis=0, concat_axis=0, tiled=True)  46.9 us
    all_gather x3, blocking collectives, gathered_by_axis(): x = lax.all_gather(x, axis, axis=dim, tiled=True)  38.7 us
    all_to_all x1, blocking collectives, copy_for_each(): lax.all_to_all(jnp.broadcast_to(x[None], (size, *x.shape)), axis, 0, 0, t...  16.8 us
    all_to_all x1, starting transfers between devices, shards(): lax.all_to_all(query_send, SEQ, split_axis=0, concat_axis=0, tiled=True)  16.3 us
    all_to_all x1, starting transfers between devices, shards(): lax.all_to_all(img_part, SEQ, split_axis=0, concat_axis=0, tiled=True)  11.2 us
    all_to_all x1, waiting for transfers between devices, shards(): lax.all_to_all(query_send, SEQ, split_axis=0, concat_axis=0, tiled=True)  9.19 us
    all_to_all x1, starting transfers between devices, shards(): lax.all_to_all(copies, SEQ, split_axis=0, concat_axis=0, tiled=True)  7.34 us
    dot_general x3, matrix products, absorb(): jnp.einsum('cqk,ckd->cqd', weights.astype(jnp.bfloat16), block_values, pr...  4.82 us
  transfers between devices with their start and end apart: 3, of which 2 were waited for; matrix products, arithmetic and copies ran while one was open for 2% of the time, Pallas kernels for 0%

commit v1 on v0

v1 whole, which is shorter than its diff:
```python
import math

import jax
import jax.numpy as jnp
import numpy as np
from jax import lax
from jax.experimental import pallas as pl
from jax.experimental.pallas import tpu as pltpu
from jax.sharding import Mesh
from jax.sharding import PartitionSpec as P

HD = 128
SEQ = ("zh", "zl", "x", "y")
CUBE = ("zl", "x", "y")
rope_base = 256.0
neg_large = -1e30
LOG2E = 1.4426950408889634
bf16 = jnp.bfloat16
f32 = jnp.float32


def vmem_spec():
    return pl.BlockSpec(memory_space=pltpu.VMEM)


def smem_spec():
    return pl.BlockSpec(memory_space=pltpu.SMEM)


def call(body, out_shape, n_in, smem=(), limit=40 * 1024 * 1024, scratch=(), name=None):
    single = not isinstance(out_shape, (tuple, list))
    outs = out_shape if not single else [out_shape]
    specs = [vmem_spec() for _ in outs]
    return pl.pallas_call(
        body,
        out_shape=out_shape,
        in_specs=[smem_spec() if i in smem else vmem_spec() for i in range(n_in)],
        out_specs=specs[0] if single else specs,
        scratch_shapes=list(scratch),
        compiler_params=pltpu.CompilerParams(vmem_limit_bytes=limit),
        name=name,
    )


def rate_table():
    table = np.zeros((8, HD), np.float32)
    frame_part = HD // 8
    second = (HD - frame_part) // 2
    at = 0
    for p, width in enumerate((frame_part, second, second)):
        ids = np.arange(width // 2, dtype=np.float32)
        rates = np.float32(rope_base) ** (np.float32(-2.0) * ids / np.float32(width))
        table[p, at : at + width] = np.repeat(rates.astype(np.float32), 2)
        at += width
    return table


def prep_body(qkv_ref, frame_ref, row_ref, col_ref, rate_ref, out_ref):
    tokens = qkv_ref.shape[1]
    sub = lax.broadcasted_iota(jnp.int32, (8, tokens), 0)
    pos = jnp.where(
        sub == 0, frame_ref[...], jnp.where(sub == 1, row_ref[...], jnp.where(sub == 2, col_ref[...], 0))
    ).astype(f32)
    angles = lax.dot_general(
        pos, rate_ref[...], (((0,), (0,)), ((), ())), precision=lax.Precision.HIGHEST,
        preferred_element_type=f32,
    )
    lane = lax.broadcasted_iota(jnp.int32, (tokens, HD), 1)
    even = (lane % 2) == 0
    cosine = jnp.cos(angles)
    sine = jnp.sin(angles)
    sine = jnp.where(even, -sine, sine)

    def rotate(v):
        v = v.astype(f32)
        partner = jnp.where(even, pltpu.roll(v, HD - 1, 1), pltpu.roll(v, 1, 1))
        return v * cosine + partner * sine

    for head in range(8):
        cols = slice(head * HD, (head + 1) * HD)
        query = rotate(qkv_ref[0, :, cols]).astype(bf16)
        key = rotate(qkv_ref[1, :, cols])
        value = qkv_ref[2, :, cols].astype(f32)
        for j in range(4):
            d = head * 4 + j
            out_ref[d, 0:32, :] = query
            pair = jnp.concatenate([key[8 * j : 8 * j + 8], value[8 * j : 8 * j + 8]], axis=0)
            out_ref[d, 32:48, :] = pair.astype(bf16)


def softmax_block(q, keys, values, live):
    scale = LOG2E / math.sqrt(HD)
    scores = lax.dot_general(q, keys, (((1,), (1,)), ((), ())), preferred_element_type=f32)
    n_img = keys.shape[0] - 128
    s_img = scores[:, :n_img]
    s_txt = jnp.where(live, scores[:, n_img:], neg_large)
    peak = jnp.maximum(
        jnp.max(s_img, axis=1, keepdims=True), jnp.max(s_txt, axis=1, keepdims=True)
    )
    w_img = jnp.exp2((s_img - peak) * scale)
    w_txt = jnp.exp2((s_txt - peak) * scale)
    total = jnp.sum(w_img, axis=1, keepdims=True) + jnp.sum(w_txt, axis=1, keepdims=True)
    weights = jnp.concatenate([w_img.astype(bf16), w_txt.astype(bf16)], axis=1)
    out = jnp.dot(weights, values, preferred_element_type=f32)
    return out / total, peak * scale + jnp.log2(total)


def three_parts(v):
    high = v.astype(bf16).astype(f32)
    rest = v - high
    mid = rest.astype(bf16).astype(f32)
    return high, mid, rest - mid


def live_mask(j, length):
    lane = lax.broadcasted_iota(jnp.int32, (1, 128), 1)
    index = lane + (j // 2) * 128
    return jnp.logical_and(index // 64 == j, index < length)


def text_body(
    where_ref, len_ref, kv0_ref, kv1_ref, kv2_ref, kv3_ref, txt_ref,
    p0_ref, p1_ref, p2_ref, p3_ref, keys_ref, values_ref,
):
    j = where_ref[0]
    length = len_ref[0]
    for b, ref in enumerate((kv0_ref, kv1_ref, kv2_ref, kv3_ref)):
        pair = ref[...].astype(f32)
        keys_ref[256 * b : 256 * b + 256, :] = pair[:, 0:8, :].reshape(256, HD).astype(bf16)
        values_ref[256 * b : 256 * b + 256, :] = pair[:, 8:16, :].reshape(256, HD).astype(bf16)
    start = pl.multiple_of((j // 2) * 128, 128)
    keys_ref[1024:1152, :] = txt_ref[1, pl.ds(start, 128), :]
    values_ref[1024:1152, :] = txt_ref[2, pl.ds(start, 128), :]
    keys = keys_ref[...]
    values = values_ref[...]
    live = live_mask(j, length)
    q = jnp.concatenate(
        [txt_ref[0, pl.ds(pl.multiple_of((j ^ s) * 64, 64), 64), :] for s in range(4)], axis=0
    )
    out, lse = softmax_block(q, keys, values, live)
    out = out.astype(bf16)
    row = lax.broadcasted_iota(jnp.int32, (64, 128), 0)
    lane = lax.broadcasted_iota(jnp.int32, (64, 128), 1)
    for s, ref in enumerate((p0_ref, p1_ref, p2_ref, p3_ref)):
        ref[0:64, :] = out[64 * s : 64 * s + 64]
        high, mid, low = three_parts(jnp.broadcast_to(lse[64 * s : 64 * s + 64], (64, 128)))
        first = jnp.where(row == lane % 64, jnp.where(lane < 64, high, mid), 0.0)
        second = jnp.where(row == lane, low, 0.0)
        first = jnp.broadcast_to(jnp.sum(first, axis=0, keepdims=True), (8, 128))
        second = jnp.broadcast_to(jnp.sum(second, axis=0, keepdims=True), (8, 128))
        ref[64:80, :] = jnp.concatenate([first, second], axis=0).astype(bf16)


def image_body(where_ref, len_ref, recv_ref, keys_ref, values_ref, out_ref):
    live = live_mask(where_ref[0], len_ref[0])
    keys = keys_ref[...]
    values = values_ref[...]
    row = lax.broadcasted_iota(jnp.int32, (8, 32, 128), 1)
    lane = lax.broadcasted_iota(jnp.int32, (8, 32, 128), 2)
    for b in range(4):
        q = recv_ref[8 * b : 8 * b + 8, 0:32, :].reshape(256, HD)
        out, lse = softmax_block(q, keys, values, live)
        out_ref[8 * b : 8 * b + 8, 0:32, :] = out.astype(bf16).reshape(8, 32, HD)
        high, mid, low = three_parts(jnp.broadcast_to(lse, (256, 128)).reshape(8, 32, 128))
        parts = jnp.where(lane < 32, high, jnp.where(lane < 64, mid, low))
        packed = jnp.where(jnp.logical_and(row == lane % 32, lane < 96), parts, 0.0)
        packed = jnp.sum(packed, axis=1, keepdims=True)
        out_ref[8 * b : 8 * b + 8, 32:48, :] = jnp.broadcast_to(packed, (8, 16, 128)).astype(bf16)


def blend(outs, lses):
    peak = lses[0]
    for v in lses[1:]:
        peak = jnp.maximum(peak, v)
    weights = [jnp.exp2(v - peak) for v in lses]
    total = weights[0]
    for w in weights[1:]:
        total = total + w
    mixed = outs[0] * weights[0]
    for o, w in zip(outs[1:], weights[1:]):
        mixed = mixed + o * w
    return mixed / total


def fill_body(where_ref, len_ref, img_ref, p0_ref, p1_ref, p2_ref, p3_ref, out_ref):
    row = lax.broadcasted_iota(jnp.int32, (64, 128), 0)
    lane = lax.broadcasted_iota(jnp.int32, (64, 128), 1)
    outs, lses = [], []
    for ref in (p0_ref, p1_ref, p2_ref, p3_ref):
        outs.append(ref[0:64, :].astype(f32))
        stats = ref[64:80, :].astype(f32)
        picked = jnp.where(row == lane % 64, stats[0:1], 0.0) + jnp.where(row == lane, stats[8:9], 0.0)
        lses.append(jnp.sum(picked, axis=1, keepdims=True))
    text = blend(outs, lses)
    text = jnp.where(where_ref[0] * 64 + row < len_ref[0], text, 0.0).astype(bf16)
    for d in range(32):
        out_ref[d, 0:48, :] = img_ref[d]
        out_ref[d, 48:112, :] = text


def tail_body(core_ref, recv_ref, w_ref, mine_ref, other_ref, txt_ref):
    row = lax.broadcasted_iota(jnp.int32, (32, 128), 0)
    lane = lax.broadcasted_iota(jnp.int32, (32, 128), 1)
    pick = jnp.logical_and(row == lane % 32, lane < 96)
    heads = []
    for head in range(8):
        outs, lses = [], []
        for j in range(4):
            s = head * 4 + j
            outs.append(recv_ref[s, 0:32, :].astype(f32))
            stats = recv_ref[s, 32:48, :].astype(f32)[0:1]
            lses.append(jnp.sum(jnp.where(pick, stats, 0.0), axis=1, keepdims=True))
            txt_ref[64 * j : 64 * j + 64, head * HD : (head + 1) * HD] = recv_ref[s, 48:112, :]
        heads.append(blend(outs, lses))
    rows = jnp.concatenate(heads, axis=1)
    flipped = jnp.concatenate([rows[16:32], rows[0:16]], axis=0)
    rows = jnp.where(core_ref[0] == 0, rows, flipped).astype(bf16)
    projected = jnp.dot(rows, w_ref[...], preferred_element_type=f32)
    mine_ref[...] = projected[0:16]
    other_ref[...] = projected[16:32].astype(bf16)


def shards(
    img_qkv, txt_qkv, frame_index, row_index, column_index, txt_len, residual, w_proj, proj_bias, gate
):
    tokens = img_qkv.shape[1]
    width = img_qkv.shape[3]
    d_model = w_proj.shape[1]
    j = lax.axis_index("y").astype(jnp.int32).reshape(1)
    head = lax.axis_index("zl") * 4 + lax.axis_index("x")
    core = lax.axis_index("tp").astype(jnp.int32).reshape(1)
    qkv = img_qkv.reshape(tokens, 3, width).transpose(1, 0, 2)
    txt = lax.dynamic_slice_in_dim(txt_qkv[0], head * HD, HD, 2).transpose(1, 0, 2)

    send = call(prep_body, jax.ShapeDtypeStruct((32, 48, HD), bf16), 5, name="prep")(
        qkv, frame_index, row_index, column_index, jnp.asarray(rate_table())
    )
    recv = lax.all_to_all(send, CUBE, 0, 0, tiled=True)
    kv = recv[:, 32:48, :]
    others = [lax.ppermute(kv, "zh", [(i, i ^ s) for i in range(4)]) for s in (1, 2, 3)]

    piece = jax.ShapeDtypeStruct((80, HD), bf16)
    keyed = jax.ShapeDtypeStruct((1152, HD), bf16)
    p0, p1, p2, p3, keys, values = call(
        text_body, [piece] * 4 + [keyed] * 2, 7, smem=(0, 1), name="text"
    )(j, txt_len, kv, *others, txt)
    got = [
        lax.ppermute(p, "y", [(i, i ^ s) for i in range(4)])
        for s, p in ((1, p1), (2, p2), (3, p3))
    ]
    img = call(image_body, jax.ShapeDtypeStruct((32, 48, HD), bf16), 5, smem=(0, 1), name="image")(
        j, txt_len, recv, keys, values
    )
    back = call(fill_body, jax.ShapeDtypeStruct((32, 112, HD), bf16), 7, smem=(0, 1), name="fill")(
        j, txt_len, img, p0, *got
    )
    home = lax.all_to_all(back, CUBE, 0, 0, tiled=True)
    half = tokens // 2
    mine, other, txt_out = call(
        tail_body,
        [
            jax.ShapeDtypeStruct((half, d_model), f32),
            jax.ShapeDtypeStruct((half, d_model), bf16),
            jax.ShapeDtypeStruct((256, width), bf16),
        ],
        3, smem=(0,), name="tail",
    )(core, home, w_proj)
    theirs = lax.ppermute(other, "tp", [(0, 1), (1, 0)])
    projected = mine + theirs.astype(f32)
    img_out = residual[0].astype(f32) + gate[None, :] * (projected + proj_bias[None, :])
    return img_out.astype(bf16)[None], txt_out[None]


def solution(mesh):
    split = Mesh(
        mesh.devices.reshape(4, 2, 4, 4, mesh.shape["tp"]), ("zh", "zl", "x", "y", "tp")
    )
    placed = (
        P(None, SEQ, None, "tp"),
        P(None, None, None, "tp"),
        P(None, SEQ),
        P(None, SEQ),
        P(None, SEQ),
        P(),
        P(None, SEQ + ("tp",), None),
        P("tp", None),
        P(),
        P(),
    )
    return jax.shard_map(
        shards,
        mesh=split,
        in_specs=placed,
        out_specs=(P(None, SEQ + ("tp",), None), P(None, None, "tp")),
        check_vma=False,
    )
```

time: 181 us -> 78.2 us (0.43)
  blocking collectives: 55.5 us -> 17.7 us
  waiting for transfers between devices: 56.1 us -> 19.6 us
  matrix products: 12.8 us -> 0 us
  starting transfers between devices: 34.9 us -> 25 us
  local copies, waits for them, and re-layouts: 14.5 us -> 6.56 us
  Pallas kernels: 0 us -> 6.93 us
  other arithmetic: 5.25 us -> 0.69 us
    all_to_all x3 -> x1, waiting for transfers between devices: 56.1 us -> 10.9 us  [shards(): home = lax.all_to_all(back, CUBE, 0, 0, tiled=True)]
    all_gather x3 -> x0, blocking collectives: 38.7 us -> none  [gathered_by_axis(): x = lax.all_gather(x, axis, axis=dim, tiled=True)]
    all_to_all x3 -> x1, starting transfers between devices: 34.9 us -> 4.62 us  [shards(): home = lax.all_to_all(back, CUBE, 0, 0, tiled=True)]
    ppermute x0 -> x7, starting transfers between devices: none -> 20.4 us  [the longest x3 7.75 us: shards(): lax.ppermute(p, 'y', [(i, i ^ s) for i in range(4)])]
    dot_general x7 -> x0, matrix products: 12.8 us -> none  [the longest x3 4.82 us: absorb(): jnp.einsum('cqk,ckd->cqd', weights.astype(jnp.bfloat16), block_values, pr...]
    ppermute x0 -> x7, waiting for transfers between devices: none -> 8.71 us  [the longest x3 7.54 us: shards(): lax.ppermute(kv, 'zh', [(i, i ^ s) for i in range(4)])]
    pallas_call x0 -> x5, Pallas kernels: none -> 6.93 us  [the longest x1 2.52 us: shards(): call(image_body, jax.ShapeDtypeStruct((32, 48, HD), bf16), 5, smem=(0, 1)...]
    unnamed x15 -> x20, local copies, waits for them, and re-layouts: 0.75 us -> 6.49 us
  transfers between devices with their start and end apart: 3 -> 8, of which waited for: 2 -> 6; matrix products, arithmetic and copies ran while one was open for 2% -> 0% of each run, Pallas kernels for 0% -> 3%
where the time goes in v1:
time: 78.2 us; the launch traced here: 77.9 us
  starting transfers between devices  25 us (32%)
  waiting for transfers between devices  19.6 us (25%)
  blocking collectives  17.7 us (23%)
  Pallas kernels  6.93 us (9%)
  local copies, waits for them, and re-layouts  6.56 us (8%)
  between operations  1.38 us (2%)
    all_to_all x1, blocking collectives, shards(): recv = lax.all_to_all(send, CUBE, 0, 0, tiled=True)  17.7 us
    all_to_all x1, waiting for transfers between devices, shards(): home = lax.all_to_all(back, CUBE, 0, 0, tiled=True)  10.9 us
    ppermute x3, starting transfers between devices, shards(): lax.ppermute(p, 'y', [(i, i ^ s) for i in range(4)])  7.75 us
    ppermute x3, waiting for transfers between devices, shards(): lax.ppermute(kv, 'zh', [(i, i ^ s) for i in range(4)])  7.54 us
    ppermute x3, starting transfers between devices, shards(): lax.ppermute(kv, 'zh', [(i, i ^ s) for i in range(4)])  7.39 us
    unnamed x20, local copies, waits for them, and re-layouts  6.49 us
    ppermute x1, starting transfers between devices, shards(): theirs = lax.ppermute(other, 'tp', [(0, 1), (1, 0)])  5.25 us
    all_to_all x1, starting transfers between devices, shards(): home = lax.all_to_all(back, CUBE, 0, 0, tiled=True)  4.62 us
  transfers between devices with their start and end apart: 8, of which 6 were waited for; matrix products, arithmetic and copies ran while one was open for 0% of the time, Pallas kernels for 3%

profile of v1, /device:TPU:1, one launch (start us, length us, event | category | flops | bytes accessed | tf_op | source)
XLA Modules:
  0.0 77.9 jit_solution(6829039524255648238)
XLA Ops:
  0.6 0.0 copy-start
  0.6 0.0 copy-start.2
  0.7 1.0 %copy-done.2 = bf16[1,32,3,1024]{3,1,2,0:T(8,128)(2,1)S(1)} copy-done((bf16[1,32,3,1024]{3,1,2,0:T(8,128)(2,1)S(1)}, bf16[1,32,3,1024]{3,1,2,0:T(8,128)(2,1)}, u32[]{:S(2)}) %copy-start.2) | copy-done | bytes 196632
  1.7 0.0 copy-start.3
  1.7 0.7 copy-done.3
  2.4 0.0 copy-start.4
  2.4 0.7 copy-done.4
  3.0 0.0 copy-start.5
  3.0 0.7 copy-done.5
  3.7 0.0 copy-start.6
  3.7 0.7 copy-done.6
  4.3 0.3 prep.1
  4.7 17.7 %all_to_all.10.recv_ref = bf16[32,48,128]{2,1,0:T(8,128)(2,1)S(1)} all-to-all(bf16[32,48,128]{2,1,0:T(8,128)(2,1)S(1)} %prep.1), channel_id=1, replica_groups=mesh['zh'=4,'zl'=2,'x'=4,'y'=4,'tp'=2] {'zl','x','y'}, dimensions={0} | all-to-all | bytes 786432 | tf_op jit(solution)/shard_map/all_to_all | solution.py:238
  22.4 5.2 %collective-permute-start.2 = (bf16[32,16,128]{2,1,0:T(8,128)(2,1)S(1)}, bf16[32,16,128]{2,1,0:T(8,128)(2,1)S(1)}, u32[]{:S(2)}, u32[]{:S(2)}) collective-permute-start(bf16[32,16,128]{2,1,0:T(8,128)(2,1)S(1)} %slice.4.kv0_ref), channel_id=1, source_target_pairs={{0,192},{64,128},{128,64},{192,0},{1,193},{65,129},{129,65},{193,1... | collective-permute-start | bytes 393224 | tf_op jit(solution)/shard_map/ppermute | solution.py:240
  27.6 1.2 %collective-permute-start.1 = (bf16[32,16,128]{2,1,0:T(8,128)(2,1)S(1)}, bf16[32,16,128]{2,1,0:T(8,128)(2,1)S(1)}, u32[]{:S(2)}, u32[]{:S(2)}) collective-permute-start(bf16[32,16,128]{2,1,0:T(8,128)(2,1)S(1)} %slice.4.kv0_ref), channel_id=1, source_target_pairs={{0,128},{64,192},{128,0},{192,64},{1,129},{65,193},{129,1},{193,65... | collective-permute-start | bytes 393224 | tf_op jit(solution)/shard_map/ppermute | solution.py:240
  28.8 1.0 %collective-permute-start = (bf16[32,16,128]{2,1,0:T(8,128)(2,1)S(1)}, bf16[32,16,128]{2,1,0:T(8,128)(2,1)S(1)}, u32[]{:S(2)}, u32[]{:S(2)}) collective-permute-start(bf16[32,16,128]{2,1,0:T(8,128)(2,1)S(1)} %slice.4.kv0_ref), channel_id=1, source_target_pairs={{0,64},{64,0},{128,192},{192,128},{1,65},{65,1},{129,193},{193,129... | collective-permute-start | bytes 393224 | tf_op jit(solution)/shard_map/ppermute | solution.py:240
  30.4 0.0 copy-done
  30.5 0.1 dynamic-slice_bitcast_fusion.txt_ref
  30.5 5.5 %collective-permute-done.2.kv3_ref = bf16[32,16,128]{2,1,0:T(8,128)(2,1)S(1)} collective-permute-done((bf16[32,16,128]{2,1,0:T(8,128)(2,1)S(1)}, bf16[32,16,128]{2,1,0:T(8,128)(2,1)S(1)}, u32[]{:S(2)}, u32[]{:S(2)}) %collective-permute-start.2) | collective-permute-done | bytes 131104 | tf_op jit(solution)/shard_map/ppermute | solution.py:240
  36.1 1.8 %collective-permute-done.1.kv2_ref = bf16[32,16,128]{2,1,0:T(8,128)(2,1)S(1)} collective-permute-done((bf16[32,16,128]{2,1,0:T(8,128)(2,1)S(1)}, bf16[32,16,128]{2,1,0:T(8,128)(2,1)S(1)}, u32[]{:S(2)}, u32[]{:S(2)}) %collective-permute-start.1) | collective-permute-done | bytes 131104 | tf_op jit(solution)/shard_map/ppermute | solution.py:240
  37.9 0.1 collective-permute-done.kv1_ref
  38.1 0.8 %text.1 = (bf16[80,128]{1,0:T(8,128)(2,1)S(1)}, bf16[80,128]{1,0:T(8,128)(2,1)S(1)}, bf16[80,128]{1,0:T(8,128)(2,1)S(1)}, bf16[80,128]{1,0:T(8,128)(2,1)S(1)}, b...) custom-call(s32[1]{0:T(128)} %bitcast.2.where_ref, s32[1]{0:T(128)S(6)} %copy.13.len_ref, ...), custom_call_target="tpu_custom_call" | custom-call | tf_op jit(solution)/shard_map/text/pallas_call | solution.py:244
  38.9 5.3 %collective-permute-start.3 = (bf16[80,128]{1,0:T(8,128)(2,1)S(1)}, bf16[80,128]{1,0:T(8,128)(2,1)S(1)}, u32[]{:S(2)}, u32[]{:S(2)}) collective-permute-start(bf16[80,128]{1,0:T(8,128)(2,1)S(1)} %get-tuple-element.14), channel_id=1, source_target_pairs={{0,2},{2,0},{4,6},{6,4},{1,3},{3,1},{5,7},{7,5},{8,10},{10,8},{12,... | collective-permute-start | bytes 61448 | tf_op jit(solution)/shard_map/ppermute | solution.py:248
  44.2 1.4 %collective-permute-start.4 = (bf16[80,128]{1,0:T(8,128)(2,1)S(1)}, bf16[80,128]{1,0:T(8,128)(2,1)S(1)}, u32[]{:S(2)}, u32[]{:S(2)}) collective-permute-start(bf16[80,128]{1,0:T(8,128)(2,1)S(1)} %get-tuple-element.15), channel_id=1, source_target_pairs={{0,4},{2,6},{4,0},{6,2},{1,5},{3,7},{5,1},{7,3},{8,12},{10,14},{12... | collective-permute-start | bytes 61448 | tf_op jit(solution)/shard_map/ppermute | solution.py:248
  45.6 1.1 %collective-permute-start.5 = (bf16[80,128]{1,0:T(8,128)(2,1)S(1)}, bf16[80,128]{1,0:T(8,128)(2,1)S(1)}, u32[]{:S(2)}, u32[]{:S(2)}) collective-permute-start(bf16[80,128]{1,0:T(8,128)(2,1)S(1)} %get-tuple-element.16), channel_id=1, source_target_pairs={{0,6},{2,4},{4,2},{6,0},{1,7},{3,5},{5,3},{7,1},{8,14},{10,12},{12... | collective-permute-start | bytes 61448 | tf_op jit(solution)/shard_map/ppermute | solution.py:248
  46.7 2.5 %image.1.img_ref = bf16[32,48,128]{2,1,0:T(8,128)(2,1)S(1)} custom-call(s32[1]{0:T(128)} %bitcast.2.where_ref, s32[1]{0:T(128)S(6)} %copy.13.len_ref, bf16[32,48,128]{2,1,0:T(8,128)(2,1)S(1)} %all_to_all.10.recv_ref, bf16[1152,128]{1,0:T(8,128)(2,1)S(1)} %get-tuple-element.11.keys_ref, bf16[1152,128]{1,0:T(8,128)(2,1)S(1)} %get-tuple-element.12.values_ref), custom_call_target="tpu_custom_call" | custom-call | tf_op jit(solution)/shard_map/image/pallas_call | solution.py:251
  49.2 0.0 collective-permute-done.3.p1_ref
  49.2 0.0 collective-permute-done.4.p2_ref
  49.2 0.2 collective-permute-done.5.p3_ref
  49.4 1.1 %fill.1 = bf16[32,112,128]{2,1,0:T(8,128)(2,1)} custom-call(s32[1]{0:T(128)} %bitcast.2.where_ref, s32[1]{0:T(128)S(6)} %copy.13.len_ref, bf16[32,48,128]{2,1,0:T(8,128)(2,1)S(1)} %image.1.img_ref, bf16[80,128]{1,0:T(8,128)(2,1)S(1)} %get-tuple-element.13.p0_ref, bf16[80,128]{1,0:T(8,128)(2,1)S(1)} %collective-permute-done.3.p1_ref, ...), custom_call_target="tpu_custom_call" | custom-call | tf_op jit(solution)/shard_map/fill/pallas_call | solution.py:254
  50.5 4.6 %all-to-all-start.1 = ((bf16[32,112,128]{2,1,0:T(8,128)(2,1)}), bf16[32,112,128]{2,1,0:T(8,128)(2,1)S(1)}, u32[]{:S(2)}, u32[]{:S(2)}) async-start(bf16[32,112,128]{2,1,0:T(8,128)(2,1)} %fill.1), calls=%async_computation.1 | async-start | bytes 1835008 | tf_op jit(solution)/shard_map/all_to_all | solution.py:257
  55.2 10.9 %all-to-all-done.1.recv_ref = bf16[32,112,128]{2,1,0:T(8,128)(2,1)S(1)} async-done(((bf16[32,112,128]{2,1,0:T(8,128)(2,1)}), bf16[32,112,128]{2,1,0:T(8,128)(2,1)S(1)}, u32[]{:S(2)}, u32[]{:S(2)}) %all-to-all-start.1) | async-done | bytes 917536 | tf_op jit(solution)/shard_map/all_to_all | solution.py:257
  66.1 0.0 copy-start.1
  66.1 2.8 %copy-done.1 = bf16[1024,3072]{1,0:T(8,128)(2,1)S(1)} copy-done((bf16[1024,3072]{1,0:T(8,128)(2,1)S(1)}, bf16[1024,3072]{1,0:T(8,128)(2,1)}, u32[]{:S(2)}) %copy-start.1) | copy-done | bytes 6291480
  68.8 0.0 copy-start.7
  68.8 0.0 copy-start.8
  68.8 0.0 copy-start.9
  68.8 2.1 %tail.1 = (f32[16,3072]{1,0:T(8,128)S(1)}, bf16[16,3072]{1,0:T(8,128)(2,1)S(1)}, bf16[256,1024]{1,0:T(8,128)(2,1)}) custom-call(s32[1]{0:T(128)} %bitcast.1.core_ref, bf16[32,112,128]{2,1,0:T(8,128)(2,1)S(1)} %all-to-all-done.1.recv_ref, bf16[1024,3072]{1,0:T(8,128)(2,1)S(1)} %copy-done.1), custom_call_target="tpu_custom_call" | custom-call | tf_op jit(solution)/shard_map/tail/pallas_call | solution.py:259
  71.0 5.2 %collective-permute-start.6 = (bf16[16,3072]{1,0:T(8,128)(2,1)S(1)}, bf16[16,3072]{1,0:T(8,128)(2,1)S(1)}, u32[]{:S(2)}, u32[]{:S(2)}) collective-permute-start(bf16[16,3072]{1,0:T(8,128)(2,1)S(1)} %get-tuple-element.18), channel_id=1, source_target_pairs={{0,1},{1,0},{2,3},{3,2},{4,5},{5,4},{6,7},{7,6},{8,9},{9,8},{10,11... | collective-permute-start | bytes 294920 | tf_op jit(solution)/shard_map/ppermute | solution.py:268
  76.2 0.9 %collective-permute-done.6 = bf16[16,3072]{1,0:T(8,128)(2,1)S(1)} collective-permute-done((bf16[16,3072]{1,0:T(8,128)(2,1)S(1)}, bf16[16,3072]{1,0:T(8,128)(2,1)S(1)}, u32[]{:S(2)}, u32[]{:S(2)}) %collective-permute-start.6) | collective-permute-done | bytes 98336 | tf_op jit(solution)/shard_map/ppermute | solution.py:268
  77.2 0.0 copy-done.7
  77.2 0.0 copy-done.8
  77.2 0.0 copy-done.9
  77.2 0.7 fusion.1
  (1 shorter events, 0.0 us)
Async XLA Ops:
  0.6 29.8 %copy-start = (bf16[1,256,3,1024]{3,1,2,0:T(8,128)(2,1)S(1)}, bf16[1,256,3,1024]{3,1,2,0:T(8,128)(2,1)}, u32[]{:S(2)}) copy-start(bf16[1,256,3,1024]{3,1,2,0:T(8,128)(2,1)} %param.12) | copy-start | bytes 4718596
  0.6 1.0 %copy-start.2 = (bf16[1,32,3,1024]{3,1,2,0:T(8,128)(2,1)S(1)}, bf16[1,32,3,1024]{3,1,2,0:T(8,128)(2,1)}, u32[]{:S(2)}) copy-start(bf16[1,32,3,1024]{3,1,2,0:T(8,128)(2,1)} %param.11) | copy-start | bytes 589828
  1.7 0.7 copy-start.3
  2.4 0.7 copy-start.4
  3.0 0.7 copy-start.5
  3.7 0.7 copy-start.6
  22.4 13.7 %collective-permute-start.2 = (bf16[32,16,128]{2,1,0:T(8,128)(2,1)S(1)}, bf16[32,16,128]{2,1,0:T(8,128)(2,1)S(1)}, u32[]{:S(2)}, u32[]{:S(2)}) collective-permute-start(bf16[32,16,128]{2,1,0:T(8,128)(2,1)S(1)} %slice.4.kv0_ref), channel_id=1, source_target_pairs={{0,192},{64,128},{128,64},{192,0},{1,193},{65,129},{129,65},{193,1... | collective-permute-start | bytes 393224 | tf_op jit(solution)/shard_map/ppermute | solution.py:240
  27.6 10.3 %collective-permute-start.1 = (bf16[32,16,128]{2,1,0:T(8,128)(2,1)S(1)}, bf16[32,16,128]{2,1,0:T(8,128)(2,1)S(1)}, u32[]{:S(2)}, u32[]{:S(2)}) collective-permute-start(bf16[32,16,128]{2,1,0:T(8,128)(2,1)S(1)} %slice.4.kv0_ref), channel_id=1, source_target_pairs={{0,128},{64,192},{128,0},{192,64},{1,129},{65,193},{129,1},{193,65... | collective-permute-start | bytes 393224 | tf_op jit(solution)/shard_map/ppermute | solution.py:240
  28.8 9.3 %collective-permute-start = (bf16[32,16,128]{2,1,0:T(8,128)(2,1)S(1)}, bf16[32,16,128]{2,1,0:T(8,128)(2,1)S(1)}, u32[]{:S(2)}, u32[]{:S(2)}) collective-permute-start(bf16[32,16,128]{2,1,0:T(8,128)(2,1)S(1)} %slice.4.kv0_ref), channel_id=1, source_target_pairs={{0,64},{64,0},{128,192},{192,128},{1,65},{65,1},{129,193},{193,129... | collective-permute-start | bytes 393224 | tf_op jit(solution)/shard_map/ppermute | solution.py:240
  38.9 10.3 %collective-permute-start.3 = (bf16[80,128]{1,0:T(8,128)(2,1)S(1)}, bf16[80,128]{1,0:T(8,128)(2,1)S(1)}, u32[]{:S(2)}, u32[]{:S(2)}) collective-permute-start(bf16[80,128]{1,0:T(8,128)(2,1)S(1)} %get-tuple-element.14), channel_id=1, source_target_pairs={{0,2},{2,0},{4,6},{6,4},{1,3},{3,1},{5,7},{7,5},{8,10},{10,8},{12,... | collective-permute-start | bytes 61448 | tf_op jit(solution)/shard_map/ppermute | solution.py:248
  44.2 5.0 %collective-permute-start.4 = (bf16[80,128]{1,0:T(8,128)(2,1)S(1)}, bf16[80,128]{1,0:T(8,128)(2,1)S(1)}, u32[]{:S(2)}, u32[]{:S(2)}) collective-permute-start(bf16[80,128]{1,0:T(8,128)(2,1)S(1)} %get-tuple-element.15), channel_id=1, source_target_pairs={{0,4},{2,6},{4,0},{6,2},{1,5},{3,7},{5,1},{7,3},{8,12},{10,14},{12... | collective-permute-start | bytes 61448 | tf_op jit(solution)/shard_map/ppermute | solution.py:248
  45.6 3.8 %collective-permute-start.5 = (bf16[80,128]{1,0:T(8,128)(2,1)S(1)}, bf16[80,128]{1,0:T(8,128)(2,1)S(1)}, u32[]{:S(2)}, u32[]{:S(2)}) collective-permute-start(bf16[80,128]{1,0:T(8,128)(2,1)S(1)} %get-tuple-element.16), channel_id=1, source_target_pairs={{0,6},{2,4},{4,2},{6,0},{1,7},{3,5},{5,3},{7,1},{8,14},{10,12},{12... | collective-permute-start | bytes 61448 | tf_op jit(solution)/shard_map/ppermute | solution.py:248
  50.5 15.5 %all-to-all-start.1 = ((bf16[32,112,128]{2,1,0:T(8,128)(2,1)}), bf16[32,112,128]{2,1,0:T(8,128)(2,1)S(1)}, u32[]{:S(2)}, u32[]{:S(2)}) async-start(bf16[32,112,128]{2,1,0:T(8,128)(2,1)} %fill.1), calls=%async_computation.1 | async-start | bytes 1835008 | tf_op jit(solution)/shard_map/all_to_all | solution.py:257
  66.1 2.8 %copy-start.1 = (bf16[1024,3072]{1,0:T(8,128)(2,1)S(1)}, bf16[1024,3072]{1,0:T(8,128)(2,1)}, u32[]{:S(2)}) copy-start(bf16[1024,3072]{1,0:T(8,128)(2,1)} %w_ref.1) | copy-start | bytes 18874372
  68.8 8.3 %copy-start.7 = (bf16[1,16,3072]{2,1,0:T(8,128)(2,1)S(1)}, bf16[1,16,3072]{2,1,0:T(8,128)(2,1)}, u32[]{:S(2)}) copy-start(bf16[1,16,3072]{2,1,0:T(8,128)(2,1)} %param.17) | copy-start | bytes 294916
  68.8 8.3 %copy-start.8 = (f32[3072]{0:T(1024)S(1)}, f32[3072]{0:T(1024)}, u32[]{:S(2)}) copy-start(f32[3072]{0:T(1024)} %param.19) | copy-start | bytes 36868
  68.8 8.3 %copy-start.9 = (f32[3072]{0:T(1024)S(1)}, f32[3072]{0:T(1024)}, u32[]{:S(2)}) copy-start(f32[3072]{0:T(1024)} %param.20) | copy-start | bytes 36868
  71.0 6.2 %collective-permute-start.6 = (bf16[16,3072]{1,0:T(8,128)(2,1)S(1)}, bf16[16,3072]{1,0:T(8,128)(2,1)S(1)}, u32[]{:S(2)}, u32[]{:S(2)}) collective-permute-start(bf16[16,3072]{1,0:T(8,128)(2,1)S(1)} %get-tuple-element.18), channel_id=1, source_target_pairs={{0,1},{1,0},{2,3},{3,2},{4,5},{5,4},{6,7},{7,6},{8,9},{9,8},{10,11... | collective-permute-start | bytes 294920 | tf_op jit(solution)/shard_map/ppermute | solution.py:268

commit v2 on v1

--- a/solution.py
+++ b/solution.py
@@ -12,6 +12,7 @@
 HD = 128
 SEQ = ("zh", "zl", "x", "y")
 CUBE = ("zl", "x", "y")
+HEAD = ("zl", "x")
 rope_base = 256.0
 neg_large = -1e30
 LOG2E = 1.4426950408889634
@@ -27,19 +28,37 @@
     return pl.BlockSpec(memory_space=pltpu.SMEM)
 
 
-def call(body, out_shape, n_in, smem=(), limit=40 * 1024 * 1024, scratch=(), name=None):
+def any_spec():
+    return pl.BlockSpec(memory_space=pltpu.HBM)
+
+
+def call(
+    body, out_shape, n_in, smem=(), hbm=(), limit=40 * 1024 * 1024, scratch=(), name=None, alias=None
+):
     single = not isinstance(out_shape, (tuple, list))
     outs = out_shape if not single else [out_shape]
     specs = [vmem_spec() for _ in outs]
-    return pl.pallas_call(
+    kernel = pl.pallas_call(
         body,
         out_shape=out_shape,
-        in_specs=[smem_spec() if i in smem else vmem_spec() for i in range(n_in)],
+        in_specs=[
+            smem_spec() if i in smem else any_spec() if i in hbm else vmem_spec() for i in range(n_in)
+        ],
         out_specs=specs[0] if single else specs,
         scratch_shapes=list(scratch),
+        input_output_aliases=alias or {},
         compiler_params=pltpu.CompilerParams(vmem_limit_bytes=limit),
         name=name,
     )
+
+    def run(*operands):
+        held = [
+            pltpu.with_memory_space_constraint(v, pltpu.HBM) if i in hbm else v
+            for i, v in enumerate(operands)
+        ]
+        return kernel(*held)
+
+    return run
 
 
 def rate_table():
@@ -55,7 +74,23 @@
     return table
 
 
-def prep_body(qkv_ref, frame_ref, row_ref, col_ref, rate_ref, out_ref):
+def prep_body(
+    qkv_hbm, frame_hbm, row_hbm, col_hbm, rate_hbm, q_out, kv_out,
+    qkv_ref, frame_ref, row_ref, col_ref, rate_ref, sems,
+):
+    copies = [
+        pltpu.make_async_copy(src, dst, sems.at[i])
+        for i, (src, dst) in enumerate(
+            (
+                (frame_hbm, frame_ref), (row_hbm, row_ref), (col_hbm, col_ref),
+                (rate_hbm, rate_ref), (qkv_hbm, qkv_ref),
+            )
+        )
+    ]
+    for c in copies:
+        c.start()
+    for c in copies[:4]:
+        c.wait()
     tokens = qkv_ref.shape[1]
     sub = lax.broadcasted_iota(jnp.int32, (8, tokens), 0)
     pos = jnp.where(
@@ -70,22 +105,20 @@
     cosine = jnp.cos(angles)
     sine = jnp.sin(angles)
     sine = jnp.where(even, -sine, sine)
+    copies[4].wait()
 
     def rotate(v):
         v = v.astype(f32)
         partner = jnp.where(even, pltpu.roll(v, HD - 1, 1), pltpu.roll(v, 1, 1))
-        return v * cosine + partner * sine
+        return (v * cosine + partner * sine).astype(bf16)
 
     for head in range(8):
         cols = slice(head * HD, (head + 1) * HD)
-        query = rotate(qkv_ref[0, :, cols]).astype(bf16)
-        key = rotate(qkv_ref[1, :, cols])
-        value = qkv_ref[2, :, cols].astype(f32)
+        kv_out[head, 0:32, :] = rotate(qkv_ref[1, :, cols])
+        kv_out[head, 32:64, :] = qkv_ref[2, :, cols]
+        query = rotate(qkv_ref[0, :, cols])
         for j in range(4):
-            d = head * 4 + j
-            out_ref[d, 0:32, :] = query
-            pair = jnp.concatenate([key[8 * j : 8 * j + 8], value[8 * j : 8 * j + 8]], axis=0)
-            out_ref[d, 32:48, :] = pair.astype(bf16)
+            q_out[head * 4 + j] = query
 
 
 def softmax_block(q, keys, values, live):
@@ -125,9 +158,8 @@
     j = where_ref[0]
     length = len_ref[0]
     for b, ref in enumerate((kv0_ref, kv1_ref, kv2_ref, kv3_ref)):
-        pair = ref[...].astype(f32)
-        keys_ref[256 * b : 256 * b + 256, :] = pair[:, 0:8, :].reshape(256, HD).astype(bf16)
-        values_ref[256 * b : 256 * b + 256, :] = pair[:, 8:16, :].reshape(256, HD).astype(bf16)
+        keys_ref[256 * b : 256 * b + 256, :] = ref[:, 0:32, :].reshape(256, HD)
+        values_ref[256 * b : 256 * b + 256, :] = ref[:, 32:64, :].reshape(256, HD)
     start = pl.multiple_of((j // 2) * 128, 128)
     keys_ref[1024:1152, :] = txt_ref[1, pl.ds(start, 128), :]
     values_ref[1024:1152, :] = txt_ref[2, pl.ds(start, 128), :]
@@ -158,14 +190,14 @@
     row = lax.broadcasted_iota(jnp.int32, (8, 32, 128), 1)
     lane = lax.broadcasted_iota(jnp.int32, (8, 32, 128), 2)
     for b in range(4):
-        q = recv_ref[8 * b : 8 * b + 8, 0:32, :].reshape(256, HD)
+        q = recv_ref[8 * b : 8 * b + 8].reshape(256, HD)
         out, lse = softmax_block(q, keys, values, live)
         out_ref[8 * b : 8 * b + 8, 0:32, :] = out.astype(bf16).reshape(8, 32, HD)
         high, mid, low = three_parts(jnp.broadcast_to(lse, (256, 128)).reshape(8, 32, 128))
         parts = jnp.where(lane < 32, high, jnp.where(lane < 64, mid, low))
         packed = jnp.where(jnp.logical_and(row == lane % 32, lane < 96), parts, 0.0)
         packed = jnp.sum(packed, axis=1, keepdims=True)
-        out_ref[8 * b : 8 * b + 8, 32:48, :] = jnp.broadcast_to(packed, (8, 16, 128)).astype(bf16)
+        out_ref[8 * b : 8 * b + 8, 32:40, :] = jnp.broadcast_to(packed, (8, 8, 128)).astype(bf16)
 
 
 def blend(outs, lses):
@@ -194,11 +226,20 @@
     text = blend(outs, lses)
     text = jnp.where(where_ref[0] * 64 + row < len_ref[0], text, 0.0).astype(bf16)
     for d in range(32):
-        out_ref[d, 0:48, :] = img_ref[d]
-        out_ref[d, 48:112, :] = text
-
-
-def tail_body(core_ref, recv_ref, w_ref, mine_ref, other_ref, txt_ref):
+        out_ref[d, 0:32, :] = img_ref[d, 0:32]
+        out_ref[d, 32:96, :] = text
+        out_ref[d, 96:104, :] = img_ref[d, 32:40]
+
+
+def tail_body(core_ref, recv_ref, w_hbm, mine_ref, other_ref, txt_ref, w_ref, sems):
+    fetches = [
+        pltpu.make_async_copy(
+            w_hbm.at[pl.ds(256 * i, 256)], w_ref.at[pl.ds(256 * i, 256)], sems.at[i]
+        )
+        for i in range(4)
+    ]
+    for c in fetches:
+        c.start()
     row = lax.broadcasted_iota(jnp.int32, (32, 128), 0)
     lane = lax.broadcasted_iota(jnp.int32, (32, 128), 1)
     pick = jnp.logical_and(row == lane % 32, lane < 96)
@@ -208,14 +249,21 @@
         for j in range(4):
             s = head * 4 + j
             outs.append(recv_ref[s, 0:32, :].astype(f32))
-            stats = recv_ref[s, 32:48, :].astype(f32)[0:1]
+            stats = recv_ref[s, 96:104, :].astype(f32)[0:1]
             lses.append(jnp.sum(jnp.where(pick, stats, 0.0), axis=1, keepdims=True))
-            txt_ref[64 * j : 64 * j + 64, head * HD : (head + 1) * HD] = recv_ref[s, 48:112, :]
+            txt_ref[64 * j : 64 * j + 64, head * HD : (head + 1) * HD] = recv_ref[s, 32:96, :]
         heads.append(blend(outs, lses))
     rows = jnp.concatenate(heads, axis=1)
     flipped = jnp.concatenate([rows[16:32], rows[0:16]], axis=0)
     rows = jnp.where(core_ref[0] == 0, rows, flipped).astype(bf16)
-    projected = jnp.dot(rows, w_ref[...], preferred_element_type=f32)
+    projected = None
+    for i in range(4):
+        fetches[i].wait()
+        part = jnp.dot(
+            rows[:, 256 * i : 256 * i + 256], w_ref[256 * i : 256 * i + 256, :],
+            preferred_element_type=f32,
+        )
+        projected = part if projected is None else projected + part
     mine_ref[...] = projected[0:16]
     other_ref[...] = projected[16:32].astype(bf16)
 
@@ -232,12 +280,23 @@
     qkv = img_qkv.reshape(tokens, 3, width).transpose(1, 0, 2)
     txt = lax.dynamic_slice_in_dim(txt_qkv[0], head * HD, HD, 2).transpose(1, 0, 2)
 
-    send = call(prep_body, jax.ShapeDtypeStruct((32, 48, HD), bf16), 5, name="prep")(
-        qkv, frame_index, row_index, column_index, jnp.asarray(rate_table())
-    )
-    recv = lax.all_to_all(send, CUBE, 0, 0, tiled=True)
-    kv = recv[:, 32:48, :]
+    q_send, kv_send = call(
+        prep_body,
+        [jax.ShapeDtypeStruct((32, 32, HD), bf16), jax.ShapeDtypeStruct((8, 64, HD), bf16)],
+        5, hbm=(0, 1, 2, 3, 4), name="prep",
+        scratch=(
+            pltpu.VMEM((3, tokens, width), bf16),
+            pltpu.VMEM((1, tokens), jnp.int32),
+            pltpu.VMEM((1, tokens), jnp.int32),
+            pltpu.VMEM((1, tokens), jnp.int32),
+            pltpu.VMEM((8, HD), f32),
+            pltpu.SemaphoreType.DMA((5,)),
+        ),
+    )(qkv, frame_index, row_index, column_index, jnp.asarray(rate_table()))
+    kv = lax.all_to_all(kv_send, HEAD, 0, 0, tiled=True)
     others = [lax.ppermute(kv, "zh", [(i, i ^ s) for i in range(4)]) for s in (1, 2, 3)]
+    q_send, _ = lax.optimization_barrier((q_send, kv))
+    recv = lax.all_to_all(q_send, CUBE, 0, 0, tiled=True)
 
     piece = jax.ShapeDtypeStruct((80, HD), bf16)
     keyed = jax.ShapeDtypeStruct((1152, HD), bf16)
@@ -248,12 +307,12 @@
         lax.ppermute(p, "y", [(i, i ^ s) for i in range(4)])
         for s, p in ((1, p1), (2, p2), (3, p3))
     ]
-    img = call(image_body, jax.ShapeDtypeStruct((32, 48, HD), bf16), 5, smem=(0, 1), name="image")(
-        j, txt_len, recv, keys, values
-    )
-    back = call(fill_body, jax.ShapeDtypeStruct((32, 112, HD), bf16), 7, smem=(0, 1), name="fill")(
-        j, txt_len, img, p0, *got
-    )
+    img = call(
+        image_body, jax.ShapeDtypeStruct((32, 40, HD), bf16), 5, smem=(0, 1), name="image"
+    )(j, txt_len, recv, keys, values)
+    back = call(
+        fill_body, jax.ShapeDtypeStruct((32, 104, HD), bf16), 7, smem=(0, 1), name="fill"
+    )(j, txt_len, img, p0, *got)
     home = lax.all_to_all(back, CUBE, 0, 0, tiled=True)
     half = tokens // 2
     mine, other, txt_out = call(
@@ -263,7 +322,8 @@
             jax.ShapeDtypeStruct((half, d_model), bf16),
             jax.ShapeDtypeStruct((256, width), bf16),
         ],
-        3, smem=(0,), name="tail",
+        3, smem=(0,), hbm=(2,), name="tail",
+        scratch=(pltpu.VMEM(w_proj.shape, bf16), pltpu.SemaphoreType.DMA((4,))),
     )(core, home, w_proj)
     theirs = lax.ppermute(other, "tp", [(0, 1), (1, 0)])
     projected = mine + theirs.astype(f32)

time: 78.2 us -> 75.2 us (0.962)
  starting transfers between devices: 25 us -> 33.4 us
  local copies, waits for them, and re-layouts: 6.56 us -> 0.08 us
  blocking collectives: 17.7 us -> 11.4 us
  Pallas kernels: 6.93 us -> 10.1 us
  waiting for transfers between devices: 19.6 us -> 17.8 us
    unnamed x20 -> x8, local copies, waits for them, and re-layouts: 6.49 us -> 0.02 us
    all_to_all x1, starting transfers between devices: 4.62 us -> 11.1 us  [shards(): home = lax.all_to_all(back, CUBE, 0, 0, tiled=True)]
    all_to_all x1, blocking collectives: 17.7 us -> 11.4 us  [shards(): kv = lax.all_to_all(kv_send, HEAD, 0, 0, tiled=True)]
    all_to_all x0 -> x1, starting transfers between devices: none -> 5.58 us  [shards(): recv = lax.all_to_all(q_send, CUBE, 0, 0, tiled=True)]
    ppermute x3, starting transfers between devices: 7.75 us -> 4.24 us  [shards(): lax.ppermute(p, 'y', [(i, i ^ s) for i in range(4)])]
    pallas_call x5, Pallas kernels: 6.93 us -> 10.1 us  [run(): return kernel(*held)]
    ppermute x3, waiting for transfers between devices: 7.54 us -> 5.16 us  [shards(): lax.ppermute(kv, 'zh', [(i, i ^ s) for i in range(4)])]
    ppermute x3, waiting for transfers between devices: 0.23 us -> 1.26 us  [shards(): lax.ppermute(p, 'y', [(i, i ^ s) for i in range(4)])]
  transfers between devices with their start and end apart: 8 -> 9, of which waited for: 6 -> 5; matrix products, arithmetic and copies ran while one was open for 0% -> 0% of each run, Pallas kernels for 3% -> 4%
where the time goes in v2:
time: 75.2 us; the launch traced here: 74.9 us
  starting transfers between devices  33.4 us (44%)
  waiting for transfers between devices  17.8 us (24%)
  blocking collectives  11.4 us (15%)
  Pallas kernels  10.1 us (13%)
  between operations  1.38 us (2%)
    all_to_all x1, blocking collectives, shards(): kv = lax.all_to_all(kv_send, HEAD, 0, 0, tiled=True)  11.4 us
    all_to_all x1, starting transfers between devices, shards(): home = lax.all_to_all(back, CUBE, 0, 0, tiled=True)  11.1 us
    all_to_all x1, waiting for transfers between devices, shards(): home = lax.all_to_all(back, CUBE, 0, 0, tiled=True)  10.5 us
    pallas_call x5, Pallas kernels, run(): return kernel(*held)  10.1 us
    ppermute x3, starting transfers between devices, shards(): lax.ppermute(kv, 'zh', [(i, i ^ s) for i in range(4)])  7.39 us
    all_to_all x1, starting transfers between devices, shards(): recv = lax.all_to_all(q_send, CUBE, 0, 0, tiled=True)  5.58 us
    ppermute x3, waiting for transfers between devices, shards(): lax.ppermute(kv, 'zh', [(i, i ^ s) for i in range(4)])  5.16 us
    ppermute x1, starting transfers between devices, shards(): theirs = lax.ppermute(other, 'tp', [(0, 1), (1, 0)])  5.14 us
  transfers between devices with their start and end apart: 9, of which 5 were waited for; matrix products, arithmetic and copies ran while one was open for 0% of the time, Pallas kernels for 4%

profile of v2, /device:TPU:1, one launch (start us, length us, event | category | flops | bytes accessed | tf_op | source)
XLA Modules:
  0.0 74.9 jit_solution(7454106795630166199)
XLA Ops:
  0.6 0.0 copy-start
  0.6 2.0 %prep.1 = (bf16[32,32,128]{2,1,0:T(8,128)(2,1)}, bf16[8,64,128]{2,1,0:T(8,128)(2,1)S(1)}) custom-call(bf16[3,32,1024]{2,1,0:T(8,128)(2,1)} %bitcast.15, s32[1,32]{1,0:T(1,128)} %frame_hbm.1, s32[1,32]{1,0:T(1,128)} %row_hbm.1, s32[1,32]{1,0:T(1,128)} %col_hbm.1, f32[8,128]{1,0:T(8,128)} %constant.26.clone.rate_hbm), custom_call_target="tpu_custom_call" | custom-call | tf_op jit(solution)/shard_map/prep/pallas_call | solution.py:59
  2.7 11.4 %all_to_all.15.kv0_ref = bf16[8,64,128]{2,1,0:T(8,128)(2,1)S(1)} all-to-all(bf16[8,64,128]{2,1,0:T(8,128)(2,1)S(1)} %get-tuple-element.15), channel_id=1, replica_groups=mesh['zh'=4,'zl'=2,'x'=4,'y'=4,'tp'=2] {'zl','x'}, dimensions={0} | all-to-all | bytes 262144 | tf_op jit(solution)/shard_map/all_to_all | solution.py:296
  14.1 5.6 %all-to-all-start.1 = ((bf16[32,32,128]{2,1,0:T(8,128)(2,1)}), bf16[32,32,128]{2,1,0:T(8,128)(2,1)S(1)}, u32[]{:S(2)}, u32[]{:S(2)}) async-start(bf16[32,32,128]{2,1,0:T(8,128)(2,1)} %get-tuple-element.16), calls=%async_computation.1 | async-start | bytes 524288 | tf_op jit(solution)/shard_map/all_to_all | solution.py:299
  19.7 5.2 %collective-permute-start.2 = (bf16[8,64,128]{2,1,0:T(8,128)(2,1)S(1)}, bf16[8,64,128]{2,1,0:T(8,128)(2,1)S(1)}, u32[]{:S(2)}, u32[]{:S(2)}) collective-permute-start(bf16[8,64,128]{2,1,0:T(8,128)(2,1)S(1)} %all_to_all.15.kv0_ref), channel_id=1, source_target_pairs={{0,192},{64,128},{128,64},{192,0},{1,193},{65,129},{129,65},{193,1... | collective-permute-start | bytes 393224 | tf_op jit(solution)/shard_map/ppermute | solution.py:297
  24.9 1.2 %collective-permute-start.1 = (bf16[8,64,128]{2,1,0:T(8,128)(2,1)S(1)}, bf16[8,64,128]{2,1,0:T(8,128)(2,1)S(1)}, u32[]{:S(2)}, u32[]{:S(2)}) collective-permute-start(bf16[8,64,128]{2,1,0:T(8,128)(2,1)S(1)} %all_to_all.15.kv0_ref), channel_id=1, source_target_pairs={{0,128},{64,192},{128,0},{192,64},{1,129},{65,193},{129,1},{193,65... | collective-permute-start | bytes 393224 | tf_op jit(solution)/shard_map/ppermute | solution.py:297
  26.1 1.0 %collective-permute-start = (bf16[8,64,128]{2,1,0:T(8,128)(2,1)S(1)}, bf16[8,64,128]{2,1,0:T(8,128)(2,1)S(1)}, u32[]{:S(2)}, u32[]{:S(2)}) collective-permute-start(bf16[8,64,128]{2,1,0:T(8,128)(2,1)S(1)} %all_to_all.15.kv0_ref), channel_id=1, source_target_pairs={{0,64},{64,0},{128,192},{192,128},{1,65},{65,1},{129,193},{193,129... | collective-permute-start | bytes 393224 | tf_op jit(solution)/shard_map/ppermute | solution.py:297
  27.8 0.0 copy-done
  27.8 0.1 dynamic-slice_bitcast_fusion.txt_ref
  27.8 1.9 %collective-permute-done.2.kv3_ref = bf16[8,64,128]{2,1,0:T(8,128)(2,1)S(1)} collective-permute-done((bf16[8,64,128]{2,1,0:T(8,128)(2,1)S(1)}, bf16[8,64,128]{2,1,0:T(8,128)(2,1)S(1)}, u32[]{:S(2)}, u32[]{:S(2)}) %collective-permute-start.2) | collective-permute-done | bytes 131104 | tf_op jit(solution)/shard_map/ppermute | solution.py:297
  29.8 3.2 %collective-permute-done.1.kv2_ref = bf16[8,64,128]{2,1,0:T(8,128)(2,1)S(1)} collective-permute-done((bf16[8,64,128]{2,1,0:T(8,128)(2,1)S(1)}, bf16[8,64,128]{2,1,0:T(8,128)(2,1)S(1)}, u32[]{:S(2)}, u32[]{:S(2)}) %collective-permute-start.1) | collective-permute-done | bytes 131104 | tf_op jit(solution)/shard_map/ppermute | solution.py:297
  33.0 0.0 collective-permute-done.kv1_ref
  33.0 0.8 %text.1 = (bf16[80,128]{1,0:T(8,128)(2,1)S(1)}, bf16[80,128]{1,0:T(8,128)(2,1)S(1)}, bf16[80,128]{1,0:T(8,128)(2,1)S(1)}, bf16[80,128]{1,0:T(8,128)(2,1)S(1)}, b...) custom-call(s32[1]{0:T(128)} %bitcast.2.where_ref, s32[1]{0:T(128)S(6)} %copy.13.len_ref, ...), custom_call_target="tpu_custom_call" | custom-call | tf_op jit(solution)/shard_map/text/pallas_call | solution.py:59
  33.8 1.7 %collective-permute-start.3 = (bf16[80,128]{1,0:T(8,128)(2,1)S(1)}, bf16[80,128]{1,0:T(8,128)(2,1)S(1)}, u32[]{:S(2)}, u32[]{:S(2)}) collective-permute-start(bf16[80,128]{1,0:T(8,128)(2,1)S(1)} %get-tuple-element.20), channel_id=1, source_target_pairs={{0,2},{2,0},{4,6},{6,4},{1,3},{3,1},{5,7},{7,5},{8,10},{10,8},{12,... | collective-permute-start | bytes 61448 | tf_op jit(solution)/shard_map/ppermute | solution.py:307
  35.6 2.4 %collective-permute-start.4 = (bf16[80,128]{1,0:T(8,128)(2,1)S(1)}, bf16[80,128]{1,0:T(8,128)(2,1)S(1)}, u32[]{:S(2)}, u32[]{:S(2)}) collective-permute-start(bf16[80,128]{1,0:T(8,128)(2,1)S(1)} %get-tuple-element.21), channel_id=1, source_target_pairs={{0,4},{2,6},{4,0},{6,2},{1,5},{3,7},{5,1},{7,3},{8,12},{10,14},{12... | collective-permute-start | bytes 61448 | tf_op jit(solution)/shard_map/ppermute | solution.py:307
  38.0 0.1 collective-permute-start.5
  38.1 0.0 all-to-all-done.1.recv_ref
  38.1 2.5 %image.1.img_ref = bf16[32,40,128]{2,1,0:T(8,128)(2,1)S(1)} custom-call(s32[1]{0:T(128)} %bitcast.2.where_ref, s32[1]{0:T(128)S(6)} %copy.13.len_ref, bf16[32,32,128]{2,1,0:T(8,128)(2,1)S(1)} %all-to-all-done.1.recv_ref, bf16[1152,128]{1,0:T(8,128)(2,1)S(1)} %get-tuple-element.17.keys_ref, bf16[1152,128]{1,0:T(8,128)(2,1)S(1)} %get-tuple-element.18.values_ref), custom_call_target="tpu_custom_call" | custom-call | tf_op jit(solution)/shard_map/image/pallas_call | solution.py:59
  40.5 0.0 collective-permute-done.3.p1_ref
  40.6 0.0 collective-permute-done.4.p2_ref
  40.6 1.3 %collective-permute-done.5.p3_ref = bf16[80,128]{1,0:T(8,128)(2,1)S(1)} collective-permute-done((bf16[80,128]{1,0:T(8,128)(2,1)S(1)}, bf16[80,128]{1,0:T(8,128)(2,1)S(1)}, u32[]{:S(2)}, u32[]{:S(2)}) %collective-permute-start.5) | collective-permute-done | bytes 20512 | tf_op jit(solution)/shard_map/ppermute | solution.py:307
  41.8 1.1 %fill.1 = bf16[32,104,128]{2,1,0:T(8,128)(2,1)} custom-call(s32[1]{0:T(128)} %bitcast.2.where_ref, s32[1]{0:T(128)S(6)} %copy.13.len_ref, bf16[32,40,128]{2,1,0:T(8,128)(2,1)S(1)} %image.1.img_ref, bf16[80,128]{1,0:T(8,128)(2,1)S(1)} %get-tuple-element.19.p0_ref, bf16[80,128]{1,0:T(8,128)(2,1)S(1)} %collective-permute-done.3.p1_ref, ...), custom_call_target="tpu_custom_call" | custom-call | tf_op jit(solution)/shard_map/fill/pallas_call | solution.py:59
  42.9 11.1 %all-to-all-start.2 = ((bf16[32,104,128]{2,1,0:T(8,128)(2,1)}), bf16[32,104,128]{2,1,0:T(8,128)(2,1)S(1)}, u32[]{:S(2)}, u32[]{:S(2)}) async-start(bf16[32,104,128]{2,1,0:T(8,128)(2,1)} %fill.1), calls=%async_computation.2 | async-start | bytes 1703936 | tf_op jit(solution)/shard_map/all_to_all | solution.py:316
  54.0 10.5 %all-to-all-done.2.recv_ref = bf16[32,104,128]{2,1,0:T(8,128)(2,1)S(1)} async-done(((bf16[32,104,128]{2,1,0:T(8,128)(2,1)}), bf16[32,104,128]{2,1,0:T(8,128)(2,1)S(1)}, u32[]{:S(2)}, u32[]{:S(2)}) %all-to-all-start.2) | async-done | bytes 852000 | tf_op jit(solution)/shard_map/all_to_all | solution.py:316
  64.4 0.0 copy-start.1
  64.4 0.0 copy-start.2
  64.4 0.0 copy-start.3
  64.4 3.7 %tail.1 = (f32[16,3072]{1,0:T(8,128)S(1)}, bf16[16,3072]{1,0:T(8,128)(2,1)S(1)}, bf16[256,1024]{1,0:T(8,128)(2,1)}) custom-call(s32[1]{0:T(128)} %bitcast.1.core_ref, bf16[32,104,128]{2,1,0:T(8,128)(2,1)S(1)} %all-to-all-done.2.recv_ref, bf16[1024,3072]{1,0:T(8,128)(2,1)} %w_hbm.1), custom_call_target="tpu_custom_call" | custom-call | tf_op jit(solution)/shard_map/tail/pallas_call | solution.py:59
  68.1 5.1 %collective-permute-start.6 = (bf16[16,3072]{1,0:T(8,128)(2,1)S(1)}, bf16[16,3072]{1,0:T(8,128)(2,1)S(1)}, u32[]{:S(2)}, u32[]{:S(2)}) collective-permute-start(bf16[16,3072]{1,0:T(8,128)(2,1)S(1)} %get-tuple-element.24), channel_id=1, source_target_pairs={{0,1},{1,0},{2,3},{3,2},{4,5},{5,4},{6,7},{7,6},{8,9},{9,8},{10,11... | collective-permute-start | bytes 294920 | tf_op jit(solution)/shard_map/ppermute | solution.py:328
  73.3 0.9 %collective-permute-done.6 = bf16[16,3072]{1,0:T(8,128)(2,1)S(1)} collective-permute-done((bf16[16,3072]{1,0:T(8,128)(2,1)S(1)}, bf16[16,3072]{1,0:T(8,128)(2,1)S(1)}, u32[]{:S(2)}, u32[]{:S(2)}) %collective-permute-start.6) | collective-permute-done | bytes 98336 | tf_op jit(solution)/shard_map/ppermute | solution.py:328
  74.2 0.0 copy-done.1
  74.2 0.0 copy-done.2
  74.2 0.0 copy-done.3
  74.2 0.7 fusion.1
Async XLA Ops:
  0.6 27.1 %copy-start = (bf16[1,256,3,1024]{3,1,2,0:T(8,128)(2,1)S(1)}, bf16[1,256,3,1024]{3,1,2,0:T(8,128)(2,1)}, u32[]{:S(2)}) copy-start(bf16[1,256,3,1024]{3,1,2,0:T(8,128)(2,1)} %param.12) | copy-start | bytes 4718596
  14.1 23.9 %all-to-all-start.1 = ((bf16[32,32,128]{2,1,0:T(8,128)(2,1)}), bf16[32,32,128]{2,1,0:T(8,128)(2,1)S(1)}, u32[]{:S(2)}, u32[]{:S(2)}) async-start(bf16[32,32,128]{2,1,0:T(8,128)(2,1)} %get-tuple-element.16), calls=%async_computation.1 | async-start | bytes 524288 | tf_op jit(solution)/shard_map/all_to_all | solution.py:299
  19.7 10.0 %collective-permute-start.2 = (bf16[8,64,128]{2,1,0:T(8,128)(2,1)S(1)}, bf16[8,64,128]{2,1,0:T(8,128)(2,1)S(1)}, u32[]{:S(2)}, u32[]{:S(2)}) collective-permute-start(bf16[8,64,128]{2,1,0:T(8,128)(2,1)S(1)} %all_to_all.15.kv0_ref), channel_id=1, source_target_pairs={{0,192},{64,128},{128,64},{192,0},{1,193},{65,129},{129,65},{193,1... | collective-permute-start | bytes 393224 | tf_op jit(solution)/shard_map/ppermute | solution.py:297
  24.9 8.1 %collective-permute-start.1 = (bf16[8,64,128]{2,1,0:T(8,128)(2,1)S(1)}, bf16[8,64,128]{2,1,0:T(8,128)(2,1)S(1)}, u32[]{:S(2)}, u32[]{:S(2)}) collective-permute-start(bf16[8,64,128]{2,1,0:T(8,128)(2,1)S(1)} %all_to_all.15.kv0_ref), channel_id=1, source_target_pairs={{0,128},{64,192},{128,0},{192,64},{1,129},{65,193},{129,1},{193,65... | collective-permute-start | bytes 393224 | tf_op jit(solution)/shard_map/ppermute | solution.py:297
  26.1 6.9 %collective-permute-start = (bf16[8,64,128]{2,1,0:T(8,128)(2,1)S(1)}, bf16[8,64,128]{2,1,0:T(8,128)(2,1)S(1)}, u32[]{:S(2)}, u32[]{:S(2)}) collective-permute-start(bf16[8,64,128]{2,1,0:T(8,128)(2,1)S(1)} %all_to_all.15.kv0_ref), channel_id=1, source_target_pairs={{0,64},{64,0},{128,192},{192,128},{1,65},{65,1},{129,193},{193,129... | collective-permute-start | bytes 393224 | tf_op jit(solution)/shard_map/ppermute | solution.py:297
  33.8 6.7 %collective-permute-start.3 = (bf16[80,128]{1,0:T(8,128)(2,1)S(1)}, bf16[80,128]{1,0:T(8,128)(2,1)S(1)}, u32[]{:S(2)}, u32[]{:S(2)}) collective-permute-start(bf16[80,128]{1,0:T(8,128)(2,1)S(1)} %get-tuple-element.20), channel_id=1, source_target_pairs={{0,2},{2,0},{4,6},{6,4},{1,3},{3,1},{5,7},{7,5},{8,10},{10,8},{12,... | collective-permute-start | bytes 61448 | tf_op jit(solution)/shard_map/ppermute | solution.py:307
  35.6 5.0 %collective-permute-start.4 = (bf16[80,128]{1,0:T(8,128)(2,1)S(1)}, bf16[80,128]{1,0:T(8,128)(2,1)S(1)}, u32[]{:S(2)}, u32[]{:S(2)}) collective-permute-start(bf16[80,128]{1,0:T(8,128)(2,1)S(1)} %get-tuple-element.21), channel_id=1, source_target_pairs={{0,4},{2,6},{4,0},{6,2},{1,5},{3,7},{5,1},{7,3},{8,12},{10,14},{12... | collective-permute-start | bytes 61448 | tf_op jit(solution)/shard_map/ppermute | solution.py:307
  38.0 3.8 %collective-permute-start.5 = (bf16[80,128]{1,0:T(8,128)(2,1)S(1)}, bf16[80,128]{1,0:T(8,128)(2,1)S(1)}, u32[]{:S(2)}, u32[]{:S(2)}) collective-permute-start(bf16[80,128]{1,0:T(8,128)(2,1)S(1)} %get-tuple-element.22), channel_id=1, source_target_pairs={{0,6},{2,4},{4,2},{6,0},{1,7},{3,5},{5,3},{7,1},{8,14},{10,12},{12... | collective-permute-start | bytes 61448 | tf_op jit(solution)/shard_map/ppermute | solution.py:307
  42.9 21.6 %all-to-all-start.2 = ((bf16[32,104,128]{2,1,0:T(8,128)(2,1)}), bf16[32,104,128]{2,1,0:T(8,128)(2,1)S(1)}, u32[]{:S(2)}, u32[]{:S(2)}) async-start(bf16[32,104,128]{2,1,0:T(8,128)(2,1)} %fill.1), calls=%async_computation.2 | async-start | bytes 1703936 | tf_op jit(solution)/shard_map/all_to_all | solution.py:316
  64.4 9.8 %copy-start.1 = (bf16[1,16,3072]{2,1,0:T(8,128)(2,1)S(1)}, bf16[1,16,3072]{2,1,0:T(8,128)(2,1)}, u32[]{:S(2)}) copy-start(bf16[1,16,3072]{2,1,0:T(8,128)(2,1)} %param.17) | copy-start | bytes 294916
  64.4 9.8 %copy-start.2 = (f32[3072]{0:T(1024)S(1)}, f32[3072]{0:T(1024)}, u32[]{:S(2)}) copy-start(f32[3072]{0:T(1024)} %param.19) | copy-start | bytes 36868
  64.4 9.8 %copy-start.3 = (f32[3072]{0:T(1024)S(1)}, f32[3072]{0:T(1024)}, u32[]{:S(2)}) copy-start(f32[3072]{0:T(1024)} %param.20) | copy-start | bytes 36868
  68.1 6.1 %collective-permute-start.6 = (bf16[16,3072]{1,0:T(8,128)(2,1)S(1)}, bf16[16,3072]{1,0:T(8,128)(2,1)S(1)}, u32[]{:S(2)}, u32[]{:S(2)}) collective-permute-start(bf16[16,3072]{1,0:T(8,128)(2,1)S(1)} %get-tuple-element.24), channel_id=1, source_target_pairs={{0,1},{1,0},{2,3},{3,2},{4,5},{5,4},{6,7},{7,6},{8,9},{9,8},{10,11... | collective-permute-start | bytes 294920 | tf_op jit(solution)/shard_map/ppermute | solution.py:328

commit v3 on v2

--- a/solution.py
+++ b/solution.py
@@ -8,6 +8,7 @@
 from jax.experimental.pallas import tpu as pltpu
 from jax.sharding import Mesh
 from jax.sharding import PartitionSpec as P
+
 
 HD = 128
 SEQ = ("zh", "zl", "x", "y")
@@ -33,7 +34,7 @@
 
 
 def call(
-    body, out_shape, n_in, smem=(), hbm=(), limit=40 * 1024 * 1024, scratch=(), name=None, alias=None
+    body, out_shape, n_in, smem=(), hbm=(), near=(), limit=40 * 1024 * 1024, scratch=(), alias=None
 ):
     single = not isinstance(out_shape, (tuple, list))
     outs = out_shape if not single else [out_shape]
@@ -48,12 +49,13 @@
         scratch_shapes=list(scratch),
         input_output_aliases=alias or {},
         compiler_params=pltpu.CompilerParams(vmem_limit_bytes=limit),
-        name=name,
     )
 
     def run(*operands):
         held = [
-            pltpu.with_memory_space_constraint(v, pltpu.HBM) if i in hbm else v
+            pltpu.with_memory_space_constraint(v, pltpu.HBM if i in hbm else pltpu.VMEM)
+            if i in hbm or i in near
+            else v
             for i, v in enumerate(operands)
         ]
         return kernel(*held)
@@ -183,7 +185,11 @@
         ref[64:80, :] = jnp.concatenate([first, second], axis=0).astype(bf16)
 
 
-def image_body(where_ref, len_ref, recv_ref, keys_ref, values_ref, out_ref):
+def image_body(
+    where_ref, len_ref, recv_ref, keys_ref, values_ref, w_hbm, out_ref, w_out, sem
+):
+    fetch = pltpu.make_async_copy(w_hbm, w_out, sem)
+    fetch.start()
     live = live_mask(where_ref[0], len_ref[0])
     keys = keys_ref[...]
     values = values_ref[...]
@@ -198,6 +204,7 @@
         packed = jnp.where(jnp.logical_and(row == lane % 32, lane < 96), parts, 0.0)
         packed = jnp.sum(packed, axis=1, keepdims=True)
         out_ref[8 * b : 8 * b + 8, 32:40, :] = jnp.broadcast_to(packed, (8, 8, 128)).astype(bf16)
+    fetch.wait()
 
 
 def blend(outs, lses):
@@ -231,15 +238,7 @@
         out_ref[d, 96:104, :] = img_ref[d, 32:40]
 
 
-def tail_body(core_ref, recv_ref, w_hbm, mine_ref, other_ref, txt_ref, w_ref, sems):
-    fetches = [
-        pltpu.make_async_copy(
-            w_hbm.at[pl.ds(256 * i, 256)], w_ref.at[pl.ds(256 * i, 256)], sems.at[i]
-        )
-        for i in range(4)
-    ]
-    for c in fetches:
-        c.start()
+def tail_body(core_ref, recv_ref, w_ref, mine_ref, other_ref, txt_ref):
     row = lax.broadcasted_iota(jnp.int32, (32, 128), 0)
     lane = lax.broadcasted_iota(jnp.int32, (32, 128), 1)
     pick = jnp.logical_and(row == lane % 32, lane < 96)
@@ -256,14 +255,7 @@
     rows = jnp.concatenate(heads, axis=1)
     flipped = jnp.concatenate([rows[16:32], rows[0:16]], axis=0)
     rows = jnp.where(core_ref[0] == 0, rows, flipped).astype(bf16)
-    projected = None
-    for i in range(4):
-        fetches[i].wait()
-        part = jnp.dot(
-            rows[:, 256 * i : 256 * i + 256], w_ref[256 * i : 256 * i + 256, :],
-            preferred_element_type=f32,
-        )
-        projected = part if projected is None else projected + part
+    projected = jnp.dot(rows, w_ref[...], preferred_element_type=f32)
     mine_ref[...] = projected[0:16]
     other_ref[...] = projected[16:32].astype(bf16)
 
@@ -277,13 +269,14 @@
     j = lax.axis_index("y").astype(jnp.int32).reshape(1)
     head = lax.axis_index("zl") * 4 + lax.axis_index("x")
     core = lax.axis_index("tp").astype(jnp.int32).reshape(1)
+    j, core, frame_index = lax.optimization_barrier((j, core, frame_index))
     qkv = img_qkv.reshape(tokens, 3, width).transpose(1, 0, 2)
     txt = lax.dynamic_slice_in_dim(txt_qkv[0], head * HD, HD, 2).transpose(1, 0, 2)
 
     q_send, kv_send = call(
         prep_body,
         [jax.ShapeDtypeStruct((32, 32, HD), bf16), jax.ShapeDtypeStruct((8, 64, HD), bf16)],
-        5, hbm=(0, 1, 2, 3, 4), name="prep",
+        5, hbm=(0, 1, 2, 3, 4),
         scratch=(
             pltpu.VMEM((3, tokens, width), bf16),
             pltpu.VMEM((1, tokens), jnp.int32),
@@ -301,17 +294,19 @@
     piece = jax.ShapeDtypeStruct((80, HD), bf16)
     keyed = jax.ShapeDtypeStruct((1152, HD), bf16)
     p0, p1, p2, p3, keys, values = call(
-        text_body, [piece] * 4 + [keyed] * 2, 7, smem=(0, 1), name="text"
+        text_body, [piece] * 4 + [keyed] * 2, 7, smem=(0, 1)
     )(j, txt_len, kv, *others, txt)
     got = [
         lax.ppermute(p, "y", [(i, i ^ s) for i in range(4)])
         for s, p in ((1, p1), (2, p2), (3, p3))
     ]
-    img = call(
-        image_body, jax.ShapeDtypeStruct((32, 40, HD), bf16), 5, smem=(0, 1), name="image"
-    )(j, txt_len, recv, keys, values)
+    img, w_near = call(
+        image_body,
+        [jax.ShapeDtypeStruct((32, 40, HD), bf16), pltpu.VMEM(w_proj.shape, bf16)],
+        6, smem=(0, 1), hbm=(5,), scratch=(pltpu.SemaphoreType.DMA,),
+    )(j, txt_len, recv, keys, values, w_proj)
     back = call(
-        fill_body, jax.ShapeDtypeStruct((32, 104, HD), bf16), 7, smem=(0, 1), name="fill"
+        fill_body, jax.ShapeDtypeStruct((32, 104, HD), bf16), 7, smem=(0, 1)
     )(j, txt_len, img, p0, *got)
     home = lax.all_to_all(back, CUBE, 0, 0, tiled=True)
     half = tokens // 2
@@ -322,9 +317,8 @@
             jax.ShapeDtypeStruct((half, d_model), bf16),
             jax.ShapeDtypeStruct((256, width), bf16),
         ],
-        3, smem=(0,), hbm=(2,), name="tail",
-        scratch=(pltpu.VMEM(w_proj.shape, bf16), pltpu.SemaphoreType.DMA((4,))),
-    )(core, home, w_proj)
+        3, smem=(0,), near=(2,),
+    )(core, home, w_near)
     theirs = lax.ppermute(other, "tp", [(0, 1), (1, 0)])
     projected = mine + theirs.astype(f32)
     img_out = residual[0].astype(f32) + gate[None, :] * (projected + proj_bias[None, :])

time: 75.2 us -> 72.9 us (0.969)
  blocking collectives: 11.4 us -> 33.2 us
  starting transfers between devices: 33.4 us -> 22.2 us
  waiting for transfers between devices: 17.8 us -> 7 us
  Pallas kernels: 10.1 us -> 7.96 us
    all_to_all x0 -> x1, blocking collectives: none -> 21.7 us  [shards(): home = lax.all_to_all(back, CUBE, 0, 0, tiled=True)]
    all_to_all x1 -> x0, starting transfers between devices: 11.1 us -> none  [shards(): home = lax.all_to_all(back, CUBE, 0, 0, tiled=True)]
    all_to_all x1 -> x0, waiting for transfers between devices: 10.5 us -> none  [shards(): home = lax.all_to_all(back, CUBE, 0, 0, tiled=True)]
    pallas_call x5, Pallas kernels: 10.1 us -> 7.96 us  [run(): return kernel(*held)]
  transfers between devices with their start and end apart: 9 -> 8, of which waited for: 5 -> 4; matrix products, arithmetic and copies ran while one was open for 0% -> 0% of each run, Pallas kernels for 4% -> 5%
where the time goes in v3:
time: 72.9 us; the launch traced here: 72.6 us
  blocking collectives  33.2 us (46%)
  starting transfers between devices  22.2 us (30%)
  Pallas kernels  7.96 us (11%)
  waiting for transfers between devices  7 us (10%)
  between operations  1.4 us (2%)
    all_to_all x1, blocking collectives, shards(): home = lax.all_to_all(back, CUBE, 0, 0, tiled=True)  21.7 us
    all_to_all x1, blocking collectives, shards(): kv = lax.all_to_all(kv_send, HEAD, 0, 0, tiled=True)  11.4 us
    pallas_call x5, Pallas kernels, run(): return kernel(*held)  7.96 us
    ppermute x3, starting transfers between devices, shards(): lax.ppermute(kv, 'zh', [(i, i ^ s) for i in range(4)])  7.39 us
    all_to_all x1, starting transfers between devices, shards(): recv = lax.all_to_all(q_send, CUBE, 0, 0, tiled=True)  5.58 us
    ppermute x3, waiting for transfers between devices, shards(): lax.ppermute(kv, 'zh', [(i, i ^ s) for i in range(4)])  5.16 us
    ppermute x1, starting transfers between devices, shards(): theirs = lax.ppermute(other, 'tp', [(0, 1), (1, 0)])  5.04 us
    ppermute x3, starting transfers between devices, shards(): lax.ppermute(p, 'y', [(i, i ^ s) for i in range(4)])  4.24 us
  transfers between devices with their start and end apart: 8, of which 4 were waited for; matrix products, arithmetic and copies ran while one was open for 0% of the time, Pallas kernels for 5%

profile of v3, /device:TPU:1, one launch (start us, length us, event | category | flops | bytes accessed | tf_op | source)
XLA Modules:
  0.0 72.6 jit_solution(9021808230237834871)
XLA Ops:
  0.6 0.0 copy-start
  0.7 2.0 %shard_map.122 = (bf16[32,32,128]{2,1,0:T(8,128)(2,1)}, bf16[8,64,128]{2,1,0:T(8,128)(2,1)S(1)}) custom-call(bf16[3,32,1024]{2,1,0:T(8,128)(2,1)} %bitcast.15, s32[1,32]{1,0:T(1,128)} %frame_hbm, s32[1,32]{1,0:T(1,128)} %row_hbm.1, s32[1,32]{1,0:T(1,128)} %col_hbm.1, f32[8,128]{1,0:T(8,128)} %constant.26.clone.rate_hbm), custom_call_target="tpu_custom_call" | custom-call | tf_op jit(solution)/shard_map/pallas_call | solution.py:61
  2.7 11.4 %all_to_all.15.kv0_ref = bf16[8,64,128]{2,1,0:T(8,128)(2,1)S(1)} all-to-all(bf16[8,64,128]{2,1,0:T(8,128)(2,1)S(1)} %get-tuple-element.23), channel_id=1, replica_groups=mesh['zh'=4,'zl'=2,'x'=4,'y'=4,'tp'=2] {'zl','x'}, dimensions={0} | all-to-all | bytes 262144 | tf_op jit(solution)/shard_map/all_to_all | solution.py:289
  14.1 5.6 %all-to-all-start.1 = ((bf16[32,32,128]{2,1,0:T(8,128)(2,1)}), bf16[32,32,128]{2,1,0:T(8,128)(2,1)S(1)}, u32[]{:S(2)}, u32[]{:S(2)}) async-start(bf16[32,32,128]{2,1,0:T(8,128)(2,1)} %get-tuple-element.24), calls=%async_computation.1 | async-start | bytes 524288 | tf_op jit(solution)/shard_map/all_to_all | solution.py:292
  19.7 5.2 %collective-permute-start.2 = (bf16[8,64,128]{2,1,0:T(8,128)(2,1)S(1)}, bf16[8,64,128]{2,1,0:T(8,128)(2,1)S(1)}, u32[]{:S(2)}, u32[]{:S(2)}) collective-permute-start(bf16[8,64,128]{2,1,0:T(8,128)(2,1)S(1)} %all_to_all.15.kv0_ref), channel_id=1, source_target_pairs={{0,192},{64,128},{128,64},{192,0},{1,193},{65,129},{129,65},{193,1... | collective-permute-start | bytes 393224 | tf_op jit(solution)/shard_map/ppermute | solution.py:290
  24.9 1.2 %collective-permute-start.1 = (bf16[8,64,128]{2,1,0:T(8,128)(2,1)S(1)}, bf16[8,64,128]{2,1,0:T(8,128)(2,1)S(1)}, u32[]{:S(2)}, u32[]{:S(2)}) collective-permute-start(bf16[8,64,128]{2,1,0:T(8,128)(2,1)S(1)} %all_to_all.15.kv0_ref), channel_id=1, source_target_pairs={{0,128},{64,192},{128,0},{192,64},{1,129},{65,193},{129,1},{193,65... | collective-permute-start | bytes 393224 | tf_op jit(solution)/shard_map/ppermute | solution.py:290
  26.1 1.0 %collective-permute-start = (bf16[8,64,128]{2,1,0:T(8,128)(2,1)S(1)}, bf16[8,64,128]{2,1,0:T(8,128)(2,1)S(1)}, u32[]{:S(2)}, u32[]{:S(2)}) collective-permute-start(bf16[8,64,128]{2,1,0:T(8,128)(2,1)S(1)} %all_to_all.15.kv0_ref), channel_id=1, source_target_pairs={{0,64},{64,0},{128,192},{192,128},{1,65},{65,1},{129,193},{193,129... | collective-permute-start | bytes 393224 | tf_op jit(solution)/shard_map/ppermute | solution.py:290
  27.8 0.0 copy-done
  27.8 0.1 dynamic-slice_bitcast_fusion.txt_ref
  27.8 1.9 %collective-permute-done.2.kv3_ref = bf16[8,64,128]{2,1,0:T(8,128)(2,1)S(1)} collective-permute-done((bf16[8,64,128]{2,1,0:T(8,128)(2,1)S(1)}, bf16[8,64,128]{2,1,0:T(8,128)(2,1)S(1)}, u32[]{:S(2)}, u32[]{:S(2)}) %collective-permute-start.2) | collective-permute-done | bytes 131104 | tf_op jit(solution)/shard_map/ppermute | solution.py:290
  29.8 3.2 %collective-permute-done.1.kv2_ref = bf16[8,64,128]{2,1,0:T(8,128)(2,1)S(1)} collective-permute-done((bf16[8,64,128]{2,1,0:T(8,128)(2,1)S(1)}, bf16[8,64,128]{2,1,0:T(8,128)(2,1)S(1)}, u32[]{:S(2)}, u32[]{:S(2)}) %collective-permute-start.1) | collective-permute-done | bytes 131104 | tf_op jit(solution)/shard_map/ppermute | solution.py:290
  33.0 0.0 collective-permute-done.kv1_ref
  33.0 0.8 %shard_map.123 = (bf16[80,128]{1,0:T(8,128)(2,1)S(1)}, bf16[80,128]{1,0:T(8,128)(2,1)S(1)}, bf16[80,128]{1,0:T(8,128)(2,1)S(1)}, bf16[80,128]{1,0:T(8,128)(2,1)S...) custom-call(s32[1]{0:T(128)} %bitcast.1.where_ref, s32[1]{0:T(128)S(6)} %copy.13.len_ref, ...), custom_call_target="tpu_custom_call" | custom-call | tf_op jit(solution)/shard_map/pallas_call | solution.py:61
  33.8 1.7 %collective-permute-start.3 = (bf16[80,128]{1,0:T(8,128)(2,1)S(1)}, bf16[80,128]{1,0:T(8,128)(2,1)S(1)}, u32[]{:S(2)}, u32[]{:S(2)}) collective-permute-start(bf16[80,128]{1,0:T(8,128)(2,1)S(1)} %get-tuple-element.29), channel_id=1, source_target_pairs={{0,2},{2,0},{4,6},{6,4},{1,3},{3,1},{5,7},{7,5},{8,10},{10,8},{12,... | collective-permute-start | bytes 61448 | tf_op jit(solution)/shard_map/ppermute | solution.py:300
  35.6 2.4 %collective-permute-start.4 = (bf16[80,128]{1,0:T(8,128)(2,1)S(1)}, bf16[80,128]{1,0:T(8,128)(2,1)S(1)}, u32[]{:S(2)}, u32[]{:S(2)}) collective-permute-start(bf16[80,128]{1,0:T(8,128)(2,1)S(1)} %get-tuple-element.30), channel_id=1, source_target_pairs={{0,4},{2,6},{4,0},{6,2},{1,5},{3,7},{5,1},{7,3},{8,12},{10,14},{12... | collective-permute-start | bytes 61448 | tf_op jit(solution)/shard_map/ppermute | solution.py:300
  38.0 0.1 collective-permute-start.5
  38.1 0.0 all-to-all-done.1.recv_ref
  38.1 2.8 %shard_map.124 = (bf16[32,40,128]{2,1,0:T(8,128)(2,1)S(1)}, bf16[1024,3072]{1,0:T(8,128)(2,1)S(1)}) custom-call(s32[1]{0:T(128)} %bitcast.1.where_ref, s32[1]{0:T(128)S(6)} %copy.13.len_ref, bf16[32,32,128]{2,1,0:T(8,128)(2,1)S(1)} %all-to-all-done.1.recv_ref, bf16[1152,128]{1,0:T(8,128)(2,1)S(1)} %get-tuple-element.25.keys_ref, ...), custom_call_target="tpu_custom_call" | custom-call | tf_op jit(solution)/shard_map/pallas_call | solution.py:61
  40.9 0.0 copy-start.1
  40.9 0.0 copy-start.2
  40.9 0.0 copy-start.3
  40.9 0.0 collective-permute-done.3.p1_ref
  40.9 0.0 collective-permute-done.4.p2_ref
  40.9 0.9 %collective-permute-done.5.p3_ref = bf16[80,128]{1,0:T(8,128)(2,1)S(1)} collective-permute-done((bf16[80,128]{1,0:T(8,128)(2,1)S(1)}, bf16[80,128]{1,0:T(8,128)(2,1)S(1)}, u32[]{:S(2)}, u32[]{:S(2)}) %collective-permute-start.5) | collective-permute-done | bytes 20512 | tf_op jit(solution)/shard_map/ppermute | solution.py:300
  41.8 0.2 shard_map.125
  42.0 21.7 %all_to_all.16.recv_ref = bf16[32,104,128]{2,1,0:T(8,128)(2,1)S(1)} all-to-all(bf16[32,104,128]{2,1,0:T(8,128)(2,1)S(1)} %shard_map.125), channel_id=1, replica_groups=mesh['zh'=4,'zl'=2,'x'=4,'y'=4,'tp'=2] {'zl','x','y'}, dimensions={0} | all-to-all | bytes 1703936 | tf_op jit(solution)/shard_map/all_to_all | solution.py:311
  63.7 2.1 %shard_map.126 = (f32[16,3072]{1,0:T(8,128)S(1)}, bf16[16,3072]{1,0:T(8,128)(2,1)S(1)}, bf16[256,1024]{1,0:T(8,128)(2,1)}) custom-call(s32[1]{0:T(128)} %bitcast.2.core_ref, bf16[32,104,128]{2,1,0:T(8,128)(2,1)S(1)} %all_to_all.16.recv_ref, bf16[1024,3072]{1,0:T(8,128)(2,1)S(1)} %get-tuple-element.32.w_ref), custom_call_target="tpu_custom_call" | custom-call | tf_op jit(solution)/shard_map/pallas_call | solution.py:61
  65.9 5.0 %collective-permute-start.6 = (bf16[16,3072]{1,0:T(8,128)(2,1)S(1)}, bf16[16,3072]{1,0:T(8,128)(2,1)S(1)}, u32[]{:S(2)}, u32[]{:S(2)}) collective-permute-start(bf16[16,3072]{1,0:T(8,128)(2,1)S(1)} %get-tuple-element.34), channel_id=1, source_target_pairs={{0,1},{1,0},{2,3},{3,2},{4,5},{5,4},{6,7},{7,6},{8,9},{9,8},{10,11... | collective-permute-start | bytes 294920 | tf_op jit(solution)/shard_map/ppermute | solution.py:322
  70.9 0.9 %collective-permute-done.6 = bf16[16,3072]{1,0:T(8,128)(2,1)S(1)} collective-permute-done((bf16[16,3072]{1,0:T(8,128)(2,1)S(1)}, bf16[16,3072]{1,0:T(8,128)(2,1)S(1)}, u32[]{:S(2)}, u32[]{:S(2)}) %collective-permute-start.6) | collective-permute-done | bytes 98336 | tf_op jit(solution)/shard_map/ppermute | solution.py:322
  71.8 0.0 copy-done.1
  71.8 0.0 copy-done.2
  71.9 0.0 copy-done.3
  71.9 0.7 fusion.1
Async XLA Ops:
  0.6 27.1 %copy-start = (bf16[1,256,3,1024]{3,1,2,0:T(8,128)(2,1)S(1)}, bf16[1,256,3,1024]{3,1,2,0:T(8,128)(2,1)}, u32[]{:S(2)}) copy-start(bf16[1,256,3,1024]{3,1,2,0:T(8,128)(2,1)} %param.12) | copy-start | bytes 4718596
  14.1 23.9 %all-to-all-start.1 = ((bf16[32,32,128]{2,1,0:T(8,128)(2,1)}), bf16[32,32,128]{2,1,0:T(8,128)(2,1)S(1)}, u32[]{:S(2)}, u32[]{:S(2)}) async-start(bf16[32,32,128]{2,1,0:T(8,128)(2,1)} %get-tuple-element.24), calls=%async_computation.1 | async-start | bytes 524288 | tf_op jit(solution)/shard_map/all_to_all | solution.py:292
  19.7 10.0 %collective-permute-start.2 = (bf16[8,64,128]{2,1,0:T(8,128)(2,1)S(1)}, bf16[8,64,128]{2,1,0:T(8,128)(2,1)S(1)}, u32[]{:S(2)}, u32[]{:S(2)}) collective-permute-start(bf16[8,64,128]{2,1,0:T(8,128)(2,1)S(1)} %all_to_all.15.kv0_ref), channel_id=1, source_target_pairs={{0,192},{64,128},{128,64},{192,0},{1,193},{65,129},{129,65},{193,1... | collective-permute-start | bytes 393224 | tf_op jit(solution)/shard_map/ppermute | solution.py:290
  24.9 8.1 %collective-permute-start.1 = (bf16[8,64,128]{2,1,0:T(8,128)(2,1)S(1)}, bf16[8,64,128]{2,1,0:T(8,128)(2,1)S(1)}, u32[]{:S(2)}, u32[]{:S(2)}) collective-permute-start(bf16[8,64,128]{2,1,0:T(8,128)(2,1)S(1)} %all_to_all.15.kv0_ref), channel_id=1, source_target_pairs={{0,128},{64,192},{128,0},{192,64},{1,129},{65,193},{129,1},{193,65... | collective-permute-start | bytes 393224 | tf_op jit(solution)/shard_map/ppermute | solution.py:290
  26.1 6.9 %collective-permute-start = (bf16[8,64,128]{2,1,0:T(8,128)(2,1)S(1)}, bf16[8,64,128]{2,1,0:T(8,128)(2,1)S(1)}, u32[]{:S(2)}, u32[]{:S(2)}) collective-permute-start(bf16[8,64,128]{2,1,0:T(8,128)(2,1)S(1)} %all_to_all.15.kv0_ref), channel_id=1, source_target_pairs={{0,64},{64,0},{128,192},{192,128},{1,65},{65,1},{129,193},{193,129... | collective-permute-start | bytes 393224 | tf_op jit(solution)/shard_map/ppermute | solution.py:290
  33.8 7.1 %collective-permute-start.3 = (bf16[80,128]{1,0:T(8,128)(2,1)S(1)}, bf16[80,128]{1,0:T(8,128)(2,1)S(1)}, u32[]{:S(2)}, u32[]{:S(2)}) collective-permute-start(bf16[80,128]{1,0:T(8,128)(2,1)S(1)} %get-tuple-element.29), channel_id=1, source_target_pairs={{0,2},{2,0},{4,6},{6,4},{1,3},{3,1},{5,7},{7,5},{8,10},{10,8},{12,... | collective-permute-start | bytes 61448 | tf_op jit(solution)/shard_map/ppermute | solution.py:300
  35.6 5.4 %collective-permute-start.4 = (bf16[80,128]{1,0:T(8,128)(2,1)S(1)}, bf16[80,128]{1,0:T(8,128)(2,1)S(1)}, u32[]{:S(2)}, u32[]{:S(2)}) collective-permute-start(bf16[80,128]{1,0:T(8,128)(2,1)S(1)} %get-tuple-element.30), channel_id=1, source_target_pairs={{0,4},{2,6},{4,0},{6,2},{1,5},{3,7},{5,1},{7,3},{8,12},{10,14},{12... | collective-permute-start | bytes 61448 | tf_op jit(solution)/shard_map/ppermute | solution.py:300
  38.0 3.8 %collective-permute-start.5 = (bf16[80,128]{1,0:T(8,128)(2,1)S(1)}, bf16[80,128]{1,0:T(8,128)(2,1)S(1)}, u32[]{:S(2)}, u32[]{:S(2)}) collective-permute-start(bf16[80,128]{1,0:T(8,128)(2,1)S(1)} %get-tuple-element.31), channel_id=1, source_target_pairs={{0,6},{2,4},{4,2},{6,0},{1,7},{3,5},{5,3},{7,1},{8,14},{10,12},{12... | collective-permute-start | bytes 61448 | tf_op jit(solution)/shard_map/ppermute | solution.py:300
  40.9 31.0 %copy-start.1 = (bf16[1,16,3072]{2,1,0:T(8,128)(2,1)S(1)}, bf16[1,16,3072]{2,1,0:T(8,128)(2,1)}, u32[]{:S(2)}) copy-start(bf16[1,16,3072]{2,1,0:T(8,128)(2,1)} %param.17) | copy-start | bytes 294916
  40.9 31.0 %copy-start.2 = (f32[3072]{0:T(1024)S(1)}, f32[3072]{0:T(1024)}, u32[]{:S(2)}) copy-start(f32[3072]{0:T(1024)} %param.19) | copy-start | bytes 36868
  40.9 30.9 %copy-start.3 = (f32[3072]{0:T(1024)S(1)}, f32[3072]{0:T(1024)}, u32[]{:S(2)}) copy-start(f32[3072]{0:T(1024)} %param.20) | copy-start | bytes 36868
  65.9 6.0 %collective-permute-start.6 = (bf16[16,3072]{1,0:T(8,128)(2,1)S(1)}, bf16[16,3072]{1,0:T(8,128)(2,1)S(1)}, u32[]{:S(2)}, u32[]{:S(2)}) collective-permute-start(bf16[16,3072]{1,0:T(8,128)(2,1)S(1)} %get-tuple-element.34), channel_id=1, source_target_pairs={{0,1},{1,0},{2,3},{3,2},{4,5},{5,4},{6,7},{7,6},{8,9},{9,8},{10,11... | collective-permute-start | bytes 294920 | tf_op jit(solution)/shard_map/ppermute | solution.py:322

commit v4 on v3

--- a/solution.py
+++ b/solution.py
@@ -11,9 +11,9 @@
 
 
 HD = 128
-SEQ = ("zh", "zl", "x", "y")
+SEQ = ("zq", "zm", "zl", "x", "y")
 CUBE = ("zl", "x", "y")
-HEAD = ("zl", "x")
+NEAR = ("zm", "zl", "x")
 rope_base = 256.0
 neg_large = -1e30
 LOG2E = 1.4426950408889634
@@ -116,11 +116,12 @@
 
     for head in range(8):
         cols = slice(head * HD, (head + 1) * HD)
-        kv_out[head, 0:32, :] = rotate(qkv_ref[1, :, cols])
-        kv_out[head, 32:64, :] = qkv_ref[2, :, cols]
-        query = rotate(qkv_ref[0, :, cols])
-        for j in range(4):
-            q_out[head * 4 + j] = query
+        key = rotate(qkv_ref[1, :, cols])
+        value = qkv_ref[2, :, cols]
+        for d in (head, head + 8):
+            kv_out[d, 0:32, :] = key
+            kv_out[d, 32:64, :] = value
+        q_out[head] = rotate(qkv_ref[0, :, cols])
 
 
 def softmax_block(q, keys, values, live):
@@ -154,14 +155,14 @@
 
 
 def text_body(
-    where_ref, len_ref, kv0_ref, kv1_ref, kv2_ref, kv3_ref, txt_ref,
+    where_ref, len_ref, kv0_ref, kv1_ref, txt_ref,
     p0_ref, p1_ref, p2_ref, p3_ref, keys_ref, values_ref,
 ):
     j = where_ref[0]
     length = len_ref[0]
-    for b, ref in enumerate((kv0_ref, kv1_ref, kv2_ref, kv3_ref)):
-        keys_ref[256 * b : 256 * b + 256, :] = ref[:, 0:32, :].reshape(256, HD)
-        values_ref[256 * b : 256 * b + 256, :] = ref[:, 32:64, :].reshape(256, HD)
+    for b, ref in enumerate((kv0_ref, kv1_ref)):
+        keys_ref[512 * b : 512 * b + 512, :] = ref[:, 0:32, :].reshape(512, HD)
+        values_ref[512 * b : 512 * b + 512, :] = ref[:, 32:64, :].reshape(512, HD)
     start = pl.multiple_of((j // 2) * 128, 128)
     keys_ref[1024:1152, :] = txt_ref[1, pl.ds(start, 128), :]
     values_ref[1024:1152, :] = txt_ref[2, pl.ds(start, 128), :]
@@ -273,9 +274,9 @@
     qkv = img_qkv.reshape(tokens, 3, width).transpose(1, 0, 2)
     txt = lax.dynamic_slice_in_dim(txt_qkv[0], head * HD, HD, 2).transpose(1, 0, 2)
 
-    q_send, kv_send = call(
+    q_mine, kv_send = call(
         prep_body,
-        [jax.ShapeDtypeStruct((32, 32, HD), bf16), jax.ShapeDtypeStruct((8, 64, HD), bf16)],
+        [jax.ShapeDtypeStruct((8, tokens, HD), bf16), jax.ShapeDtypeStruct((16, 64, HD), bf16)],
         5, hbm=(0, 1, 2, 3, 4),
         scratch=(
             pltpu.VMEM((3, tokens, width), bf16),
@@ -286,16 +287,17 @@
             pltpu.SemaphoreType.DMA((5,)),
         ),
     )(qkv, frame_index, row_index, column_index, jnp.asarray(rate_table()))
-    kv = lax.all_to_all(kv_send, HEAD, 0, 0, tiled=True)
-    others = [lax.ppermute(kv, "zh", [(i, i ^ s) for i in range(4)]) for s in (1, 2, 3)]
-    q_send, _ = lax.optimization_barrier((q_send, kv))
+    kv = lax.all_to_all(kv_send, NEAR, 0, 0, tiled=True)
+    other = lax.ppermute(kv, "zq", [(0, 1), (1, 0)])
+    q_mine, _ = lax.optimization_barrier((q_mine, kv))
+    q_send = jnp.broadcast_to(q_mine[:, None], (8, 4, tokens, HD)).reshape(32, tokens, HD)
     recv = lax.all_to_all(q_send, CUBE, 0, 0, tiled=True)
 
     piece = jax.ShapeDtypeStruct((80, HD), bf16)
     keyed = jax.ShapeDtypeStruct((1152, HD), bf16)
     p0, p1, p2, p3, keys, values = call(
-        text_body, [piece] * 4 + [keyed] * 2, 7, smem=(0, 1)
-    )(j, txt_len, kv, *others, txt)
+        text_body, [piece] * 4 + [keyed] * 2, 5, smem=(0, 1)
+    )(j, txt_len, kv, other, txt)
     got = [
         lax.ppermute(p, "y", [(i, i ^ s) for i in range(4)])
         for s, p in ((1, p1), (2, p2), (3, p3))
@@ -310,7 +312,7 @@
     )(j, txt_len, img, p0, *got)
     home = lax.all_to_all(back, CUBE, 0, 0, tiled=True)
     half = tokens // 2
-    mine, other, txt_out = call(
+    mine, given, txt_out = call(
         tail_body,
         [
             jax.ShapeDtypeStruct((half, d_model), f32),
@@ -319,7 +321,7 @@
         ],
         3, smem=(0,), near=(2,),
     )(core, home, w_near)
-    theirs = lax.ppermute(other, "tp", [(0, 1), (1, 0)])
+    theirs = lax.ppermute(given, "tp", [(0, 1), (1, 0)])
     projected = mine + theirs.astype(f32)
     img_out = residual[0].astype(f32) + gate[None, :] * (projected + proj_bias[None, :])
     return img_out.astype(bf16)[None], txt_out[None]
@@ -327,7 +329,7 @@
 
 def solution(mesh):
     split = Mesh(
-        mesh.devices.reshape(4, 2, 4, 4, mesh.shape["tp"]), ("zh", "zl", "x", "y", "tp")
+        mesh.devices.reshape(2, 2, 2, 4, 4, mesh.shape["tp"]), ("zq", "zm", "zl", "x", "y", "tp")
     )
     placed = (
         P(None, SEQ, None, "tp"),

time: 72.9 us -> 76.7 us (1.052)
  blocking collectives: 33.2 us -> 36.3 us
  waiting for transfers between devices: 7 us -> 7.85 us
    all_to_all x1, blocking collectives: 11.4 us -> 18.4 us  [shards(): kv = lax.all_to_all(kv_send, NEAR, 0, 0, tiled=True)]
    all_to_all x1, blocking collectives: 21.7 us -> 17.9 us  [shards(): home = lax.all_to_all(back, CUBE, 0, 0, tiled=True)]
    ppermute x4 -> x2, waiting for transfers between devices: 6.11 us -> 7.32 us  [the longest x1 6.38 us: shards(): other = lax.ppermute(kv, 'zq', [(0, 1), (1, 0)])]
    ppermute x4 -> x2, starting transfers between devices: 12.4 us -> 12.7 us  [the longest x1 8.36 us: shards(): theirs = lax.ppermute(given, 'tp', [(0, 1), (1, 0)])]
  transfers between devices with their start and end apart: 8 -> 6, of which waited for: 4 -> 3; matrix products, arithmetic and copies ran while one was open for 0% -> 0% of each run, Pallas kernels for 5% -> 5%
where the time goes in v4:
time: 76.7 us; the launch traced here: 76.4 us
  blocking collectives  36.3 us (47%)
  starting transfers between devices  22.1 us (29%)
  waiting for transfers between devices  7.85 us (10%)
  Pallas kernels  7.27 us (9%)
  between operations  1.4 us (2%)
  local copies, waits for them, and re-layouts  0.83 us (1%)
    all_to_all x1, blocking collectives, shards(): kv = lax.all_to_all(kv_send, NEAR, 0, 0, tiled=True)  18.4 us
    all_to_all x1, blocking collectives, shards(): home = lax.all_to_all(back, CUBE, 0, 0, tiled=True)  17.9 us
    ppermute x1, starting transfers between devices, shards(): theirs = lax.ppermute(given, 'tp', [(0, 1), (1, 0)])  8.36 us
    pallas_call x5, Pallas kernels, run(): return kernel(*held)  7.27 us
    ppermute x1, waiting for transfers between devices, shards(): other = lax.ppermute(kv, 'zq', [(0, 1), (1, 0)])  6.38 us
    all_to_all x1, starting transfers between devices, shards(): recv = lax.all_to_all(q_send, CUBE, 0, 0, tiled=True)  5.46 us
    ppermute x1, starting transfers between devices, shards(): other = lax.ppermute(kv, 'zq', [(0, 1), (1, 0)])  4.3 us
    ppermute x3, starting transfers between devices, shards(): lax.ppermute(p, 'y', [(i, i ^ s) for i in range(4)])  3.95 us
  transfers between devices with their start and end apart: 6, of which 3 were waited for; matrix products, arithmetic and copies ran while one was open for 0% of the time, Pallas kernels for 5%

profile of v4, /device:TPU:1, one launch (start us, length us, event | category | flops | bytes accessed | tf_op | source)
XLA Modules:
  0.0 76.4 jit_solution(15160165677755892152)
XLA Ops:
  0.6 0.0 copy-start
  0.7 1.3 %shard_map.122 = (bf16[8,32,128]{2,1,0:T(8,128)(2,1)S(1)}, bf16[16,64,128]{2,1,0:T(8,128)(2,1)S(1)}) custom-call(bf16[3,32,1024]{2,1,0:T(8,128)(2,1)} %bitcast.16, s32[1,32]{1,0:T(1,128)} %frame_hbm, s32[1,32]{1,0:T(1,128)} %row_hbm.1, s32[1,32]{1,0:T(1,128)} %col_hbm.1, f32[8,128]{1,0:T(8,128)} %constant.26.clone.rate_hbm), custom_call_target="tpu_custom_call" | custom-call | tf_op jit(solution)/shard_map/pallas_call | solution.py:61
  2.0 18.4 %all_to_all.15.kv0_ref = bf16[16,64,128]{2,1,0:T(8,128)(2,1)S(1)} all-to-all(bf16[16,64,128]{2,1,0:T(8,128)(2,1)S(1)} %get-tuple-element.23), channel_id=1, replica_groups=mesh['zq'=2,'zm'=2,'zl'=2,'x'=4,'y'=4,'tp'=2] {'zm','zl','x'}, dimensions={0} | all-to-all | bytes 524288 | tf_op jit(solution)/shard_map/all_to_all | solution.py:290
  20.4 0.7 broadcast_in_dim.6
  21.1 5.5 %all-to-all-start.1 = ((bf16[32,32,128]{2,1,0:T(8,128)(2,1)}), bf16[32,32,128]{2,1,0:T(8,128)(2,1)S(1)}, u32[]{:S(2)}, u32[]{:S(2)}) async-start(bf16[32,32,128]{2,1,0:T(8,128)(2,1)} %bitcast.5), calls=%async_computation.1 | async-start | bytes 524288 | tf_op jit(solution)/shard_map/all_to_all | solution.py:294
  26.6 4.3 %collective-permute-start = (bf16[16,64,128]{2,1,0:T(8,128)(2,1)S(1)}, bf16[16,64,128]{2,1,0:T(8,128)(2,1)S(1)}, u32[]{:S(2)}, u32[]{:S(2)}) collective-permute-start(bf16[16,64,128]{2,1,0:T(8,128)(2,1)S(1)} %all_to_all.15.kv0_ref), channel_id=1, source_target_pairs={{0,128},{128,0},{1,129},{129,1},{2,130},{130,2},{3,131},{131,3},{4... | collective-permute-start | bytes 786440 | tf_op jit(solution)/shard_map/ppermute | solution.py:291
  31.6 0.0 copy-done
  31.6 0.1 dynamic-slice_bitcast_fusion.txt_ref
  31.6 6.4 %collective-permute-done.kv1_ref = bf16[16,64,128]{2,1,0:T(8,128)(2,1)S(1)} collective-permute-done((bf16[16,64,128]{2,1,0:T(8,128)(2,1)S(1)}, bf16[16,64,128]{2,1,0:T(8,128)(2,1)S(1)}, u32[]{:S(2)}, u32[]{:S(2)}) %collective-permute-start) | collective-permute-done | bytes 262176 | tf_op jit(solution)/shard_map/ppermute | solution.py:291
  38.0 0.8 %shard_map.123 = (bf16[80,128]{1,0:T(8,128)(2,1)S(1)}, bf16[80,128]{1,0:T(8,128)(2,1)S(1)}, bf16[80,128]{1,0:T(8,128)(2,1)S(1)}, bf16[80,128]{1,0:T(8,128)(2,1)S...) custom-call(s32[1]{0:T(128)} %bitcast.1.where_ref, s32[1]{0:T(128)S(6)} %copy.13.len_ref, ...), custom_call_target="tpu_custom_call" | custom-call | tf_op jit(solution)/shard_map/pallas_call | solution.py:61
  38.8 1.1 %collective-permute-start.1 = (bf16[80,128]{1,0:T(8,128)(2,1)S(1)}, bf16[80,128]{1,0:T(8,128)(2,1)S(1)}, u32[]{:S(2)}, u32[]{:S(2)}) collective-permute-start(bf16[80,128]{1,0:T(8,128)(2,1)S(1)} %get-tuple-element.29), channel_id=1, source_target_pairs={{0,2},{2,0},{4,6},{6,4},{1,3},{3,1},{5,7},{7,5},{8,10},{10,8},{12,... | collective-permute-start | bytes 61448 | tf_op jit(solution)/shard_map/ppermute | solution.py:302
  39.9 2.4 %collective-permute-start.2 = (bf16[80,128]{1,0:T(8,128)(2,1)S(1)}, bf16[80,128]{1,0:T(8,128)(2,1)S(1)}, u32[]{:S(2)}, u32[]{:S(2)}) collective-permute-start(bf16[80,128]{1,0:T(8,128)(2,1)S(1)} %get-tuple-element.30), channel_id=1, source_target_pairs={{0,4},{2,6},{4,0},{6,2},{1,5},{3,7},{5,1},{7,3},{8,12},{10,14},{12... | collective-permute-start | bytes 61448 | tf_op jit(solution)/shard_map/ppermute | solution.py:302
  42.3 0.5 collective-permute-start.3
  42.8 0.0 all-to-all-done.1.recv_ref
  42.8 2.8 %shard_map.124 = (bf16[32,40,128]{2,1,0:T(8,128)(2,1)S(1)}, bf16[1024,3072]{1,0:T(8,128)(2,1)S(1)}) custom-call(s32[1]{0:T(128)} %bitcast.1.where_ref, s32[1]{0:T(128)S(6)} %copy.13.len_ref, bf16[32,32,128]{2,1,0:T(8,128)(2,1)S(1)} %all-to-all-done.1.recv_ref, bf16[1152,128]{1,0:T(8,128)(2,1)S(1)} %get-tuple-element.25.keys_ref, ...), custom_call_target="tpu_custom_call" | custom-call | tf_op jit(solution)/shard_map/pallas_call | solution.py:61
  45.6 0.0 copy-start.1
  45.6 0.0 copy-start.2
  45.6 0.0 copy-start.3
  45.6 0.0 collective-permute-done.1.p1_ref
  45.6 0.0 collective-permute-done.2.p2_ref
  45.6 0.5 collective-permute-done.3.p3_ref
  46.2 0.2 shard_map.125
  46.3 17.9 %all_to_all.16.recv_ref = bf16[32,104,128]{2,1,0:T(8,128)(2,1)S(1)} all-to-all(bf16[32,104,128]{2,1,0:T(8,128)(2,1)S(1)} %shard_map.125), channel_id=1, replica_groups=mesh['zq'=2,'zm'=2,'zl'=2,'x'=4,'y'=4,'tp'=2] {'zl','x','y'}, dimensions={0} | all-to-all | bytes 1703936 | tf_op jit(solution)/shard_map/all_to_all | solution.py:313
  64.2 2.1 %shard_map.126 = (f32[16,3072]{1,0:T(8,128)S(1)}, bf16[16,3072]{1,0:T(8,128)(2,1)S(1)}, bf16[256,1024]{1,0:T(8,128)(2,1)}) custom-call(s32[1]{0:T(128)} %bitcast.2.core_ref, bf16[32,104,128]{2,1,0:T(8,128)(2,1)S(1)} %all_to_all.16.recv_ref, bf16[1024,3072]{1,0:T(8,128)(2,1)S(1)} %get-tuple-element.32.w_ref), custom_call_target="tpu_custom_call" | custom-call | tf_op jit(solution)/shard_map/pallas_call | solution.py:61
  66.4 8.4 %collective-permute-start.4 = (bf16[16,3072]{1,0:T(8,128)(2,1)S(1)}, bf16[16,3072]{1,0:T(8,128)(2,1)S(1)}, u32[]{:S(2)}, u32[]{:S(2)}) collective-permute-start(bf16[16,3072]{1,0:T(8,128)(2,1)S(1)} %get-tuple-element.34), channel_id=1, source_target_pairs={{0,1},{1,0},{2,3},{3,2},{4,5},{5,4},{6,7},{7,6},{8,9},{9,8},{10,11... | collective-permute-start | bytes 294920 | tf_op jit(solution)/shard_map/ppermute | solution.py:324
  74.7 0.9 %collective-permute-done.4 = bf16[16,3072]{1,0:T(8,128)(2,1)S(1)} collective-permute-done((bf16[16,3072]{1,0:T(8,128)(2,1)S(1)}, bf16[16,3072]{1,0:T(8,128)(2,1)S(1)}, u32[]{:S(2)}, u32[]{:S(2)}) %collective-permute-start.4) | collective-permute-done | bytes 98336 | tf_op jit(solution)/shard_map/ppermute | solution.py:324
  75.7 0.0 copy-done.1
  75.7 0.0 copy-done.2
  75.7 0.0 copy-done.3
  75.7 0.7 fusion.1
Async XLA Ops:
  0.6 30.9 %copy-start = (bf16[1,256,3,1024]{3,1,2,0:T(8,128)(2,1)S(1)}, bf16[1,256,3,1024]{3,1,2,0:T(8,128)(2,1)}, u32[]{:S(2)}) copy-start(bf16[1,256,3,1024]{3,1,2,0:T(8,128)(2,1)} %param.12) | copy-start | bytes 4718596
  21.1 21.6 %all-to-all-start.1 = ((bf16[32,32,128]{2,1,0:T(8,128)(2,1)}), bf16[32,32,128]{2,1,0:T(8,128)(2,1)S(1)}, u32[]{:S(2)}, u32[]{:S(2)}) async-start(bf16[32,32,128]{2,1,0:T(8,128)(2,1)} %bitcast.5), calls=%async_computation.1 | async-start | bytes 524288 | tf_op jit(solution)/shard_map/all_to_all | solution.py:294
  26.6 11.4 %collective-permute-start = (bf16[16,64,128]{2,1,0:T(8,128)(2,1)S(1)}, bf16[16,64,128]{2,1,0:T(8,128)(2,1)S(1)}, u32[]{:S(2)}, u32[]{:S(2)}) collective-permute-start(bf16[16,64,128]{2,1,0:T(8,128)(2,1)S(1)} %all_to_all.15.kv0_ref), channel_id=1, source_target_pairs={{0,128},{128,0},{1,129},{129,1},{2,130},{130,2},{3,131},{131,3},{4... | collective-permute-start | bytes 786440 | tf_op jit(solution)/shard_map/ppermute | solution.py:291
  38.8 6.8 %collective-permute-start.1 = (bf16[80,128]{1,0:T(8,128)(2,1)S(1)}, bf16[80,128]{1,0:T(8,128)(2,1)S(1)}, u32[]{:S(2)}, u32[]{:S(2)}) collective-permute-start(bf16[80,128]{1,0:T(8,128)(2,1)S(1)} %get-tuple-element.29), channel_id=1, source_target_pairs={{0,2},{2,0},{4,6},{6,4},{1,3},{3,1},{5,7},{7,5},{8,10},{10,8},{12,... | collective-permute-start | bytes 61448 | tf_op jit(solution)/shard_map/ppermute | solution.py:302
  39.9 5.7 %collective-permute-start.2 = (bf16[80,128]{1,0:T(8,128)(2,1)S(1)}, bf16[80,128]{1,0:T(8,128)(2,1)S(1)}, u32[]{:S(2)}, u32[]{:S(2)}) collective-permute-start(bf16[80,128]{1,0:T(8,128)(2,1)S(1)} %get-tuple-element.30), channel_id=1, source_target_pairs={{0,4},{2,6},{4,0},{6,2},{1,5},{3,7},{5,1},{7,3},{8,12},{10,14},{12... | collective-permute-start | bytes 61448 | tf_op jit(solution)/shard_map/ppermute | solution.py:302
  42.3 3.8 %collective-permute-start.3 = (bf16[80,128]{1,0:T(8,128)(2,1)S(1)}, bf16[80,128]{1,0:T(8,128)(2,1)S(1)}, u32[]{:S(2)}, u32[]{:S(2)}) collective-permute-start(bf16[80,128]{1,0:T(8,128)(2,1)S(1)} %get-tuple-element.31), channel_id=1, source_target_pairs={{0,6},{2,4},{4,2},{6,0},{1,7},{3,5},{5,3},{7,1},{8,14},{10,12},{12... | collective-permute-start | bytes 61448 | tf_op jit(solution)/shard_map/ppermute | solution.py:302
  45.6 30.1 %copy-start.1 = (bf16[1,16,3072]{2,1,0:T(8,128)(2,1)S(1)}, bf16[1,16,3072]{2,1,0:T(8,128)(2,1)}, u32[]{:S(2)}) copy-start(bf16[1,16,3072]{2,1,0:T(8,128)(2,1)} %param.17) | copy-start | bytes 294916
  45.6 30.1 %copy-start.2 = (f32[3072]{0:T(1024)S(1)}, f32[3072]{0:T(1024)}, u32[]{:S(2)}) copy-start(f32[3072]{0:T(1024)} %param.19) | copy-start | bytes 36868
  45.6 30.1 %copy-start.3 = (f32[3072]{0:T(1024)S(1)}, f32[3072]{0:T(1024)}, u32[]{:S(2)}) copy-start(f32[3072]{0:T(1024)} %param.20) | copy-start | bytes 36868
  66.4 9.3 %collective-permute-start.4 = (bf16[16,3072]{1,0:T(8,128)(2,1)S(1)}, bf16[16,3072]{1,0:T(8,128)(2,1)S(1)}, u32[]{:S(2)}, u32[]{:S(2)}) collective-permute-start(bf16[16,3072]{1,0:T(8,128)(2,1)S(1)} %get-tuple-element.34), channel_id=1, source_target_pairs={{0,1},{1,0},{2,3},{3,2},{4,5},{5,4},{6,7},{7,6},{8,9},{9,8},{10,11... | collective-permute-start | bytes 294920 | tf_op jit(solution)/shard_map/ppermute | solution.py:324

commit v5 on v3

--- a/solution.py
+++ b/solution.py
@@ -1,3 +1,4 @@
+import functools
 import math
 
 import jax
@@ -118,9 +119,7 @@
         cols = slice(head * HD, (head + 1) * HD)
         kv_out[head, 0:32, :] = rotate(qkv_ref[1, :, cols])
         kv_out[head, 32:64, :] = qkv_ref[2, :, cols]
-        query = rotate(qkv_ref[0, :, cols])
-        for j in range(4):
-            q_out[head * 4 + j] = query
+        q_out[head] = rotate(qkv_ref[0, :, cols])
 
 
 def softmax_block(q, keys, values, live):
@@ -155,7 +154,7 @@
 
 def text_body(
     where_ref, len_ref, kv0_ref, kv1_ref, kv2_ref, kv3_ref, txt_ref,
-    p0_ref, p1_ref, p2_ref, p3_ref, keys_ref, values_ref,
+    send_ref, keep_ref, keys_ref, values_ref,
 ):
     j = where_ref[0]
     length = len_ref[0]
@@ -169,34 +168,65 @@
     values = values_ref[...]
     live = live_mask(j, length)
     q = jnp.concatenate(
-        [txt_ref[0, pl.ds(pl.multiple_of((j ^ s) * 64, 64), 64), :] for s in range(4)], axis=0
+        [txt_ref[0, pl.ds(pl.multiple_of((j ^ s) * 64, 64), 64), :] for s in (2, 3, 0, 1)], axis=0
     )
     out, lse = softmax_block(q, keys, values, live)
-    out = out.astype(bf16)
-    row = lax.broadcasted_iota(jnp.int32, (64, 128), 0)
-    lane = lax.broadcasted_iota(jnp.int32, (64, 128), 1)
-    for s, ref in enumerate((p0_ref, p1_ref, p2_ref, p3_ref)):
-        ref[0:64, :] = out[64 * s : 64 * s + 64]
-        high, mid, low = three_parts(jnp.broadcast_to(lse[64 * s : 64 * s + 64], (64, 128)))
-        first = jnp.where(row == lane % 64, jnp.where(lane < 64, high, mid), 0.0)
-        second = jnp.where(row == lane, low, 0.0)
-        first = jnp.broadcast_to(jnp.sum(first, axis=0, keepdims=True), (8, 128))
-        second = jnp.broadcast_to(jnp.sum(second, axis=0, keepdims=True), (8, 128))
-        ref[64:80, :] = jnp.concatenate([first, second], axis=0).astype(bf16)
+    send_ref[0:128, :] = out[0:128].astype(bf16)
+    send_ref[128:136, :] = stat_rows(lse[0:128]).astype(bf16)
+    keep_ref[0] = out[128:256]
+    keep_ref[1] = jnp.broadcast_to(lse[128:256], (128, 128))
+
+
+def stat_rows(lse):
+    rows = lse.shape[0]
+    row = lax.broadcasted_iota(jnp.int32, (rows, 128), 0)
+    lane = lax.broadcasted_iota(jnp.int32, (rows, 128), 1)
+    sub = lax.broadcasted_iota(jnp.int32, (8, 128), 0)
+    packed = jnp.zeros((8, 128), f32)
+    for p, part in enumerate(three_parts(jnp.broadcast_to(lse, (rows, 128)))):
+        line = jnp.sum(jnp.where(row == lane, part, 0.0), axis=0, keepdims=True)
+        packed = jnp.where(sub == p, line, packed)
+    return packed
+
+
+def stat_column(packed, rows):
+    row = lax.broadcasted_iota(jnp.int32, (rows, 128), 0)
+    lane = lax.broadcasted_iota(jnp.int32, (rows, 128), 1)
+    line = packed[0:1] + packed[1:2] + packed[2:3]
+    return jnp.sum(jnp.where(row == lane, line, 0.0), axis=1, keepdims=True)
+
+
+def middle_body(keep_ref, got_ref, send_ref, out_ref):
+    outs = (keep_ref[0], got_ref[0:128, :].astype(f32))
+    lses = (keep_ref[1], stat_column(got_ref[128:136, :].astype(f32), 128))
+    mixed, lse = blend_pair(outs, lses)
+    out_ref[0] = mixed[0:64]
+    out_ref[1] = lse[0:64]
+    send_ref[0:64, :] = mixed[64:128].astype(bf16)
+    send_ref[64:72, :] = stat_rows(lse[64:128, 0:1]).astype(bf16)
+
+
+def blend_pair(outs, lses):
+    peak = jnp.maximum(lses[0], lses[1])
+    first = jnp.exp2(lses[0] - peak)
+    second = jnp.exp2(lses[1] - peak)
+    total = first + second
+    return (outs[0] * first + outs[1] * second) / total, peak + jnp.log2(total)
 
 
 def image_body(
-    where_ref, len_ref, recv_ref, keys_ref, values_ref, w_hbm, out_ref, w_out, sem
-):
-    fetch = pltpu.make_async_copy(w_hbm, w_out, sem)
+    half, where_ref, len_ref, recv_ref, keys_ref, values_ref, w_hbm, out_ref, w_out, sem
+):
+    fetch = pltpu.make_async_copy(w_hbm.at[pl.ds(512 * half, 512)], w_out, sem)
     fetch.start()
     live = live_mask(where_ref[0], len_ref[0])
     keys = keys_ref[...]
     values = values_ref[...]
     row = lax.broadcasted_iota(jnp.int32, (8, 32, 128), 1)
     lane = lax.broadcasted_iota(jnp.int32, (8, 32, 128), 2)
-    for b in range(4):
-        q = recv_ref[8 * b : 8 * b + 8].reshape(256, HD)
+    for b in range(2):
+        at = 16 * half + 8 * b
+        q = recv_ref[at : at + 8].reshape(256, HD)
         out, lse = softmax_block(q, keys, values, live)
         out_ref[8 * b : 8 * b + 8, 0:32, :] = out.astype(bf16).reshape(8, 32, HD)
         high, mid, low = three_parts(jnp.broadcast_to(lse, (256, 128)).reshape(8, 32, 128))
@@ -221,24 +251,20 @@
     return mixed / total
 
 
-def fill_body(where_ref, len_ref, img_ref, p0_ref, p1_ref, p2_ref, p3_ref, out_ref):
+def fill_body(where_ref, len_ref, img0_ref, img1_ref, keep_ref, got_ref, out_ref):
     row = lax.broadcasted_iota(jnp.int32, (64, 128), 0)
-    lane = lax.broadcasted_iota(jnp.int32, (64, 128), 1)
-    outs, lses = [], []
-    for ref in (p0_ref, p1_ref, p2_ref, p3_ref):
-        outs.append(ref[0:64, :].astype(f32))
-        stats = ref[64:80, :].astype(f32)
-        picked = jnp.where(row == lane % 64, stats[0:1], 0.0) + jnp.where(row == lane, stats[8:9], 0.0)
-        lses.append(jnp.sum(picked, axis=1, keepdims=True))
-    text = blend(outs, lses)
+    outs = (keep_ref[0], got_ref[0:64, :].astype(f32))
+    lses = (keep_ref[1], stat_column(got_ref[64:72, :].astype(f32), 64))
+    text, _ = blend_pair(outs, lses)
     text = jnp.where(where_ref[0] * 64 + row < len_ref[0], text, 0.0).astype(bf16)
     for d in range(32):
-        out_ref[d, 0:32, :] = img_ref[d, 0:32]
+        src = (img0_ref, img1_ref)[d // 16]
+        out_ref[d, 0:32, :] = src[d % 16, 0:32]
         out_ref[d, 32:96, :] = text
-        out_ref[d, 96:104, :] = img_ref[d, 32:40]
-
-
-def tail_body(core_ref, recv_ref, w_ref, mine_ref, other_ref, txt_ref):
+        out_ref[d, 96:104, :] = src[d % 16, 32:40]
+
+
+def tail_body(core_ref, recv_ref, w0_ref, w1_ref, mine_ref, other_ref, txt_ref):
     row = lax.broadcasted_iota(jnp.int32, (32, 128), 0)
     lane = lax.broadcasted_iota(jnp.int32, (32, 128), 1)
     pick = jnp.logical_and(row == lane % 32, lane < 96)
@@ -255,7 +281,9 @@
     rows = jnp.concatenate(heads, axis=1)
     flipped = jnp.concatenate([rows[16:32], rows[0:16]], axis=0)
     rows = jnp.where(core_ref[0] == 0, rows, flipped).astype(bf16)
-    projected = jnp.dot(rows, w_ref[...], preferred_element_type=f32)
+    projected = jnp.dot(rows[:, 0:512], w0_ref[...], preferred_element_type=f32) + jnp.dot(
+        rows[:, 512:1024], w1_ref[...], preferred_element_type=f32
+    )
     mine_ref[...] = projected[0:16]
     other_ref[...] = projected[16:32].astype(bf16)
 
@@ -273,9 +301,9 @@
     qkv = img_qkv.reshape(tokens, 3, width).transpose(1, 0, 2)
     txt = lax.dynamic_slice_in_dim(txt_qkv[0], head * HD, HD, 2).transpose(1, 0, 2)
 
-    q_send, kv_send = call(
+    q_mine, kv_send = call(
         prep_body,
-        [jax.ShapeDtypeStruct((32, 32, HD), bf16), jax.ShapeDtypeStruct((8, 64, HD), bf16)],
+        [jax.ShapeDtypeStruct((8, tokens, HD), bf16), jax.ShapeDtypeStruct((8, 64, HD), bf16)],
         5, hbm=(0, 1, 2, 3, 4),
         scratch=(
             pltpu.VMEM((3, tokens, width), bf16),
@@ -288,26 +316,39 @@
     )(qkv, frame_index, row_index, column_index, jnp.asarray(rate_table()))
     kv = lax.all_to_all(kv_send, HEAD, 0, 0, tiled=True)
     others = [lax.ppermute(kv, "zh", [(i, i ^ s) for i in range(4)]) for s in (1, 2, 3)]
-    q_send, _ = lax.optimization_barrier((q_send, kv))
+    q_mine, _ = lax.optimization_barrier((q_mine, kv))
+    q_send = jnp.broadcast_to(q_mine[:, None], (8, 4, tokens, HD)).reshape(32, tokens, HD)
     recv = lax.all_to_all(q_send, CUBE, 0, 0, tiled=True)
 
-    piece = jax.ShapeDtypeStruct((80, HD), bf16)
     keyed = jax.ShapeDtypeStruct((1152, HD), bf16)
-    p0, p1, p2, p3, keys, values = call(
-        text_body, [piece] * 4 + [keyed] * 2, 7, smem=(0, 1)
+    send, keep, keys, values = call(
+        text_body,
+        [jax.ShapeDtypeStruct((136, HD), bf16), jax.ShapeDtypeStruct((2, 128, HD), f32)] + [keyed] * 2,
+        7, smem=(0, 1),
     )(j, txt_len, kv, *others, txt)
-    got = [
-        lax.ppermute(p, "y", [(i, i ^ s) for i in range(4)])
-        for s, p in ((1, p1), (2, p2), (3, p3))
-    ]
-    img, w_near = call(
-        image_body,
-        [jax.ShapeDtypeStruct((32, 40, HD), bf16), pltpu.VMEM(w_proj.shape, bf16)],
-        6, smem=(0, 1), hbm=(5,), scratch=(pltpu.SemaphoreType.DMA,),
-    )(j, txt_len, recv, keys, values, w_proj)
-    back = call(
-        fill_body, jax.ShapeDtypeStruct((32, 104, HD), bf16), 7, smem=(0, 1)
-    )(j, txt_len, img, p0, *got)
+
+    def image_half(half):
+        return call(
+            functools.partial(image_body, half),
+            [
+                jax.ShapeDtypeStruct((16, 40, HD), bf16),
+                pltpu.VMEM((w_proj.shape[0] // 2, d_model), bf16),
+            ],
+            6, smem=(0, 1), hbm=(5,), scratch=(pltpu.SemaphoreType.DMA,),
+        )(j, txt_len, recv, keys, values, w_proj)
+
+    got = lax.ppermute(send, "y", [(i, i ^ 2) for i in range(4)])
+    img0, w0 = image_half(0)
+    send, keep = call(
+        middle_body,
+        [jax.ShapeDtypeStruct((72, HD), bf16), jax.ShapeDtypeStruct((2, 64, HD), f32)],
+        2,
+    )(keep, got)
+    got = lax.ppermute(send, "y", [(i, i ^ 1) for i in range(4)])
+    img1, w1 = image_half(1)
+    back = call(fill_body, jax.ShapeDtypeStruct((32, 104, HD), bf16), 6, smem=(0, 1))(
+        j, txt_len, img0, img1, keep, got
+    )
     home = lax.all_to_all(back, CUBE, 0, 0, tiled=True)
     half = tokens // 2
     mine, other, txt_out = call(
@@ -317,8 +358,8 @@
             jax.ShapeDtypeStruct((half, d_model), bf16),
             jax.ShapeDtypeStruct((256, width), bf16),
         ],
-        3, smem=(0,), near=(2,),
-    )(core, home, w_near)
+        4, smem=(0,), near=(2, 3),
+    )(core, home, w0, w1)
     theirs = lax.ppermute(other, "tp", [(0, 1), (1, 0)])
     projected = mine + theirs.astype(f32)
     img_out = residual[0].astype(f32) + gate[None, :] * (projected + proj_bias[None, :])

time: 72.9 us -> 76.1 us (1.044)
  starting transfers between devices: 22.2 us -> 23.4 us
    ppermute x3 -> x2, starting transfers between devices: 4.24 us -> 5.09 us  [the longest x1 3.25 us: shards(): got = lax.ppermute(send, 'y', [(i, i ^ 2) for i in range(4)])]
    pallas_call x5 -> x7, Pallas kernels: 7.96 us -> 8.45 us  [run(): return kernel(*held)]
  transfers between devices with their start and end apart: 8 -> 7, of which waited for: 4 -> 4; matrix products, arithmetic and copies ran while one was open for 0% -> 0% of each run, Pallas kernels for 5% -> 6%
where the time goes in v5:
time: 76.1 us; the launch traced here: 75.7 us
  blocking collectives  33.5 us (44%)
  starting transfers between devices  23.4 us (31%)
  Pallas kernels  8.45 us (11%)
  waiting for transfers between devices  7.44 us (10%)
  between operations  1.38 us (2%)
  local copies, waits for them, and re-layouts  0.82 us (1%)
    all_to_all x1, blocking collectives, shards(): home = lax.all_to_all(back, CUBE, 0, 0, tiled=True)  22.1 us
    all_to_all x1, blocking collectives, shards(): kv = lax.all_to_all(kv_send, HEAD, 0, 0, tiled=True)  11.4 us
    pallas_call x7, Pallas kernels, run(): return kernel(*held)  8.45 us
    ppermute x3, starting transfers between devices, shards(): lax.ppermute(kv, 'zh', [(i, i ^ s) for i in range(4)])  7.39 us
    all_to_all x1, starting transfers between devices, shards(): recv = lax.all_to_all(q_send, CUBE, 0, 0, tiled=True)  5.58 us
    ppermute x1, starting transfers between devices, shards(): theirs = lax.ppermute(other, 'tp', [(0, 1), (1, 0)])  5.39 us
    ppermute x3, waiting for transfers between devices, shards(): lax.ppermute(kv, 'zh', [(i, i ^ s) for i in range(4)])  5.16 us
    ppermute x1, starting transfers between devices, shards(): got = lax.ppermute(send, 'y', [(i, i ^ 2) for i in range(4)])  3.25 us
  transfers between devices with their start and end apart: 7, of which 4 were waited for; matrix products, arithmetic and copies ran while one was open for 0% of the time, Pallas kernels for 6%

profile of v5, /device:TPU:1, one launch (start us, length us, event | category | flops | bytes accessed | tf_op | source)
XLA Modules:
  0.0 75.7 jit_solution(16881228114588671372)
XLA Ops:
  0.6 0.0 copy-start
  0.7 1.3 %shard_map.122 = (bf16[8,32,128]{2,1,0:T(8,128)(2,1)S(1)}, bf16[8,64,128]{2,1,0:T(8,128)(2,1)S(1)}) custom-call(bf16[3,32,1024]{2,1,0:T(8,128)(2,1)} %bitcast.16, s32[1,32]{1,0:T(1,128)} %frame_hbm, s32[1,32]{1,0:T(1,128)} %row_hbm.1, s32[1,32]{1,0:T(1,128)} %col_hbm.1, f32[8,128]{1,0:T(8,128)} %constant.26.clone.rate_hbm), custom_call_target="tpu_custom_call" | custom-call | tf_op jit(solution)/shard_map/pallas_call | solution.py:62
  2.0 11.4 %all_to_all.15.kv0_ref = bf16[8,64,128]{2,1,0:T(8,128)(2,1)S(1)} all-to-all(bf16[8,64,128]{2,1,0:T(8,128)(2,1)S(1)} %get-tuple-element.25), channel_id=1, replica_groups=mesh['zh'=4,'zl'=2,'x'=4,'y'=4,'tp'=2] {'zl','x'}, dimensions={0} | all-to-all | bytes 262144 | tf_op jit(solution)/shard_map/all_to_all | solution.py:317
  13.4 0.7 broadcast_in_dim.6
  14.2 5.6 %all-to-all-start.1 = ((bf16[32,32,128]{2,1,0:T(8,128)(2,1)}), bf16[32,32,128]{2,1,0:T(8,128)(2,1)S(1)}, u32[]{:S(2)}, u32[]{:S(2)}) async-start(bf16[32,32,128]{2,1,0:T(8,128)(2,1)} %bitcast.5), calls=%async_computation.1 | async-start | bytes 524288 | tf_op jit(solution)/shard_map/all_to_all | solution.py:321
  19.8 5.2 %collective-permute-start.2 = (bf16[8,64,128]{2,1,0:T(8,128)(2,1)S(1)}, bf16[8,64,128]{2,1,0:T(8,128)(2,1)S(1)}, u32[]{:S(2)}, u32[]{:S(2)}) collective-permute-start(bf16[8,64,128]{2,1,0:T(8,128)(2,1)S(1)} %all_to_all.15.kv0_ref), channel_id=1, source_target_pairs={{0,192},{64,128},{128,64},{192,0},{1,193},{65,129},{129,65},{193,1... | collective-permute-start | bytes 393224 | tf_op jit(solution)/shard_map/ppermute | solution.py:318
  25.0 1.2 %collective-permute-start.1 = (bf16[8,64,128]{2,1,0:T(8,128)(2,1)S(1)}, bf16[8,64,128]{2,1,0:T(8,128)(2,1)S(1)}, u32[]{:S(2)}, u32[]{:S(2)}) collective-permute-start(bf16[8,64,128]{2,1,0:T(8,128)(2,1)S(1)} %all_to_all.15.kv0_ref), channel_id=1, source_target_pairs={{0,128},{64,192},{128,0},{192,64},{1,129},{65,193},{129,1},{193,65... | collective-permute-start | bytes 393224 | tf_op jit(solution)/shard_map/ppermute | solution.py:318
  26.1 1.0 %collective-permute-start = (bf16[8,64,128]{2,1,0:T(8,128)(2,1)S(1)}, bf16[8,64,128]{2,1,0:T(8,128)(2,1)S(1)}, u32[]{:S(2)}, u32[]{:S(2)}) collective-permute-start(bf16[8,64,128]{2,1,0:T(8,128)(2,1)S(1)} %all_to_all.15.kv0_ref), channel_id=1, source_target_pairs={{0,64},{64,0},{128,192},{192,128},{1,65},{65,1},{129,193},{193,129... | collective-permute-start | bytes 393224 | tf_op jit(solution)/shard_map/ppermute | solution.py:318
  27.8 0.0 copy-done
  27.8 0.1 dynamic-slice_bitcast_fusion.txt_ref
  27.9 1.9 %collective-permute-done.2.kv3_ref = bf16[8,64,128]{2,1,0:T(8,128)(2,1)S(1)} collective-permute-done((bf16[8,64,128]{2,1,0:T(8,128)(2,1)S(1)}, bf16[8,64,128]{2,1,0:T(8,128)(2,1)S(1)}, u32[]{:S(2)}, u32[]{:S(2)}) %collective-permute-start.2) | collective-permute-done | bytes 131104 | tf_op jit(solution)/shard_map/ppermute | solution.py:318
  29.8 3.2 %collective-permute-done.1.kv2_ref = bf16[8,64,128]{2,1,0:T(8,128)(2,1)S(1)} collective-permute-done((bf16[8,64,128]{2,1,0:T(8,128)(2,1)S(1)}, bf16[8,64,128]{2,1,0:T(8,128)(2,1)S(1)}, u32[]{:S(2)}, u32[]{:S(2)}) %collective-permute-start.1) | collective-permute-done | bytes 131104 | tf_op jit(solution)/shard_map/ppermute | solution.py:318
  33.1 0.0 collective-permute-done.kv1_ref
  33.1 0.8 %shard_map.123 = (bf16[136,128]{1,0:T(8,128)(2,1)S(1)}, f32[2,128,128]{2,1,0:T(8,128)S(1)}, bf16[1152,128]{1,0:T(8,128)(2,1)S(1)}, bf16[1152,128]{1,0:T(8,128)(2,1)S(1)}) custom-call(s32[1]{0:T(128)} %bitcast.1.where_ref, s32[1]{0:T(128)S(6)} %copy.13.len_ref, bf16[8,64,128]{2,1,0:T(8,128)(2,1)S(1)} %all_to_all.15.kv0_ref, ...), custom_call_target="tpu_custom_call" | custom-call | tf_op jit(solution)/shard_map/pallas_call | solution.py:62
  33.9 3.2 %collective-permute-start.3 = (bf16[136,128]{1,0:T(8,128)(2,1)S(1)}, bf16[136,128]{1,0:T(8,128)(2,1)S(1)}, u32[]{:S(2)}, u32[]{:S(2)}) collective-permute-start(bf16[136,128]{1,0:T(8,128)(2,1)S(1)} %get-tuple-element.32), channel_id=1, source_target_pairs={{0,4},{2,6},{4,0},{6,2},{1,5},{3,7},{5,1},{7,3},{8,12},{10,14},{12... | collective-permute-start | bytes 104456 | tf_op jit(solution)/shard_map/ppermute | solution.py:340
  37.1 1.3 %collective-permute-done.3.got_ref = bf16[136,128]{1,0:T(8,128)(2,1)S(1)} collective-permute-done((bf16[136,128]{1,0:T(8,128)(2,1)S(1)}, bf16[136,128]{1,0:T(8,128)(2,1)S(1)}, u32[]{:S(2)}, u32[]{:S(2)}) %collective-permute-start.3) | collective-permute-done | bytes 34848 | tf_op jit(solution)/shard_map/ppermute | solution.py:340
  38.5 0.2 shard_map.126
  38.7 1.8 %collective-permute-start.4 = (bf16[72,128]{1,0:T(8,128)(2,1)S(1)}, bf16[72,128]{1,0:T(8,128)(2,1)S(1)}, u32[]{:S(2)}, u32[]{:S(2)}) collective-permute-start(bf16[72,128]{1,0:T(8,128)(2,1)S(1)} %get-tuple-element.34), channel_id=1, source_target_pairs={{0,2},{2,0},{4,6},{6,4},{1,3},{3,1},{5,7},{7,5},{8,10},{10,8},{12,... | collective-permute-start | bytes 55304 | tf_op jit(solution)/shard_map/ppermute | solution.py:347
  40.5 0.0 all-to-all-done.1.recv_ref
  40.5 1.9 %shard_map.125 = (bf16[16,40,128]{2,1,0:T(8,128)(2,1)S(1)}, bf16[512,3072]{1,0:T(8,128)(2,1)S(1)}) custom-call(s32[1]{0:T(128)} %bitcast.1.where_ref, s32[1]{0:T(128)S(6)} %copy.13.len_ref, bf16[32,32,128]{2,1,0:T(8,128)(2,1)S(1)} %all-to-all-done.1.recv_ref, bf16[1152,128]{1,0:T(8,128)(2,1)S(1)} %get-tuple-element.27.keys_ref, ...), custom_call_target="tpu_custom_call" | custom-call | tf_op jit(solution)/shard_map/pallas_call | solution.py:62
  42.4 1.9 %shard_map.124 = (bf16[16,40,128]{2,1,0:T(8,128)(2,1)S(1)}, bf16[512,3072]{1,0:T(8,128)(2,1)S(1)}) custom-call(s32[1]{0:T(128)} %bitcast.1.where_ref, s32[1]{0:T(128)S(6)} %copy.13.len_ref, bf16[32,32,128]{2,1,0:T(8,128)(2,1)S(1)} %all-to-all-done.1.recv_ref, bf16[1152,128]{1,0:T(8,128)(2,1)S(1)} %get-tuple-element.27.keys_ref, ...), custom_call_target="tpu_custom_call" | custom-call | tf_op jit(solution)/shard_map/pallas_call | solution.py:62
  44.4 0.0 collective-permute-done.4.got_ref
  44.4 0.1 shard_map.127
  44.5 22.1 %all_to_all.16.recv_ref = bf16[32,104,128]{2,1,0:T(8,128)(2,1)S(1)} all-to-all(bf16[32,104,128]{2,1,0:T(8,128)(2,1)S(1)} %shard_map.127), channel_id=1, replica_groups=mesh['zh'=4,'zl'=2,'x'=4,'y'=4,'tp'=2] {'zl','x','y'}, dimensions={0} | all-to-all | bytes 1703936 | tf_op jit(solution)/shard_map/all_to_all | solution.py:352
  66.6 0.0 copy-start.1
  66.6 0.0 copy-start.2
  66.6 0.0 copy-start.3
  66.6 2.1 %shard_map.128 = (f32[16,3072]{1,0:T(8,128)S(1)}, bf16[16,3072]{1,0:T(8,128)(2,1)S(1)}, bf16[256,1024]{1,0:T(8,128)(2,1)}) custom-call(s32[1]{0:T(128)} %bitcast.2.core_ref, bf16[32,104,128]{2,1,0:T(8,128)(2,1)S(1)} %all_to_all.16.recv_ref, bf16[512,3072]{1,0:T(8,128)(2,1)S(1)} %get-tuple-element.35.w0_ref, bf16[512,3072]{1,0:T(8,128)(2,1)S(1)} %get-tuple-element.36.w1_ref), custom_call_target="tpu_custom_call" | custom-call | tf_op jit(solution)/shard_map/pallas_call | solution.py:62
  68.7 5.4 %collective-permute-start.5 = (bf16[16,3072]{1,0:T(8,128)(2,1)S(1)}, bf16[16,3072]{1,0:T(8,128)(2,1)S(1)}, u32[]{:S(2)}, u32[]{:S(2)}) collective-permute-start(bf16[16,3072]{1,0:T(8,128)(2,1)S(1)} %get-tuple-element.38), channel_id=1, source_target_pairs={{0,1},{1,0},{2,3},{3,2},{4,5},{5,4},{6,7},{7,6},{8,9},{9,8},{10,11... | collective-permute-start | bytes 294920 | tf_op jit(solution)/shard_map/ppermute | solution.py:363
  74.1 0.9 %collective-permute-done.5 = bf16[16,3072]{1,0:T(8,128)(2,1)S(1)} collective-permute-done((bf16[16,3072]{1,0:T(8,128)(2,1)S(1)}, bf16[16,3072]{1,0:T(8,128)(2,1)S(1)}, u32[]{:S(2)}, u32[]{:S(2)}) %collective-permute-start.5) | collective-permute-done | bytes 98336 | tf_op jit(solution)/shard_map/ppermute | solution.py:363
  75.0 0.0 copy-done.1
  75.0 0.0 copy-done.2
  75.0 0.0 copy-done.3
  75.0 0.7 fusion.1
Async XLA Ops:
  0.6 27.2 %copy-start = (bf16[1,256,3,1024]{3,1,2,0:T(8,128)(2,1)S(1)}, bf16[1,256,3,1024]{3,1,2,0:T(8,128)(2,1)}, u32[]{:S(2)}) copy-start(bf16[1,256,3,1024]{3,1,2,0:T(8,128)(2,1)} %param.12) | copy-start | bytes 4718596
  14.2 26.3 %all-to-all-start.1 = ((bf16[32,32,128]{2,1,0:T(8,128)(2,1)}), bf16[32,32,128]{2,1,0:T(8,128)(2,1)S(1)}, u32[]{:S(2)}, u32[]{:S(2)}) async-start(bf16[32,32,128]{2,1,0:T(8,128)(2,1)} %bitcast.5), calls=%async_computation.1 | async-start | bytes 524288 | tf_op jit(solution)/shard_map/all_to_all | solution.py:321
  19.8 10.0 %collective-permute-start.2 = (bf16[8,64,128]{2,1,0:T(8,128)(2,1)S(1)}, bf16[8,64,128]{2,1,0:T(8,128)(2,1)S(1)}, u32[]{:S(2)}, u32[]{:S(2)}) collective-permute-start(bf16[8,64,128]{2,1,0:T(8,128)(2,1)S(1)} %all_to_all.15.kv0_ref), channel_id=1, source_target_pairs={{0,192},{64,128},{128,64},{192,0},{1,193},{65,129},{129,65},{193,1... | collective-permute-start | bytes 393224 | tf_op jit(solution)/shard_map/ppermute | solution.py:318
  25.0 8.1 %collective-permute-start.1 = (bf16[8,64,128]{2,1,0:T(8,128)(2,1)S(1)}, bf16[8,64,128]{2,1,0:T(8,128)(2,1)S(1)}, u32[]{:S(2)}, u32[]{:S(2)}) collective-permute-start(bf16[8,64,128]{2,1,0:T(8,128)(2,1)S(1)} %all_to_all.15.kv0_ref), channel_id=1, source_target_pairs={{0,128},{64,192},{128,0},{192,64},{1,129},{65,193},{129,1},{193,65... | collective-permute-start | bytes 393224 | tf_op jit(solution)/shard_map/ppermute | solution.py:318
  26.1 6.9 %collective-permute-start = (bf16[8,64,128]{2,1,0:T(8,128)(2,1)S(1)}, bf16[8,64,128]{2,1,0:T(8,128)(2,1)S(1)}, u32[]{:S(2)}, u32[]{:S(2)}) collective-permute-start(bf16[8,64,128]{2,1,0:T(8,128)(2,1)S(1)} %all_to_all.15.kv0_ref), channel_id=1, source_target_pairs={{0,64},{64,0},{128,192},{192,128},{1,65},{65,1},{129,193},{193,129... | collective-permute-start | bytes 393224 | tf_op jit(solution)/shard_map/ppermute | solution.py:318
  33.9 4.6 %collective-permute-start.3 = (bf16[136,128]{1,0:T(8,128)(2,1)S(1)}, bf16[136,128]{1,0:T(8,128)(2,1)S(1)}, u32[]{:S(2)}, u32[]{:S(2)}) collective-permute-start(bf16[136,128]{1,0:T(8,128)(2,1)S(1)} %get-tuple-element.32), channel_id=1, source_target_pairs={{0,4},{2,6},{4,0},{6,2},{1,5},{3,7},{5,1},{7,3},{8,12},{10,14},{12... | collective-permute-start | bytes 104456 | tf_op jit(solution)/shard_map/ppermute | solution.py:340
  38.7 5.7 %collective-permute-start.4 = (bf16[72,128]{1,0:T(8,128)(2,1)S(1)}, bf16[72,128]{1,0:T(8,128)(2,1)S(1)}, u32[]{:S(2)}, u32[]{:S(2)}) collective-permute-start(bf16[72,128]{1,0:T(8,128)(2,1)S(1)} %get-tuple-element.34), channel_id=1, source_target_pairs={{0,2},{2,0},{4,6},{6,4},{1,3},{3,1},{5,7},{7,5},{8,10},{10,8},{12,... | collective-permute-start | bytes 55304 | tf_op jit(solution)/shard_map/ppermute | solution.py:347
  66.6 8.5 %copy-start.1 = (bf16[1,16,3072]{2,1,0:T(8,128)(2,1)S(1)}, bf16[1,16,3072]{2,1,0:T(8,128)(2,1)}, u32[]{:S(2)}) copy-start(bf16[1,16,3072]{2,1,0:T(8,128)(2,1)} %param.17) | copy-start | bytes 294916
  66.6 8.5 %copy-start.2 = (f32[3072]{0:T(1024)S(1)}, f32[3072]{0:T(1024)}, u32[]{:S(2)}) copy-start(f32[3072]{0:T(1024)} %param.19) | copy-start | bytes 36868
  66.6 8.5 %copy-start.3 = (f32[3072]{0:T(1024)S(1)}, f32[3072]{0:T(1024)}, u32[]{:S(2)}) copy-start(f32[3072]{0:T(1024)} %param.20) | copy-start | bytes 36868
  68.7 6.3 %collective-permute-start.5 = (bf16[16,3072]{1,0:T(8,128)(2,1)S(1)}, bf16[16,3072]{1,0:T(8,128)(2,1)S(1)}, u32[]{:S(2)}, u32[]{:S(2)}) collective-permute-start(bf16[16,3072]{1,0:T(8,128)(2,1)S(1)} %get-tuple-element.38), channel_id=1, source_target_pairs={{0,1},{1,0},{2,3},{3,2},{4,5},{5,4},{6,7},{7,6},{8,9},{9,8},{10,11... | collective-permute-start | bytes 294920 | tf_op jit(solution)/shard_map/ppermute | solution.py:363

commit v6 on v5

--- a/solution.py
+++ b/solution.py
@@ -1,4 +1,3 @@
-import functools
 import math
 
 import jax
@@ -78,7 +77,7 @@
 
 
 def prep_body(
-    qkv_hbm, frame_hbm, row_hbm, col_hbm, rate_hbm, q_out, kv_out,
+    qkv_hbm, frame_hbm, row_hbm, col_hbm, rate_hbm, out_ref,
     qkv_ref, frame_ref, row_ref, col_ref, rate_ref, sems,
 ):
     copies = [
@@ -117,9 +116,9 @@
 
     for head in range(8):
         cols = slice(head * HD, (head + 1) * HD)
-        kv_out[head, 0:32, :] = rotate(qkv_ref[1, :, cols])
-        kv_out[head, 32:64, :] = qkv_ref[2, :, cols]
-        q_out[head] = rotate(qkv_ref[0, :, cols])
+        out_ref[head, 0:32, :] = rotate(qkv_ref[0, :, cols])
+        out_ref[head, 32:64, :] = rotate(qkv_ref[1, :, cols])
+        out_ref[head, 64:96, :] = qkv_ref[2, :, cols]
 
 
 def softmax_block(q, keys, values, live):
@@ -214,27 +213,34 @@
     return (outs[0] * first + outs[1] * second) / total, peak + jnp.log2(total)
 
 
-def image_body(
-    half, where_ref, len_ref, recv_ref, keys_ref, values_ref, w_hbm, out_ref, w_out, sem
-):
-    fetch = pltpu.make_async_copy(w_hbm.at[pl.ds(512 * half, 512)], w_out, sem)
-    fetch.start()
+def image_body(where_ref, len_ref, q0_ref, q1_ref, keys_ref, values_ref, out0_ref, out1_ref):
     live = live_mask(where_ref[0], len_ref[0])
     keys = keys_ref[...]
     values = values_ref[...]
     row = lax.broadcasted_iota(jnp.int32, (8, 32, 128), 1)
     lane = lax.broadcasted_iota(jnp.int32, (8, 32, 128), 2)
-    for b in range(2):
-        at = 16 * half + 8 * b
-        q = recv_ref[at : at + 8].reshape(256, HD)
-        out, lse = softmax_block(q, keys, values, live)
-        out_ref[8 * b : 8 * b + 8, 0:32, :] = out.astype(bf16).reshape(8, 32, HD)
+    for q_ref, out_ref in ((q0_ref, out0_ref), (q1_ref, out1_ref)):
+        out, lse = softmax_block(q_ref[...].reshape(256, HD), keys, values, live)
+        out_ref[:, 0:32, :] = out.astype(bf16).reshape(8, 32, HD)
         high, mid, low = three_parts(jnp.broadcast_to(lse, (256, 128)).reshape(8, 32, 128))
         parts = jnp.where(lane < 32, high, jnp.where(lane < 64, mid, low))
         packed = jnp.where(jnp.logical_and(row == lane % 32, lane < 96), parts, 0.0)
         packed = jnp.sum(packed, axis=1, keepdims=True)
-        out_ref[8 * b : 8 * b + 8, 32:40, :] = jnp.broadcast_to(packed, (8, 8, 128)).astype(bf16)
-    fetch.wait()
+        out_ref[:, 32:40, :] = jnp.broadcast_to(packed, (8, 8, 128)).astype(bf16)
+
+
+def weights_body(w_hbm, w_out, sems):
+    share = w_hbm.shape[0] // 8
+    copies = [
+        pltpu.make_async_copy(
+            w_hbm.at[pl.ds(share * i, share)], w_out.at[pl.ds(share * i, share)], sems.at[i]
+        )
+        for i in range(8)
+    ]
+    for c in copies:
+        c.start()
+    for c in copies:
+        c.wait()
 
 
 def blend(outs, lses):
@@ -251,20 +257,23 @@
     return mixed / total
 
 
-def fill_body(where_ref, len_ref, img0_ref, img1_ref, keep_ref, got_ref, out_ref):
+def fill_body(
+    where_ref, len_ref, img0_ref, img1_ref, img2_ref, img3_ref, keep_ref, got_ref, out_ref
+):
     row = lax.broadcasted_iota(jnp.int32, (64, 128), 0)
     outs = (keep_ref[0], got_ref[0:64, :].astype(f32))
     lses = (keep_ref[1], stat_column(got_ref[64:72, :].astype(f32), 64))
     text, _ = blend_pair(outs, lses)
     text = jnp.where(where_ref[0] * 64 + row < len_ref[0], text, 0.0).astype(bf16)
-    for d in range(32):
-        src = (img0_ref, img1_ref)[d // 16]
-        out_ref[d, 0:32, :] = src[d % 16, 0:32]
-        out_ref[d, 32:96, :] = text
-        out_ref[d, 96:104, :] = src[d % 16, 32:40]
-
-
-def tail_body(core_ref, recv_ref, w0_ref, w1_ref, mine_ref, other_ref, txt_ref):
+    for s, src in enumerate((img0_ref, img1_ref, img2_ref, img3_ref)):
+        for i in range(8):
+            d = 4 * i + (where_ref[0] ^ s)
+            out_ref[d, 0:32, :] = src[i, 0:32]
+            out_ref[d, 32:96, :] = text
+            out_ref[d, 96:104, :] = src[i, 32:40]
+
+
+def tail_body(core_ref, recv_ref, w_ref, mine_ref, other_ref, txt_ref):
     row = lax.broadcasted_iota(jnp.int32, (32, 128), 0)
     lane = lax.broadcasted_iota(jnp.int32, (32, 128), 1)
     pick = jnp.logical_and(row == lane % 32, lane < 96)
@@ -281,9 +290,7 @@
     rows = jnp.concatenate(heads, axis=1)
     flipped = jnp.concatenate([rows[16:32], rows[0:16]], axis=0)
     rows = jnp.where(core_ref[0] == 0, rows, flipped).astype(bf16)
-    projected = jnp.dot(rows[:, 0:512], w0_ref[...], preferred_element_type=f32) + jnp.dot(
-        rows[:, 512:1024], w1_ref[...], preferred_element_type=f32
-    )
+    projected = jnp.dot(rows, w_ref[...], preferred_element_type=f32)
     mine_ref[...] = projected[0:16]
     other_ref[...] = projected[16:32].astype(bf16)
 
@@ -301,9 +308,9 @@
     qkv = img_qkv.reshape(tokens, 3, width).transpose(1, 0, 2)
     txt = lax.dynamic_slice_in_dim(txt_qkv[0], head * HD, HD, 2).transpose(1, 0, 2)
 
-    q_mine, kv_send = call(
+    send = call(
         prep_body,
-        [jax.ShapeDtypeStruct((8, tokens, HD), bf16), jax.ShapeDtypeStruct((8, 64, HD), bf16)],
+        jax.ShapeDtypeStruct((8, 96, HD), bf16),
         5, hbm=(0, 1, 2, 3, 4),
         scratch=(
             pltpu.VMEM((3, tokens, width), bf16),
@@ -314,12 +321,15 @@
             pltpu.SemaphoreType.DMA((5,)),
         ),
     )(qkv, frame_index, row_index, column_index, jnp.asarray(rate_table()))
-    kv = lax.all_to_all(kv_send, HEAD, 0, 0, tiled=True)
+    recv = lax.all_to_all(send, HEAD, 0, 0, tiled=True)
+    kv = recv[:, 32:96]
+    q = recv[:, 0:32]
     others = [lax.ppermute(kv, "zh", [(i, i ^ s) for i in range(4)]) for s in (1, 2, 3)]
-    q_mine, _ = lax.optimization_barrier((q_mine, kv))
-    q_send = jnp.broadcast_to(q_mine[:, None], (8, 4, tokens, HD)).reshape(32, tokens, HD)
-    recv = lax.all_to_all(q_send, CUBE, 0, 0, tiled=True)
-
+    queries = [q] + [lax.ppermute(q, "y", [(i, i ^ s) for i in range(4)]) for s in (1, 2, 3)]
+    w_near = call(
+        weights_body, pltpu.VMEM(w_proj.shape, bf16), 1, hbm=(0,),
+        scratch=(pltpu.SemaphoreType.DMA((8,)),),
+    )(w_proj)
     keyed = jax.ShapeDtypeStruct((1152, HD), bf16)
     send, keep, keys, values = call(
         text_body,
@@ -327,27 +337,22 @@
         7, smem=(0, 1),
     )(j, txt_len, kv, *others, txt)
 
-    def image_half(half):
+    def image_half(q0, q1):
         return call(
-            functools.partial(image_body, half),
-            [
-                jax.ShapeDtypeStruct((16, 40, HD), bf16),
-                pltpu.VMEM((w_proj.shape[0] // 2, d_model), bf16),
-            ],
-            6, smem=(0, 1), hbm=(5,), scratch=(pltpu.SemaphoreType.DMA,),
-        )(j, txt_len, recv, keys, values, w_proj)
+            image_body, [jax.ShapeDtypeStruct((8, 40, HD), bf16)] * 2, 6, smem=(0, 1)
+        )(j, txt_len, q0, q1, keys, values)
 
     got = lax.ppermute(send, "y", [(i, i ^ 2) for i in range(4)])
-    img0, w0 = image_half(0)
+    img0, img1 = image_half(queries[0], queries[1])
     send, keep = call(
         middle_body,
         [jax.ShapeDtypeStruct((72, HD), bf16), jax.ShapeDtypeStruct((2, 64, HD), f32)],
         2,
     )(keep, got)
     got = lax.ppermute(send, "y", [(i, i ^ 1) for i in range(4)])
-    img1, w1 = image_half(1)
-    back = call(fill_body, jax.ShapeDtypeStruct((32, 104, HD), bf16), 6, smem=(0, 1))(
-        j, txt_len, img0, img1, keep, got
+    img2, img3 = image_half(queries[2], queries[3])
+    back = call(fill_body, jax.ShapeDtypeStruct((32, 104, HD), bf16), 8, smem=(0, 1))(
+        j, txt_len, img0, img1, img2, img3, keep, got
     )
     home = lax.all_to_all(back, CUBE, 0, 0, tiled=True)
     half = tokens // 2
@@ -358,8 +363,8 @@
             jax.ShapeDtypeStruct((half, d_model), bf16),
             jax.ShapeDtypeStruct((256, width), bf16),
         ],
-        4, smem=(0,), near=(2, 3),
-    )(core, home, w0, w1)
+        3, smem=(0,), near=(2,),
+    )(core, home, w_near)
     theirs = lax.ppermute(other, "tp", [(0, 1), (1, 0)])
     projected = mine + theirs.astype(f32)
     img_out = residual[0].astype(f32) + gate[None, :] * (projected + proj_bias[None, :])

time: 76.1 us -> 71.5 us (0.940)
  blocking collectives: 33.5 us -> 11.9 us
  waiting for transfers between devices: 7.44 us -> 15.2 us
  local copies, waits for them, and re-layouts: 0.82 us -> 5.53 us
  Pallas kernels: 8.45 us -> 11.2 us
  starting transfers between devices: 23.4 us -> 25.2 us
    all_to_all x2 -> x1, blocking collectives: 33.5 us -> 11.9 us  [shards(): recv = lax.all_to_all(send, HEAD, 0, 0, tiled=True)]
    unnamed x8 -> x12, local copies, waits for them, and re-layouts: 0.02 us -> 5.46 us
    all_to_all x1, waiting for transfers between devices: 0.01 us -> 5.2 us  [shards(): home = lax.all_to_all(back, CUBE, 0, 0, tiled=True)]
    ppermute x0 -> x3, starting transfers between devices: none -> 4.38 us  [shards(): lax.ppermute(q, 'y', [(i, i ^ s) for i in range(4)])]
    pallas_call x7 -> x8, Pallas kernels: 8.45 us -> 11.2 us  [run(): return kernel(*held)]
    ppermute x3, waiting for transfers between devices: 5.16 us -> 7.71 us  [shards(): lax.ppermute(kv, 'zh', [(i, i ^ s) for i in range(4)])]
    all_to_all x1, starting transfers between devices: 5.58 us -> 4.29 us  [shards(): home = lax.all_to_all(back, CUBE, 0, 0, tiled=True)]
  transfers between devices with their start and end apart: 7 -> 10, of which waited for: 4 -> 5; matrix products, arithmetic and copies ran while one was open for 0% -> 0% of each run, Pallas kernels for 6% -> 9%
where the time goes in v6:
time: 71.5 us; the launch traced here: 71.2 us
  starting transfers between devices  25.2 us (35%)
  waiting for transfers between devices  15.2 us (21%)
  blocking collectives  11.9 us (17%)
  Pallas kernels  11.2 us (16%)
  local copies, waits for them, and re-layouts  5.53 us (8%)
  between operations  1.41 us (2%)
    all_to_all x1, blocking collectives, shards(): recv = lax.all_to_all(send, HEAD, 0, 0, tiled=True)  11.9 us
    pallas_call x8, Pallas kernels, run(): return kernel(*held)  11.2 us
    ppermute x3, waiting for transfers between devices, shards(): lax.ppermute(kv, 'zh', [(i, i ^ s) for i in range(4)])  7.71 us
    ppermute x3, starting transfers between devices, shards(): lax.ppermute(kv, 'zh', [(i, i ^ s) for i in range(4)])  7.39 us
    unnamed x12, local copies, waits for them, and re-layouts  5.46 us
    all_to_all x1, waiting for transfers between devices, shards(): home = lax.all_to_all(back, CUBE, 0, 0, tiled=True)  5.2 us
    ppermute x1, starting transfers between devices, shards(): theirs = lax.ppermute(other, 'tp', [(0, 1), (1, 0)])  4.8 us
    ppermute x3, starting transfers between devices, shards(): lax.ppermute(q, 'y', [(i, i ^ s) for i in range(4)])  4.38 us
  transfers between devices with their start and end apart: 10, of which 5 were waited for; matrix products, arithmetic and copies ran while one was open for 0% of the time, Pallas kernels for 9%

profile of v6, /device:TPU:1, one launch (start us, length us, event | category | flops | bytes accessed | tf_op | source)
XLA Modules:
  0.0 71.2 jit_solution(9068818309500248849)
XLA Ops:
  0.6 0.0 copy-start
  0.7 1.3 %shard_map.122 = bf16[8,96,128]{2,1,0:T(8,128)(2,1)S(1)} custom-call(bf16[3,32,1024]{2,1,0:T(8,128)(2,1)} %bitcast.15, s32[1,32]{1,0:T(1,128)} %frame_hbm, s32[1,32]{1,0:T(1,128)} %row_hbm.1, s32[1,32]{1,0:T(1,128)} %col_hbm.1, f32[8,128]{1,0:T(8,128)} %constant.26.clone.rate_hbm), custom_call_target="tpu_custom_call" | custom-call | tf_op jit(solution)/shard_map/pallas_call | solution.py:61
  2.0 11.9 %all_to_all.10 = bf16[8,96,128]{2,1,0:T(8,128)(2,1)S(1)} all-to-all(bf16[8,96,128]{2,1,0:T(8,128)(2,1)S(1)} %shard_map.122), channel_id=1, replica_groups=mesh['zh'=4,'zl'=2,'x'=4,'y'=4,'tp'=2] {'zl','x'}, dimensions={0} | all-to-all | bytes 393216 | tf_op jit(solution)/shard_map/all_to_all | solution.py:324
  13.9 5.2 %collective-permute-start.3 = (bf16[8,64,128]{2,1,0:T(8,128)(2,1)S(1)}, bf16[8,64,128]{2,1,0:T(8,128)(2,1)S(1)}, u32[]{:S(2)}, u32[]{:S(2)}) collective-permute-start(bf16[8,64,128]{2,1,0:T(8,128)(2,1)S(1)} %slice.9.kv0_ref), channel_id=1, source_target_pairs={{0,192},{64,128},{128,64},{192,0},{1,193},{65,129},{129,65},{193,1... | collective-permute-start | bytes 393224 | tf_op jit(solution)/shard_map/ppermute | solution.py:327
  19.1 1.2 %collective-permute-start.2 = (bf16[8,64,128]{2,1,0:T(8,128)(2,1)S(1)}, bf16[8,64,128]{2,1,0:T(8,128)(2,1)S(1)}, u32[]{:S(2)}, u32[]{:S(2)}) collective-permute-start(bf16[8,64,128]{2,1,0:T(8,128)(2,1)S(1)} %slice.9.kv0_ref), channel_id=1, source_target_pairs={{0,128},{64,192},{128,0},{192,64},{1,129},{65,193},{129,1},{193,65... | collective-permute-start | bytes 393224 | tf_op jit(solution)/shard_map/ppermute | solution.py:327
  20.3 1.0 %collective-permute-start.1 = (bf16[8,64,128]{2,1,0:T(8,128)(2,1)S(1)}, bf16[8,64,128]{2,1,0:T(8,128)(2,1)S(1)}, u32[]{:S(2)}, u32[]{:S(2)}) collective-permute-start(bf16[8,64,128]{2,1,0:T(8,128)(2,1)S(1)} %slice.9.kv0_ref), channel_id=1, source_target_pairs={{0,64},{64,0},{128,192},{192,128},{1,65},{65,1},{129,193},{193,129... | collective-permute-start | bytes 393224 | tf_op jit(solution)/shard_map/ppermute | solution.py:327
  21.3 2.7 %collective-permute-start.5 = (bf16[8,32,128]{2,1,0:T(8,128)(2,1)S(1)}, bf16[8,32,128]{2,1,0:T(8,128)(2,1)S(1)}, u32[]{:S(2)}, u32[]{:S(2)}) collective-permute-start(bf16[8,32,128]{2,1,0:T(8,128)(2,1)S(1)} %slice.8.q0_ref), channel_id=1, source_target_pairs={{0,6},{2,4},{4,2},{6,0},{1,7},{3,5},{5,3},{7,1},{8,14},{10,12},{12... | collective-permute-start | bytes 196616 | tf_op jit(solution)/shard_map/ppermute | solution.py:328
  24.0 0.3 collective-permute-start.4
  24.4 6.0 %collective-permute-done.3.kv3_ref = bf16[8,64,128]{2,1,0:T(8,128)(2,1)S(1)} collective-permute-done((bf16[8,64,128]{2,1,0:T(8,128)(2,1)S(1)}, bf16[8,64,128]{2,1,0:T(8,128)(2,1)S(1)}, u32[]{:S(2)}, u32[]{:S(2)}) %collective-permute-start.3) | collective-permute-done | bytes 131104 | tf_op jit(solution)/shard_map/ppermute | solution.py:327
  30.4 1.3 %collective-permute-start = (bf16[8,32,128]{2,1,0:T(8,128)(2,1)S(1)}, bf16[8,32,128]{2,1,0:T(8,128)(2,1)S(1)}, u32[]{:S(2)}, u32[]{:S(2)}) collective-permute-start(bf16[8,32,128]{2,1,0:T(8,128)(2,1)S(1)} %slice.8.q0_ref), channel_id=1, source_target_pairs={{0,2},{2,0},{4,6},{6,4},{1,3},{3,1},{5,7},{7,5},{8,10},{10,8},{12,... | collective-permute-start | bytes 196616 | tf_op jit(solution)/shard_map/ppermute | solution.py:328
  31.7 0.0 copy-done
  31.7 0.1 dynamic-slice_bitcast_fusion.txt_ref
  32.4 0.0 collective-permute-done.2.kv2_ref
  32.4 1.7 %collective-permute-done.1.kv1_ref = bf16[8,64,128]{2,1,0:T(8,128)(2,1)S(1)} collective-permute-done((bf16[8,64,128]{2,1,0:T(8,128)(2,1)S(1)}, bf16[8,64,128]{2,1,0:T(8,128)(2,1)S(1)}, u32[]{:S(2)}, u32[]{:S(2)}) %collective-permute-start.1) | collective-permute-done | bytes 131104 | tf_op jit(solution)/shard_map/ppermute | solution.py:327
  34.1 0.8 %shard_map.123 = (bf16[136,128]{1,0:T(8,128)(2,1)S(1)}, f32[2,128,128]{2,1,0:T(8,128)S(1)}, bf16[1152,128]{1,0:T(8,128)(2,1)S(1)}, bf16[1152,128]{1,0:T(8,128)(2,1)S(1)}) custom-call(s32[1]{0:T(128)} %bitcast.1.where_ref, s32[1]{0:T(128)S(6)} %copy.13.len_ref, bf16[8,64,128]{2,1,0:T(8,128)(2,1)S(1)} %slice.9.kv0_ref, ...), custom_call_target="tpu_custom_call" | custom-call | tf_op jit(solution)/shard_map/pallas_call | solution.py:61
  34.9 3.0 %collective-permute-start.6 = (bf16[136,128]{1,0:T(8,128)(2,1)S(1)}, bf16[136,128]{1,0:T(8,128)(2,1)S(1)}, u32[]{:S(2)}, u32[]{:S(2)}) collective-permute-start(bf16[136,128]{1,0:T(8,128)(2,1)S(1)} %get-tuple-element.28), channel_id=1, source_target_pairs={{0,4},{2,6},{4,0},{6,2},{1,5},{3,7},{5,1},{7,3},{8,12},{10,14},{12... | collective-permute-start | bytes 104456 | tf_op jit(solution)/shard_map/ppermute | solution.py:345
  37.9 1.4 %collective-permute-done.6.got_ref = bf16[136,128]{1,0:T(8,128)(2,1)S(1)} collective-permute-done((bf16[136,128]{1,0:T(8,128)(2,1)S(1)}, bf16[136,128]{1,0:T(8,128)(2,1)S(1)}, u32[]{:S(2)}, u32[]{:S(2)}) %collective-permute-start.6) | collective-permute-done | bytes 34848 | tf_op jit(solution)/shard_map/ppermute | solution.py:345
  39.3 0.2 shard_map.126
  39.5 1.4 %collective-permute-start.7 = (bf16[72,128]{1,0:T(8,128)(2,1)S(1)}, bf16[72,128]{1,0:T(8,128)(2,1)S(1)}, u32[]{:S(2)}, u32[]{:S(2)}) collective-permute-start(bf16[72,128]{1,0:T(8,128)(2,1)S(1)} %get-tuple-element.30), channel_id=1, source_target_pairs={{0,2},{2,0},{4,6},{6,4},{1,3},{3,1},{5,7},{7,5},{8,10},{10,8},{12,... | collective-permute-start | bytes 55304 | tf_op jit(solution)/shard_map/ppermute | solution.py:352
  40.9 0.0 collective-permute-done.q1_ref
  40.9 1.4 %shard_map.124 = (bf16[8,40,128]{2,1,0:T(8,128)(2,1)S(1)}, bf16[8,40,128]{2,1,0:T(8,128)(2,1)S(1)}) custom-call(s32[1]{0:T(128)} %bitcast.1.where_ref, s32[1]{0:T(128)S(6)} %copy.13.len_ref, bf16[8,32,128]{2,1,0:T(8,128)(2,1)S(1)} %slice.8.q0_ref, bf16[8,32,128]{2,1,0:T(8,128)(2,1)S(1)} %collective-permute-done.q1_ref, ...), custom_call_target="tpu_custom_call" | custom-call | tf_op jit(solution)/shard_map/pallas_call | solution.py:61
  42.3 0.0 collective-permute-done.5.q1_ref
  42.3 0.0 collective-permute-done.4.q0_ref
  42.3 1.4 %shard_map.125 = (bf16[8,40,128]{2,1,0:T(8,128)(2,1)S(1)}, bf16[8,40,128]{2,1,0:T(8,128)(2,1)S(1)}) custom-call(s32[1]{0:T(128)} %bitcast.1.where_ref, s32[1]{0:T(128)S(6)} %copy.13.len_ref, bf16[8,32,128]{2,1,0:T(8,128)(2,1)S(1)} %collective-permute-done.4.q0_ref, bf16[8,32,128]{2,1,0:T(8,128)(2,1)S(1)} %collective-permute-done.5.q1_ref, ...), custom_call_target="tpu_custom_call" | custom-call | tf_op jit(solution)/shard_map/pallas_call | solution.py:61
  43.7 0.0 collective-permute-done.7.got_ref
  43.7 1.1 %shard_map.127 = bf16[32,104,128]{2,1,0:T(8,128)(2,1)} custom-call(s32[1]{0:T(128)} %bitcast.1.where_ref, s32[1]{0:T(128)S(6)} %copy.13.len_ref, bf16[8,40,128]{2,1,0:T(8,128)(2,1)S(1)} %get-tuple-element.23.img0_ref, bf16[8,40,128]{2,1,0:T(8,128)(2,1)S(1)} %get-tuple-element.24.img1_ref, bf16[8,40,128]{2,1,0:T(8,128)(2,1)S(1)} %get-tuple-element.25.img2_ref, ...), custom_call_target="tpu_custom_call" | custom-call | tf_op jit(solution)/shard_map/pallas_call | solution.py:61
  44.8 4.3 %all-to-all-start.1 = ((bf16[32,104,128]{2,1,0:T(8,128)(2,1)}), bf16[32,104,128]{2,1,0:T(8,128)(2,1)S(1)}, u32[]{:S(2)}, u32[]{:S(2)}) async-start(bf16[32,104,128]{2,1,0:T(8,128)(2,1)} %shard_map.127), calls=%async_computation.1 | async-start | bytes 1703936 | tf_op jit(solution)/shard_map/all_to_all | solution.py:357
  49.1 2.9 %shard_map.128.w_ref = bf16[1024,3072]{1,0:T(8,128)(2,1)S(1)} custom-call(bf16[1024,3072]{1,0:T(8,128)(2,1)} %w_hbm.1), custom_call_target="tpu_custom_call" | custom-call | tf_op jit(solution)/shard_map/pallas_call | solution.py:61
  51.9 0.0 copy-start.1
  52.0 2.7 %copy-done.1 = bf16[1024,3072]{1,0:T(8,128)(2,1)} copy-done((bf16[1024,3072]{1,0:T(8,128)(2,1)}, bf16[1024,3072]{1,0:T(8,128)(2,1)S(1)}, u32[]{:S(2)}) %copy-start.1) | copy-done | bytes 6291480
  54.6 5.2 %all-to-all-done.1.recv_ref = bf16[32,104,128]{2,1,0:T(8,128)(2,1)S(1)} async-done(((bf16[32,104,128]{2,1,0:T(8,128)(2,1)}), bf16[32,104,128]{2,1,0:T(8,128)(2,1)S(1)}, u32[]{:S(2)}, u32[]{:S(2)}) %all-to-all-start.1) | async-done | bytes 852000 | tf_op jit(solution)/shard_map/all_to_all | solution.py:357
  59.8 0.0 copy-start.2
  59.8 2.8 %copy-done.2 = bf16[1024,3072]{1,0:T(8,128)(2,1)S(1)} copy-done((bf16[1024,3072]{1,0:T(8,128)(2,1)S(1)}, bf16[1024,3072]{1,0:T(8,128)(2,1)}, u32[]{:S(2)}) %copy-start.2) | copy-done | bytes 6291480
  62.6 0.0 copy-start.3
  62.6 0.0 copy-start.4
  62.6 0.0 copy-start.5
  62.6 2.1 %shard_map.129 = (f32[16,3072]{1,0:T(8,128)S(1)}, bf16[16,3072]{1,0:T(8,128)(2,1)S(1)}, bf16[256,1024]{1,0:T(8,128)(2,1)}) custom-call(s32[1]{0:T(128)} %bitcast.2.core_ref, bf16[32,104,128]{2,1,0:T(8,128)(2,1)S(1)} %all-to-all-done.1.recv_ref, bf16[1024,3072]{1,0:T(8,128)(2,1)S(1)} %copy-done.2), custom_call_target="tpu_custom_call" | custom-call | tf_op jit(solution)/shard_map/pallas_call | solution.py:61
  64.7 4.8 %collective-permute-start.8 = (bf16[16,3072]{1,0:T(8,128)(2,1)S(1)}, bf16[16,3072]{1,0:T(8,128)(2,1)S(1)}, u32[]{:S(2)}, u32[]{:S(2)}) collective-permute-start(bf16[16,3072]{1,0:T(8,128)(2,1)S(1)} %get-tuple-element.32), channel_id=1, source_target_pairs={{0,1},{1,0},{2,3},{3,2},{4,5},{5,4},{6,7},{7,6},{8,9},{9,8},{10,11... | collective-permute-start | bytes 294920 | tf_op jit(solution)/shard_map/ppermute | solution.py:368
  69.5 0.9 %collective-permute-done.8 = bf16[16,3072]{1,0:T(8,128)(2,1)S(1)} collective-permute-done((bf16[16,3072]{1,0:T(8,128)(2,1)S(1)}, bf16[16,3072]{1,0:T(8,128)(2,1)S(1)}, u32[]{:S(2)}, u32[]{:S(2)}) %collective-permute-start.8) | collective-permute-done | bytes 98336 | tf_op jit(solution)/shard_map/ppermute | solution.py:368
  70.5 0.0 copy-done.3
  70.5 0.0 copy-done.4
  70.5 0.0 copy-done.5
  70.5 0.7 fusion.1
  (2 shorter events, 0.0 us)
Async XLA Ops:
  0.6 31.0 %copy-start = (bf16[1,256,3,1024]{3,1,2,0:T(8,128)(2,1)S(1)}, bf16[1,256,3,1024]{3,1,2,0:T(8,128)(2,1)}, u32[]{:S(2)}) copy-start(bf16[1,256,3,1024]{3,1,2,0:T(8,128)(2,1)} %param.12) | copy-start | bytes 4718596
  13.9 16.5 %collective-permute-start.3 = (bf16[8,64,128]{2,1,0:T(8,128)(2,1)S(1)}, bf16[8,64,128]{2,1,0:T(8,128)(2,1)S(1)}, u32[]{:S(2)}, u32[]{:S(2)}) collective-permute-start(bf16[8,64,128]{2,1,0:T(8,128)(2,1)S(1)} %slice.9.kv0_ref), channel_id=1, source_target_pairs={{0,192},{64,128},{128,64},{192,0},{1,193},{65,129},{129,65},{193,1... | collective-permute-start | bytes 393224 | tf_op jit(solution)/shard_map/ppermute | solution.py:327
  19.1 13.3 %collective-permute-start.2 = (bf16[8,64,128]{2,1,0:T(8,128)(2,1)S(1)}, bf16[8,64,128]{2,1,0:T(8,128)(2,1)S(1)}, u32[]{:S(2)}, u32[]{:S(2)}) collective-permute-start(bf16[8,64,128]{2,1,0:T(8,128)(2,1)S(1)} %slice.9.kv0_ref), channel_id=1, source_target_pairs={{0,128},{64,192},{128,0},{192,64},{1,129},{65,193},{129,1},{193,65... | collective-permute-start | bytes 393224 | tf_op jit(solution)/shard_map/ppermute | solution.py:327
  20.3 13.8 %collective-permute-start.1 = (bf16[8,64,128]{2,1,0:T(8,128)(2,1)S(1)}, bf16[8,64,128]{2,1,0:T(8,128)(2,1)S(1)}, u32[]{:S(2)}, u32[]{:S(2)}) collective-permute-start(bf16[8,64,128]{2,1,0:T(8,128)(2,1)S(1)} %slice.9.kv0_ref), channel_id=1, source_target_pairs={{0,64},{64,0},{128,192},{192,128},{1,65},{65,1},{129,193},{193,129... | collective-permute-start | bytes 393224 | tf_op jit(solution)/shard_map/ppermute | solution.py:327
  21.3 21.0 %collective-permute-start.5 = (bf16[8,32,128]{2,1,0:T(8,128)(2,1)S(1)}, bf16[8,32,128]{2,1,0:T(8,128)(2,1)S(1)}, u32[]{:S(2)}, u32[]{:S(2)}) collective-permute-start(bf16[8,32,128]{2,1,0:T(8,128)(2,1)S(1)} %slice.8.q0_ref), channel_id=1, source_target_pairs={{0,6},{2,4},{4,2},{6,0},{1,7},{3,5},{5,3},{7,1},{8,14},{10,12},{12... | collective-permute-start | bytes 196616 | tf_op jit(solution)/shard_map/ppermute | solution.py:328
  24.0 18.3 %collective-permute-start.4 = (bf16[8,32,128]{2,1,0:T(8,128)(2,1)S(1)}, bf16[8,32,128]{2,1,0:T(8,128)(2,1)S(1)}, u32[]{:S(2)}, u32[]{:S(2)}) collective-permute-start(bf16[8,32,128]{2,1,0:T(8,128)(2,1)S(1)} %slice.8.q0_ref), channel_id=1, source_target_pairs={{0,4},{2,6},{4,0},{6,2},{1,5},{3,7},{5,1},{7,3},{8,12},{10,14},{12... | collective-permute-start | bytes 196616 | tf_op jit(solution)/shard_map/ppermute | solution.py:328
  30.4 10.5 %collective-permute-start = (bf16[8,32,128]{2,1,0:T(8,128)(2,1)S(1)}, bf16[8,32,128]{2,1,0:T(8,128)(2,1)S(1)}, u32[]{:S(2)}, u32[]{:S(2)}) collective-permute-start(bf16[8,32,128]{2,1,0:T(8,128)(2,1)S(1)} %slice.8.q0_ref), channel_id=1, source_target_pairs={{0,2},{2,0},{4,6},{6,4},{1,3},{3,1},{5,7},{7,5},{8,10},{10,8},{12,... | collective-permute-start | bytes 196616 | tf_op jit(solution)/shard_map/ppermute | solution.py:328
  34.9 4.4 %collective-permute-start.6 = (bf16[136,128]{1,0:T(8,128)(2,1)S(1)}, bf16[136,128]{1,0:T(8,128)(2,1)S(1)}, u32[]{:S(2)}, u32[]{:S(2)}) collective-permute-start(bf16[136,128]{1,0:T(8,128)(2,1)S(1)} %get-tuple-element.28), channel_id=1, source_target_pairs={{0,4},{2,6},{4,0},{6,2},{1,5},{3,7},{5,1},{7,3},{8,12},{10,14},{12... | collective-permute-start | bytes 104456 | tf_op jit(solution)/shard_map/ppermute | solution.py:345
  39.5 4.1 %collective-permute-start.7 = (bf16[72,128]{1,0:T(8,128)(2,1)S(1)}, bf16[72,128]{1,0:T(8,128)(2,1)S(1)}, u32[]{:S(2)}, u32[]{:S(2)}) collective-permute-start(bf16[72,128]{1,0:T(8,128)(2,1)S(1)} %get-tuple-element.30), channel_id=1, source_target_pairs={{0,2},{2,0},{4,6},{6,4},{1,3},{3,1},{5,7},{7,5},{8,10},{10,8},{12,... | collective-permute-start | bytes 55304 | tf_op jit(solution)/shard_map/ppermute | solution.py:352
  44.8 15.0 %all-to-all-start.1 = ((bf16[32,104,128]{2,1,0:T(8,128)(2,1)}), bf16[32,104,128]{2,1,0:T(8,128)(2,1)S(1)}, u32[]{:S(2)}, u32[]{:S(2)}) async-start(bf16[32,104,128]{2,1,0:T(8,128)(2,1)} %shard_map.127), calls=%async_computation.1 | async-start | bytes 1703936 | tf_op jit(solution)/shard_map/all_to_all | solution.py:357
  51.9 2.7 %copy-start.1 = (bf16[1024,3072]{1,0:T(8,128)(2,1)}, bf16[1024,3072]{1,0:T(8,128)(2,1)S(1)}, u32[]{:S(2)}) copy-start(bf16[1024,3072]{1,0:T(8,128)(2,1)S(1)} %shard_map.128.w_ref) | copy-start | bytes 18874372
  59.8 2.8 %copy-start.2 = (bf16[1024,3072]{1,0:T(8,128)(2,1)S(1)}, bf16[1024,3072]{1,0:T(8,128)(2,1)}, u32[]{:S(2)}) copy-start(bf16[1024,3072]{1,0:T(8,128)(2,1)} %copy-done.1) | copy-start | bytes 18874372
  62.6 7.9 %copy-start.3 = (bf16[1,16,3072]{2,1,0:T(8,128)(2,1)S(1)}, bf16[1,16,3072]{2,1,0:T(8,128)(2,1)}, u32[]{:S(2)}) copy-start(bf16[1,16,3072]{2,1,0:T(8,128)(2,1)} %param.17) | copy-start | bytes 294916
  62.6 7.9 %copy-start.4 = (f32[3072]{0:T(1024)S(1)}, f32[3072]{0:T(1024)}, u32[]{:S(2)}) copy-start(f32[3072]{0:T(1024)} %param.19) | copy-start | bytes 36868
  62.6 7.9 %copy-start.5 = (f32[3072]{0:T(1024)S(1)}, f32[3072]{0:T(1024)}, u32[]{:S(2)}) copy-start(f32[3072]{0:T(1024)} %param.20) | copy-start | bytes 36868
  64.7 5.7 %collective-permute-start.8 = (bf16[16,3072]{1,0:T(8,128)(2,1)S(1)}, bf16[16,3072]{1,0:T(8,128)(2,1)S(1)}, u32[]{:S(2)}, u32[]{:S(2)}) collective-permute-start(bf16[16,3072]{1,0:T(8,128)(2,1)S(1)} %get-tuple-element.32), channel_id=1, source_target_pairs={{0,1},{1,0},{2,3},{3,2},{4,5},{5,4},{6,7},{7,6},{8,9},{9,8},{10,11... | collective-permute-start | bytes 294920 | tf_op jit(solution)/shard_map/ppermute | solution.py:368

commit v7 on v3

--- a/solution.py
+++ b/solution.py
@@ -77,7 +77,7 @@
 
 
 def prep_body(
-    qkv_hbm, frame_hbm, row_hbm, col_hbm, rate_hbm, q_out, kv_out,
+    qkv_hbm, frame_hbm, row_hbm, col_hbm, rate_hbm, out_ref,
     qkv_ref, frame_ref, row_ref, col_ref, rate_ref, sems,
 ):
     copies = [
@@ -116,11 +116,9 @@
 
     for head in range(8):
         cols = slice(head * HD, (head + 1) * HD)
-        kv_out[head, 0:32, :] = rotate(qkv_ref[1, :, cols])
-        kv_out[head, 32:64, :] = qkv_ref[2, :, cols]
-        query = rotate(qkv_ref[0, :, cols])
-        for j in range(4):
-            q_out[head * 4 + j] = query
+        out_ref[head, 0:32, :] = rotate(qkv_ref[0, :, cols])
+        out_ref[head, 32:64, :] = rotate(qkv_ref[1, :, cols])
+        out_ref[head, 64:96, :] = qkv_ref[2, :, cols]
 
 
 def softmax_block(q, keys, values, live):
@@ -186,25 +184,36 @@
 
 
 def image_body(
-    where_ref, len_ref, recv_ref, keys_ref, values_ref, w_hbm, out_ref, w_out, sem
-):
-    fetch = pltpu.make_async_copy(w_hbm, w_out, sem)
-    fetch.start()
+    where_ref, len_ref, q0_ref, q1_ref, q2_ref, q3_ref, keys_ref, values_ref, out_ref
+):
     live = live_mask(where_ref[0], len_ref[0])
     keys = keys_ref[...]
     values = values_ref[...]
     row = lax.broadcasted_iota(jnp.int32, (8, 32, 128), 1)
     lane = lax.broadcasted_iota(jnp.int32, (8, 32, 128), 2)
-    for b in range(4):
-        q = recv_ref[8 * b : 8 * b + 8].reshape(256, HD)
-        out, lse = softmax_block(q, keys, values, live)
-        out_ref[8 * b : 8 * b + 8, 0:32, :] = out.astype(bf16).reshape(8, 32, HD)
+    for s, q_ref in enumerate((q0_ref, q1_ref, q2_ref, q3_ref)):
+        out, lse = softmax_block(q_ref[...].reshape(256, HD), keys, values, live)
+        at = slice(8 * s, 8 * s + 8)
+        out_ref[at, 0:32, :] = out.astype(bf16).reshape(8, 32, HD)
         high, mid, low = three_parts(jnp.broadcast_to(lse, (256, 128)).reshape(8, 32, 128))
         parts = jnp.where(lane < 32, high, jnp.where(lane < 64, mid, low))
         packed = jnp.where(jnp.logical_and(row == lane % 32, lane < 96), parts, 0.0)
         packed = jnp.sum(packed, axis=1, keepdims=True)
-        out_ref[8 * b : 8 * b + 8, 32:40, :] = jnp.broadcast_to(packed, (8, 8, 128)).astype(bf16)
-    fetch.wait()
+        out_ref[at, 32:40, :] = jnp.broadcast_to(packed, (8, 8, 128)).astype(bf16)
+
+
+def weights_body(w_hbm, w_out, sems):
+    share = w_hbm.shape[0] // 8
+    copies = [
+        pltpu.make_async_copy(
+            w_hbm.at[pl.ds(share * i, share)], w_out.at[pl.ds(share * i, share)], sems.at[i]
+        )
+        for i in range(8)
+    ]
+    for c in copies:
+        c.start()
+    for c in copies:
+        c.wait()
 
 
 def blend(outs, lses):
@@ -232,10 +241,12 @@
         lses.append(jnp.sum(picked, axis=1, keepdims=True))
     text = blend(outs, lses)
     text = jnp.where(where_ref[0] * 64 + row < len_ref[0], text, 0.0).astype(bf16)
-    for d in range(32):
-        out_ref[d, 0:32, :] = img_ref[d, 0:32]
-        out_ref[d, 32:96, :] = text
-        out_ref[d, 96:104, :] = img_ref[d, 32:40]
+    for s in range(4):
+        for i in range(8):
+            d = 4 * i + (where_ref[0] ^ s)
+            out_ref[d, 0:32, :] = img_ref[8 * s + i, 0:32]
+            out_ref[d, 32:96, :] = text
+            out_ref[d, 96:104, :] = img_ref[8 * s + i, 32:40]
 
 
 def tail_body(core_ref, recv_ref, w_ref, mine_ref, other_ref, txt_ref):
@@ -273,9 +284,9 @@
     qkv = img_qkv.reshape(tokens, 3, width).transpose(1, 0, 2)
     txt = lax.dynamic_slice_in_dim(txt_qkv[0], head * HD, HD, 2).transpose(1, 0, 2)
 
-    q_send, kv_send = call(
+    send = call(
         prep_body,
-        [jax.ShapeDtypeStruct((32, 32, HD), bf16), jax.ShapeDtypeStruct((8, 64, HD), bf16)],
+        jax.ShapeDtypeStruct((8, 96, HD), bf16),
         5, hbm=(0, 1, 2, 3, 4),
         scratch=(
             pltpu.VMEM((3, tokens, width), bf16),
@@ -286,11 +297,15 @@
             pltpu.SemaphoreType.DMA((5,)),
         ),
     )(qkv, frame_index, row_index, column_index, jnp.asarray(rate_table()))
-    kv = lax.all_to_all(kv_send, HEAD, 0, 0, tiled=True)
+    recv = lax.all_to_all(send, HEAD, 0, 0, tiled=True)
+    kv = recv[:, 32:96]
+    q = recv[:, 0:32]
     others = [lax.ppermute(kv, "zh", [(i, i ^ s) for i in range(4)]) for s in (1, 2, 3)]
-    q_send, _ = lax.optimization_barrier((q_send, kv))
-    recv = lax.all_to_all(q_send, CUBE, 0, 0, tiled=True)
-
+    queries = [q] + [lax.ppermute(q, "y", [(i, i ^ s) for i in range(4)]) for s in (1, 2, 3)]
+    w_near = call(
+        weights_body, pltpu.VMEM(w_proj.shape, bf16), 1, hbm=(0,),
+        scratch=(pltpu.SemaphoreType.DMA((8,)),),
+    )(w_proj)
     piece = jax.ShapeDtypeStruct((80, HD), bf16)
     keyed = jax.ShapeDtypeStruct((1152, HD), bf16)
     p0, p1, p2, p3, keys, values = call(
@@ -300,14 +315,12 @@
         lax.ppermute(p, "y", [(i, i ^ s) for i in range(4)])
         for s, p in ((1, p1), (2, p2), (3, p3))
     ]
-    img, w_near = call(
-        image_body,
-        [jax.ShapeDtypeStruct((32, 40, HD), bf16), pltpu.VMEM(w_proj.shape, bf16)],
-        6, smem=(0, 1), hbm=(5,), scratch=(pltpu.SemaphoreType.DMA,),
-    )(j, txt_len, recv, keys, values, w_proj)
-    back = call(
-        fill_body, jax.ShapeDtypeStruct((32, 104, HD), bf16), 7, smem=(0, 1)
-    )(j, txt_len, img, p0, *got)
+    img = call(
+        image_body, jax.ShapeDtypeStruct((32, 40, HD), bf16), 8, smem=(0, 1)
+    )(j, txt_len, *queries, keys, values)
+    back = call(fill_body, jax.ShapeDtypeStruct((32, 104, HD), bf16), 7, smem=(0, 1))(
+        j, txt_len, img, p0, *got
+    )
     home = lax.all_to_all(back, CUBE, 0, 0, tiled=True)
     half = tokens // 2
     mine, other, txt_out = call(

time: 72.9 us -> 70.2 us (0.963)
  blocking collectives: 33.2 us -> 11.9 us
  waiting for transfers between devices: 7 us -> 15.6 us
  local copies, waits for them, and re-layouts: 0.09 us -> 5.54 us
  Pallas kernels: 7.96 us -> 10.8 us
  starting transfers between devices: 22.2 us -> 24 us
    all_to_all x2 -> x1, blocking collectives: 33.2 us -> 11.9 us  [shards(): recv = lax.all_to_all(send, HEAD, 0, 0, tiled=True)]
    all_to_all x1, waiting for transfers between devices: 0.01 us -> 5.63 us  [shards(): home = lax.all_to_all(back, CUBE, 0, 0, tiled=True)]
    unnamed x8 -> x12, local copies, waits for them, and re-layouts: 0.03 us -> 5.47 us
    ppermute x0 -> x3, starting transfers between devices: none -> 4.38 us  [shards(): lax.ppermute(q, 'y', [(i, i ^ s) for i in range(4)])]
    pallas_call x5 -> x6, Pallas kernels: 7.96 us -> 10.8 us  [run(): return kernel(*held)]
    ppermute x3, waiting for transfers between devices: 5.16 us -> 7.71 us  [shards(): lax.ppermute(kv, 'zh', [(i, i ^ s) for i in range(4)])]
    all_to_all x1, starting transfers between devices: 5.58 us -> 3.92 us  [shards(): home = lax.all_to_all(back, CUBE, 0, 0, tiled=True)]
  transfers between devices with their start and end apart: 8 -> 11, of which waited for: 4 -> 5; matrix products, arithmetic and copies ran while one was open for 0% -> 0% of each run, Pallas kernels for 5% -> 9%
where the time goes in v7:
time: 70.2 us; the launch traced here: 69.9 us
  starting transfers between devices  24 us (34%)
  waiting for transfers between devices  15.6 us (22%)
  blocking collectives  11.9 us (17%)
  Pallas kernels  10.8 us (15%)
  local copies, waits for them, and re-layouts  5.54 us (8%)
  between operations  1.4 us (2%)
    all_to_all x1, blocking collectives, shards(): recv = lax.all_to_all(send, HEAD, 0, 0, tiled=True)  11.9 us
    pallas_call x6, Pallas kernels, run(): return kernel(*held)  10.8 us
    ppermute x3, waiting for transfers between devices, shards(): lax.ppermute(kv, 'zh', [(i, i ^ s) for i in range(4)])  7.71 us
    ppermute x3, starting transfers between devices, shards(): lax.ppermute(kv, 'zh', [(i, i ^ s) for i in range(4)])  7.39 us
    all_to_all x1, waiting for transfers between devices, shards(): home = lax.all_to_all(back, CUBE, 0, 0, tiled=True)  5.63 us
    unnamed x12, local copies, waits for them, and re-layouts  5.47 us
    ppermute x3, starting transfers between devices, shards(): lax.ppermute(q, 'y', [(i, i ^ s) for i in range(4)])  4.38 us
    ppermute x1, starting transfers between devices, shards(): theirs = lax.ppermute(other, 'tp', [(0, 1), (1, 0)])  4.36 us
  transfers between devices with their start and end apart: 11, of which 5 were waited for; matrix products, arithmetic and copies ran while one was open for 0% of the time, Pallas kernels for 9%

profile of v7, /device:TPU:1, one launch (start us, length us, event | category | flops | bytes accessed | tf_op | source)
XLA Modules:
  0.0 69.9 jit_solution(14639381148164163634)
XLA Ops:
  0.6 0.0 copy-start
  0.7 1.3 %shard_map.122 = bf16[8,96,128]{2,1,0:T(8,128)(2,1)S(1)} custom-call(bf16[3,32,1024]{2,1,0:T(8,128)(2,1)} %bitcast.15, s32[1,32]{1,0:T(1,128)} %frame_hbm, s32[1,32]{1,0:T(1,128)} %row_hbm.1, s32[1,32]{1,0:T(1,128)} %col_hbm.1, f32[8,128]{1,0:T(8,128)} %constant.26.clone.rate_hbm), custom_call_target="tpu_custom_call" | custom-call | tf_op jit(solution)/shard_map/pallas_call | solution.py:61
  2.0 11.9 %all_to_all.10 = bf16[8,96,128]{2,1,0:T(8,128)(2,1)S(1)} all-to-all(bf16[8,96,128]{2,1,0:T(8,128)(2,1)S(1)} %shard_map.122), channel_id=1, replica_groups=mesh['zh'=4,'zl'=2,'x'=4,'y'=4,'tp'=2] {'zl','x'}, dimensions={0} | all-to-all | bytes 393216 | tf_op jit(solution)/shard_map/all_to_all | solution.py:300
  13.9 5.2 %collective-permute-start.5 = (bf16[8,64,128]{2,1,0:T(8,128)(2,1)S(1)}, bf16[8,64,128]{2,1,0:T(8,128)(2,1)S(1)}, u32[]{:S(2)}, u32[]{:S(2)}) collective-permute-start(bf16[8,64,128]{2,1,0:T(8,128)(2,1)S(1)} %slice.9.kv0_ref), channel_id=1, source_target_pairs={{0,192},{64,128},{128,64},{192,0},{1,193},{65,129},{129,65},{193,1... | collective-permute-start | bytes 393224 | tf_op jit(solution)/shard_map/ppermute | solution.py:303
  19.1 1.2 %collective-permute-start.4 = (bf16[8,64,128]{2,1,0:T(8,128)(2,1)S(1)}, bf16[8,64,128]{2,1,0:T(8,128)(2,1)S(1)}, u32[]{:S(2)}, u32[]{:S(2)}) collective-permute-start(bf16[8,64,128]{2,1,0:T(8,128)(2,1)S(1)} %slice.9.kv0_ref), channel_id=1, source_target_pairs={{0,128},{64,192},{128,0},{192,64},{1,129},{65,193},{129,1},{193,65... | collective-permute-start | bytes 393224 | tf_op jit(solution)/shard_map/ppermute | solution.py:303
  20.3 1.0 %collective-permute-start.3 = (bf16[8,64,128]{2,1,0:T(8,128)(2,1)S(1)}, bf16[8,64,128]{2,1,0:T(8,128)(2,1)S(1)}, u32[]{:S(2)}, u32[]{:S(2)}) collective-permute-start(bf16[8,64,128]{2,1,0:T(8,128)(2,1)S(1)} %slice.9.kv0_ref), channel_id=1, source_target_pairs={{0,64},{64,0},{128,192},{192,128},{1,65},{65,1},{129,193},{193,129... | collective-permute-start | bytes 393224 | tf_op jit(solution)/shard_map/ppermute | solution.py:303
  21.3 2.7 %collective-permute-start.2 = (bf16[8,32,128]{2,1,0:T(8,128)(2,1)S(1)}, bf16[8,32,128]{2,1,0:T(8,128)(2,1)S(1)}, u32[]{:S(2)}, u32[]{:S(2)}) collective-permute-start(bf16[8,32,128]{2,1,0:T(8,128)(2,1)S(1)} %slice.8.q0_ref), channel_id=1, source_target_pairs={{0,6},{2,4},{4,2},{6,0},{1,7},{3,5},{5,3},{7,1},{8,14},{10,12},{12... | collective-permute-start | bytes 196616 | tf_op jit(solution)/shard_map/ppermute | solution.py:304
  24.0 0.3 collective-permute-start.1
  24.4 6.0 %collective-permute-done.5.kv3_ref = bf16[8,64,128]{2,1,0:T(8,128)(2,1)S(1)} collective-permute-done((bf16[8,64,128]{2,1,0:T(8,128)(2,1)S(1)}, bf16[8,64,128]{2,1,0:T(8,128)(2,1)S(1)}, u32[]{:S(2)}, u32[]{:S(2)}) %collective-permute-start.5) | collective-permute-done | bytes 131104 | tf_op jit(solution)/shard_map/ppermute | solution.py:303
  30.4 1.3 %collective-permute-start = (bf16[8,32,128]{2,1,0:T(8,128)(2,1)S(1)}, bf16[8,32,128]{2,1,0:T(8,128)(2,1)S(1)}, u32[]{:S(2)}, u32[]{:S(2)}) collective-permute-start(bf16[8,32,128]{2,1,0:T(8,128)(2,1)S(1)} %slice.8.q0_ref), channel_id=1, source_target_pairs={{0,2},{2,0},{4,6},{6,4},{1,3},{3,1},{5,7},{7,5},{8,10},{10,8},{12,... | collective-permute-start | bytes 196616 | tf_op jit(solution)/shard_map/ppermute | solution.py:304
  31.7 0.0 copy-done
  31.7 0.1 dynamic-slice_bitcast_fusion.txt_ref
  32.4 0.0 collective-permute-done.4.kv2_ref
  32.4 1.7 %collective-permute-done.3.kv1_ref = bf16[8,64,128]{2,1,0:T(8,128)(2,1)S(1)} collective-permute-done((bf16[8,64,128]{2,1,0:T(8,128)(2,1)S(1)}, bf16[8,64,128]{2,1,0:T(8,128)(2,1)S(1)}, u32[]{:S(2)}, u32[]{:S(2)}) %collective-permute-start.3) | collective-permute-done | bytes 131104 | tf_op jit(solution)/shard_map/ppermute | solution.py:303
  34.1 0.8 %shard_map.123 = (bf16[80,128]{1,0:T(8,128)(2,1)S(1)}, bf16[80,128]{1,0:T(8,128)(2,1)S(1)}, bf16[80,128]{1,0:T(8,128)(2,1)S(1)}, bf16[80,128]{1,0:T(8,128)(2,1)S...) custom-call(s32[1]{0:T(128)} %bitcast.1.where_ref, s32[1]{0:T(128)S(6)} %copy.13.len_ref, ...), custom_call_target="tpu_custom_call" | custom-call | tf_op jit(solution)/shard_map/pallas_call | solution.py:61
  34.9 1.4 %collective-permute-start.6 = (bf16[80,128]{1,0:T(8,128)(2,1)S(1)}, bf16[80,128]{1,0:T(8,128)(2,1)S(1)}, u32[]{:S(2)}, u32[]{:S(2)}) collective-permute-start(bf16[80,128]{1,0:T(8,128)(2,1)S(1)} %get-tuple-element.20), channel_id=1, source_target_pairs={{0,2},{2,0},{4,6},{6,4},{1,3},{3,1},{5,7},{7,5},{8,10},{10,8},{12,... | collective-permute-start | bytes 61448 | tf_op jit(solution)/shard_map/ppermute | solution.py:315
  36.3 2.6 %collective-permute-start.7 = (bf16[80,128]{1,0:T(8,128)(2,1)S(1)}, bf16[80,128]{1,0:T(8,128)(2,1)S(1)}, u32[]{:S(2)}, u32[]{:S(2)}) collective-permute-start(bf16[80,128]{1,0:T(8,128)(2,1)S(1)} %get-tuple-element.21), channel_id=1, source_target_pairs={{0,4},{2,6},{4,0},{6,2},{1,5},{3,7},{5,1},{7,3},{8,12},{10,14},{12... | collective-permute-start | bytes 61448 | tf_op jit(solution)/shard_map/ppermute | solution.py:315
  38.9 0.0 collective-permute-done.2.q3_ref
  38.9 0.0 collective-permute-start.8
  38.9 0.0 collective-permute-done.1.q2_ref
  38.9 0.0 collective-permute-done.q1_ref
  39.0 2.5 %shard_map.124.img_ref = bf16[32,40,128]{2,1,0:T(8,128)(2,1)S(1)} custom-call(s32[1]{0:T(128)} %bitcast.1.where_ref, s32[1]{0:T(128)S(6)} %copy.13.len_ref, bf16[8,32,128]{2,1,0:T(8,128)(2,1)S(1)} %slice.8.q0_ref, bf16[8,32,128]{2,1,0:T(8,128)(2,1)S(1)} %collective-permute-done.q1_ref, bf16[8,32,128]{2,1,0:T(8,128)(2,1)S(1)} %collective-permute-done.1.q2_ref, ...), custom_call_target="tpu_custom_call" | custom-call | tf_op jit(solution)/shard_map/pallas_call | solution.py:61
  41.5 0.0 collective-permute-done.6.p1_ref
  41.5 0.0 collective-permute-done.7.p2_ref
  41.5 1.3 %collective-permute-done.8.p3_ref = bf16[80,128]{1,0:T(8,128)(2,1)S(1)} collective-permute-done((bf16[80,128]{1,0:T(8,128)(2,1)S(1)}, bf16[80,128]{1,0:T(8,128)(2,1)S(1)}, u32[]{:S(2)}, u32[]{:S(2)}) %collective-permute-start.8) | collective-permute-done | bytes 20512 | tf_op jit(solution)/shard_map/ppermute | solution.py:315
  42.8 1.1 %shard_map.125 = bf16[32,104,128]{2,1,0:T(8,128)(2,1)} custom-call(s32[1]{0:T(128)} %bitcast.1.where_ref, s32[1]{0:T(128)S(6)} %copy.13.len_ref, bf16[32,40,128]{2,1,0:T(8,128)(2,1)S(1)} %shard_map.124.img_ref, bf16[80,128]{1,0:T(8,128)(2,1)S(1)} %get-tuple-element.19.p0_ref, bf16[80,128]{1,0:T(8,128)(2,1)S(1)} %collective-permute-done.6.p1_ref, ...), custom_call_target="tpu_custom_call" | custom-call | tf_op jit(solution)/shard_map/pallas_call | solution.py:61
  43.9 3.9 %all-to-all-start.1 = ((bf16[32,104,128]{2,1,0:T(8,128)(2,1)}), bf16[32,104,128]{2,1,0:T(8,128)(2,1)S(1)}, u32[]{:S(2)}, u32[]{:S(2)}) async-start(bf16[32,104,128]{2,1,0:T(8,128)(2,1)} %shard_map.125), calls=%async_computation.1 | async-start | bytes 1703936 | tf_op jit(solution)/shard_map/all_to_all | solution.py:324
  47.8 2.9 %shard_map.126.w_ref = bf16[1024,3072]{1,0:T(8,128)(2,1)S(1)} custom-call(bf16[1024,3072]{1,0:T(8,128)(2,1)} %w_hbm.1), custom_call_target="tpu_custom_call" | custom-call | tf_op jit(solution)/shard_map/pallas_call | solution.py:61
  50.7 0.0 copy-start.1
  50.7 2.7 %copy-done.1 = bf16[1024,3072]{1,0:T(8,128)(2,1)} copy-done((bf16[1024,3072]{1,0:T(8,128)(2,1)}, bf16[1024,3072]{1,0:T(8,128)(2,1)S(1)}, u32[]{:S(2)}) %copy-start.1) | copy-done | bytes 6291480
  53.4 5.6 %all-to-all-done.1.recv_ref = bf16[32,104,128]{2,1,0:T(8,128)(2,1)S(1)} async-done(((bf16[32,104,128]{2,1,0:T(8,128)(2,1)}), bf16[32,104,128]{2,1,0:T(8,128)(2,1)S(1)}, u32[]{:S(2)}, u32[]{:S(2)}) %all-to-all-start.1) | async-done | bytes 852000 | tf_op jit(solution)/shard_map/all_to_all | solution.py:324
  59.0 0.0 copy-start.2
  59.0 2.8 %copy-done.2 = bf16[1024,3072]{1,0:T(8,128)(2,1)S(1)} copy-done((bf16[1024,3072]{1,0:T(8,128)(2,1)S(1)}, bf16[1024,3072]{1,0:T(8,128)(2,1)}, u32[]{:S(2)}) %copy-start.2) | copy-done | bytes 6291480
  61.8 0.0 copy-start.3
  61.8 0.0 copy-start.4
  61.8 0.0 copy-start.5
  61.8 2.1 %shard_map.127 = (f32[16,3072]{1,0:T(8,128)S(1)}, bf16[16,3072]{1,0:T(8,128)(2,1)S(1)}, bf16[256,1024]{1,0:T(8,128)(2,1)}) custom-call(s32[1]{0:T(128)} %bitcast.2.core_ref, bf16[32,104,128]{2,1,0:T(8,128)(2,1)S(1)} %all-to-all-done.1.recv_ref, bf16[1024,3072]{1,0:T(8,128)(2,1)S(1)} %copy-done.2), custom_call_target="tpu_custom_call" | custom-call | tf_op jit(solution)/shard_map/pallas_call | solution.py:61
  63.9 4.4 %collective-permute-start.9 = (bf16[16,3072]{1,0:T(8,128)(2,1)S(1)}, bf16[16,3072]{1,0:T(8,128)(2,1)S(1)}, u32[]{:S(2)}, u32[]{:S(2)}) collective-permute-start(bf16[16,3072]{1,0:T(8,128)(2,1)S(1)} %get-tuple-element.24), channel_id=1, source_target_pairs={{0,1},{1,0},{2,3},{3,2},{4,5},{5,4},{6,7},{7,6},{8,9},{9,8},{10,11... | collective-permute-start | bytes 294920 | tf_op jit(solution)/shard_map/ppermute | solution.py:335
  68.3 0.9 %collective-permute-done.9 = bf16[16,3072]{1,0:T(8,128)(2,1)S(1)} collective-permute-done((bf16[16,3072]{1,0:T(8,128)(2,1)S(1)}, bf16[16,3072]{1,0:T(8,128)(2,1)S(1)}, u32[]{:S(2)}, u32[]{:S(2)}) %collective-permute-start.9) | collective-permute-done | bytes 98336 | tf_op jit(solution)/shard_map/ppermute | solution.py:335
  69.2 0.0 copy-done.3
  69.2 0.0 copy-done.4
  69.2 0.0 copy-done.5
  69.2 0.7 fusion.1
  (2 shorter events, 0.0 us)
Async XLA Ops:
  0.6 31.0 %copy-start = (bf16[1,256,3,1024]{3,1,2,0:T(8,128)(2,1)S(1)}, bf16[1,256,3,1024]{3,1,2,0:T(8,128)(2,1)}, u32[]{:S(2)}) copy-start(bf16[1,256,3,1024]{3,1,2,0:T(8,128)(2,1)} %param.12) | copy-start | bytes 4718596
  13.9 16.5 %collective-permute-start.5 = (bf16[8,64,128]{2,1,0:T(8,128)(2,1)S(1)}, bf16[8,64,128]{2,1,0:T(8,128)(2,1)S(1)}, u32[]{:S(2)}, u32[]{:S(2)}) collective-permute-start(bf16[8,64,128]{2,1,0:T(8,128)(2,1)S(1)} %slice.9.kv0_ref), channel_id=1, source_target_pairs={{0,192},{64,128},{128,64},{192,0},{1,193},{65,129},{129,65},{193,1... | collective-permute-start | bytes 393224 | tf_op jit(solution)/shard_map/ppermute | solution.py:303
  19.1 13.3 %collective-permute-start.4 = (bf16[8,64,128]{2,1,0:T(8,128)(2,1)S(1)}, bf16[8,64,128]{2,1,0:T(8,128)(2,1)S(1)}, u32[]{:S(2)}, u32[]{:S(2)}) collective-permute-start(bf16[8,64,128]{2,1,0:T(8,128)(2,1)S(1)} %slice.9.kv0_ref), channel_id=1, source_target_pairs={{0,128},{64,192},{128,0},{192,64},{1,129},{65,193},{129,1},{193,65... | collective-permute-start | bytes 393224 | tf_op jit(solution)/shard_map/ppermute | solution.py:303
  20.3 13.8 %collective-permute-start.3 = (bf16[8,64,128]{2,1,0:T(8,128)(2,1)S(1)}, bf16[8,64,128]{2,1,0:T(8,128)(2,1)S(1)}, u32[]{:S(2)}, u32[]{:S(2)}) collective-permute-start(bf16[8,64,128]{2,1,0:T(8,128)(2,1)S(1)} %slice.9.kv0_ref), channel_id=1, source_target_pairs={{0,64},{64,0},{128,192},{192,128},{1,65},{65,1},{129,193},{193,129... | collective-permute-start | bytes 393224 | tf_op jit(solution)/shard_map/ppermute | solution.py:303
  21.3 17.7 %collective-permute-start.2 = (bf16[8,32,128]{2,1,0:T(8,128)(2,1)S(1)}, bf16[8,32,128]{2,1,0:T(8,128)(2,1)S(1)}, u32[]{:S(2)}, u32[]{:S(2)}) collective-permute-start(bf16[8,32,128]{2,1,0:T(8,128)(2,1)S(1)} %slice.8.q0_ref), channel_id=1, source_target_pairs={{0,6},{2,4},{4,2},{6,0},{1,7},{3,5},{5,3},{7,1},{8,14},{10,12},{12... | collective-permute-start | bytes 196616 | tf_op jit(solution)/shard_map/ppermute | solution.py:304
  24.0 14.9 %collective-permute-start.1 = (bf16[8,32,128]{2,1,0:T(8,128)(2,1)S(1)}, bf16[8,32,128]{2,1,0:T(8,128)(2,1)S(1)}, u32[]{:S(2)}, u32[]{:S(2)}) collective-permute-start(bf16[8,32,128]{2,1,0:T(8,128)(2,1)S(1)} %slice.8.q0_ref), channel_id=1, source_target_pairs={{0,4},{2,6},{4,0},{6,2},{1,5},{3,7},{5,1},{7,3},{8,12},{10,14},{12... | collective-permute-start | bytes 196616 | tf_op jit(solution)/shard_map/ppermute | solution.py:304
  30.4 8.6 %collective-permute-start = (bf16[8,32,128]{2,1,0:T(8,128)(2,1)S(1)}, bf16[8,32,128]{2,1,0:T(8,128)(2,1)S(1)}, u32[]{:S(2)}, u32[]{:S(2)}) collective-permute-start(bf16[8,32,128]{2,1,0:T(8,128)(2,1)S(1)} %slice.8.q0_ref), channel_id=1, source_target_pairs={{0,2},{2,0},{4,6},{6,4},{1,3},{3,1},{5,7},{7,5},{8,10},{10,8},{12,... | collective-permute-start | bytes 196616 | tf_op jit(solution)/shard_map/ppermute | solution.py:304
  34.9 6.6 %collective-permute-start.6 = (bf16[80,128]{1,0:T(8,128)(2,1)S(1)}, bf16[80,128]{1,0:T(8,128)(2,1)S(1)}, u32[]{:S(2)}, u32[]{:S(2)}) collective-permute-start(bf16[80,128]{1,0:T(8,128)(2,1)S(1)} %get-tuple-element.20), channel_id=1, source_target_pairs={{0,2},{2,0},{4,6},{6,4},{1,3},{3,1},{5,7},{7,5},{8,10},{10,8},{12,... | collective-permute-start | bytes 61448 | tf_op jit(solution)/shard_map/ppermute | solution.py:315
  36.3 5.2 %collective-permute-start.7 = (bf16[80,128]{1,0:T(8,128)(2,1)S(1)}, bf16[80,128]{1,0:T(8,128)(2,1)S(1)}, u32[]{:S(2)}, u32[]{:S(2)}) collective-permute-start(bf16[80,128]{1,0:T(8,128)(2,1)S(1)} %get-tuple-element.21), channel_id=1, source_target_pairs={{0,4},{2,6},{4,0},{6,2},{1,5},{3,7},{5,1},{7,3},{8,12},{10,14},{12... | collective-permute-start | bytes 61448 | tf_op jit(solution)/shard_map/ppermute | solution.py:315
  38.9 3.8 %collective-permute-start.8 = (bf16[80,128]{1,0:T(8,128)(2,1)S(1)}, bf16[80,128]{1,0:T(8,128)(2,1)S(1)}, u32[]{:S(2)}, u32[]{:S(2)}) collective-permute-start(bf16[80,128]{1,0:T(8,128)(2,1)S(1)} %get-tuple-element.22), channel_id=1, source_target_pairs={{0,6},{2,4},{4,2},{6,0},{1,7},{3,5},{5,3},{7,1},{8,14},{10,12},{12... | collective-permute-start | bytes 61448 | tf_op jit(solution)/shard_map/ppermute | solution.py:315
  43.9 15.1 %all-to-all-start.1 = ((bf16[32,104,128]{2,1,0:T(8,128)(2,1)}), bf16[32,104,128]{2,1,0:T(8,128)(2,1)S(1)}, u32[]{:S(2)}, u32[]{:S(2)}) async-start(bf16[32,104,128]{2,1,0:T(8,128)(2,1)} %shard_map.125), calls=%async_computation.1 | async-start | bytes 1703936 | tf_op jit(solution)/shard_map/all_to_all | solution.py:324
  50.7 2.7 %copy-start.1 = (bf16[1024,3072]{1,0:T(8,128)(2,1)}, bf16[1024,3072]{1,0:T(8,128)(2,1)S(1)}, u32[]{:S(2)}) copy-start(bf16[1024,3072]{1,0:T(8,128)(2,1)S(1)} %shard_map.126.w_ref) | copy-start | bytes 18874372
  59.0 2.8 %copy-start.2 = (bf16[1024,3072]{1,0:T(8,128)(2,1)S(1)}, bf16[1024,3072]{1,0:T(8,128)(2,1)}, u32[]{:S(2)}) copy-start(bf16[1024,3072]{1,0:T(8,128)(2,1)} %copy-done.1) | copy-start | bytes 18874372
  61.8 7.4 %copy-start.3 = (bf16[1,16,3072]{2,1,0:T(8,128)(2,1)S(1)}, bf16[1,16,3072]{2,1,0:T(8,128)(2,1)}, u32[]{:S(2)}) copy-start(bf16[1,16,3072]{2,1,0:T(8,128)(2,1)} %param.17) | copy-start | bytes 294916
  61.8 7.4 %copy-start.4 = (f32[3072]{0:T(1024)S(1)}, f32[3072]{0:T(1024)}, u32[]{:S(2)}) copy-start(f32[3072]{0:T(1024)} %param.19) | copy-start | bytes 36868
  61.8 7.4 %copy-start.5 = (f32[3072]{0:T(1024)S(1)}, f32[3072]{0:T(1024)}, u32[]{:S(2)}) copy-start(f32[3072]{0:T(1024)} %param.20) | copy-start | bytes 36868
  63.9 5.3 %collective-permute-start.9 = (bf16[16,3072]{1,0:T(8,128)(2,1)S(1)}, bf16[16,3072]{1,0:T(8,128)(2,1)S(1)}, u32[]{:S(2)}, u32[]{:S(2)}) collective-permute-start(bf16[16,3072]{1,0:T(8,128)(2,1)S(1)} %get-tuple-element.24), channel_id=1, source_target_pairs={{0,1},{1,0},{2,3},{3,2},{4,5},{5,4},{6,7},{7,6},{8,9},{9,8},{10,11... | collective-permute-start | bytes 294920 | tf_op jit(solution)/shard_map/ppermute | solution.py:335

commit v8 on v7

--- a/solution.py
+++ b/solution.py
@@ -145,54 +145,88 @@
     return high, mid, rest - mid
 
 
-def live_mask(j, length):
+def live_mask(block, size, length):
     lane = lax.broadcasted_iota(jnp.int32, (1, 128), 1)
-    index = lane + (j // 2) * 128
-    return jnp.logical_and(index // 64 == j, index < length)
-
-
-def text_body(
-    where_ref, len_ref, kv0_ref, kv1_ref, kv2_ref, kv3_ref, txt_ref,
-    p0_ref, p1_ref, p2_ref, p3_ref, keys_ref, values_ref,
+    index = lane + (block * size // 128) * 128
+    return jnp.logical_and(index // size == block, index < length)
+
+
+def stat_rows(lse):
+    rows = lse.shape[0]
+    row = lax.broadcasted_iota(jnp.int32, (rows, 128), 0)
+    lane = lax.broadcasted_iota(jnp.int32, (rows, 128), 1)
+    sub = lax.broadcasted_iota(jnp.int32, (8, 128), 0)
+    packed = jnp.zeros((8, 128), f32)
+    for p, part in enumerate(three_parts(jnp.broadcast_to(lse, (rows, 128)))):
+        line = jnp.sum(jnp.where(row == lane, part, 0.0), axis=0, keepdims=True)
+        packed = jnp.where(sub == p, line, packed)
+    return packed.astype(bf16)
+
+
+def stat_column(packed, rows):
+    packed = packed.astype(f32)
+    row = lax.broadcasted_iota(jnp.int32, (rows, 128), 0)
+    lane = lax.broadcasted_iota(jnp.int32, (rows, 128), 1)
+    line = packed[0:1] + packed[1:2] + packed[2:3]
+    return jnp.sum(jnp.where(row == lane, line, 0.0), axis=1, keepdims=True)
+
+
+def text_body(where_ref, len_ref, recv_ref, txt_ref, m1_ref, m2_ref, m3_ref, keep_ref):
+    j = where_ref[0]
+    block = where_ref[1] * 4 + j
+    start = pl.multiple_of((block // 8) * 128, 128)
+    keys = jnp.concatenate(
+        [recv_ref[:, 32:64, :].reshape(256, HD), txt_ref[1, pl.ds(start, 128), :]], axis=0
+    )
+    values = jnp.concatenate(
+        [recv_ref[:, 64:96, :].reshape(256, HD), txt_ref[2, pl.ds(start, 128), :]], axis=0
+    )
+    q = jnp.concatenate(
+        [txt_ref[0, pl.ds(pl.multiple_of((j ^ s) * 64, 64), 64), :] for s in range(4)], axis=0
+    )
+    out, lse = softmax_block(q, keys, values, live_mask(block, 16, len_ref[0]))
+    keep_ref[0] = out[0:64]
+    keep_ref[1] = jnp.broadcast_to(lse[0:64], (64, 128))
+    for s, ref in ((1, m1_ref), (2, m2_ref), (3, m3_ref)):
+        ref[0:256, :] = recv_ref[:, 0:32, :].reshape(256, HD)
+        ref[256:320, :] = out[64 * s : 64 * s + 64].astype(bf16)
+        ref[320:328, :] = stat_rows(lse[64 * s : 64 * s + 64])
+
+
+def level_body(keep_ref, g1_ref, g2_ref, g3_ref, send_ref, out_ref):
+    outs = [keep_ref[0]] + [g[256:320, :].astype(f32) for g in (g1_ref, g2_ref, g3_ref)]
+    lses = [keep_ref[1]] + [stat_column(g[320:328, :], 64) for g in (g1_ref, g2_ref, g3_ref)]
+    mixed, lse = blend(outs, lses)
+    out_ref[0] = mixed
+    out_ref[1] = lse
+    send_ref[0:64, :] = mixed.astype(bf16)
+    send_ref[64:72, :] = stat_rows(lse[:, 0:1])
+
+
+def image_body(
+    where_ref, len_ref, recv_ref, kv1_ref, kv2_ref, kv3_ref, m1_ref, m2_ref, m3_ref, txt_ref,
+    out_ref, keys_ref, values_ref,
 ):
     j = where_ref[0]
-    length = len_ref[0]
-    for b, ref in enumerate((kv0_ref, kv1_ref, kv2_ref, kv3_ref)):
+    keys_ref[0:256, :] = recv_ref[:, 32:64, :].reshape(256, HD)
+    values_ref[0:256, :] = recv_ref[:, 64:96, :].reshape(256, HD)
+    for b, ref in ((1, kv1_ref), (2, kv2_ref), (3, kv3_ref)):
         keys_ref[256 * b : 256 * b + 256, :] = ref[:, 0:32, :].reshape(256, HD)
         values_ref[256 * b : 256 * b + 256, :] = ref[:, 32:64, :].reshape(256, HD)
     start = pl.multiple_of((j // 2) * 128, 128)
     keys_ref[1024:1152, :] = txt_ref[1, pl.ds(start, 128), :]
     values_ref[1024:1152, :] = txt_ref[2, pl.ds(start, 128), :]
-    keys = keys_ref[...]
-    values = values_ref[...]
-    live = live_mask(j, length)
-    q = jnp.concatenate(
-        [txt_ref[0, pl.ds(pl.multiple_of((j ^ s) * 64, 64), 64), :] for s in range(4)], axis=0
-    )
-    out, lse = softmax_block(q, keys, values, live)
-    out = out.astype(bf16)
-    row = lax.broadcasted_iota(jnp.int32, (64, 128), 0)
-    lane = lax.broadcasted_iota(jnp.int32, (64, 128), 1)
-    for s, ref in enumerate((p0_ref, p1_ref, p2_ref, p3_ref)):
-        ref[0:64, :] = out[64 * s : 64 * s + 64]
-        high, mid, low = three_parts(jnp.broadcast_to(lse[64 * s : 64 * s + 64], (64, 128)))
-        first = jnp.where(row == lane % 64, jnp.where(lane < 64, high, mid), 0.0)
-        second = jnp.where(row == lane, low, 0.0)
-        first = jnp.broadcast_to(jnp.sum(first, axis=0, keepdims=True), (8, 128))
-        second = jnp.broadcast_to(jnp.sum(second, axis=0, keepdims=True), (8, 128))
-        ref[64:80, :] = jnp.concatenate([first, second], axis=0).astype(bf16)
-
-
-def image_body(
-    where_ref, len_ref, q0_ref, q1_ref, q2_ref, q3_ref, keys_ref, values_ref, out_ref
-):
-    live = live_mask(where_ref[0], len_ref[0])
+    live = live_mask(j, 64, len_ref[0])
     keys = keys_ref[...]
     values = values_ref[...]
     row = lax.broadcasted_iota(jnp.int32, (8, 32, 128), 1)
     lane = lax.broadcasted_iota(jnp.int32, (8, 32, 128), 2)
-    for s, q_ref in enumerate((q0_ref, q1_ref, q2_ref, q3_ref)):
-        out, lse = softmax_block(q_ref[...].reshape(256, HD), keys, values, live)
+    for s in range(4):
+        if s == 0:
+            q = recv_ref[:, 0:32, :].reshape(256, HD)
+        else:
+            q = (m1_ref, m2_ref, m3_ref)[s - 1][0:256, :]
+        out, lse = softmax_block(q, keys, values, live)
         at = slice(8 * s, 8 * s + 8)
         out_ref[at, 0:32, :] = out.astype(bf16).reshape(8, 32, HD)
         high, mid, low = three_parts(jnp.broadcast_to(lse, (256, 128)).reshape(8, 32, 128))
@@ -227,19 +261,14 @@
     mixed = outs[0] * weights[0]
     for o, w in zip(outs[1:], weights[1:]):
         mixed = mixed + o * w
-    return mixed / total
-
-
-def fill_body(where_ref, len_ref, img_ref, p0_ref, p1_ref, p2_ref, p3_ref, out_ref):
+    return mixed / total, peak + jnp.log2(total)
+
+
+def fill_body(where_ref, len_ref, img_ref, keep_ref, g1_ref, g2_ref, g3_ref, out_ref):
     row = lax.broadcasted_iota(jnp.int32, (64, 128), 0)
-    lane = lax.broadcasted_iota(jnp.int32, (64, 128), 1)
-    outs, lses = [], []
-    for ref in (p0_ref, p1_ref, p2_ref, p3_ref):
-        outs.append(ref[0:64, :].astype(f32))
-        stats = ref[64:80, :].astype(f32)
-        picked = jnp.where(row == lane % 64, stats[0:1], 0.0) + jnp.where(row == lane, stats[8:9], 0.0)
-        lses.append(jnp.sum(picked, axis=1, keepdims=True))
-    text = blend(outs, lses)
+    outs = [keep_ref[0]] + [g[0:64, :].astype(f32) for g in (g1_ref, g2_ref, g3_ref)]
+    lses = [keep_ref[1]] + [stat_column(g[64:72, :], 64) for g in (g1_ref, g2_ref, g3_ref)]
+    text, _ = blend(outs, lses)
     text = jnp.where(where_ref[0] * 64 + row < len_ref[0], text, 0.0).astype(bf16)
     for s in range(4):
         for i in range(8):
@@ -262,7 +291,7 @@
             stats = recv_ref[s, 96:104, :].astype(f32)[0:1]
             lses.append(jnp.sum(jnp.where(pick, stats, 0.0), axis=1, keepdims=True))
             txt_ref[64 * j : 64 * j + 64, head * HD : (head + 1) * HD] = recv_ref[s, 32:96, :]
-        heads.append(blend(outs, lses))
+        heads.append(blend(outs, lses)[0])
     rows = jnp.concatenate(heads, axis=1)
     flipped = jnp.concatenate([rows[16:32], rows[0:16]], axis=0)
     rows = jnp.where(core_ref[0] == 0, rows, flipped).astype(bf16)
@@ -277,10 +306,10 @@
     tokens = img_qkv.shape[1]
     width = img_qkv.shape[3]
     d_model = w_proj.shape[1]
-    j = lax.axis_index("y").astype(jnp.int32).reshape(1)
+    where = jnp.stack([lax.axis_index("y"), lax.axis_index("zh")]).astype(jnp.int32)
     head = lax.axis_index("zl") * 4 + lax.axis_index("x")
     core = lax.axis_index("tp").astype(jnp.int32).reshape(1)
-    j, core, frame_index = lax.optimization_barrier((j, core, frame_index))
+    where, core, head, frame_index = lax.optimization_barrier((where, core, head, frame_index))
     qkv = img_qkv.reshape(tokens, 3, width).transpose(1, 0, 2)
     txt = lax.dynamic_slice_in_dim(txt_qkv[0], head * HD, HD, 2).transpose(1, 0, 2)
 
@@ -299,27 +328,34 @@
     )(qkv, frame_index, row_index, column_index, jnp.asarray(rate_table()))
     recv = lax.all_to_all(send, HEAD, 0, 0, tiled=True)
     kv = recv[:, 32:96]
-    q = recv[:, 0:32]
+    rows = 8 * tokens
     others = [lax.ppermute(kv, "zh", [(i, i ^ s) for i in range(4)]) for s in (1, 2, 3)]
-    queries = [q] + [lax.ppermute(q, "y", [(i, i ^ s) for i in range(4)]) for s in (1, 2, 3)]
+    m1, m2, m3, keep = call(
+        text_body,
+        [jax.ShapeDtypeStruct((rows + 72, HD), bf16)] * 3
+        + [jax.ShapeDtypeStruct((2, 64, HD), f32)],
+        4, smem=(0, 1),
+    )(where, txt_len, recv, txt)
+    messages = [
+        lax.ppermute(m, "y", [(i, i ^ s) for i in range(4)])
+        for s, m in ((1, m1), (2, m2), (3, m3))
+    ]
     w_near = call(
         weights_body, pltpu.VMEM(w_proj.shape, bf16), 1, hbm=(0,),
         scratch=(pltpu.SemaphoreType.DMA((8,)),),
     )(w_proj)
-    piece = jax.ShapeDtypeStruct((80, HD), bf16)
-    keyed = jax.ShapeDtypeStruct((1152, HD), bf16)
-    p0, p1, p2, p3, keys, values = call(
-        text_body, [piece] * 4 + [keyed] * 2, 7, smem=(0, 1)
-    )(j, txt_len, kv, *others, txt)
-    got = [
-        lax.ppermute(p, "y", [(i, i ^ s) for i in range(4)])
-        for s, p in ((1, p1), (2, p2), (3, p3))
-    ]
+    send, keep = call(
+        level_body,
+        [jax.ShapeDtypeStruct((72, HD), bf16), jax.ShapeDtypeStruct((2, 64, HD), f32)],
+        4,
+    )(keep, *messages)
+    got = [lax.ppermute(send, "zh", [(i, i ^ s) for i in range(4)]) for s in (1, 2, 3)]
     img = call(
-        image_body, jax.ShapeDtypeStruct((32, 40, HD), bf16), 8, smem=(0, 1)
-    )(j, txt_len, *queries, keys, values)
+        image_body, jax.ShapeDtypeStruct((32, 40, HD), bf16), 10, smem=(0, 1),
+        scratch=(pltpu.VMEM((1152, HD), bf16), pltpu.VMEM((1152, HD), bf16)),
+    )(where, txt_len, recv, *others, *messages, txt)
     back = call(fill_body, jax.ShapeDtypeStruct((32, 104, HD), bf16), 7, smem=(0, 1))(
-        j, txt_len, img, p0, *got
+        where, txt_len, img, keep, *got
     )
     home = lax.all_to_all(back, CUBE, 0, 0, tiled=True)
     half = tokens // 2

time: 70.2 us -> 72 us (1.026)
  blocking collectives: 11.9 us -> 0 us
  starting transfers between devices: 24 us -> 34.2 us
  Pallas kernels: 10.8 us -> 12.9 us
  waiting for transfers between devices: 15.6 us -> 16.8 us
    all_to_all x1 -> x0, blocking collectives: 11.9 us -> none  [shards(): recv = lax.all_to_all(send, HEAD, 0, 0, tiled=True)]
    ppermute x3, waiting for transfers between devices: 7.71 us -> 0.01 us  [shards(): lax.ppermute(kv, 'zh', [(i, i ^ s) for i in range(4)])]
    all_to_all x0 -> x1, starting transfers between devices: none -> 6.2 us  [shards(): recv = lax.all_to_all(send, HEAD, 0, 0, tiled=True)]
    all_to_all x0 -> x1, waiting for transfers between devices: none -> 5.15 us  [shards(): recv = lax.all_to_all(send, HEAD, 0, 0, tiled=True)]
    ppermute x6, waiting for transfers between devices: 1.29 us -> 5.95 us  [the longest x3 4.66 us: shards(): lax.ppermute(m, 'y', [(i, i ^ s) for i in range(4)])]
    ppermute x1, starting transfers between devices: 4.36 us -> 6.81 us  [shards(): theirs = lax.ppermute(other, 'tp', [(0, 1), (1, 0)])]
    pallas_call x6 -> x7, Pallas kernels: 10.8 us -> 12.9 us  [run(): return kernel(*held)]
    ppermute x6, starting transfers between devices: 8.39 us -> 9.9 us  [the longest x3 5.9 us: shards(): lax.ppermute(send, 'zh', [(i, i ^ s) for i in range(4)])]
  transfers between devices with their start and end apart: 11 -> 12, of which waited for: 5 -> 6; matrix products, arithmetic and copies ran while one was open for 0% -> 0% of each run, Pallas kernels for 9% -> 9%
where the time goes in v8:
time: 72 us; the launch traced here: 71.6 us
  starting transfers between devices  34.2 us (48%)
  waiting for transfers between devices  16.8 us (23%)
  Pallas kernels  12.9 us (18%)
  local copies, waits for them, and re-layouts  5.52 us (8%)
  between operations  1.4 us (2%)
  other arithmetic  0.77 us (1%)
    pallas_call x7, Pallas kernels, run(): return kernel(*held)  12.9 us
    ppermute x3, starting transfers between devices, shards(): lax.ppermute(kv, 'zh', [(i, i ^ s) for i in range(4)])  7.39 us
    ppermute x1, starting transfers between devices, shards(): theirs = lax.ppermute(other, 'tp', [(0, 1), (1, 0)])  6.81 us
    all_to_all x1, starting transfers between devices, shards(): recv = lax.all_to_all(send, HEAD, 0, 0, tiled=True)  6.2 us
    ppermute x3, starting transfers between devices, shards(): lax.ppermute(send, 'zh', [(i, i ^ s) for i in range(4)])  5.9 us
    unnamed x12, local copies, waits for them, and re-layouts  5.45 us
    all_to_all x1, waiting for transfers between devices, shards(): recv = lax.all_to_all(send, HEAD, 0, 0, tiled=True)  5.15 us
    all_to_all x1, waiting for transfers between devices, shards(): home = lax.all_to_all(back, CUBE, 0, 0, tiled=True)  4.77 us
  transfers between devices with their start and end apart: 12, of which 6 were waited for; matrix products, arithmetic and copies ran while one was open for 0% of the time, Pallas kernels for 9%

profile of v8, /device:TPU:1, one launch (start us, length us, event | category | flops | bytes accessed | tf_op | source)
XLA Modules:
  0.0 71.6 jit_solution(8024462837763215573)
XLA Ops:
  0.6 0.0 copy-start
  0.7 0.1 pad_add_fusion.where_ref
  0.7 2.0 %shard_map.122 = bf16[8,96,128]{2,1,0:T(8,128)(2,1)} custom-call(bf16[3,32,1024]{2,1,0:T(8,128)(2,1)} %bitcast.16, s32[1,32]{1,0:T(1,128)} %frame_hbm, s32[1,32]{1,0:T(1,128)} %row_hbm.1, s32[1,32]{1,0:T(1,128)} %col_hbm.1, f32[8,128]{1,0:T(8,128)} %constant.30.clone.rate_hbm), custom_call_target="tpu_custom_call" | custom-call | tf_op jit(solution)/shard_map/pallas_call | solution.py:61
  2.7 6.2 %all-to-all-start = ((bf16[8,96,128]{2,1,0:T(8,128)(2,1)}), bf16[8,96,128]{2,1,0:T(8,128)(2,1)S(1)}, u32[]{:S(2)}, u32[]{:S(2)}) async-start(bf16[8,96,128]{2,1,0:T(8,128)(2,1)} %shard_map.122), calls=%async_computation | async-start | bytes 393216 | tf_op jit(solution)/shard_map/all_to_all | solution.py:329
  9.6 0.0 copy-done
  9.6 0.1 dynamic-slice_bitcast_fusion.txt_ref
  9.7 5.2 %all-to-all-done.recv_ref = bf16[8,96,128]{2,1,0:T(8,128)(2,1)S(1)} async-done(((bf16[8,96,128]{2,1,0:T(8,128)(2,1)}), bf16[8,96,128]{2,1,0:T(8,128)(2,1)S(1)}, u32[]{:S(2)}, u32[]{:S(2)}) %all-to-all-start) | async-done | bytes 196640 | tf_op jit(solution)/shard_map/all_to_all | solution.py:329
  14.8 1.0 %shard_map.123 = (bf16[328,128]{1,0:T(8,128)(2,1)S(1)}, bf16[328,128]{1,0:T(8,128)(2,1)S(1)}, bf16[328,128]{1,0:T(8,128)(2,1)S(1)}, f32[2,64,128]{2,1,0:T(8,128)S(1)}) custom-call(s32[2]{0:T(128)S(1)} %pad_add_fusion.where_ref, s32[1]{0:T(128)S(6)} %copy.13.len_ref, bf16[8,96,128]{2,1,0:T(8,128)(2,1)S(1)} %all-to-all-done.recv_ref, ...), custom_call_target="tpu_custom_call" | custom-call | tf_op jit(solution)/shard_map/pallas_call | solution.py:61
  15.8 1.4 %collective-permute-start.3 = (bf16[328,128]{1,0:T(8,128)(2,1)S(1)}, bf16[328,128]{1,0:T(8,128)(2,1)S(1)}, u32[]{:S(2)}, u32[]{:S(2)}) collective-permute-start(bf16[328,128]{1,0:T(8,128)(2,1)S(1)} %get-tuple-element.19), channel_id=1, source_target_pairs={{0,2},{2,0},{4,6},{6,4},{1,3},{3,1},{5,7},{7,5},{8,10},{10,8},{12,... | collective-permute-start | bytes 251912 | tf_op jit(solution)/shard_map/ppermute | solution.py:340
  17.2 5.2 %collective-permute-start.2 = (bf16[8,64,128]{2,1,0:T(8,128)(2,1)S(1)}, bf16[8,64,128]{2,1,0:T(8,128)(2,1)S(1)}, u32[]{:S(2)}, u32[]{:S(2)}) collective-permute-start(bf16[8,64,128]{2,1,0:T(8,128)(2,1)S(1)} %slice.4), channel_id=1, source_target_pairs={{0,192},{64,128},{128,64},{192,0},{1,193},{65,129},{129,65},{193,1... | collective-permute-start | bytes 393224 | tf_op jit(solution)/shard_map/ppermute | solution.py:332
  22.4 1.2 %collective-permute-start.1 = (bf16[8,64,128]{2,1,0:T(8,128)(2,1)S(1)}, bf16[8,64,128]{2,1,0:T(8,128)(2,1)S(1)}, u32[]{:S(2)}, u32[]{:S(2)}) collective-permute-start(bf16[8,64,128]{2,1,0:T(8,128)(2,1)S(1)} %slice.4), channel_id=1, source_target_pairs={{0,128},{64,192},{128,0},{192,64},{1,129},{65,193},{129,1},{193,65... | collective-permute-start | bytes 393224 | tf_op jit(solution)/shard_map/ppermute | solution.py:332
  23.6 1.0 %collective-permute-start = (bf16[8,64,128]{2,1,0:T(8,128)(2,1)S(1)}, bf16[8,64,128]{2,1,0:T(8,128)(2,1)S(1)}, u32[]{:S(2)}, u32[]{:S(2)}) collective-permute-start(bf16[8,64,128]{2,1,0:T(8,128)(2,1)S(1)} %slice.4), channel_id=1, source_target_pairs={{0,64},{64,0},{128,192},{192,128},{1,65},{65,1},{129,193},{193,129... | collective-permute-start | bytes 393224 | tf_op jit(solution)/shard_map/ppermute | solution.py:332
  24.6 2.6 %collective-permute-start.4 = (bf16[328,128]{1,0:T(8,128)(2,1)S(1)}, bf16[328,128]{1,0:T(8,128)(2,1)S(1)}, u32[]{:S(2)}, u32[]{:S(2)}) collective-permute-start(bf16[328,128]{1,0:T(8,128)(2,1)S(1)} %get-tuple-element.20), channel_id=1, source_target_pairs={{0,4},{2,6},{4,0},{6,2},{1,5},{3,7},{5,1},{7,3},{8,12},{10,14},{12... | collective-permute-start | bytes 251912 | tf_op jit(solution)/shard_map/ppermute | solution.py:340
  27.2 0.0 collective-permute-done.3.m1_ref.g1_ref
  27.2 0.0 collective-permute-start.5
  27.2 2.2 %collective-permute-done.4.m2_ref.g2_ref = bf16[328,128]{1,0:T(8,128)(2,1)S(1)} collective-permute-done((bf16[328,128]{1,0:T(8,128)(2,1)S(1)}, bf16[328,128]{1,0:T(8,128)(2,1)S(1)}, u32[]{:S(2)}, u32[]{:S(2)}) %collective-permute-start.4) | collective-permute-done | bytes 84000 | tf_op jit(solution)/shard_map/ppermute | solution.py:340
  29.4 2.5 %collective-permute-done.5.m3_ref.g3_ref = bf16[328,128]{1,0:T(8,128)(2,1)S(1)} collective-permute-done((bf16[328,128]{1,0:T(8,128)(2,1)S(1)}, bf16[328,128]{1,0:T(8,128)(2,1)S(1)}, u32[]{:S(2)}, u32[]{:S(2)}) %collective-permute-start.5) | collective-permute-done | bytes 84000 | tf_op jit(solution)/shard_map/ppermute | solution.py:340
  31.9 0.2 shard_map.125
  32.1 3.7 %collective-permute-start.8 = (bf16[72,128]{1,0:T(8,128)(2,1)S(1)}, bf16[72,128]{1,0:T(8,128)(2,1)S(1)}, u32[]{:S(2)}, u32[]{:S(2)}) collective-permute-start(bf16[72,128]{1,0:T(8,128)(2,1)S(1)} %get-tuple-element.24), channel_id=1, source_target_pairs={{0,192},{64,128},{128,64},{192,0},{1,193},{65,129},{129,65},{193,1... | collective-permute-start | bytes 55304 | tf_op jit(solution)/shard_map/ppermute | solution.py:352
  35.9 1.2 %collective-permute-start.7 = (bf16[72,128]{1,0:T(8,128)(2,1)S(1)}, bf16[72,128]{1,0:T(8,128)(2,1)S(1)}, u32[]{:S(2)}, u32[]{:S(2)}) collective-permute-start(bf16[72,128]{1,0:T(8,128)(2,1)S(1)} %get-tuple-element.24), channel_id=1, source_target_pairs={{0,128},{64,192},{128,0},{192,64},{1,129},{65,193},{129,1},{193,65... | collective-permute-start | bytes 55304 | tf_op jit(solution)/shard_map/ppermute | solution.py:352
  37.0 0.0 collective-permute-done.2.kv3_ref
  37.0 1.0 %collective-permute-start.6 = (bf16[72,128]{1,0:T(8,128)(2,1)S(1)}, bf16[72,128]{1,0:T(8,128)(2,1)S(1)}, u32[]{:S(2)}, u32[]{:S(2)}) collective-permute-start(bf16[72,128]{1,0:T(8,128)(2,1)S(1)} %get-tuple-element.24), channel_id=1, source_target_pairs={{0,64},{64,0},{128,192},{192,128},{1,65},{65,1},{129,193},{193,129... | collective-permute-start | bytes 55304 | tf_op jit(solution)/shard_map/ppermute | solution.py:352
  38.0 0.0 collective-permute-done.1.kv2_ref
  38.0 0.0 collective-permute-done.kv1_ref
  38.0 3.0 %shard_map.124.img_ref = bf16[32,40,128]{2,1,0:T(8,128)(2,1)S(1)} custom-call(s32[2]{0:T(128)S(1)} %pad_add_fusion.where_ref, s32[1]{0:T(128)S(6)} %copy.13.len_ref, bf16[8,96,128]{2,1,0:T(8,128)(2,1)S(1)} %all-to-all-done.recv_ref, bf16[8,64,128]{2,1,0:T(8,128)(2,1)S(1)} %collective-permute-done.kv1_ref, ...), custom_call_target="tpu_custom_call" | custom-call | tf_op jit(solution)/shard_map/pallas_call | solution.py:61
  41.1 0.0 collective-permute-done.8.g3_ref
  41.1 1.3 %collective-permute-done.7.g2_ref = bf16[72,128]{1,0:T(8,128)(2,1)S(1)} collective-permute-done((bf16[72,128]{1,0:T(8,128)(2,1)S(1)}, bf16[72,128]{1,0:T(8,128)(2,1)S(1)}, u32[]{:S(2)}, u32[]{:S(2)}) %collective-permute-start.7) | collective-permute-done | bytes 18464 | tf_op jit(solution)/shard_map/ppermute | solution.py:352
  42.4 0.0 collective-permute-done.6.g1_ref
  42.4 1.6 %shard_map.126 = bf16[32,104,128]{2,1,0:T(8,128)(2,1)} custom-call(s32[2]{0:T(128)S(1)} %pad_add_fusion.where_ref, s32[1]{0:T(128)S(6)} %copy.13.len_ref, bf16[32,40,128]{2,1,0:T(8,128)(2,1)S(1)} %shard_map.124.img_ref, f32[2,64,128]{2,1,0:T(8,128)S(1)} %get-tuple-element.23.keep_ref, bf16[72,128]{1,0:T(8,128)(2,1)S(1)} %collective-permute-done.6.g1_ref, ...), custom_call_target="tpu_custom_call" | custom-call | tf_op jit(solution)/shard_map/pallas_call | solution.py:61
  44.0 3.9 %all-to-all-start.1 = ((bf16[32,104,128]{2,1,0:T(8,128)(2,1)}), bf16[32,104,128]{2,1,0:T(8,128)(2,1)S(1)}, u32[]{:S(2)}, u32[]{:S(2)}) async-start(bf16[32,104,128]{2,1,0:T(8,128)(2,1)} %shard_map.126), calls=%async_computation.1 | async-start | bytes 1703936 | tf_op jit(solution)/shard_map/all_to_all | solution.py:360
  48.0 2.9 %shard_map.127.w_ref = bf16[1024,3072]{1,0:T(8,128)(2,1)S(1)} custom-call(bf16[1024,3072]{1,0:T(8,128)(2,1)} %w_hbm.1), custom_call_target="tpu_custom_call" | custom-call | tf_op jit(solution)/shard_map/pallas_call | solution.py:61
  50.8 0.0 copy-start.1
  50.8 2.6 %copy-done.1 = bf16[1024,3072]{1,0:T(8,128)(2,1)} copy-done((bf16[1024,3072]{1,0:T(8,128)(2,1)}, bf16[1024,3072]{1,0:T(8,128)(2,1)S(1)}, u32[]{:S(2)}) %copy-start.1) | copy-done | bytes 6291480
  53.5 4.8 %all-to-all-done.1.recv_ref = bf16[32,104,128]{2,1,0:T(8,128)(2,1)S(1)} async-done(((bf16[32,104,128]{2,1,0:T(8,128)(2,1)}), bf16[32,104,128]{2,1,0:T(8,128)(2,1)S(1)}, u32[]{:S(2)}, u32[]{:S(2)}) %all-to-all-start.1) | async-done | bytes 852000 | tf_op jit(solution)/shard_map/all_to_all | solution.py:360
  58.3 0.0 copy-start.2
  58.3 2.8 %copy-done.2 = bf16[1024,3072]{1,0:T(8,128)(2,1)S(1)} copy-done((bf16[1024,3072]{1,0:T(8,128)(2,1)S(1)}, bf16[1024,3072]{1,0:T(8,128)(2,1)}, u32[]{:S(2)}) %copy-start.2) | copy-done | bytes 6291480
  61.0 0.0 copy-start.3
  61.0 0.0 copy-start.4
  61.0 0.0 copy-start.5
  61.0 2.1 %shard_map.128 = (f32[16,3072]{1,0:T(8,128)S(1)}, bf16[16,3072]{1,0:T(8,128)(2,1)S(1)}, bf16[256,1024]{1,0:T(8,128)(2,1)}) custom-call(s32[1]{0:T(128)} %bitcast.3.core_ref, bf16[32,104,128]{2,1,0:T(8,128)(2,1)S(1)} %all-to-all-done.1.recv_ref, bf16[1024,3072]{1,0:T(8,128)(2,1)S(1)} %copy-done.2), custom_call_target="tpu_custom_call" | custom-call | tf_op jit(solution)/shard_map/pallas_call | solution.py:61
  63.2 6.8 %collective-permute-start.9 = (bf16[16,3072]{1,0:T(8,128)(2,1)S(1)}, bf16[16,3072]{1,0:T(8,128)(2,1)S(1)}, u32[]{:S(2)}, u32[]{:S(2)}) collective-permute-start(bf16[16,3072]{1,0:T(8,128)(2,1)S(1)} %get-tuple-element.26), channel_id=1, source_target_pairs={{0,1},{1,0},{2,3},{3,2},{4,5},{5,4},{6,7},{7,6},{8,9},{9,8},{10,11... | collective-permute-start | bytes 294920 | tf_op jit(solution)/shard_map/ppermute | solution.py:371
  70.0 0.9 %collective-permute-done.9 = bf16[16,3072]{1,0:T(8,128)(2,1)S(1)} collective-permute-done((bf16[16,3072]{1,0:T(8,128)(2,1)S(1)}, bf16[16,3072]{1,0:T(8,128)(2,1)S(1)}, u32[]{:S(2)}, u32[]{:S(2)}) %collective-permute-start.9) | collective-permute-done | bytes 98336 | tf_op jit(solution)/shard_map/ppermute | solution.py:371
  70.9 0.0 copy-done.3
  70.9 0.0 copy-done.4
  70.9 0.0 copy-done.5
  70.9 0.7 fusion.1
  (1 shorter events, 0.0 us)
Async XLA Ops:
  0.6 9.0 %copy-start = (bf16[1,256,3,1024]{3,1,2,0:T(8,128)(2,1)S(1)}, bf16[1,256,3,1024]{3,1,2,0:T(8,128)(2,1)}, u32[]{:S(2)}) copy-start(bf16[1,256,3,1024]{3,1,2,0:T(8,128)(2,1)} %param.12) | copy-start | bytes 4718596
  2.7 12.1 %all-to-all-start = ((bf16[8,96,128]{2,1,0:T(8,128)(2,1)}), bf16[8,96,128]{2,1,0:T(8,128)(2,1)S(1)}, u32[]{:S(2)}, u32[]{:S(2)}) async-start(bf16[8,96,128]{2,1,0:T(8,128)(2,1)} %shard_map.122), calls=%async_computation | async-start | bytes 393216 | tf_op jit(solution)/shard_map/all_to_all | solution.py:329
  15.8 11.4 %collective-permute-start.3 = (bf16[328,128]{1,0:T(8,128)(2,1)S(1)}, bf16[328,128]{1,0:T(8,128)(2,1)S(1)}, u32[]{:S(2)}, u32[]{:S(2)}) collective-permute-start(bf16[328,128]{1,0:T(8,128)(2,1)S(1)} %get-tuple-element.19), channel_id=1, source_target_pairs={{0,2},{2,0},{4,6},{6,4},{1,3},{3,1},{5,7},{7,5},{8,10},{10,8},{12,... | collective-permute-start | bytes 251912 | tf_op jit(solution)/shard_map/ppermute | solution.py:340
  17.2 19.8 %collective-permute-start.2 = (bf16[8,64,128]{2,1,0:T(8,128)(2,1)S(1)}, bf16[8,64,128]{2,1,0:T(8,128)(2,1)S(1)}, u32[]{:S(2)}, u32[]{:S(2)}) collective-permute-start(bf16[8,64,128]{2,1,0:T(8,128)(2,1)S(1)} %slice.4), channel_id=1, source_target_pairs={{0,192},{64,128},{128,64},{192,0},{1,193},{65,129},{129,65},{193,1... | collective-permute-start | bytes 393224 | tf_op jit(solution)/shard_map/ppermute | solution.py:332
  22.4 15.6 %collective-permute-start.1 = (bf16[8,64,128]{2,1,0:T(8,128)(2,1)S(1)}, bf16[8,64,128]{2,1,0:T(8,128)(2,1)S(1)}, u32[]{:S(2)}, u32[]{:S(2)}) collective-permute-start(bf16[8,64,128]{2,1,0:T(8,128)(2,1)S(1)} %slice.4), channel_id=1, source_target_pairs={{0,128},{64,192},{128,0},{192,64},{1,129},{65,193},{129,1},{193,65... | collective-permute-start | bytes 393224 | tf_op jit(solution)/shard_map/ppermute | solution.py:332
  23.6 14.4 %collective-permute-start = (bf16[8,64,128]{2,1,0:T(8,128)(2,1)S(1)}, bf16[8,64,128]{2,1,0:T(8,128)(2,1)S(1)}, u32[]{:S(2)}, u32[]{:S(2)}) collective-permute-start(bf16[8,64,128]{2,1,0:T(8,128)(2,1)S(1)} %slice.4), channel_id=1, source_target_pairs={{0,64},{64,0},{128,192},{192,128},{1,65},{65,1},{129,193},{193,129... | collective-permute-start | bytes 393224 | tf_op jit(solution)/shard_map/ppermute | solution.py:332
  24.6 4.8 %collective-permute-start.4 = (bf16[328,128]{1,0:T(8,128)(2,1)S(1)}, bf16[328,128]{1,0:T(8,128)(2,1)S(1)}, u32[]{:S(2)}, u32[]{:S(2)}) collective-permute-start(bf16[328,128]{1,0:T(8,128)(2,1)S(1)} %get-tuple-element.20), channel_id=1, source_target_pairs={{0,4},{2,6},{4,0},{6,2},{1,5},{3,7},{5,1},{7,3},{8,12},{10,14},{12... | collective-permute-start | bytes 251912 | tf_op jit(solution)/shard_map/ppermute | solution.py:340
  27.2 4.7 %collective-permute-start.5 = (bf16[328,128]{1,0:T(8,128)(2,1)S(1)}, bf16[328,128]{1,0:T(8,128)(2,1)S(1)}, u32[]{:S(2)}, u32[]{:S(2)}) collective-permute-start(bf16[328,128]{1,0:T(8,128)(2,1)S(1)} %get-tuple-element.21), channel_id=1, source_target_pairs={{0,6},{2,4},{4,2},{6,0},{1,7},{3,5},{5,3},{7,1},{8,14},{10,12},{12... | collective-permute-start | bytes 251912 | tf_op jit(solution)/shard_map/ppermute | solution.py:340
  32.1 9.0 %collective-permute-start.8 = (bf16[72,128]{1,0:T(8,128)(2,1)S(1)}, bf16[72,128]{1,0:T(8,128)(2,1)S(1)}, u32[]{:S(2)}, u32[]{:S(2)}) collective-permute-start(bf16[72,128]{1,0:T(8,128)(2,1)S(1)} %get-tuple-element.24), channel_id=1, source_target_pairs={{0,192},{64,128},{128,64},{192,0},{1,193},{65,129},{129,65},{193,1... | collective-permute-start | bytes 55304 | tf_op jit(solution)/shard_map/ppermute | solution.py:352
  35.9 6.5 %collective-permute-start.7 = (bf16[72,128]{1,0:T(8,128)(2,1)S(1)}, bf16[72,128]{1,0:T(8,128)(2,1)S(1)}, u32[]{:S(2)}, u32[]{:S(2)}) collective-permute-start(bf16[72,128]{1,0:T(8,128)(2,1)S(1)} %get-tuple-element.24), channel_id=1, source_target_pairs={{0,128},{64,192},{128,0},{192,64},{1,129},{65,193},{129,1},{193,65... | collective-permute-start | bytes 55304 | tf_op jit(solution)/shard_map/ppermute | solution.py:352
  37.0 5.4 %collective-permute-start.6 = (bf16[72,128]{1,0:T(8,128)(2,1)S(1)}, bf16[72,128]{1,0:T(8,128)(2,1)S(1)}, u32[]{:S(2)}, u32[]{:S(2)}) collective-permute-start(bf16[72,128]{1,0:T(8,128)(2,1)S(1)} %get-tuple-element.24), channel_id=1, source_target_pairs={{0,64},{64,0},{128,192},{192,128},{1,65},{65,1},{129,193},{193,129... | collective-permute-start | bytes 55304 | tf_op jit(solution)/shard_map/ppermute | solution.py:352
  44.0 14.2 %all-to-all-start.1 = ((bf16[32,104,128]{2,1,0:T(8,128)(2,1)}), bf16[32,104,128]{2,1,0:T(8,128)(2,1)S(1)}, u32[]{:S(2)}, u32[]{:S(2)}) async-start(bf16[32,104,128]{2,1,0:T(8,128)(2,1)} %shard_map.126), calls=%async_computation.1 | async-start | bytes 1703936 | tf_op jit(solution)/shard_map/all_to_all | solution.py:360
  50.8 2.7 %copy-start.1 = (bf16[1024,3072]{1,0:T(8,128)(2,1)}, bf16[1024,3072]{1,0:T(8,128)(2,1)S(1)}, u32[]{:S(2)}) copy-start(bf16[1024,3072]{1,0:T(8,128)(2,1)S(1)} %shard_map.127.w_ref) | copy-start | bytes 18874372
  58.3 2.8 %copy-start.2 = (bf16[1024,3072]{1,0:T(8,128)(2,1)S(1)}, bf16[1024,3072]{1,0:T(8,128)(2,1)}, u32[]{:S(2)}) copy-start(bf16[1024,3072]{1,0:T(8,128)(2,1)} %copy-done.1) | copy-start | bytes 18874372
  61.0 9.9 %copy-start.3 = (bf16[1,16,3072]{2,1,0:T(8,128)(2,1)S(1)}, bf16[1,16,3072]{2,1,0:T(8,128)(2,1)}, u32[]{:S(2)}) copy-start(bf16[1,16,3072]{2,1,0:T(8,128)(2,1)} %param.17) | copy-start | bytes 294916
  61.0 9.9 %copy-start.4 = (f32[3072]{0:T(1024)S(1)}, f32[3072]{0:T(1024)}, u32[]{:S(2)}) copy-start(f32[3072]{0:T(1024)} %param.19) | copy-start | bytes 36868
  61.0 9.9 %copy-start.5 = (f32[3072]{0:T(1024)S(1)}, f32[3072]{0:T(1024)}, u32[]{:S(2)}) copy-start(f32[3072]{0:T(1024)} %param.20) | copy-start | bytes 36868
  63.2 7.8 %collective-permute-start.9 = (bf16[16,3072]{1,0:T(8,128)(2,1)S(1)}, bf16[16,3072]{1,0:T(8,128)(2,1)S(1)}, u32[]{:S(2)}, u32[]{:S(2)}) collective-permute-start(bf16[16,3072]{1,0:T(8,128)(2,1)S(1)} %get-tuple-element.26), channel_id=1, source_target_pairs={{0,1},{1,0},{2,3},{3,2},{4,5},{5,4},{6,7},{7,6},{8,9},{9,8},{10,11... | collective-permute-start | bytes 294920 | tf_op jit(solution)/shard_map/ppermute | solution.py:371

commit v9 on v7

--- a/solution.py
+++ b/solution.py
@@ -34,11 +34,11 @@
 
 
 def call(
-    body, out_shape, n_in, smem=(), hbm=(), near=(), limit=40 * 1024 * 1024, scratch=(), alias=None
+    body, out_shape, n_in, smem=(), hbm=(), near=(), far_outs=(), limit=40 * 1024 * 1024, scratch=(), alias=None
 ):
     single = not isinstance(out_shape, (tuple, list))
     outs = out_shape if not single else [out_shape]
-    specs = [vmem_spec() for _ in outs]
+    specs = [any_spec() if i in far_outs else vmem_spec() for i in range(len(outs))]
     kernel = pl.pallas_call(
         body,
         out_shape=out_shape,
@@ -151,25 +151,62 @@
     return jnp.logical_and(index // 64 == j, index < length)
 
 
+SCALE = LOG2E / math.sqrt(HD)
+
+
+def text_queries(txt_ref, j):
+    return jnp.concatenate(
+        [txt_ref[0, pl.ds(pl.multiple_of((j ^ s) * 64, 64), 64), :] for s in range(4)], axis=0
+    )
+
+
+def early_body(where_ref, len_ref, recv_ref, kv_ref, txt_ref, acc_ref, stat_ref):
+    j = where_ref[0]
+    start = pl.multiple_of((j // 2) * 128, 128)
+    keys = jnp.concatenate(
+        [
+            recv_ref[:, 32:64, :].reshape(256, HD), kv_ref[:, 0:32, :].reshape(256, HD),
+            txt_ref[1, pl.ds(start, 128), :],
+        ],
+        axis=0,
+    )
+    values = jnp.concatenate(
+        [
+            recv_ref[:, 64:96, :].reshape(256, HD), kv_ref[:, 32:64, :].reshape(256, HD),
+            txt_ref[2, pl.ds(start, 128), :],
+        ],
+        axis=0,
+    )
+    q = text_queries(txt_ref, j)
+    scores = lax.dot_general(q, keys, (((1,), (1,)), ((), ())), preferred_element_type=f32)
+    s_txt = jnp.where(live_mask(j, len_ref[0]), scores[:, 512:], neg_large)
+    peak = jnp.maximum(
+        jnp.max(scores[:, :512], axis=1, keepdims=True), jnp.max(s_txt, axis=1, keepdims=True)
+    )
+    w_img = jnp.exp2((scores[:, :512] - peak) * SCALE)
+    w_txt = jnp.exp2((s_txt - peak) * SCALE)
+    total = jnp.sum(w_img, axis=1, keepdims=True) + jnp.sum(w_txt, axis=1, keepdims=True)
+    weights = jnp.concatenate([w_img.astype(bf16), w_txt.astype(bf16)], axis=1)
+    acc_ref[...] = jnp.dot(weights, values, preferred_element_type=f32)
+    stat_ref[0] = jnp.broadcast_to(peak, (256, 128))
+    stat_ref[1] = jnp.broadcast_to(total, (256, 128))
+
+
 def text_body(
-    where_ref, len_ref, kv0_ref, kv1_ref, kv2_ref, kv3_ref, txt_ref,
-    p0_ref, p1_ref, p2_ref, p3_ref, keys_ref, values_ref,
+    where_ref, kv0_ref, kv1_ref, txt_ref, acc_ref, stat_ref, p0_ref, p1_ref, p2_ref, p3_ref
 ):
-    j = where_ref[0]
-    length = len_ref[0]
-    for b, ref in enumerate((kv0_ref, kv1_ref, kv2_ref, kv3_ref)):
-        keys_ref[256 * b : 256 * b + 256, :] = ref[:, 0:32, :].reshape(256, HD)
-        values_ref[256 * b : 256 * b + 256, :] = ref[:, 32:64, :].reshape(256, HD)
-    start = pl.multiple_of((j // 2) * 128, 128)
-    keys_ref[1024:1152, :] = txt_ref[1, pl.ds(start, 128), :]
-    values_ref[1024:1152, :] = txt_ref[2, pl.ds(start, 128), :]
-    keys = keys_ref[...]
-    values = values_ref[...]
-    live = live_mask(j, length)
-    q = jnp.concatenate(
-        [txt_ref[0, pl.ds(pl.multiple_of((j ^ s) * 64, 64), 64), :] for s in range(4)], axis=0
-    )
-    out, lse = softmax_block(q, keys, values, live)
+    keys = jnp.concatenate([r[:, 0:32, :].reshape(256, HD) for r in (kv0_ref, kv1_ref)], axis=0)
+    values = jnp.concatenate([r[:, 32:64, :].reshape(256, HD) for r in (kv0_ref, kv1_ref)], axis=0)
+    q = text_queries(txt_ref, where_ref[0])
+    scores = lax.dot_general(q, keys, (((1,), (1,)), ((), ())), preferred_element_type=f32)
+    before = stat_ref[0][:, 0:1]
+    peak = jnp.maximum(before, jnp.max(scores, axis=1, keepdims=True))
+    shrink = jnp.exp2((before - peak) * SCALE)
+    weights = jnp.exp2((scores - peak) * SCALE)
+    total = stat_ref[1][:, 0:1] * shrink + jnp.sum(weights, axis=1, keepdims=True)
+    out = acc_ref[...] * shrink + jnp.dot(weights.astype(bf16), values, preferred_element_type=f32)
+    out = out / total
+    lse = peak * SCALE + jnp.log2(total)
     out = out.astype(bf16)
     row = lax.broadcasted_iota(jnp.int32, (64, 128), 0)
     lane = lax.broadcasted_iota(jnp.int32, (64, 128), 1)
@@ -184,15 +221,26 @@
 
 
 def image_body(
-    where_ref, len_ref, q0_ref, q1_ref, q2_ref, q3_ref, keys_ref, values_ref, out_ref
+    where_ref, len_ref, recv_ref, kv1_ref, kv2_ref, kv3_ref, q1_ref, q2_ref, q3_ref, txt_ref,
+    out_ref, keys_ref, values_ref,
 ):
-    live = live_mask(where_ref[0], len_ref[0])
+    j = where_ref[0]
+    keys_ref[0:256, :] = recv_ref[:, 32:64, :].reshape(256, HD)
+    values_ref[0:256, :] = recv_ref[:, 64:96, :].reshape(256, HD)
+    for b, ref in ((1, kv1_ref), (2, kv2_ref), (3, kv3_ref)):
+        keys_ref[256 * b : 256 * b + 256, :] = ref[:, 0:32, :].reshape(256, HD)
+        values_ref[256 * b : 256 * b + 256, :] = ref[:, 32:64, :].reshape(256, HD)
+    start = pl.multiple_of((j // 2) * 128, 128)
+    keys_ref[1024:1152, :] = txt_ref[1, pl.ds(start, 128), :]
+    values_ref[1024:1152, :] = txt_ref[2, pl.ds(start, 128), :]
+    live = live_mask(j, len_ref[0])
     keys = keys_ref[...]
     values = values_ref[...]
     row = lax.broadcasted_iota(jnp.int32, (8, 32, 128), 1)
     lane = lax.broadcasted_iota(jnp.int32, (8, 32, 128), 2)
-    for s, q_ref in enumerate((q0_ref, q1_ref, q2_ref, q3_ref)):
-        out, lse = softmax_block(q_ref[...].reshape(256, HD), keys, values, live)
+    for s in range(4):
+        q = recv_ref[:, 0:32, :] if s == 0 else (q1_ref, q2_ref, q3_ref)[s - 1][...]
+        out, lse = softmax_block(q.reshape(256, HD), keys, values, live)
         at = slice(8 * s, 8 * s + 8)
         out_ref[at, 0:32, :] = out.astype(bf16).reshape(8, 32, HD)
         high, mid, low = three_parts(jnp.broadcast_to(lse, (256, 128)).reshape(8, 32, 128))
@@ -249,7 +297,7 @@
             out_ref[d, 96:104, :] = img_ref[8 * s + i, 32:40]
 
 
-def tail_body(core_ref, recv_ref, w_ref, mine_ref, other_ref, txt_ref):
+def tail_body(core_ref, recv_ref, w_ref, mine_ref, other_ref, txt_out, txt_ref, sem):
     row = lax.broadcasted_iota(jnp.int32, (32, 128), 0)
     lane = lax.broadcasted_iota(jnp.int32, (32, 128), 1)
     pick = jnp.logical_and(row == lane % 32, lane < 96)
@@ -263,12 +311,15 @@
             lses.append(jnp.sum(jnp.where(pick, stats, 0.0), axis=1, keepdims=True))
             txt_ref[64 * j : 64 * j + 64, head * HD : (head + 1) * HD] = recv_ref[s, 32:96, :]
         heads.append(blend(outs, lses))
+    leave = pltpu.make_async_copy(txt_ref, txt_out, sem)
+    leave.start()
     rows = jnp.concatenate(heads, axis=1)
     flipped = jnp.concatenate([rows[16:32], rows[0:16]], axis=0)
     rows = jnp.where(core_ref[0] == 0, rows, flipped).astype(bf16)
     projected = jnp.dot(rows, w_ref[...], preferred_element_type=f32)
     mine_ref[...] = projected[0:16]
     other_ref[...] = projected[16:32].astype(bf16)
+    leave.wait()
 
 
 def shards(
@@ -280,7 +331,7 @@
     j = lax.axis_index("y").astype(jnp.int32).reshape(1)
     head = lax.axis_index("zl") * 4 + lax.axis_index("x")
     core = lax.axis_index("tp").astype(jnp.int32).reshape(1)
-    j, core, frame_index = lax.optimization_barrier((j, core, frame_index))
+    j, core, head, frame_index = lax.optimization_barrier((j, core, head, frame_index))
     qkv = img_qkv.reshape(tokens, 3, width).transpose(1, 0, 2)
     txt = lax.dynamic_slice_in_dim(txt_qkv[0], head * HD, HD, 2).transpose(1, 0, 2)
 
@@ -300,26 +351,30 @@
     recv = lax.all_to_all(send, HEAD, 0, 0, tiled=True)
     kv = recv[:, 32:96]
     q = recv[:, 0:32]
-    others = [lax.ppermute(kv, "zh", [(i, i ^ s) for i in range(4)]) for s in (1, 2, 3)]
-    queries = [q] + [lax.ppermute(q, "y", [(i, i ^ s) for i in range(4)]) for s in (1, 2, 3)]
+    others = {}
+    for s in (2, 3, 1):
+        others[s] = lax.ppermute(kv, "zh", [(i, i ^ s) for i in range(4)])
+    queries = [lax.ppermute(q, "y", [(i, i ^ s) for i in range(4)]) for s in (1, 2, 3)]
     w_near = call(
         weights_body, pltpu.VMEM(w_proj.shape, bf16), 1, hbm=(0,),
         scratch=(pltpu.SemaphoreType.DMA((8,)),),
     )(w_proj)
     piece = jax.ShapeDtypeStruct((80, HD), bf16)
-    keyed = jax.ShapeDtypeStruct((1152, HD), bf16)
-    p0, p1, p2, p3, keys, values = call(
-        text_body, [piece] * 4 + [keyed] * 2, 7, smem=(0, 1)
-    )(j, txt_len, kv, *others, txt)
-    got = [
-        lax.ppermute(p, "y", [(i, i ^ s) for i in range(4)])
-        for s, p in ((1, p1), (2, p2), (3, p3))
-    ]
+    got = {}
+    acc, stat = call(
+        early_body,
+        [jax.ShapeDtypeStruct((256, HD), f32), jax.ShapeDtypeStruct((2, 256, 128), f32)],
+        5, smem=(0, 1),
+    )(j, txt_len, recv, others[2], txt)
+    pieces = call(text_body, [piece] * 4, 6, smem=(0,))(j, others[3], others[1], txt, acc, stat)
+    for s in (2, 3, 1):
+        got[s] = lax.ppermute(pieces[s], "y", [(i, i ^ s) for i in range(4)])
     img = call(
-        image_body, jax.ShapeDtypeStruct((32, 40, HD), bf16), 8, smem=(0, 1)
-    )(j, txt_len, *queries, keys, values)
+        image_body, jax.ShapeDtypeStruct((32, 40, HD), bf16), 10, smem=(0, 1),
+        scratch=(pltpu.VMEM((1152, HD), bf16), pltpu.VMEM((1152, HD), bf16)),
+    )(j, txt_len, recv, others[1], others[2], others[3], *queries, txt)
     back = call(fill_body, jax.ShapeDtypeStruct((32, 104, HD), bf16), 7, smem=(0, 1))(
-        j, txt_len, img, p0, *got
+        j, txt_len, img, pieces[0], got[1], got[2], got[3]
     )
     home = lax.all_to_all(back, CUBE, 0, 0, tiled=True)
     half = tokens // 2
@@ -328,9 +383,10 @@
         [
             jax.ShapeDtypeStruct((half, d_model), f32),
             jax.ShapeDtypeStruct((half, d_model), bf16),
-            jax.ShapeDtypeStruct((256, width), bf16),
+            pltpu.HBM((256, width), bf16),
         ],
-        3, smem=(0,), near=(2,),
+        3, smem=(0,), near=(2,), far_outs=(2,),
+        scratch=(pltpu.VMEM((256, width), bf16), pltpu.SemaphoreType.DMA),
     )(core, home, w_near)
     theirs = lax.ppermute(other, "tp", [(0, 1), (1, 0)])
     projected = mine + theirs.astype(f32)

time: 70.2 us -> 68.8 us (0.980)
  starting transfers between devices: 24 us -> 22.4 us
    ppermute x6, waiting for transfers between devices: 9 us -> 7.79 us  [the longest x3 6.49 us: shards(): others[s] = lax.ppermute(kv, 'zh', [(i, i ^ s) for i in range(4)])]
    all_to_all x1, waiting for transfers between devices: 5.63 us -> 6.73 us  [shards(): home = lax.all_to_all(back, CUBE, 0, 0, tiled=True)]
    ppermute x1, starting transfers between devices: 4.36 us -> 3.35 us  [shards(): theirs = lax.ppermute(other, 'tp', [(0, 1), (1, 0)])]
    ppermute x3, starting transfers between devices: 4.38 us -> 3.4 us  [shards(): lax.ppermute(q, 'y', [(i, i ^ s) for i in range(4)])]
    pallas_call x6 -> x7, Pallas kernels: 10.8 us -> 11.2 us  [run(): return kernel(*held)]
  transfers between devices with their start and end apart: 11 -> 11, of which waited for: 5 -> 5; matrix products, arithmetic and copies ran while one was open for 0% -> 0% of each run, Pallas kernels for 9% -> 10%
where the time goes in v9:
time: 68.8 us; the launch traced here: 68.5 us
  starting transfers between devices  22.4 us (33%)
  waiting for transfers between devices  15.5 us (23%)
  blocking collectives  11.9 us (17%)
  Pallas kernels  11.2 us (16%)
  local copies, waits for them, and re-layouts  5.53 us (8%)
  between operations  1.41 us (2%)
  other arithmetic  0.69 us (1%)
    all_to_all x1, blocking collectives, shards(): recv = lax.all_to_all(send, HEAD, 0, 0, tiled=True)  11.9 us
    pallas_call x7, Pallas kernels, run(): return kernel(*held)  11.2 us
    ppermute x3, starting transfers between devices, shards(): others[s] = lax.ppermute(kv, 'zh', [(i, i ^ s) for i in range(4)])  7.29 us
    all_to_all x1, waiting for transfers between devices, shards(): home = lax.all_to_all(back, CUBE, 0, 0, tiled=True)  6.73 us
    ppermute x3, waiting for transfers between devices, shards(): others[s] = lax.ppermute(kv, 'zh', [(i, i ^ s) for i in range(4)])  6.49 us
    unnamed x12, local copies, waits for them, and re-layouts  5.46 us
    all_to_all x1, starting transfers between devices, shards(): home = lax.all_to_all(back, CUBE, 0, 0, tiled=True)  4.3 us
    ppermute x3, starting transfers between devices, shards(): got[s] = lax.ppermute(pieces[s], 'y', [(i, i ^ s) for i in range(4)])  4.01 us
  transfers between devices with their start and end apart: 11, of which 5 were waited for; matrix products, arithmetic and copies ran while one was open for 0% of the time, Pallas kernels for 10%

profile of v9, /device:TPU:1, one launch (start us, length us, event | category | flops | bytes accessed | tf_op | source)
XLA Modules:
  0.0 68.5 jit_solution(8482552966400620747)
XLA Ops:
  0.6 0.0 copy-start
  0.7 1.3 %shard_map.122 = bf16[8,96,128]{2,1,0:T(8,128)(2,1)S(1)} custom-call(bf16[3,32,1024]{2,1,0:T(8,128)(2,1)} %bitcast.15, s32[1,32]{1,0:T(1,128)} %frame_hbm, s32[1,32]{1,0:T(1,128)} %row_hbm.1, s32[1,32]{1,0:T(1,128)} %col_hbm.1, f32[8,128]{1,0:T(8,128)} %constant.26.clone.rate_hbm), custom_call_target="tpu_custom_call" | custom-call | tf_op jit(solution)/shard_map/pallas_call | solution.py:61
  2.0 11.9 %all_to_all.10.recv_ref = bf16[8,96,128]{2,1,0:T(8,128)(2,1)S(1)} all-to-all(bf16[8,96,128]{2,1,0:T(8,128)(2,1)S(1)} %shard_map.122), channel_id=1, replica_groups=mesh['zh'=4,'zl'=2,'x'=4,'y'=4,'tp'=2] {'zl','x'}, dimensions={0} | all-to-all | bytes 393216 | tf_op jit(solution)/shard_map/all_to_all | solution.py:351
  13.9 6.1 %collective-permute-start.1 = (bf16[8,64,128]{2,1,0:T(8,128)(2,1)S(1)}, bf16[8,64,128]{2,1,0:T(8,128)(2,1)S(1)}, u32[]{:S(2)}, u32[]{:S(2)}) collective-permute-start(bf16[8,64,128]{2,1,0:T(8,128)(2,1)S(1)} %slice.8), channel_id=1, source_target_pairs={{0,128},{64,192},{128,0},{192,64},{1,129},{65,193},{129,1},{193,65... | collective-permute-start | bytes 393224 | tf_op jit(solution)/shard_map/ppermute | solution.py:356
  20.0 0.3 collective-permute-start.2
  20.3 0.9 %collective-permute-start = (bf16[8,64,128]{2,1,0:T(8,128)(2,1)S(1)}, bf16[8,64,128]{2,1,0:T(8,128)(2,1)S(1)}, u32[]{:S(2)}, u32[]{:S(2)}) collective-permute-start(bf16[8,64,128]{2,1,0:T(8,128)(2,1)S(1)} %slice.8), channel_id=1, source_target_pairs={{0,64},{64,0},{128,192},{192,128},{1,65},{65,1},{129,193},{193,129... | collective-permute-start | bytes 393224 | tf_op jit(solution)/shard_map/ppermute | solution.py:356
  21.2 2.7 %collective-permute-start.5 = (bf16[8,32,128]{2,1,0:T(8,128)(2,1)S(1)}, bf16[8,32,128]{2,1,0:T(8,128)(2,1)S(1)}, u32[]{:S(2)}, u32[]{:S(2)}) collective-permute-start(bf16[8,32,128]{2,1,0:T(8,128)(2,1)S(1)} %slice.9), channel_id=1, source_target_pairs={{0,6},{2,4},{4,2},{6,0},{1,7},{3,5},{5,3},{7,1},{8,14},{10,12},{12... | collective-permute-start | bytes 196616 | tf_op jit(solution)/shard_map/ppermute | solution.py:357
  23.9 0.3 collective-permute-start.4
  24.3 0.0 collective-permute-done.1.kv2_ref.kv_ref
  24.3 0.3 collective-permute-start.3
  24.6 0.0 copy-done
  24.6 0.1 dynamic-slice_bitcast_fusion.txt_ref
  25.3 0.6 shard_map.124
  25.9 5.5 %collective-permute-done.2.kv3_ref.kv0_ref = bf16[8,64,128]{2,1,0:T(8,128)(2,1)S(1)} collective-permute-done((bf16[8,64,128]{2,1,0:T(8,128)(2,1)S(1)}, bf16[8,64,128]{2,1,0:T(8,128)(2,1)S(1)}, u32[]{:S(2)}, u32[]{:S(2)}) %collective-permute-start.2) | collective-permute-done | bytes 131104 | tf_op jit(solution)/shard_map/ppermute | solution.py:356
  31.4 1.0 %collective-permute-done.kv1_ref = bf16[8,64,128]{2,1,0:T(8,128)(2,1)S(1)} collective-permute-done((bf16[8,64,128]{2,1,0:T(8,128)(2,1)S(1)}, bf16[8,64,128]{2,1,0:T(8,128)(2,1)S(1)}, u32[]{:S(2)}, u32[]{:S(2)}) %collective-permute-start) | collective-permute-done | bytes 131104 | tf_op jit(solution)/shard_map/ppermute | solution.py:356
  32.4 0.6 shard_map.125
  33.0 1.4 %collective-permute-start.6 = (bf16[80,128]{1,0:T(8,128)(2,1)S(1)}, bf16[80,128]{1,0:T(8,128)(2,1)S(1)}, u32[]{:S(2)}, u32[]{:S(2)}) collective-permute-start(bf16[80,128]{1,0:T(8,128)(2,1)S(1)} %get-tuple-element.22), channel_id=1, source_target_pairs={{0,2},{2,0},{4,6},{6,4},{1,3},{3,1},{5,7},{7,5},{8,10},{10,8},{12,... | collective-permute-start | bytes 61448 | tf_op jit(solution)/shard_map/ppermute | solution.py:371
  34.4 2.6 %collective-permute-start.7 = (bf16[80,128]{1,0:T(8,128)(2,1)S(1)}, bf16[80,128]{1,0:T(8,128)(2,1)S(1)}, u32[]{:S(2)}, u32[]{:S(2)}) collective-permute-start(bf16[80,128]{1,0:T(8,128)(2,1)S(1)} %get-tuple-element.23), channel_id=1, source_target_pairs={{0,4},{2,6},{4,0},{6,2},{1,5},{3,7},{5,1},{7,3},{8,12},{10,14},{12... | collective-permute-start | bytes 61448 | tf_op jit(solution)/shard_map/ppermute | solution.py:371
  37.0 0.0 collective-permute-done.5.q3_ref
  37.0 0.0 collective-permute-start.8
  37.0 0.0 collective-permute-done.4.q2_ref
  37.0 0.0 collective-permute-done.3.q1_ref
  37.0 2.5 %shard_map.123.img_ref = bf16[32,40,128]{2,1,0:T(8,128)(2,1)S(1)} custom-call(s32[1]{0:T(128)} %bitcast.1.where_ref, s32[1]{0:T(128)S(6)} %copy.13.len_ref, bf16[8,96,128]{2,1,0:T(8,128)(2,1)S(1)} %all_to_all.10.recv_ref, bf16[8,64,128]{2,1,0:T(8,128)(2,1)S(1)} %collective-permute-done.kv1_ref, ...), custom_call_target="tpu_custom_call" | custom-call | tf_op jit(solution)/shard_map/pallas_call | solution.py:61
  39.5 0.0 collective-permute-done.6.p1_ref
  39.5 0.0 collective-permute-done.7.p2_ref
  39.6 1.3 %collective-permute-done.8.p3_ref = bf16[80,128]{1,0:T(8,128)(2,1)S(1)} collective-permute-done((bf16[80,128]{1,0:T(8,128)(2,1)S(1)}, bf16[80,128]{1,0:T(8,128)(2,1)S(1)}, u32[]{:S(2)}, u32[]{:S(2)}) %collective-permute-start.8) | collective-permute-done | bytes 20512 | tf_op jit(solution)/shard_map/ppermute | solution.py:371
  40.8 1.1 %shard_map.126 = bf16[32,104,128]{2,1,0:T(8,128)(2,1)} custom-call(s32[1]{0:T(128)} %bitcast.1.where_ref, s32[1]{0:T(128)S(6)} %copy.13.len_ref, bf16[32,40,128]{2,1,0:T(8,128)(2,1)S(1)} %shard_map.123.img_ref, bf16[80,128]{1,0:T(8,128)(2,1)S(1)} %get-tuple-element.21.p0_ref, bf16[80,128]{1,0:T(8,128)(2,1)S(1)} %collective-permute-done.6.p1_ref, ...), custom_call_target="tpu_custom_call" | custom-call | tf_op jit(solution)/shard_map/pallas_call | solution.py:61
  42.0 4.3 %all-to-all-start.1 = ((bf16[32,104,128]{2,1,0:T(8,128)(2,1)}), bf16[32,104,128]{2,1,0:T(8,128)(2,1)S(1)}, u32[]{:S(2)}, u32[]{:S(2)}) async-start(bf16[32,104,128]{2,1,0:T(8,128)(2,1)} %shard_map.126), calls=%async_computation.1 | async-start | bytes 1703936 | tf_op jit(solution)/shard_map/all_to_all | solution.py:379
  46.3 2.9 %shard_map.127.w_ref = bf16[1024,3072]{1,0:T(8,128)(2,1)S(1)} custom-call(bf16[1024,3072]{1,0:T(8,128)(2,1)} %w_hbm.1), custom_call_target="tpu_custom_call" | custom-call | tf_op jit(solution)/shard_map/pallas_call | solution.py:61
  49.1 0.0 copy-start.1
  49.2 2.7 %copy-done.1 = bf16[1024,3072]{1,0:T(8,128)(2,1)} copy-done((bf16[1024,3072]{1,0:T(8,128)(2,1)}, bf16[1024,3072]{1,0:T(8,128)(2,1)S(1)}, u32[]{:S(2)}) %copy-start.1) | copy-done | bytes 6291480
  51.8 6.7 %all-to-all-done.1.recv_ref = bf16[32,104,128]{2,1,0:T(8,128)(2,1)S(1)} async-done(((bf16[32,104,128]{2,1,0:T(8,128)(2,1)}), bf16[32,104,128]{2,1,0:T(8,128)(2,1)S(1)}, u32[]{:S(2)}, u32[]{:S(2)}) %all-to-all-start.1) | async-done | bytes 852000 | tf_op jit(solution)/shard_map/all_to_all | solution.py:379
  58.5 0.0 copy-start.2
  58.5 2.8 %copy-done.2 = bf16[1024,3072]{1,0:T(8,128)(2,1)S(1)} copy-done((bf16[1024,3072]{1,0:T(8,128)(2,1)S(1)}, bf16[1024,3072]{1,0:T(8,128)(2,1)}, u32[]{:S(2)}) %copy-start.2) | copy-done | bytes 6291480
  61.3 0.0 copy-start.3
  61.3 0.0 copy-start.4
  61.3 0.0 copy-start.5
  61.3 2.1 %shard_map.128 = (f32[16,3072]{1,0:T(8,128)S(1)}, bf16[16,3072]{1,0:T(8,128)(2,1)S(1)}, bf16[256,1024]{1,0:T(8,128)(2,1)}) custom-call(s32[1]{0:T(128)} %bitcast.2.core_ref, bf16[32,104,128]{2,1,0:T(8,128)(2,1)S(1)} %all-to-all-done.1.recv_ref, bf16[1024,3072]{1,0:T(8,128)(2,1)S(1)} %copy-done.2), custom_call_target="tpu_custom_call" | custom-call | tf_op jit(solution)/shard_map/pallas_call | solution.py:61
  63.5 3.4 %collective-permute-start.9 = (bf16[16,3072]{1,0:T(8,128)(2,1)S(1)}, bf16[16,3072]{1,0:T(8,128)(2,1)S(1)}, u32[]{:S(2)}, u32[]{:S(2)}) collective-permute-start(bf16[16,3072]{1,0:T(8,128)(2,1)S(1)} %get-tuple-element.26), channel_id=1, source_target_pairs={{0,1},{1,0},{2,3},{3,2},{4,5},{5,4},{6,7},{7,6},{8,9},{9,8},{10,11... | collective-permute-start | bytes 294920 | tf_op jit(solution)/shard_map/ppermute | solution.py:391
  66.8 0.9 %collective-permute-done.9 = bf16[16,3072]{1,0:T(8,128)(2,1)S(1)} collective-permute-done((bf16[16,3072]{1,0:T(8,128)(2,1)S(1)}, bf16[16,3072]{1,0:T(8,128)(2,1)S(1)}, u32[]{:S(2)}, u32[]{:S(2)}) %collective-permute-start.9) | collective-permute-done | bytes 98336 | tf_op jit(solution)/shard_map/ppermute | solution.py:391
  67.8 0.0 copy-done.3
  67.8 0.0 copy-done.4
  67.8 0.0 copy-done.5
  67.8 0.7 %fusion.1 = bf16[1,16,3072]{2,1,0:T(8,128)(2,1)} fusion(f32[16,3072]{1,0:T(8,128)S(1)} %get-tuple-element.25, bf16[16,3072]{1,0:T(8,128)(2,1)S(1)} %collective-permute-done.9, bf16[1,16,3072]{2,1,0:T(8,128)(2,1)S(1)} %copy-done.3, f32[3072]{0:T(1024)S(1)} %copy-done.4, f32[3072]{0:T(1024)S(1)} %copy-done.5), kind=kLoop, calls=%fused_computation.3 | loop fusion | flops 344064 | bytes 516096 | tf_op jit(solution)/shard_map/broadcast_in_dim | solution.py:394
  (2 shorter events, 0.0 us)
Async XLA Ops:
  0.6 24.0 %copy-start = (bf16[1,256,3,1024]{3,1,2,0:T(8,128)(2,1)S(1)}, bf16[1,256,3,1024]{3,1,2,0:T(8,128)(2,1)}, u32[]{:S(2)}) copy-start(bf16[1,256,3,1024]{3,1,2,0:T(8,128)(2,1)} %param.12) | copy-start | bytes 4718596
  13.9 10.4 %collective-permute-start.1 = (bf16[8,64,128]{2,1,0:T(8,128)(2,1)S(1)}, bf16[8,64,128]{2,1,0:T(8,128)(2,1)S(1)}, u32[]{:S(2)}, u32[]{:S(2)}) collective-permute-start(bf16[8,64,128]{2,1,0:T(8,128)(2,1)S(1)} %slice.8), channel_id=1, source_target_pairs={{0,128},{64,192},{128,0},{192,64},{1,129},{65,193},{129,1},{193,65... | collective-permute-start | bytes 393224 | tf_op jit(solution)/shard_map/ppermute | solution.py:356
  20.0 11.4 %collective-permute-start.2 = (bf16[8,64,128]{2,1,0:T(8,128)(2,1)S(1)}, bf16[8,64,128]{2,1,0:T(8,128)(2,1)S(1)}, u32[]{:S(2)}, u32[]{:S(2)}) collective-permute-start(bf16[8,64,128]{2,1,0:T(8,128)(2,1)S(1)} %slice.8), channel_id=1, source_target_pairs={{0,192},{64,128},{128,64},{192,0},{1,193},{65,129},{129,65},{193,1... | collective-permute-start | bytes 393224 | tf_op jit(solution)/shard_map/ppermute | solution.py:356
  20.3 12.1 %collective-permute-start = (bf16[8,64,128]{2,1,0:T(8,128)(2,1)S(1)}, bf16[8,64,128]{2,1,0:T(8,128)(2,1)S(1)}, u32[]{:S(2)}, u32[]{:S(2)}) collective-permute-start(bf16[8,64,128]{2,1,0:T(8,128)(2,1)S(1)} %slice.8), channel_id=1, source_target_pairs={{0,64},{64,0},{128,192},{192,128},{1,65},{65,1},{129,193},{193,129... | collective-permute-start | bytes 393224 | tf_op jit(solution)/shard_map/ppermute | solution.py:356
  21.2 15.8 %collective-permute-start.5 = (bf16[8,32,128]{2,1,0:T(8,128)(2,1)S(1)}, bf16[8,32,128]{2,1,0:T(8,128)(2,1)S(1)}, u32[]{:S(2)}, u32[]{:S(2)}) collective-permute-start(bf16[8,32,128]{2,1,0:T(8,128)(2,1)S(1)} %slice.9), channel_id=1, source_target_pairs={{0,6},{2,4},{4,2},{6,0},{1,7},{3,5},{5,3},{7,1},{8,14},{10,12},{12... | collective-permute-start | bytes 196616 | tf_op jit(solution)/shard_map/ppermute | solution.py:357
  23.9 13.1 %collective-permute-start.4 = (bf16[8,32,128]{2,1,0:T(8,128)(2,1)S(1)}, bf16[8,32,128]{2,1,0:T(8,128)(2,1)S(1)}, u32[]{:S(2)}, u32[]{:S(2)}) collective-permute-start(bf16[8,32,128]{2,1,0:T(8,128)(2,1)S(1)} %slice.9), channel_id=1, source_target_pairs={{0,4},{2,6},{4,0},{6,2},{1,5},{3,7},{5,1},{7,3},{8,12},{10,14},{12... | collective-permute-start | bytes 196616 | tf_op jit(solution)/shard_map/ppermute | solution.py:357
  24.3 12.7 %collective-permute-start.3 = (bf16[8,32,128]{2,1,0:T(8,128)(2,1)S(1)}, bf16[8,32,128]{2,1,0:T(8,128)(2,1)S(1)}, u32[]{:S(2)}, u32[]{:S(2)}) collective-permute-start(bf16[8,32,128]{2,1,0:T(8,128)(2,1)S(1)} %slice.9), channel_id=1, source_target_pairs={{0,2},{2,0},{4,6},{6,4},{1,3},{3,1},{5,7},{7,5},{8,10},{10,8},{12,... | collective-permute-start | bytes 196616 | tf_op jit(solution)/shard_map/ppermute | solution.py:357
  33.0 6.5 %collective-permute-start.6 = (bf16[80,128]{1,0:T(8,128)(2,1)S(1)}, bf16[80,128]{1,0:T(8,128)(2,1)S(1)}, u32[]{:S(2)}, u32[]{:S(2)}) collective-permute-start(bf16[80,128]{1,0:T(8,128)(2,1)S(1)} %get-tuple-element.22), channel_id=1, source_target_pairs={{0,2},{2,0},{4,6},{6,4},{1,3},{3,1},{5,7},{7,5},{8,10},{10,8},{12,... | collective-permute-start | bytes 61448 | tf_op jit(solution)/shard_map/ppermute | solution.py:371
  34.4 5.2 %collective-permute-start.7 = (bf16[80,128]{1,0:T(8,128)(2,1)S(1)}, bf16[80,128]{1,0:T(8,128)(2,1)S(1)}, u32[]{:S(2)}, u32[]{:S(2)}) collective-permute-start(bf16[80,128]{1,0:T(8,128)(2,1)S(1)} %get-tuple-element.23), channel_id=1, source_target_pairs={{0,4},{2,6},{4,0},{6,2},{1,5},{3,7},{5,1},{7,3},{8,12},{10,14},{12... | collective-permute-start | bytes 61448 | tf_op jit(solution)/shard_map/ppermute | solution.py:371
  37.0 3.8 %collective-permute-start.8 = (bf16[80,128]{1,0:T(8,128)(2,1)S(1)}, bf16[80,128]{1,0:T(8,128)(2,1)S(1)}, u32[]{:S(2)}, u32[]{:S(2)}) collective-permute-start(bf16[80,128]{1,0:T(8,128)(2,1)S(1)} %get-tuple-element.24), channel_id=1, source_target_pairs={{0,6},{2,4},{4,2},{6,0},{1,7},{3,5},{5,3},{7,1},{8,14},{10,12},{12... | collective-permute-start | bytes 61448 | tf_op jit(solution)/shard_map/ppermute | solution.py:371
  42.0 16.6 %all-to-all-start.1 = ((bf16[32,104,128]{2,1,0:T(8,128)(2,1)}), bf16[32,104,128]{2,1,0:T(8,128)(2,1)S(1)}, u32[]{:S(2)}, u32[]{:S(2)}) async-start(bf16[32,104,128]{2,1,0:T(8,128)(2,1)} %shard_map.126), calls=%async_computation.1 | async-start | bytes 1703936 | tf_op jit(solution)/shard_map/all_to_all | solution.py:379
  49.1 2.7 %copy-start.1 = (bf16[1024,3072]{1,0:T(8,128)(2,1)}, bf16[1024,3072]{1,0:T(8,128)(2,1)S(1)}, u32[]{:S(2)}) copy-start(bf16[1024,3072]{1,0:T(8,128)(2,1)S(1)} %shard_map.127.w_ref) | copy-start | bytes 18874372
  58.5 2.8 %copy-start.2 = (bf16[1024,3072]{1,0:T(8,128)(2,1)S(1)}, bf16[1024,3072]{1,0:T(8,128)(2,1)}, u32[]{:S(2)}) copy-start(bf16[1024,3072]{1,0:T(8,128)(2,1)} %copy-done.1) | copy-start | bytes 18874372
  61.3 6.5 %copy-start.3 = (bf16[1,16,3072]{2,1,0:T(8,128)(2,1)S(1)}, bf16[1,16,3072]{2,1,0:T(8,128)(2,1)}, u32[]{:S(2)}) copy-start(bf16[1,16,3072]{2,1,0:T(8,128)(2,1)} %param.17) | copy-start | bytes 294916
  61.3 6.5 %copy-start.4 = (f32[3072]{0:T(1024)S(1)}, f32[3072]{0:T(1024)}, u32[]{:S(2)}) copy-start(f32[3072]{0:T(1024)} %param.19) | copy-start | bytes 36868
  61.3 6.5 %copy-start.5 = (f32[3072]{0:T(1024)S(1)}, f32[3072]{0:T(1024)}, u32[]{:S(2)}) copy-start(f32[3072]{0:T(1024)} %param.20) | copy-start | bytes 36868
  63.5 4.3 %collective-permute-start.9 = (bf16[16,3072]{1,0:T(8,128)(2,1)S(1)}, bf16[16,3072]{1,0:T(8,128)(2,1)S(1)}, u32[]{:S(2)}, u32[]{:S(2)}) collective-permute-start(bf16[16,3072]{1,0:T(8,128)(2,1)S(1)} %get-tuple-element.26), channel_id=1, source_target_pairs={{0,1},{1,0},{2,3},{3,2},{4,5},{5,4},{6,7},{7,6},{8,9},{9,8},{10,11... | collective-permute-start | bytes 294920 | tf_op jit(solution)/shard_map/ppermute | solution.py:391

commit v10 on v9

--- a/solution.py
+++ b/solution.py
@@ -352,7 +352,7 @@
     kv = recv[:, 32:96]
     q = recv[:, 0:32]
     others = {}
-    for s in (2, 3, 1):
+    for s in (3, 2, 1):
         others[s] = lax.ppermute(kv, "zh", [(i, i ^ s) for i in range(4)])
     queries = [lax.ppermute(q, "y", [(i, i ^ s) for i in range(4)]) for s in (1, 2, 3)]
     w_near = call(
@@ -365,8 +365,8 @@
         early_body,
         [jax.ShapeDtypeStruct((256, HD), f32), jax.ShapeDtypeStruct((2, 256, 128), f32)],
         5, smem=(0, 1),
-    )(j, txt_len, recv, others[2], txt)
-    pieces = call(text_body, [piece] * 4, 6, smem=(0,))(j, others[3], others[1], txt, acc, stat)
+    )(j, txt_len, recv, others[3], txt)
+    pieces = call(text_body, [piece] * 4, 6, smem=(0,))(j, others[2], others[1], txt, acc, stat)
     for s in (2, 3, 1):
         got[s] = lax.ppermute(pieces[s], "y", [(i, i ^ s) for i in range(4)])
     img = call(

time: 68.8 us -> 70.1 us (1.019)
  starting transfers between devices: 22.4 us -> 24.1 us
    all_to_all x1, waiting for transfers between devices: 6.73 us -> 5.64 us  [shards(): home = lax.all_to_all(back, CUBE, 0, 0, tiled=True)]
    ppermute x1, starting transfers between devices: 3.35 us -> 4.44 us  [shards(): theirs = lax.ppermute(other, 'tp', [(0, 1), (1, 0)])]
    ppermute x3, starting transfers between devices: 3.4 us -> 4.38 us  [shards(): lax.ppermute(q, 'y', [(i, i ^ s) for i in range(4)])]
  transfers between devices with their start and end apart: 11 -> 11, of which waited for: 5 -> 5; matrix products, arithmetic and copies ran while one was open for 0% -> 0% of each run, Pallas kernels for 10% -> 9%
where the time goes in v10:
time: 70.1 us; the launch traced here: 69.8 us
  starting transfers between devices  24.1 us (34%)
  waiting for transfers between devices  15 us (21%)
  blocking collectives  11.9 us (17%)
  Pallas kernels  11.1 us (16%)
  local copies, waits for them, and re-layouts  5.53 us (8%)
  between operations  1.41 us (2%)
    all_to_all x1, blocking collectives, shards(): recv = lax.all_to_all(send, HEAD, 0, 0, tiled=True)  11.9 us
    pallas_call x7, Pallas kernels, run(): return kernel(*held)  11.1 us
    ppermute x3, starting transfers between devices, shards(): others[s] = lax.ppermute(kv, 'zh', [(i, i ^ s) for i in range(4)])  7.39 us
    ppermute x3, waiting for transfers between devices, shards(): others[s] = lax.ppermute(kv, 'zh', [(i, i ^ s) for i in range(4)])  7.13 us
    all_to_all x1, waiting for transfers between devices, shards(): home = lax.all_to_all(back, CUBE, 0, 0, tiled=True)  5.64 us
    unnamed x12, local copies, waits for them, and re-layouts  5.46 us
    ppermute x1, starting transfers between devices, shards(): theirs = lax.ppermute(other, 'tp', [(0, 1), (1, 0)])  4.44 us
    ppermute x3, starting transfers between devices, shards(): lax.ppermute(q, 'y', [(i, i ^ s) for i in range(4)])  4.38 us
  transfers between devices with their start and end apart: 11, of which 5 were waited for; matrix products, arithmetic and copies ran while one was open for 0% of the time, Pallas kernels for 9%

profile of v10, /device:TPU:1, one launch (start us, length us, event | category | flops | bytes accessed | tf_op | source)
XLA Modules:
  0.0 69.8 jit_solution(6951543711554927649)
XLA Ops:
  0.6 0.0 copy-start
  0.7 1.3 %shard_map.122 = bf16[8,96,128]{2,1,0:T(8,128)(2,1)S(1)} custom-call(bf16[3,32,1024]{2,1,0:T(8,128)(2,1)} %bitcast.15, s32[1,32]{1,0:T(1,128)} %frame_hbm, s32[1,32]{1,0:T(1,128)} %row_hbm.1, s32[1,32]{1,0:T(1,128)} %col_hbm.1, f32[8,128]{1,0:T(8,128)} %constant.26.clone.rate_hbm), custom_call_target="tpu_custom_call" | custom-call | tf_op jit(solution)/shard_map/pallas_call | solution.py:61
  2.0 11.9 %all_to_all.10.recv_ref = bf16[8,96,128]{2,1,0:T(8,128)(2,1)S(1)} all-to-all(bf16[8,96,128]{2,1,0:T(8,128)(2,1)S(1)} %shard_map.122), channel_id=1, replica_groups=mesh['zh'=4,'zl'=2,'x'=4,'y'=4,'tp'=2] {'zl','x'}, dimensions={0} | all-to-all | bytes 393216 | tf_op jit(solution)/shard_map/all_to_all | solution.py:351
  13.9 5.2 %collective-permute-start.2 = (bf16[8,64,128]{2,1,0:T(8,128)(2,1)S(1)}, bf16[8,64,128]{2,1,0:T(8,128)(2,1)S(1)}, u32[]{:S(2)}, u32[]{:S(2)}) collective-permute-start(bf16[8,64,128]{2,1,0:T(8,128)(2,1)S(1)} %slice.8), channel_id=1, source_target_pairs={{0,192},{64,128},{128,64},{192,0},{1,193},{65,129},{129,65},{193,1... | collective-permute-start | bytes 393224 | tf_op jit(solution)/shard_map/ppermute | solution.py:356
  19.1 1.2 %collective-permute-start.1 = (bf16[8,64,128]{2,1,0:T(8,128)(2,1)S(1)}, bf16[8,64,128]{2,1,0:T(8,128)(2,1)S(1)}, u32[]{:S(2)}, u32[]{:S(2)}) collective-permute-start(bf16[8,64,128]{2,1,0:T(8,128)(2,1)S(1)} %slice.8), channel_id=1, source_target_pairs={{0,128},{64,192},{128,0},{192,64},{1,129},{65,193},{129,1},{193,65... | collective-permute-start | bytes 393224 | tf_op jit(solution)/shard_map/ppermute | solution.py:356
  20.3 1.0 %collective-permute-start = (bf16[8,64,128]{2,1,0:T(8,128)(2,1)S(1)}, bf16[8,64,128]{2,1,0:T(8,128)(2,1)S(1)}, u32[]{:S(2)}, u32[]{:S(2)}) collective-permute-start(bf16[8,64,128]{2,1,0:T(8,128)(2,1)S(1)} %slice.8), channel_id=1, source_target_pairs={{0,64},{64,0},{128,192},{192,128},{1,65},{65,1},{129,193},{193,129... | collective-permute-start | bytes 393224 | tf_op jit(solution)/shard_map/ppermute | solution.py:356
  21.3 2.7 %collective-permute-start.5 = (bf16[8,32,128]{2,1,0:T(8,128)(2,1)S(1)}, bf16[8,32,128]{2,1,0:T(8,128)(2,1)S(1)}, u32[]{:S(2)}, u32[]{:S(2)}) collective-permute-start(bf16[8,32,128]{2,1,0:T(8,128)(2,1)S(1)} %slice.9), channel_id=1, source_target_pairs={{0,6},{2,4},{4,2},{6,0},{1,7},{3,5},{5,3},{7,1},{8,14},{10,12},{12... | collective-permute-start | bytes 196616 | tf_op jit(solution)/shard_map/ppermute | solution.py:357
  24.0 0.3 collective-permute-start.4
  24.4 6.0 %collective-permute-done.2.kv3_ref.kv_ref = bf16[8,64,128]{2,1,0:T(8,128)(2,1)S(1)} collective-permute-done((bf16[8,64,128]{2,1,0:T(8,128)(2,1)S(1)}, bf16[8,64,128]{2,1,0:T(8,128)(2,1)S(1)}, u32[]{:S(2)}, u32[]{:S(2)}) %collective-permute-start.2) | collective-permute-done | bytes 131104 | tf_op jit(solution)/shard_map/ppermute | solution.py:356
  30.4 1.3 %collective-permute-start.3 = (bf16[8,32,128]{2,1,0:T(8,128)(2,1)S(1)}, bf16[8,32,128]{2,1,0:T(8,128)(2,1)S(1)}, u32[]{:S(2)}, u32[]{:S(2)}) collective-permute-start(bf16[8,32,128]{2,1,0:T(8,128)(2,1)S(1)} %slice.9), channel_id=1, source_target_pairs={{0,2},{2,0},{4,6},{6,4},{1,3},{3,1},{5,7},{7,5},{8,10},{10,8},{12,... | collective-permute-start | bytes 196616 | tf_op jit(solution)/shard_map/ppermute | solution.py:357
  31.7 0.0 copy-done
  31.7 0.1 dynamic-slice_bitcast_fusion.txt_ref
  32.4 0.6 shard_map.124
  33.0 0.0 collective-permute-done.1.kv2_ref.kv0_ref
  33.0 1.1 %collective-permute-done.kv1_ref = bf16[8,64,128]{2,1,0:T(8,128)(2,1)S(1)} collective-permute-done((bf16[8,64,128]{2,1,0:T(8,128)(2,1)S(1)}, bf16[8,64,128]{2,1,0:T(8,128)(2,1)S(1)}, u32[]{:S(2)}, u32[]{:S(2)}) %collective-permute-start) | collective-permute-done | bytes 131104 | tf_op jit(solution)/shard_map/ppermute | solution.py:356
  34.1 0.6 shard_map.125
  34.7 1.4 %collective-permute-start.6 = (bf16[80,128]{1,0:T(8,128)(2,1)S(1)}, bf16[80,128]{1,0:T(8,128)(2,1)S(1)}, u32[]{:S(2)}, u32[]{:S(2)}) collective-permute-start(bf16[80,128]{1,0:T(8,128)(2,1)S(1)} %get-tuple-element.22), channel_id=1, source_target_pairs={{0,2},{2,0},{4,6},{6,4},{1,3},{3,1},{5,7},{7,5},{8,10},{10,8},{12,... | collective-permute-start | bytes 61448 | tf_op jit(solution)/shard_map/ppermute | solution.py:371
  36.1 2.6 %collective-permute-start.7 = (bf16[80,128]{1,0:T(8,128)(2,1)S(1)}, bf16[80,128]{1,0:T(8,128)(2,1)S(1)}, u32[]{:S(2)}, u32[]{:S(2)}) collective-permute-start(bf16[80,128]{1,0:T(8,128)(2,1)S(1)} %get-tuple-element.23), channel_id=1, source_target_pairs={{0,4},{2,6},{4,0},{6,2},{1,5},{3,7},{5,1},{7,3},{8,12},{10,14},{12... | collective-permute-start | bytes 61448 | tf_op jit(solution)/shard_map/ppermute | solution.py:371
  38.7 0.0 collective-permute-done.5.q3_ref
  38.7 0.0 collective-permute-start.8
  38.7 0.0 collective-permute-done.4.q2_ref
  38.7 0.0 collective-permute-done.3.q1_ref
  38.7 2.5 %shard_map.123.img_ref = bf16[32,40,128]{2,1,0:T(8,128)(2,1)S(1)} custom-call(s32[1]{0:T(128)} %bitcast.1.where_ref, s32[1]{0:T(128)S(6)} %copy.13.len_ref, bf16[8,96,128]{2,1,0:T(8,128)(2,1)S(1)} %all_to_all.10.recv_ref, bf16[8,64,128]{2,1,0:T(8,128)(2,1)S(1)} %collective-permute-done.kv1_ref, ...), custom_call_target="tpu_custom_call" | custom-call | tf_op jit(solution)/shard_map/pallas_call | solution.py:61
  41.2 0.0 collective-permute-done.6.p1_ref
  41.3 0.0 collective-permute-done.7.p2_ref
  41.3 1.3 %collective-permute-done.8.p3_ref = bf16[80,128]{1,0:T(8,128)(2,1)S(1)} collective-permute-done((bf16[80,128]{1,0:T(8,128)(2,1)S(1)}, bf16[80,128]{1,0:T(8,128)(2,1)S(1)}, u32[]{:S(2)}, u32[]{:S(2)}) %collective-permute-start.8) | collective-permute-done | bytes 20512 | tf_op jit(solution)/shard_map/ppermute | solution.py:371
  42.6 1.1 %shard_map.126 = bf16[32,104,128]{2,1,0:T(8,128)(2,1)} custom-call(s32[1]{0:T(128)} %bitcast.1.where_ref, s32[1]{0:T(128)S(6)} %copy.13.len_ref, bf16[32,40,128]{2,1,0:T(8,128)(2,1)S(1)} %shard_map.123.img_ref, bf16[80,128]{1,0:T(8,128)(2,1)S(1)} %get-tuple-element.21.p0_ref, bf16[80,128]{1,0:T(8,128)(2,1)S(1)} %collective-permute-done.6.p1_ref, ...), custom_call_target="tpu_custom_call" | custom-call | tf_op jit(solution)/shard_map/pallas_call | solution.py:61
  43.7 3.9 %all-to-all-start.1 = ((bf16[32,104,128]{2,1,0:T(8,128)(2,1)}), bf16[32,104,128]{2,1,0:T(8,128)(2,1)S(1)}, u32[]{:S(2)}, u32[]{:S(2)}) async-start(bf16[32,104,128]{2,1,0:T(8,128)(2,1)} %shard_map.126), calls=%async_computation.1 | async-start | bytes 1703936 | tf_op jit(solution)/shard_map/all_to_all | solution.py:379
  47.6 2.9 %shard_map.127.w_ref = bf16[1024,3072]{1,0:T(8,128)(2,1)S(1)} custom-call(bf16[1024,3072]{1,0:T(8,128)(2,1)} %w_hbm.1), custom_call_target="tpu_custom_call" | custom-call | tf_op jit(solution)/shard_map/pallas_call | solution.py:61
  50.5 0.0 copy-start.1
  50.5 2.7 %copy-done.1 = bf16[1024,3072]{1,0:T(8,128)(2,1)} copy-done((bf16[1024,3072]{1,0:T(8,128)(2,1)}, bf16[1024,3072]{1,0:T(8,128)(2,1)S(1)}, u32[]{:S(2)}) %copy-start.1) | copy-done | bytes 6291480
  53.1 5.6 %all-to-all-done.1.recv_ref = bf16[32,104,128]{2,1,0:T(8,128)(2,1)S(1)} async-done(((bf16[32,104,128]{2,1,0:T(8,128)(2,1)}), bf16[32,104,128]{2,1,0:T(8,128)(2,1)S(1)}, u32[]{:S(2)}, u32[]{:S(2)}) %all-to-all-start.1) | async-done | bytes 852000 | tf_op jit(solution)/shard_map/all_to_all | solution.py:379
  58.8 0.0 copy-start.2
  58.8 2.8 %copy-done.2 = bf16[1024,3072]{1,0:T(8,128)(2,1)S(1)} copy-done((bf16[1024,3072]{1,0:T(8,128)(2,1)S(1)}, bf16[1024,3072]{1,0:T(8,128)(2,1)}, u32[]{:S(2)}) %copy-start.2) | copy-done | bytes 6291480
  61.6 0.0 copy-start.3
  61.6 0.0 copy-start.4
  61.6 0.0 copy-start.5
  61.6 2.1 %shard_map.128 = (f32[16,3072]{1,0:T(8,128)S(1)}, bf16[16,3072]{1,0:T(8,128)(2,1)S(1)}, bf16[256,1024]{1,0:T(8,128)(2,1)}) custom-call(s32[1]{0:T(128)} %bitcast.2.core_ref, bf16[32,104,128]{2,1,0:T(8,128)(2,1)S(1)} %all-to-all-done.1.recv_ref, bf16[1024,3072]{1,0:T(8,128)(2,1)S(1)} %copy-done.2), custom_call_target="tpu_custom_call" | custom-call | tf_op jit(solution)/shard_map/pallas_call | solution.py:61
  63.7 4.4 %collective-permute-start.9 = (bf16[16,3072]{1,0:T(8,128)(2,1)S(1)}, bf16[16,3072]{1,0:T(8,128)(2,1)S(1)}, u32[]{:S(2)}, u32[]{:S(2)}) collective-permute-start(bf16[16,3072]{1,0:T(8,128)(2,1)S(1)} %get-tuple-element.26), channel_id=1, source_target_pairs={{0,1},{1,0},{2,3},{3,2},{4,5},{5,4},{6,7},{7,6},{8,9},{9,8},{10,11... | collective-permute-start | bytes 294920 | tf_op jit(solution)/shard_map/ppermute | solution.py:391
  68.2 0.9 %collective-permute-done.9 = bf16[16,3072]{1,0:T(8,128)(2,1)S(1)} collective-permute-done((bf16[16,3072]{1,0:T(8,128)(2,1)S(1)}, bf16[16,3072]{1,0:T(8,128)(2,1)S(1)}, u32[]{:S(2)}, u32[]{:S(2)}) %collective-permute-start.9) | collective-permute-done | bytes 98336 | tf_op jit(solution)/shard_map/ppermute | solution.py:391
  69.1 0.0 copy-done.3
  69.1 0.0 copy-done.4
  69.1 0.0 copy-done.5
  69.1 0.7 fusion.1
  (2 shorter events, 0.0 us)
Async XLA Ops:
  0.6 31.1 %copy-start = (bf16[1,256,3,1024]{3,1,2,0:T(8,128)(2,1)S(1)}, bf16[1,256,3,1024]{3,1,2,0:T(8,128)(2,1)}, u32[]{:S(2)}) copy-start(bf16[1,256,3,1024]{3,1,2,0:T(8,128)(2,1)} %param.12) | copy-start | bytes 4718596
  13.9 16.5 %collective-permute-start.2 = (bf16[8,64,128]{2,1,0:T(8,128)(2,1)S(1)}, bf16[8,64,128]{2,1,0:T(8,128)(2,1)S(1)}, u32[]{:S(2)}, u32[]{:S(2)}) collective-permute-start(bf16[8,64,128]{2,1,0:T(8,128)(2,1)S(1)} %slice.8), channel_id=1, source_target_pairs={{0,192},{64,128},{128,64},{192,0},{1,193},{65,129},{129,65},{193,1... | collective-permute-start | bytes 393224 | tf_op jit(solution)/shard_map/ppermute | solution.py:356
  19.1 13.9 %collective-permute-start.1 = (bf16[8,64,128]{2,1,0:T(8,128)(2,1)S(1)}, bf16[8,64,128]{2,1,0:T(8,128)(2,1)S(1)}, u32[]{:S(2)}, u32[]{:S(2)}) collective-permute-start(bf16[8,64,128]{2,1,0:T(8,128)(2,1)S(1)} %slice.8), channel_id=1, source_target_pairs={{0,128},{64,192},{128,0},{192,64},{1,129},{65,193},{129,1},{193,65... | collective-permute-start | bytes 393224 | tf_op jit(solution)/shard_map/ppermute | solution.py:356
  20.3 13.8 %collective-permute-start = (bf16[8,64,128]{2,1,0:T(8,128)(2,1)S(1)}, bf16[8,64,128]{2,1,0:T(8,128)(2,1)S(1)}, u32[]{:S(2)}, u32[]{:S(2)}) collective-permute-start(bf16[8,64,128]{2,1,0:T(8,128)(2,1)S(1)} %slice.8), channel_id=1, source_target_pairs={{0,64},{64,0},{128,192},{192,128},{1,65},{65,1},{129,193},{193,129... | collective-permute-start | bytes 393224 | tf_op jit(solution)/shard_map/ppermute | solution.py:356
  21.3 17.4 %collective-permute-start.5 = (bf16[8,32,128]{2,1,0:T(8,128)(2,1)S(1)}, bf16[8,32,128]{2,1,0:T(8,128)(2,1)S(1)}, u32[]{:S(2)}, u32[]{:S(2)}) collective-permute-start(bf16[8,32,128]{2,1,0:T(8,128)(2,1)S(1)} %slice.9), channel_id=1, source_target_pairs={{0,6},{2,4},{4,2},{6,0},{1,7},{3,5},{5,3},{7,1},{8,14},{10,12},{12... | collective-permute-start | bytes 196616 | tf_op jit(solution)/shard_map/ppermute | solution.py:357
  24.0 14.7 %collective-permute-start.4 = (bf16[8,32,128]{2,1,0:T(8,128)(2,1)S(1)}, bf16[8,32,128]{2,1,0:T(8,128)(2,1)S(1)}, u32[]{:S(2)}, u32[]{:S(2)}) collective-permute-start(bf16[8,32,128]{2,1,0:T(8,128)(2,1)S(1)} %slice.9), channel_id=1, source_target_pairs={{0,4},{2,6},{4,0},{6,2},{1,5},{3,7},{5,1},{7,3},{8,12},{10,14},{12... | collective-permute-start | bytes 196616 | tf_op jit(solution)/shard_map/ppermute | solution.py:357
  30.4 8.3 %collective-permute-start.3 = (bf16[8,32,128]{2,1,0:T(8,128)(2,1)S(1)}, bf16[8,32,128]{2,1,0:T(8,128)(2,1)S(1)}, u32[]{:S(2)}, u32[]{:S(2)}) collective-permute-start(bf16[8,32,128]{2,1,0:T(8,128)(2,1)S(1)} %slice.9), channel_id=1, source_target_pairs={{0,2},{2,0},{4,6},{6,4},{1,3},{3,1},{5,7},{7,5},{8,10},{10,8},{12,... | collective-permute-start | bytes 196616 | tf_op jit(solution)/shard_map/ppermute | solution.py:357
  34.7 6.5 %collective-permute-start.6 = (bf16[80,128]{1,0:T(8,128)(2,1)S(1)}, bf16[80,128]{1,0:T(8,128)(2,1)S(1)}, u32[]{:S(2)}, u32[]{:S(2)}) collective-permute-start(bf16[80,128]{1,0:T(8,128)(2,1)S(1)} %get-tuple-element.22), channel_id=1, source_target_pairs={{0,2},{2,0},{4,6},{6,4},{1,3},{3,1},{5,7},{7,5},{8,10},{10,8},{12,... | collective-permute-start | bytes 61448 | tf_op jit(solution)/shard_map/ppermute | solution.py:371
  36.1 5.2 %collective-permute-start.7 = (bf16[80,128]{1,0:T(8,128)(2,1)S(1)}, bf16[80,128]{1,0:T(8,128)(2,1)S(1)}, u32[]{:S(2)}, u32[]{:S(2)}) collective-permute-start(bf16[80,128]{1,0:T(8,128)(2,1)S(1)} %get-tuple-element.23), channel_id=1, source_target_pairs={{0,4},{2,6},{4,0},{6,2},{1,5},{3,7},{5,1},{7,3},{8,12},{10,14},{12... | collective-permute-start | bytes 61448 | tf_op jit(solution)/shard_map/ppermute | solution.py:371
  38.7 3.8 %collective-permute-start.8 = (bf16[80,128]{1,0:T(8,128)(2,1)S(1)}, bf16[80,128]{1,0:T(8,128)(2,1)S(1)}, u32[]{:S(2)}, u32[]{:S(2)}) collective-permute-start(bf16[80,128]{1,0:T(8,128)(2,1)S(1)} %get-tuple-element.24), channel_id=1, source_target_pairs={{0,6},{2,4},{4,2},{6,0},{1,7},{3,5},{5,3},{7,1},{8,14},{10,12},{12... | collective-permute-start | bytes 61448 | tf_op jit(solution)/shard_map/ppermute | solution.py:371
  43.7 15.1 %all-to-all-start.1 = ((bf16[32,104,128]{2,1,0:T(8,128)(2,1)}), bf16[32,104,128]{2,1,0:T(8,128)(2,1)S(1)}, u32[]{:S(2)}, u32[]{:S(2)}) async-start(bf16[32,104,128]{2,1,0:T(8,128)(2,1)} %shard_map.126), calls=%async_computation.1 | async-start | bytes 1703936 | tf_op jit(solution)/shard_map/all_to_all | solution.py:379
  50.5 2.7 %copy-start.1 = (bf16[1024,3072]{1,0:T(8,128)(2,1)}, bf16[1024,3072]{1,0:T(8,128)(2,1)S(1)}, u32[]{:S(2)}) copy-start(bf16[1024,3072]{1,0:T(8,128)(2,1)S(1)} %shard_map.127.w_ref) | copy-start | bytes 18874372
  58.8 2.8 %copy-start.2 = (bf16[1024,3072]{1,0:T(8,128)(2,1)S(1)}, bf16[1024,3072]{1,0:T(8,128)(2,1)}, u32[]{:S(2)}) copy-start(bf16[1024,3072]{1,0:T(8,128)(2,1)} %copy-done.1) | copy-start | bytes 18874372
  61.6 7.5 %copy-start.3 = (bf16[1,16,3072]{2,1,0:T(8,128)(2,1)S(1)}, bf16[1,16,3072]{2,1,0:T(8,128)(2,1)}, u32[]{:S(2)}) copy-start(bf16[1,16,3072]{2,1,0:T(8,128)(2,1)} %param.17) | copy-start | bytes 294916
  61.6 7.5 %copy-start.4 = (f32[3072]{0:T(1024)S(1)}, f32[3072]{0:T(1024)}, u32[]{:S(2)}) copy-start(f32[3072]{0:T(1024)} %param.19) | copy-start | bytes 36868
  61.6 7.5 %copy-start.5 = (f32[3072]{0:T(1024)S(1)}, f32[3072]{0:T(1024)}, u32[]{:S(2)}) copy-start(f32[3072]{0:T(1024)} %param.20) | copy-start | bytes 36868
  63.7 5.4 %collective-permute-start.9 = (bf16[16,3072]{1,0:T(8,128)(2,1)S(1)}, bf16[16,3072]{1,0:T(8,128)(2,1)S(1)}, u32[]{:S(2)}, u32[]{:S(2)}) collective-permute-start(bf16[16,3072]{1,0:T(8,128)(2,1)S(1)} %get-tuple-element.26), channel_id=1, source_target_pairs={{0,1},{1,0},{2,3},{3,2},{4,5},{5,4},{6,7},{7,6},{8,9},{9,8},{10,11... | collective-permute-start | bytes 294920 | tf_op jit(solution)/shard_map/ppermute | solution.py:391

commit v11 on v9

--- a/solution.py
+++ b/solution.py
@@ -221,9 +221,18 @@
 
 
 def image_body(
-    where_ref, len_ref, recv_ref, kv1_ref, kv2_ref, kv3_ref, q1_ref, q2_ref, q3_ref, txt_ref,
-    out_ref, keys_ref, values_ref,
+    where_ref, len_ref, recv_ref, kv1_ref, kv2_ref, kv3_ref, q1_ref, q2_ref, q3_ref, txt_ref, w_hbm,
+    out_ref, w_out, keys_ref, values_ref, sems,
 ):
+    share = w_hbm.shape[0] // 8
+    fetches = [
+        pltpu.make_async_copy(
+            w_hbm.at[pl.ds(share * i, share)], w_out.at[pl.ds(share * i, share)], sems.at[i]
+        )
+        for i in range(8)
+    ]
+    for c in fetches:
+        c.start()
     j = where_ref[0]
     keys_ref[0:256, :] = recv_ref[:, 32:64, :].reshape(256, HD)
     values_ref[0:256, :] = recv_ref[:, 64:96, :].reshape(256, HD)
@@ -248,19 +257,7 @@
         packed = jnp.where(jnp.logical_and(row == lane % 32, lane < 96), parts, 0.0)
         packed = jnp.sum(packed, axis=1, keepdims=True)
         out_ref[at, 32:40, :] = jnp.broadcast_to(packed, (8, 8, 128)).astype(bf16)
-
-
-def weights_body(w_hbm, w_out, sems):
-    share = w_hbm.shape[0] // 8
-    copies = [
-        pltpu.make_async_copy(
-            w_hbm.at[pl.ds(share * i, share)], w_out.at[pl.ds(share * i, share)], sems.at[i]
-        )
-        for i in range(8)
-    ]
-    for c in copies:
-        c.start()
-    for c in copies:
+    for c in fetches:
         c.wait()
 
 
@@ -301,22 +298,29 @@
     row = lax.broadcasted_iota(jnp.int32, (32, 128), 0)
     lane = lax.broadcasted_iota(jnp.int32, (32, 128), 1)
     pick = jnp.logical_and(row == lane % 32, lane < 96)
-    heads = []
     for head in range(8):
-        outs, lses = [], []
         for j in range(4):
-            s = head * 4 + j
-            outs.append(recv_ref[s, 0:32, :].astype(f32))
-            stats = recv_ref[s, 96:104, :].astype(f32)[0:1]
-            lses.append(jnp.sum(jnp.where(pick, stats, 0.0), axis=1, keepdims=True))
-            txt_ref[64 * j : 64 * j + 64, head * HD : (head + 1) * HD] = recv_ref[s, 32:96, :]
-        heads.append(blend(outs, lses))
+            txt_ref[64 * j : 64 * j + 64, head * HD : (head + 1) * HD] = recv_ref[head * 4 + j, 32:96, :]
     leave = pltpu.make_async_copy(txt_ref, txt_out, sem)
     leave.start()
-    rows = jnp.concatenate(heads, axis=1)
-    flipped = jnp.concatenate([rows[16:32], rows[0:16]], axis=0)
-    rows = jnp.where(core_ref[0] == 0, rows, flipped).astype(bf16)
-    projected = jnp.dot(rows, w_ref[...], preferred_element_type=f32)
+    projected = None
+    for pair in range(4):
+        heads = []
+        for head in (2 * pair, 2 * pair + 1):
+            outs, lses = [], []
+            for j in range(4):
+                s = head * 4 + j
+                outs.append(recv_ref[s, 0:32, :].astype(f32))
+                stats = recv_ref[s, 96:104, :].astype(f32)[0:1]
+                lses.append(jnp.sum(jnp.where(pick, stats, 0.0), axis=1, keepdims=True))
+            heads.append(blend(outs, lses))
+        rows = jnp.concatenate(heads, axis=1)
+        flipped = jnp.concatenate([rows[16:32], rows[0:16]], axis=0)
+        rows = jnp.where(core_ref[0] == 0, rows, flipped).astype(bf16)
+        part = jnp.dot(
+            rows, w_ref[256 * pair : 256 * pair + 256, :], preferred_element_type=f32
+        )
+        projected = part if projected is None else projected + part
     mine_ref[...] = projected[0:16]
     other_ref[...] = projected[16:32].astype(bf16)
     leave.wait()
@@ -355,10 +359,7 @@
     for s in (2, 3, 1):
         others[s] = lax.ppermute(kv, "zh", [(i, i ^ s) for i in range(4)])
     queries = [lax.ppermute(q, "y", [(i, i ^ s) for i in range(4)]) for s in (1, 2, 3)]
-    w_near = call(
-        weights_body, pltpu.VMEM(w_proj.shape, bf16), 1, hbm=(0,),
-        scratch=(pltpu.SemaphoreType.DMA((8,)),),
-    )(w_proj)
+
     piece = jax.ShapeDtypeStruct((80, HD), bf16)
     got = {}
     acc, stat = call(
@@ -369,10 +370,14 @@
     pieces = call(text_body, [piece] * 4, 6, smem=(0,))(j, others[3], others[1], txt, acc, stat)
     for s in (2, 3, 1):
         got[s] = lax.ppermute(pieces[s], "y", [(i, i ^ s) for i in range(4)])
-    img = call(
-        image_body, jax.ShapeDtypeStruct((32, 40, HD), bf16), 10, smem=(0, 1),
-        scratch=(pltpu.VMEM((1152, HD), bf16), pltpu.VMEM((1152, HD), bf16)),
-    )(j, txt_len, recv, others[1], others[2], others[3], *queries, txt)
+    img, w_near = call(
+        image_body,
+        [jax.ShapeDtypeStruct((32, 40, HD), bf16), pltpu.VMEM(w_proj.shape, bf16)],
+        11, smem=(0, 1), hbm=(10,),
+        scratch=(
+            pltpu.VMEM((1152, HD), bf16), pltpu.VMEM((1152, HD), bf16), pltpu.SemaphoreType.DMA((8,)),
+        ),
+    )(j, txt_len, recv, others[1], others[2], others[3], *queries, txt, w_proj)
     back = call(fill_body, jax.ShapeDtypeStruct((32, 104, HD), bf16), 7, smem=(0, 1))(
         j, txt_len, img, pieces[0], got[1], got[2], got[3]
     )

time: 68.8 us -> 65.7 us (0.955)
  blocking collectives: 11.9 us -> 29.3 us
  waiting for transfers between devices: 15.5 us -> 7.81 us
  local copies, waits for them, and re-layouts: 5.53 us -> 0.09 us
  starting transfers between devices: 22.4 us -> 18 us
  Pallas kernels: 11.2 us -> 8.22 us
    all_to_all x0 -> x1, blocking collectives: none -> 17.4 us  [shards(): home = lax.all_to_all(back, CUBE, 0, 0, tiled=True)]
    all_to_all x1 -> x0, waiting for transfers between devices: 6.73 us -> none  [shards(): home = lax.all_to_all(back, CUBE, 0, 0, tiled=True)]
    unnamed x12 -> x8, local copies, waits for them, and re-layouts: 5.46 us -> 0.03 us
    all_to_all x1 -> x0, starting transfers between devices: 4.3 us -> none  [shards(): home = lax.all_to_all(back, CUBE, 0, 0, tiled=True)]
    pallas_call x7 -> x6, Pallas kernels: 11.2 us -> 8.22 us  [run(): return kernel(*held)]
    ppermute x3, waiting for transfers between devices: 1.3 us -> 0.37 us  [shards(): got[s] = lax.ppermute(pieces[s], 'y', [(i, i ^ s) for i in range(4)])]
  transfers between devices with their start and end apart: 11 -> 10, of which waited for: 5 -> 4; matrix products, arithmetic and copies ran while one was open for 0% -> 0% of each run, Pallas kernels for 10% -> 7%
where the time goes in v11:
time: 65.7 us; the launch traced here: 65.5 us
  blocking collectives  29.3 us (45%)
  starting transfers between devices  18 us (27%)
  Pallas kernels  8.22 us (13%)
  waiting for transfers between devices  7.81 us (12%)
  between operations  1.41 us (2%)
  other arithmetic  0.7 us (1%)
    all_to_all x1, blocking collectives, shards(): home = lax.all_to_all(back, CUBE, 0, 0, tiled=True)  17.4 us
    all_to_all x1, blocking collectives, shards(): recv = lax.all_to_all(send, HEAD, 0, 0, tiled=True)  11.9 us
    pallas_call x6, Pallas kernels, run(): return kernel(*held)  8.22 us
    ppermute x3, starting transfers between devices, shards(): others[s] = lax.ppermute(kv, 'zh', [(i, i ^ s) for i in range(4)])  7.29 us
    ppermute x3, waiting for transfers between devices, shards(): others[s] = lax.ppermute(kv, 'zh', [(i, i ^ s) for i in range(4)])  6.49 us
    ppermute x3, starting transfers between devices, shards(): got[s] = lax.ppermute(pieces[s], 'y', [(i, i ^ s) for i in range(4)])  4.01 us
    ppermute x3, starting transfers between devices, shards(): lax.ppermute(q, 'y', [(i, i ^ s) for i in range(4)])  3.4 us
    ppermute x1, starting transfers between devices, shards(): theirs = lax.ppermute(other, 'tp', [(0, 1), (1, 0)])  3.26 us
  transfers between devices with their start and end apart: 10, of which 4 were waited for; matrix products, arithmetic and copies ran while one was open for 0% of the time, Pallas kernels for 7%

profile of v11, /device:TPU:1, one launch (start us, length us, event | category | flops | bytes accessed | tf_op | source)
XLA Modules:
  0.0 65.5 jit_solution(10538072419241342216)
XLA Ops:
  0.6 0.0 copy-start
  0.7 1.3 %shard_map.122 = bf16[8,96,128]{2,1,0:T(8,128)(2,1)S(1)} custom-call(bf16[3,32,1024]{2,1,0:T(8,128)(2,1)} %bitcast.15, s32[1,32]{1,0:T(1,128)} %frame_hbm, s32[1,32]{1,0:T(1,128)} %row_hbm.1, s32[1,32]{1,0:T(1,128)} %col_hbm.1, f32[8,128]{1,0:T(8,128)} %constant.26.clone.rate_hbm), custom_call_target="tpu_custom_call" | custom-call | tf_op jit(solution)/shard_map/pallas_call | solution.py:61
  2.0 11.9 %all_to_all.10.recv_ref = bf16[8,96,128]{2,1,0:T(8,128)(2,1)S(1)} all-to-all(bf16[8,96,128]{2,1,0:T(8,128)(2,1)S(1)} %shard_map.122), channel_id=1, replica_groups=mesh['zh'=4,'zl'=2,'x'=4,'y'=4,'tp'=2] {'zl','x'}, dimensions={0} | all-to-all | bytes 393216 | tf_op jit(solution)/shard_map/all_to_all | solution.py:355
  13.9 6.1 %collective-permute-start.1 = (bf16[8,64,128]{2,1,0:T(8,128)(2,1)S(1)}, bf16[8,64,128]{2,1,0:T(8,128)(2,1)S(1)}, u32[]{:S(2)}, u32[]{:S(2)}) collective-permute-start(bf16[8,64,128]{2,1,0:T(8,128)(2,1)S(1)} %slice.8), channel_id=1, source_target_pairs={{0,128},{64,192},{128,0},{192,64},{1,129},{65,193},{129,1},{193,65... | collective-permute-start | bytes 393224 | tf_op jit(solution)/shard_map/ppermute | solution.py:360
  20.0 0.3 collective-permute-start.2
  20.3 0.9 %collective-permute-start = (bf16[8,64,128]{2,1,0:T(8,128)(2,1)S(1)}, bf16[8,64,128]{2,1,0:T(8,128)(2,1)S(1)}, u32[]{:S(2)}, u32[]{:S(2)}) collective-permute-start(bf16[8,64,128]{2,1,0:T(8,128)(2,1)S(1)} %slice.8), channel_id=1, source_target_pairs={{0,64},{64,0},{128,192},{192,128},{1,65},{65,1},{129,193},{193,129... | collective-permute-start | bytes 393224 | tf_op jit(solution)/shard_map/ppermute | solution.py:360
  21.2 2.7 %collective-permute-start.5 = (bf16[8,32,128]{2,1,0:T(8,128)(2,1)S(1)}, bf16[8,32,128]{2,1,0:T(8,128)(2,1)S(1)}, u32[]{:S(2)}, u32[]{:S(2)}) collective-permute-start(bf16[8,32,128]{2,1,0:T(8,128)(2,1)S(1)} %slice.9), channel_id=1, source_target_pairs={{0,6},{2,4},{4,2},{6,0},{1,7},{3,5},{5,3},{7,1},{8,14},{10,12},{12... | collective-permute-start | bytes 196616 | tf_op jit(solution)/shard_map/ppermute | solution.py:361
  23.9 0.3 collective-permute-start.4
  24.3 0.0 collective-permute-done.1.kv2_ref.kv_ref
  24.3 0.3 collective-permute-start.3
  24.6 0.0 copy-done
  24.6 0.1 dynamic-slice_bitcast_fusion.txt_ref
  25.3 0.6 shard_map.124
  25.9 5.5 %collective-permute-done.2.kv3_ref.kv0_ref = bf16[8,64,128]{2,1,0:T(8,128)(2,1)S(1)} collective-permute-done((bf16[8,64,128]{2,1,0:T(8,128)(2,1)S(1)}, bf16[8,64,128]{2,1,0:T(8,128)(2,1)S(1)}, u32[]{:S(2)}, u32[]{:S(2)}) %collective-permute-start.2) | collective-permute-done | bytes 131104 | tf_op jit(solution)/shard_map/ppermute | solution.py:360
  31.4 1.0 %collective-permute-done.kv1_ref = bf16[8,64,128]{2,1,0:T(8,128)(2,1)S(1)} collective-permute-done((bf16[8,64,128]{2,1,0:T(8,128)(2,1)S(1)}, bf16[8,64,128]{2,1,0:T(8,128)(2,1)S(1)}, u32[]{:S(2)}, u32[]{:S(2)}) %collective-permute-start) | collective-permute-done | bytes 131104 | tf_op jit(solution)/shard_map/ppermute | solution.py:360
  32.4 0.6 shard_map.125
  33.0 1.4 %collective-permute-start.6 = (bf16[80,128]{1,0:T(8,128)(2,1)S(1)}, bf16[80,128]{1,0:T(8,128)(2,1)S(1)}, u32[]{:S(2)}, u32[]{:S(2)}) collective-permute-start(bf16[80,128]{1,0:T(8,128)(2,1)S(1)} %get-tuple-element.25), channel_id=1, source_target_pairs={{0,2},{2,0},{4,6},{6,4},{1,3},{3,1},{5,7},{7,5},{8,10},{10,8},{12,... | collective-permute-start | bytes 61448 | tf_op jit(solution)/shard_map/ppermute | solution.py:372
  34.4 2.6 %collective-permute-start.7 = (bf16[80,128]{1,0:T(8,128)(2,1)S(1)}, bf16[80,128]{1,0:T(8,128)(2,1)S(1)}, u32[]{:S(2)}, u32[]{:S(2)}) collective-permute-start(bf16[80,128]{1,0:T(8,128)(2,1)S(1)} %get-tuple-element.26), channel_id=1, source_target_pairs={{0,4},{2,6},{4,0},{6,2},{1,5},{3,7},{5,1},{7,3},{8,12},{10,14},{12... | collective-permute-start | bytes 61448 | tf_op jit(solution)/shard_map/ppermute | solution.py:372
  37.0 0.0 collective-permute-done.5.q3_ref
  37.0 0.0 collective-permute-start.8
  37.0 0.0 collective-permute-done.4.q2_ref
  37.0 0.0 collective-permute-done.3.q1_ref
  37.0 3.4 %shard_map.123 = (bf16[32,40,128]{2,1,0:T(8,128)(2,1)S(1)}, bf16[1024,3072]{1,0:T(8,128)(2,1)S(1)}) custom-call(s32[1]{0:T(128)} %bitcast.1.where_ref, s32[1]{0:T(128)S(6)} %copy.13.len_ref, bf16[8,96,128]{2,1,0:T(8,128)(2,1)S(1)} %all_to_all.10.recv_ref, bf16[8,64,128]{2,1,0:T(8,128)(2,1)S(1)} %collective-permute-done.kv1_ref, ...), custom_call_target="tpu_custom_call" | custom-call | tf_op jit(solution)/shard_map/pallas_call | solution.py:61
  40.4 0.0 copy-start.1
  40.4 0.0 copy-start.2
  40.4 0.0 copy-start.3
  40.5 0.0 collective-permute-done.6.p1_ref
  40.5 0.0 collective-permute-done.7.p2_ref
  40.5 0.4 collective-permute-done.8.p3_ref
  40.8 0.2 shard_map.126
  41.0 17.4 %all_to_all.11.recv_ref = bf16[32,104,128]{2,1,0:T(8,128)(2,1)S(1)} all-to-all(bf16[32,104,128]{2,1,0:T(8,128)(2,1)S(1)} %shard_map.126), channel_id=1, replica_groups=mesh['zh'=4,'zl'=2,'x'=4,'y'=4,'tp'=2] {'zl','x','y'}, dimensions={0} | all-to-all | bytes 1703936 | tf_op jit(solution)/shard_map/all_to_all | solution.py:384
  58.4 2.1 %shard_map.127 = (f32[16,3072]{1,0:T(8,128)S(1)}, bf16[16,3072]{1,0:T(8,128)(2,1)S(1)}, bf16[256,1024]{1,0:T(8,128)(2,1)}) custom-call(s32[1]{0:T(128)} %bitcast.2.core_ref, bf16[32,104,128]{2,1,0:T(8,128)(2,1)S(1)} %all_to_all.11.recv_ref, bf16[1024,3072]{1,0:T(8,128)(2,1)S(1)} %get-tuple-element.28.w_ref), custom_call_target="tpu_custom_call" | custom-call | tf_op jit(solution)/shard_map/pallas_call | solution.py:61
  60.6 3.3 %collective-permute-start.9 = (bf16[16,3072]{1,0:T(8,128)(2,1)S(1)}, bf16[16,3072]{1,0:T(8,128)(2,1)S(1)}, u32[]{:S(2)}, u32[]{:S(2)}) collective-permute-start(bf16[16,3072]{1,0:T(8,128)(2,1)S(1)} %get-tuple-element.30), channel_id=1, source_target_pairs={{0,1},{1,0},{2,3},{3,2},{4,5},{5,4},{6,7},{7,6},{8,9},{9,8},{10,11... | collective-permute-start | bytes 294920 | tf_op jit(solution)/shard_map/ppermute | solution.py:396
  63.8 0.9 %collective-permute-done.9 = bf16[16,3072]{1,0:T(8,128)(2,1)S(1)} collective-permute-done((bf16[16,3072]{1,0:T(8,128)(2,1)S(1)}, bf16[16,3072]{1,0:T(8,128)(2,1)S(1)}, u32[]{:S(2)}, u32[]{:S(2)}) %collective-permute-start.9) | collective-permute-done | bytes 98336 | tf_op jit(solution)/shard_map/ppermute | solution.py:396
  64.8 0.0 copy-done.1
  64.8 0.0 copy-done.2
  64.8 0.0 copy-done.3
  64.8 0.7 %fusion.1 = bf16[1,16,3072]{2,1,0:T(8,128)(2,1)} fusion(f32[16,3072]{1,0:T(8,128)S(1)} %get-tuple-element.29, bf16[16,3072]{1,0:T(8,128)(2,1)S(1)} %collective-permute-done.9, bf16[1,16,3072]{2,1,0:T(8,128)(2,1)S(1)} %copy-done.1, f32[3072]{0:T(1024)S(1)} %copy-done.2, f32[3072]{0:T(1024)S(1)} %copy-done.3), kind=kLoop, calls=%fused_computation.3 | loop fusion | flops 344064 | bytes 516096 | tf_op jit(solution)/shard_map/broadcast_in_dim | solution.py:399
  (2 shorter events, 0.0 us)
Async XLA Ops:
  0.6 24.0 %copy-start = (bf16[1,256,3,1024]{3,1,2,0:T(8,128)(2,1)S(1)}, bf16[1,256,3,1024]{3,1,2,0:T(8,128)(2,1)}, u32[]{:S(2)}) copy-start(bf16[1,256,3,1024]{3,1,2,0:T(8,128)(2,1)} %param.12) | copy-start | bytes 4718596
  13.9 10.4 %collective-permute-start.1 = (bf16[8,64,128]{2,1,0:T(8,128)(2,1)S(1)}, bf16[8,64,128]{2,1,0:T(8,128)(2,1)S(1)}, u32[]{:S(2)}, u32[]{:S(2)}) collective-permute-start(bf16[8,64,128]{2,1,0:T(8,128)(2,1)S(1)} %slice.8), channel_id=1, source_target_pairs={{0,128},{64,192},{128,0},{192,64},{1,129},{65,193},{129,1},{193,65... | collective-permute-start | bytes 393224 | tf_op jit(solution)/shard_map/ppermute | solution.py:360
  20.0 11.4 %collective-permute-start.2 = (bf16[8,64,128]{2,1,0:T(8,128)(2,1)S(1)}, bf16[8,64,128]{2,1,0:T(8,128)(2,1)S(1)}, u32[]{:S(2)}, u32[]{:S(2)}) collective-permute-start(bf16[8,64,128]{2,1,0:T(8,128)(2,1)S(1)} %slice.8), channel_id=1, source_target_pairs={{0,192},{64,128},{128,64},{192,0},{1,193},{65,129},{129,65},{193,1... | collective-permute-start | bytes 393224 | tf_op jit(solution)/shard_map/ppermute | solution.py:360
  20.3 12.1 %collective-permute-start = (bf16[8,64,128]{2,1,0:T(8,128)(2,1)S(1)}, bf16[8,64,128]{2,1,0:T(8,128)(2,1)S(1)}, u32[]{:S(2)}, u32[]{:S(2)}) collective-permute-start(bf16[8,64,128]{2,1,0:T(8,128)(2,1)S(1)} %slice.8), channel_id=1, source_target_pairs={{0,64},{64,0},{128,192},{192,128},{1,65},{65,1},{129,193},{193,129... | collective-permute-start | bytes 393224 | tf_op jit(solution)/shard_map/ppermute | solution.py:360
  21.2 15.8 %collective-permute-start.5 = (bf16[8,32,128]{2,1,0:T(8,128)(2,1)S(1)}, bf16[8,32,128]{2,1,0:T(8,128)(2,1)S(1)}, u32[]{:S(2)}, u32[]{:S(2)}) collective-permute-start(bf16[8,32,128]{2,1,0:T(8,128)(2,1)S(1)} %slice.9), channel_id=1, source_target_pairs={{0,6},{2,4},{4,2},{6,0},{1,7},{3,5},{5,3},{7,1},{8,14},{10,12},{12... | collective-permute-start | bytes 196616 | tf_op jit(solution)/shard_map/ppermute | solution.py:361
  23.9 13.1 %collective-permute-start.4 = (bf16[8,32,128]{2,1,0:T(8,128)(2,1)S(1)}, bf16[8,32,128]{2,1,0:T(8,128)(2,1)S(1)}, u32[]{:S(2)}, u32[]{:S(2)}) collective-permute-start(bf16[8,32,128]{2,1,0:T(8,128)(2,1)S(1)} %slice.9), channel_id=1, source_target_pairs={{0,4},{2,6},{4,0},{6,2},{1,5},{3,7},{5,1},{7,3},{8,12},{10,14},{12... | collective-permute-start | bytes 196616 | tf_op jit(solution)/shard_map/ppermute | solution.py:361
  24.3 12.7 %collective-permute-start.3 = (bf16[8,32,128]{2,1,0:T(8,128)(2,1)S(1)}, bf16[8,32,128]{2,1,0:T(8,128)(2,1)S(1)}, u32[]{:S(2)}, u32[]{:S(2)}) collective-permute-start(bf16[8,32,128]{2,1,0:T(8,128)(2,1)S(1)} %slice.9), channel_id=1, source_target_pairs={{0,2},{2,0},{4,6},{6,4},{1,3},{3,1},{5,7},{7,5},{8,10},{10,8},{12,... | collective-permute-start | bytes 196616 | tf_op jit(solution)/shard_map/ppermute | solution.py:361
  33.0 7.5 %collective-permute-start.6 = (bf16[80,128]{1,0:T(8,128)(2,1)S(1)}, bf16[80,128]{1,0:T(8,128)(2,1)S(1)}, u32[]{:S(2)}, u32[]{:S(2)}) collective-permute-start(bf16[80,128]{1,0:T(8,128)(2,1)S(1)} %get-tuple-element.25), channel_id=1, source_target_pairs={{0,2},{2,0},{4,6},{6,4},{1,3},{3,1},{5,7},{7,5},{8,10},{10,8},{12,... | collective-permute-start | bytes 61448 | tf_op jit(solution)/shard_map/ppermute | solution.py:372
  34.4 6.1 %collective-permute-start.7 = (bf16[80,128]{1,0:T(8,128)(2,1)S(1)}, bf16[80,128]{1,0:T(8,128)(2,1)S(1)}, u32[]{:S(2)}, u32[]{:S(2)}) collective-permute-start(bf16[80,128]{1,0:T(8,128)(2,1)S(1)} %get-tuple-element.26), channel_id=1, source_target_pairs={{0,4},{2,6},{4,0},{6,2},{1,5},{3,7},{5,1},{7,3},{8,12},{10,14},{12... | collective-permute-start | bytes 61448 | tf_op jit(solution)/shard_map/ppermute | solution.py:372
  37.0 3.8 %collective-permute-start.8 = (bf16[80,128]{1,0:T(8,128)(2,1)S(1)}, bf16[80,128]{1,0:T(8,128)(2,1)S(1)}, u32[]{:S(2)}, u32[]{:S(2)}) collective-permute-start(bf16[80,128]{1,0:T(8,128)(2,1)S(1)} %get-tuple-element.27), channel_id=1, source_target_pairs={{0,6},{2,4},{4,2},{6,0},{1,7},{3,5},{5,3},{7,1},{8,14},{10,12},{12... | collective-permute-start | bytes 61448 | tf_op jit(solution)/shard_map/ppermute | solution.py:372
  40.4 24.3 %copy-start.1 = (bf16[1,16,3072]{2,1,0:T(8,128)(2,1)S(1)}, bf16[1,16,3072]{2,1,0:T(8,128)(2,1)}, u32[]{:S(2)}) copy-start(bf16[1,16,3072]{2,1,0:T(8,128)(2,1)} %param.17) | copy-start | bytes 294916
  40.4 24.3 %copy-start.2 = (f32[3072]{0:T(1024)S(1)}, f32[3072]{0:T(1024)}, u32[]{:S(2)}) copy-start(f32[3072]{0:T(1024)} %param.19) | copy-start | bytes 36868
  40.4 24.3 %copy-start.3 = (f32[3072]{0:T(1024)S(1)}, f32[3072]{0:T(1024)}, u32[]{:S(2)}) copy-start(f32[3072]{0:T(1024)} %param.20) | copy-start | bytes 36868
  60.6 4.2 %collective-permute-start.9 = (bf16[16,3072]{1,0:T(8,128)(2,1)S(1)}, bf16[16,3072]{1,0:T(8,128)(2,1)S(1)}, u32[]{:S(2)}, u32[]{:S(2)}) collective-permute-start(bf16[16,3072]{1,0:T(8,128)(2,1)S(1)} %get-tuple-element.30), channel_id=1, source_target_pairs={{0,1},{1,0},{2,3},{3,2},{4,5},{5,4},{6,7},{7,6},{8,9},{9,8},{10,11... | collective-permute-start | bytes 294920 | tf_op jit(solution)/shard_map/ppermute | solution.py:396

commit v12 on v9

v12 whole, which is shorter than its diff:
```python
import math

import jax
import jax.numpy as jnp
import numpy as np
from jax import lax
from jax.experimental import pallas as pl
from jax.experimental.pallas import tpu as pltpu
from jax.sharding import Mesh
from jax.sharding import PartitionSpec as P


HD = 128
SEQ = ("zh", "zl", "x", "y")
HEAD = ("zl", "x")
rope_base = 256.0
neg_large = -1e30
LOG2E = 1.4426950408889634
bf16 = jnp.bfloat16
f32 = jnp.float32


def vmem_spec():
    return pl.BlockSpec(memory_space=pltpu.VMEM)


def smem_spec():
    return pl.BlockSpec(memory_space=pltpu.SMEM)


def any_spec():
    return pl.BlockSpec(memory_space=pltpu.HBM)


def call(
    body, out_shape, n_in, smem=(), hbm=(), near=(), far_outs=(), limit=40 * 1024 * 1024, scratch=(), alias=None
):
    single = not isinstance(out_shape, (tuple, list))
    outs = out_shape if not single else [out_shape]
    specs = [any_spec() if i in far_outs else vmem_spec() for i in range(len(outs))]
    kernel = pl.pallas_call(
        body,
        out_shape=out_shape,
        in_specs=[
            smem_spec() if i in smem else any_spec() if i in hbm else vmem_spec() for i in range(n_in)
        ],
        out_specs=specs[0] if single else specs,
        scratch_shapes=list(scratch),
        input_output_aliases=alias or {},
        compiler_params=pltpu.CompilerParams(vmem_limit_bytes=limit),
    )

    def run(*operands):
        held = [
            pltpu.with_memory_space_constraint(v, pltpu.HBM if i in hbm else pltpu.VMEM)
            if i in hbm or i in near
            else v
            for i, v in enumerate(operands)
        ]
        return kernel(*held)

    return run


def rate_table():
    table = np.zeros((8, HD), np.float32)
    frame_part = HD // 8
    second = (HD - frame_part) // 2
    at = 0
    for p, width in enumerate((frame_part, second, second)):
        ids = np.arange(width // 2, dtype=np.float32)
        rates = np.float32(rope_base) ** (np.float32(-2.0) * ids / np.float32(width))
        table[p, at : at + width] = np.repeat(rates.astype(np.float32), 2)
        at += width
    return table


def prep_body(
    qkv_hbm, frame_hbm, row_hbm, col_hbm, rate_hbm, out_ref,
    qkv_ref, frame_ref, row_ref, col_ref, rate_ref, sems,
):
    copies = [
        pltpu.make_async_copy(src, dst, sems.at[i])
        for i, (src, dst) in enumerate(
            (
                (frame_hbm, frame_ref), (row_hbm, row_ref), (col_hbm, col_ref),
                (rate_hbm, rate_ref), (qkv_hbm, qkv_ref),
            )
        )
    ]
    for c in copies:
        c.start()
    for c in copies[:4]:
        c.wait()
    tokens = qkv_ref.shape[1]
    sub = lax.broadcasted_iota(jnp.int32, (8, tokens), 0)
    pos = jnp.where(
        sub == 0, frame_ref[...], jnp.where(sub == 1, row_ref[...], jnp.where(sub == 2, col_ref[...], 0))
    ).astype(f32)
    angles = lax.dot_general(
        pos, rate_ref[...], (((0,), (0,)), ((), ())), precision=lax.Precision.HIGHEST,
        preferred_element_type=f32,
    )
    lane = lax.broadcasted_iota(jnp.int32, (tokens, HD), 1)
    even = (lane % 2) == 0
    cosine = jnp.cos(angles)
    sine = jnp.sin(angles)
    sine = jnp.where(even, -sine, sine)
    copies[4].wait()

    def rotate(v):
        v = v.astype(f32)
        partner = jnp.where(even, pltpu.roll(v, HD - 1, 1), pltpu.roll(v, 1, 1))
        return (v * cosine + partner * sine).astype(bf16)

    for head in range(8):
        cols = slice(head * HD, (head + 1) * HD)
        out_ref[head, 0:32, :] = rotate(qkv_ref[0, :, cols])
        out_ref[head, 32:64, :] = rotate(qkv_ref[1, :, cols])
        out_ref[head, 64:96, :] = qkv_ref[2, :, cols]


def three_parts(v):
    high = v.astype(bf16).astype(f32)
    rest = v - high
    mid = rest.astype(bf16).astype(f32)
    return high, mid, rest - mid


def live_mask(j, length):
    lane = lax.broadcasted_iota(jnp.int32, (1, 128), 1)
    index = lane + (j // 2) * 128
    return jnp.logical_and(index // 64 == j, index < length)


SCALE = LOG2E / math.sqrt(HD)


def stat_rows(lse):
    row = lax.broadcasted_iota(jnp.int32, (128, 128), 0)
    lane = lax.broadcasted_iota(jnp.int32, (128, 128), 1)
    sub = lax.broadcasted_iota(jnp.int32, (8, 128), 0)
    packed = jnp.zeros((8, 128), f32)
    for half in range(2):
        column = jnp.broadcast_to(lse[128 * half : 128 * half + 128], (128, 128))
        for p, part in enumerate(three_parts(column)):
            line = jnp.sum(jnp.where(row == lane, part, 0.0), axis=0, keepdims=True)
            packed = jnp.where(sub == 2 * p + half, line, packed)
    return packed.astype(bf16)


def stat_column(packed):
    packed = packed.astype(f32)
    row = lax.broadcasted_iota(jnp.int32, (128, 128), 0)
    lane = lax.broadcasted_iota(jnp.int32, (128, 128), 1)
    halves = []
    for half in range(2):
        line = packed[half : half + 1] + packed[2 + half : 3 + half] + packed[4 + half : 5 + half]
        halves.append(jnp.sum(jnp.where(row == lane, line, 0.0), axis=1, keepdims=True))
    return jnp.concatenate(halves, axis=0)


def query_block(b, recv_ref, q_refs, txt_ref):
    if b == 4:
        return txt_ref[0]
    q = recv_ref[:, 0:32, :] if b == 0 else q_refs[b - 1][...]
    return q.reshape(256, HD)


def early_body(
    where_ref, len_ref, recv_ref, kv_ref, q1_ref, q2_ref, q3_ref, txt_ref, acc_ref, stat_ref
):
    j = where_ref[0]
    start = pl.multiple_of((j // 2) * 128, 128)
    keys = jnp.concatenate(
        [
            recv_ref[:, 32:64, :].reshape(256, HD), kv_ref[:, 0:32, :].reshape(256, HD),
            txt_ref[1, pl.ds(start, 128), :],
        ],
        axis=0,
    )
    values = jnp.concatenate(
        [
            recv_ref[:, 64:96, :].reshape(256, HD), kv_ref[:, 32:64, :].reshape(256, HD),
            txt_ref[2, pl.ds(start, 128), :],
        ],
        axis=0,
    )
    live = live_mask(j, len_ref[0])
    for b in range(5):
        q = query_block(b, recv_ref, (q1_ref, q2_ref, q3_ref), txt_ref)
        scores = lax.dot_general(q, keys, (((1,), (1,)), ((), ())), preferred_element_type=f32)
        s_txt = jnp.where(live, scores[:, 512:], neg_large)
        peak = jnp.maximum(
            jnp.max(scores[:, :512], axis=1, keepdims=True), jnp.max(s_txt, axis=1, keepdims=True)
        )
        w_img = jnp.exp2((scores[:, :512] - peak) * SCALE)
        w_txt = jnp.exp2((s_txt - peak) * SCALE)
        total = jnp.sum(w_img, axis=1, keepdims=True) + jnp.sum(w_txt, axis=1, keepdims=True)
        weights = jnp.concatenate([w_img.astype(bf16), w_txt.astype(bf16)], axis=1)
        at = slice(256 * b, 256 * b + 256)
        acc_ref[at, :] = jnp.dot(weights, values, preferred_element_type=f32)
        stat_ref[0, at, :] = jnp.broadcast_to(peak, (256, 128))
        stat_ref[1, at, :] = jnp.broadcast_to(total, (256, 128))


def late_body(
    recv_ref, kv0_ref, kv1_ref, q1_ref, q2_ref, q3_ref, txt_ref, acc_ref, stat_ref,
    m1_ref, m2_ref, m3_ref, keep_ref,
):
    keys = jnp.concatenate([r[:, 0:32, :].reshape(256, HD) for r in (kv0_ref, kv1_ref)], axis=0)
    values = jnp.concatenate([r[:, 32:64, :].reshape(256, HD) for r in (kv0_ref, kv1_ref)], axis=0)
    messages = (m1_ref, m2_ref, m3_ref)
    for b in range(5):
        q = query_block(b, recv_ref, (q1_ref, q2_ref, q3_ref), txt_ref)
        at = slice(256 * b, 256 * b + 256)
        scores = lax.dot_general(q, keys, (((1,), (1,)), ((), ())), preferred_element_type=f32)
        before = stat_ref[0, at, 0:1]
        peak = jnp.maximum(before, jnp.max(scores, axis=1, keepdims=True))
        shrink = jnp.exp2((before - peak) * SCALE)
        weights = jnp.exp2((scores - peak) * SCALE)
        total = stat_ref[1, at, 0:1] * shrink + jnp.sum(weights, axis=1, keepdims=True)
        out = acc_ref[at, :] * shrink + jnp.dot(
            weights.astype(bf16), values, preferred_element_type=f32
        )
        out = out / total
        lse = peak * SCALE + jnp.log2(total)
        if b in (0, 4):
            rows = slice(0, 256) if b == 0 else slice(256, 512)
            keep_ref[0, rows, :] = out
            keep_ref[1, rows, :] = jnp.broadcast_to(lse, (256, 128))
        if b in (1, 2, 3):
            messages[b - 1][0:256, :] = out.astype(bf16)
            messages[b - 1][512:520, :] = stat_rows(lse)
        if b == 4:
            stats = stat_rows(lse)
            for m in messages:
                m[256:512, :] = out.astype(bf16)
                m[520:528, :] = stats


def weights_body(w_hbm, w_out, sems):
    share = w_hbm.shape[0] // 8
    copies = [
        pltpu.make_async_copy(
            w_hbm.at[pl.ds(share * i, share)], w_out.at[pl.ds(share * i, share)], sems.at[i]
        )
        for i in range(8)
    ]
    for c in copies:
        c.start()
    for c in copies:
        c.wait()


def blend(outs, lses):
    peak = lses[0]
    for v in lses[1:]:
        peak = jnp.maximum(peak, v)
    weights = [jnp.exp2(v - peak) for v in lses]
    total = weights[0]
    for w in weights[1:]:
        total = total + w
    mixed = outs[0] * weights[0]
    for o, w in zip(outs[1:], weights[1:]):
        mixed = mixed + o * w
    return mixed / total


def mix_body(len_ref, keep_ref, g1_ref, g2_ref, g3_ref, out_ref):
    got = (g1_ref, g2_ref, g3_ref)
    for part in range(2):
        rows = slice(256 * part, 256 * part + 256)
        outs = [keep_ref[0, rows, :]] + [g[rows, :].astype(f32) for g in got]
        lses = [keep_ref[1, rows, 0:1]]
        lses += [stat_column(g[512 + 8 * part : 520 + 8 * part, :]) for g in got]
        mixed = blend(outs, lses)
        if part == 0:
            out_ref[:, 0:32, :] = mixed.astype(bf16).reshape(8, 32, HD)
        else:
            row = lax.broadcasted_iota(jnp.int32, (256, 128), 0)
            text = jnp.where(row < len_ref[0], mixed, 0.0).astype(bf16)
            for d in range(8):
                out_ref[d, 32:288, :] = text


def tail_body(core_ref, recv_ref, w_ref, mine_ref, other_ref, txt_out, sems):
    leave = [
        pltpu.make_async_copy(
            recv_ref.at[h, pl.ds(32, 256)], txt_out.at[:, pl.ds(h * HD, HD)], sems.at[h]
        )
        for h in range(8)
    ]
    for c in leave:
        c.start()
    rows = jnp.concatenate([recv_ref[h, 0:32, :] for h in range(8)], axis=1).astype(f32)
    flipped = jnp.concatenate([rows[16:32], rows[0:16]], axis=0)
    rows = jnp.where(core_ref[0] == 0, rows, flipped).astype(bf16)
    projected = jnp.dot(rows, w_ref[...], preferred_element_type=f32)
    mine_ref[...] = projected[0:16]
    other_ref[...] = projected[16:32].astype(bf16)
    for c in leave:
        c.wait()


def shards(
    img_qkv, txt_qkv, frame_index, row_index, column_index, txt_len, residual, w_proj, proj_bias, gate
):
    tokens = img_qkv.shape[1]
    width = img_qkv.shape[3]
    d_model = w_proj.shape[1]
    j = lax.axis_index("y").astype(jnp.int32).reshape(1)
    head = lax.axis_index("zl") * 4 + lax.axis_index("x")
    core = lax.axis_index("tp").astype(jnp.int32).reshape(1)
    j, core, head, frame_index = lax.optimization_barrier((j, core, head, frame_index))
    qkv = img_qkv.reshape(tokens, 3, width).transpose(1, 0, 2)
    txt = lax.dynamic_slice_in_dim(txt_qkv[0], head * HD, HD, 2).transpose(1, 0, 2)

    send = call(
        prep_body,
        jax.ShapeDtypeStruct((8, 96, HD), bf16),
        5, hbm=(0, 1, 2, 3, 4),
        scratch=(
            pltpu.VMEM((3, tokens, width), bf16),
            pltpu.VMEM((1, tokens), jnp.int32),
            pltpu.VMEM((1, tokens), jnp.int32),
            pltpu.VMEM((1, tokens), jnp.int32),
            pltpu.VMEM((8, HD), f32),
            pltpu.SemaphoreType.DMA((5,)),
        ),
    )(qkv, frame_index, row_index, column_index, jnp.asarray(rate_table()))
    recv = lax.all_to_all(send, HEAD, 0, 0, tiled=True)
    kv = recv[:, 32:96]
    q = recv[:, 0:32]
    others = {}
    for s in (2, 3, 1):
        others[s] = lax.ppermute(kv, "zh", [(i, i ^ s) for i in range(4)])
    queries = [lax.ppermute(q, "y", [(i, i ^ s) for i in range(4)]) for s in (1, 2, 3)]
    w_near = call(
        weights_body, pltpu.VMEM(w_proj.shape, bf16), 1, hbm=(0,),
        scratch=(pltpu.SemaphoreType.DMA((8,)),),
    )(w_proj)
    acc, stat = call(
        early_body,
        [jax.ShapeDtypeStruct((1280, HD), f32), jax.ShapeDtypeStruct((2, 1280, 128), f32)],
        8, smem=(0, 1),
    )(j, txt_len, recv, others[2], *queries, txt)
    *messages, keep = call(
        late_body,
        [jax.ShapeDtypeStruct((528, HD), bf16)] * 3 + [jax.ShapeDtypeStruct((2, 512, 128), f32)],
        9,
    )(recv, others[3], others[1], *queries, txt, acc, stat)
    got = {}
    for s in (2, 3, 1):
        got[s] = lax.ppermute(messages[s - 1], "y", [(i, i ^ s) for i in range(4)])
    back = call(mix_body, jax.ShapeDtypeStruct((8, 288, HD), bf16), 5, smem=(0,))(
        txt_len, keep, got[1], got[2], got[3]
    )
    home = lax.all_to_all(back, HEAD, 0, 0, tiled=True)
    half = tokens // 2
    mine, other, txt_out = call(
        tail_body,
        [
            jax.ShapeDtypeStruct((half, d_model), f32),
            jax.ShapeDtypeStruct((half, d_model), bf16),
            pltpu.HBM((256, width), bf16),
        ],
        3, smem=(0,), near=(2,), far_outs=(2,),
        scratch=(pltpu.SemaphoreType.DMA((8,)),),
    )(core, home, w_near)
    theirs = lax.ppermute(other, "tp", [(0, 1), (1, 0)])
    projected = mine + theirs.astype(f32)
    img_out = residual[0].astype(f32) + gate[None, :] * (projected + proj_bias[None, :])
    return img_out.astype(bf16)[None], txt_out[None]


def solution(mesh):
    split = Mesh(
        mesh.devices.reshape(4, 2, 4, 4, mesh.shape["tp"]), ("zh", "zl", "x", "y", "tp")
    )
    placed = (
        P(None, SEQ, None, "tp"),
        P(None, None, None, "tp"),
        P(None, SEQ),
        P(None, SEQ),
        P(None, SEQ),
        P(),
        P(None, SEQ + ("tp",), None),
        P("tp", None),
        P(),
        P(),
    )
    return jax.shard_map(
        shards,
        mesh=split,
        in_specs=placed,
        out_specs=(P(None, SEQ + ("tp",), None), P(None, None, "tp")),
        check_vma=False,
    )
```

time: 68.8 us -> 69.5 us (1.010)
  waiting for transfers between devices: 15.5 us -> 17.3 us
  starting transfers between devices: 22.4 us -> 21.3 us
    ppermute x3, waiting for transfers between devices: 1.3 us -> 5.6 us  [shards(): got[s] = lax.ppermute(messages[s - 1], 'y', [(i, i ^ s) for i in range(4)])]
    ppermute x3, waiting for transfers between devices: 0.01 us -> 4.27 us  [shards(): lax.ppermute(q, 'y', [(i, i ^ s) for i in range(4)])]
    all_to_all x1, waiting for transfers between devices: 6.73 us -> 3.04 us  [shards(): home = lax.all_to_all(back, HEAD, 0, 0, tiled=True)]
    ppermute x3, waiting for transfers between devices: 6.49 us -> 3.4 us  [shards(): others[s] = lax.ppermute(kv, 'zh', [(i, i ^ s) for i in range(4)])]
    pallas_call x7 -> x6, Pallas kernels: 11.2 us -> 11.2 us  [run(): return kernel(*held)]
  transfers between devices with their start and end apart: 11 -> 11, of which waited for: 5 -> 7; matrix products, arithmetic and copies ran while one was open for 0% -> 0% of each run, Pallas kernels for 10% -> 7%
where the time goes in v12:
time: 69.5 us; the launch traced here: 69.3 us
  starting transfers between devices  21.3 us (31%)
  waiting for transfers between devices  17.3 us (25%)
  blocking collectives  11.9 us (17%)
  Pallas kernels  11.2 us (16%)
  local copies, waits for them, and re-layouts  5.53 us (8%)
  between operations  1.38 us (2%)
    all_to_all x1, blocking collectives, shards(): recv = lax.all_to_all(send, HEAD, 0, 0, tiled=True)  11.9 us
    pallas_call x6, Pallas kernels, run(): return kernel(*held)  11.2 us
    ppermute x3, starting transfers between devices, shards(): others[s] = lax.ppermute(kv, 'zh', [(i, i ^ s) for i in range(4)])  7.29 us
    ppermute x3, waiting for transfers between devices, shards(): got[s] = lax.ppermute(messages[s - 1], 'y', [(i, i ^ s) for i in range(4)])  5.6 us
    unnamed x12, local copies, waits for them, and re-layouts  5.46 us
    ppermute x3, waiting for transfers between devices, shards(): lax.ppermute(q, 'y', [(i, i ^ s) for i in range(4)])  4.27 us
    all_to_all x1, starting transfers between devices, shards(): home = lax.all_to_all(back, HEAD, 0, 0, tiled=True)  3.96 us
    ppermute x3, starting transfers between devices, shards(): got[s] = lax.ppermute(messages[s - 1], 'y', [(i, i ^ s) for i in range(4)])  3.94 us
  transfers between devices with their start and end apart: 11, of which 7 were waited for; matrix products, arithmetic and copies ran while one was open for 0% of the time, Pallas kernels for 7%

profile of v12, /device:TPU:1, one launch (start us, length us, event | category | flops | bytes accessed | tf_op | source)
XLA Modules:
  0.0 69.3 jit_solution(2386491608850007584)
XLA Ops:
  0.6 0.0 copy-start
  0.7 1.3 %shard_map.122 = bf16[8,96,128]{2,1,0:T(8,128)(2,1)S(1)} custom-call(bf16[3,32,1024]{2,1,0:T(8,128)(2,1)} %bitcast.15, s32[1,32]{1,0:T(1,128)} %frame_hbm, s32[1,32]{1,0:T(1,128)} %row_hbm.1, s32[1,32]{1,0:T(1,128)} %col_hbm.1, f32[8,128]{1,0:T(8,128)} %constant.26.clone.rate_hbm), custom_call_target="tpu_custom_call" | custom-call | tf_op jit(solution)/shard_map/pallas_call | solution.py:60
  2.0 11.9 %all_to_all.10.recv_ref = bf16[8,96,128]{2,1,0:T(8,128)(2,1)S(1)} all-to-all(bf16[8,96,128]{2,1,0:T(8,128)(2,1)S(1)} %shard_map.122), channel_id=1, replica_groups=mesh['zh'=4,'zl'=2,'x'=4,'y'=4,'tp'=2] {'zl','x'}, dimensions={0} | all-to-all | bytes 393216 | tf_op jit(solution)/shard_map/all_to_all | solution.py:332
  13.9 2.7 %collective-permute-start.4 = (bf16[8,32,128]{2,1,0:T(8,128)(2,1)S(1)}, bf16[8,32,128]{2,1,0:T(8,128)(2,1)S(1)}, u32[]{:S(2)}, u32[]{:S(2)}) collective-permute-start(bf16[8,32,128]{2,1,0:T(8,128)(2,1)S(1)} %slice.9), channel_id=1, source_target_pairs={{0,6},{2,4},{4,2},{6,0},{1,7},{3,5},{5,3},{7,1},{8,14},{10,12},{12... | collective-permute-start | bytes 196616 | tf_op jit(solution)/shard_map/ppermute | solution.py:338
  16.6 6.1 %collective-permute-start.5 = (bf16[8,64,128]{2,1,0:T(8,128)(2,1)S(1)}, bf16[8,64,128]{2,1,0:T(8,128)(2,1)S(1)}, u32[]{:S(2)}, u32[]{:S(2)}) collective-permute-start(bf16[8,64,128]{2,1,0:T(8,128)(2,1)S(1)} %slice.8), channel_id=1, source_target_pairs={{0,128},{64,192},{128,0},{192,64},{1,129},{65,193},{129,1},{193,65... | collective-permute-start | bytes 393224 | tf_op jit(solution)/shard_map/ppermute | solution.py:337
  22.7 1.2 %collective-permute-start.1 = (bf16[8,64,128]{2,1,0:T(8,128)(2,1)S(1)}, bf16[8,64,128]{2,1,0:T(8,128)(2,1)S(1)}, u32[]{:S(2)}, u32[]{:S(2)}) collective-permute-start(bf16[8,64,128]{2,1,0:T(8,128)(2,1)S(1)} %slice.8), channel_id=1, source_target_pairs={{0,64},{64,0},{128,192},{192,128},{1,65},{65,1},{129,193},{193,129... | collective-permute-start | bytes 393224 | tf_op jit(solution)/shard_map/ppermute | solution.py:337
  23.9 0.0 collective-permute-start
  24.6 0.4 collective-permute-start.3
  25.0 0.0 collective-permute-done.4.q3_ref
  25.0 0.2 collective-permute-start.2
  25.3 0.0 copy-done
  25.3 0.1 dynamic-slice_bitcast_fusion.txt_ref
  25.3 4.3 %collective-permute-done.3.q2_ref = bf16[8,32,128]{2,1,0:T(8,128)(2,1)S(1)} collective-permute-done((bf16[8,32,128]{2,1,0:T(8,128)(2,1)S(1)}, bf16[8,32,128]{2,1,0:T(8,128)(2,1)S(1)}, u32[]{:S(2)}, u32[]{:S(2)}) %collective-permute-start.3) | collective-permute-done | bytes 65568 | tf_op jit(solution)/shard_map/ppermute | solution.py:338
  29.6 0.0 collective-permute-done.2.q1_ref
  29.6 0.0 collective-permute-done.5.kv_ref
  29.6 2.1 %shard_map.123 = (f32[1280,128]{1,0:T(8,128)S(1)}, f32[2,1280,128]{2,1,0:T(8,128)S(1)}) custom-call(s32[1]{0:T(128)} %bitcast.1.where_ref, s32[1]{0:T(128)S(6)} %copy.13.len_ref, bf16[8,96,128]{2,1,0:T(8,128)(2,1)S(1)} %all_to_all.10.recv_ref, bf16[8,64,128]{2,1,0:T(8,128)(2,1)S(1)} %collective-permute-done.5.kv_ref, ...), custom_call_target="tpu_custom_call" | custom-call | tf_op jit(solution)/shard_map/pallas_call | solution.py:60
  31.7 3.4 %collective-permute-done.1.kv1_ref = bf16[8,64,128]{2,1,0:T(8,128)(2,1)S(1)} collective-permute-done((bf16[8,64,128]{2,1,0:T(8,128)(2,1)S(1)}, bf16[8,64,128]{2,1,0:T(8,128)(2,1)S(1)}, u32[]{:S(2)}, u32[]{:S(2)}) %collective-permute-start.1) | collective-permute-done | bytes 131104 | tf_op jit(solution)/shard_map/ppermute | solution.py:337
  35.1 0.0 collective-permute-done.kv0_ref
  35.1 2.1 %shard_map.124 = (bf16[528,128]{1,0:T(8,128)(2,1)S(1)}, bf16[528,128]{1,0:T(8,128)(2,1)S(1)}, bf16[528,128]{1,0:T(8,128)(2,1)S(1)}, f32[2,512,128]{2,1,0:T(8,128)S(1)}) custom-call(bf16[8,96,128]{2,1,0:T(8,128)(2,1)S(1)} %all_to_all.10.recv_ref, bf16[8,64,128]{2,1,0:T(8,128)(2,1)S(1)} %collective-permute-done.kv0_ref, ...), custom_call_target="tpu_custom_call" | custom-call | tf_op jit(solution)/shard_map/pallas_call | solution.py:60
  37.2 0.1 collective-permute-start.6
  37.3 1.2 %collective-permute-start.7 = (bf16[528,128]{1,0:T(8,128)(2,1)S(1)}, bf16[528,128]{1,0:T(8,128)(2,1)S(1)}, u32[]{:S(2)}, u32[]{:S(2)}) collective-permute-start(bf16[528,128]{1,0:T(8,128)(2,1)S(1)} %get-tuple-element.23), channel_id=1, source_target_pairs={{0,4},{2,6},{4,0},{6,2},{1,5},{3,7},{5,1},{7,3},{8,12},{10,14},{12... | collective-permute-start | bytes 405512 | tf_op jit(solution)/shard_map/ppermute | solution.py:355
  38.5 2.7 %collective-permute-start.8 = (bf16[528,128]{1,0:T(8,128)(2,1)S(1)}, bf16[528,128]{1,0:T(8,128)(2,1)S(1)}, u32[]{:S(2)}, u32[]{:S(2)}) collective-permute-start(bf16[528,128]{1,0:T(8,128)(2,1)S(1)} %get-tuple-element.24), channel_id=1, source_target_pairs={{0,6},{2,4},{4,2},{6,0},{1,7},{3,5},{5,3},{7,1},{8,14},{10,12},{12... | collective-permute-start | bytes 405512 | tf_op jit(solution)/shard_map/ppermute | solution.py:355
  41.2 0.8 %collective-permute-done.6.g1_ref = bf16[528,128]{1,0:T(8,128)(2,1)S(1)} collective-permute-done((bf16[528,128]{1,0:T(8,128)(2,1)S(1)}, bf16[528,128]{1,0:T(8,128)(2,1)S(1)}, u32[]{:S(2)}, u32[]{:S(2)}) %collective-permute-start.6) | collective-permute-done | bytes 135200 | tf_op jit(solution)/shard_map/ppermute | solution.py:355
  41.9 2.6 %collective-permute-done.7.g2_ref = bf16[528,128]{1,0:T(8,128)(2,1)S(1)} collective-permute-done((bf16[528,128]{1,0:T(8,128)(2,1)S(1)}, bf16[528,128]{1,0:T(8,128)(2,1)S(1)}, u32[]{:S(2)}, u32[]{:S(2)}) %collective-permute-start.7) | collective-permute-done | bytes 135200 | tf_op jit(solution)/shard_map/ppermute | solution.py:355
  44.5 2.3 %collective-permute-done.8.g3_ref = bf16[528,128]{1,0:T(8,128)(2,1)S(1)} collective-permute-done((bf16[528,128]{1,0:T(8,128)(2,1)S(1)}, bf16[528,128]{1,0:T(8,128)(2,1)S(1)}, u32[]{:S(2)}, u32[]{:S(2)}) %collective-permute-start.8) | collective-permute-done | bytes 135200 | tf_op jit(solution)/shard_map/ppermute | solution.py:355
  46.8 1.5 %shard_map.125 = bf16[8,288,128]{2,1,0:T(8,128)(2,1)} custom-call(s32[1]{0:T(128)S(6)} %copy.13.len_ref, f32[2,512,128]{2,1,0:T(8,128)S(1)} %get-tuple-element.21.keep_ref, bf16[528,128]{1,0:T(8,128)(2,1)S(1)} %collective-permute-done.6.g1_ref, bf16[528,128]{1,0:T(8,128)(2,1)S(1)} %collective-permute-done.7.g2_ref, ...), custom_call_target="tpu_custom_call" | custom-call | tf_op jit(solution)/shard_map/pallas_call | solution.py:60
  48.3 4.0 %all-to-all-start.1 = ((bf16[8,288,128]{2,1,0:T(8,128)(2,1)}), bf16[8,288,128]{2,1,0:T(8,128)(2,1)S(1)}, u32[]{:S(2)}, u32[]{:S(2)}) async-start(bf16[8,288,128]{2,1,0:T(8,128)(2,1)} %shard_map.125), calls=%async_computation.1 | async-start | bytes 1179648 | tf_op jit(solution)/shard_map/all_to_all | solution.py:359
  52.3 2.9 %shard_map.126.w_ref = bf16[1024,3072]{1,0:T(8,128)(2,1)S(1)} custom-call(bf16[1024,3072]{1,0:T(8,128)(2,1)} %w_hbm.1), custom_call_target="tpu_custom_call" | custom-call | tf_op jit(solution)/shard_map/pallas_call | solution.py:60
  55.1 0.0 copy-start.1
  55.1 2.7 %copy-done.1 = bf16[1024,3072]{1,0:T(8,128)(2,1)} copy-done((bf16[1024,3072]{1,0:T(8,128)(2,1)}, bf16[1024,3072]{1,0:T(8,128)(2,1)S(1)}, u32[]{:S(2)}) %copy-start.1) | copy-done | bytes 6291480
  57.8 3.0 %all-to-all-done.1.recv_ref = bf16[8,288,128]{2,1,0:T(8,128)(2,1)S(1)} async-done(((bf16[8,288,128]{2,1,0:T(8,128)(2,1)}), bf16[8,288,128]{2,1,0:T(8,128)(2,1)S(1)}, u32[]{:S(2)}, u32[]{:S(2)}) %all-to-all-start.1) | async-done | bytes 589856 | tf_op jit(solution)/shard_map/all_to_all | solution.py:359
  60.8 0.0 copy-start.2
  60.8 2.8 %copy-done.2 = bf16[1024,3072]{1,0:T(8,128)(2,1)S(1)} copy-done((bf16[1024,3072]{1,0:T(8,128)(2,1)S(1)}, bf16[1024,3072]{1,0:T(8,128)(2,1)}, u32[]{:S(2)}) %copy-start.2) | copy-done | bytes 6291480
  63.6 0.0 copy-start.3
  63.6 0.0 copy-start.4
  63.6 0.0 copy-start.5
  63.6 1.3 %shard_map.127 = (f32[16,3072]{1,0:T(8,128)S(1)}, bf16[16,3072]{1,0:T(8,128)(2,1)S(1)}, bf16[256,1024]{1,0:T(8,128)(2,1)}) custom-call(s32[1]{0:T(128)} %bitcast.2.core_ref, bf16[8,288,128]{2,1,0:T(8,128)(2,1)S(1)} %all-to-all-done.1.recv_ref, bf16[1024,3072]{1,0:T(8,128)(2,1)S(1)} %copy-done.2), custom_call_target="tpu_custom_call" | custom-call | tf_op jit(solution)/shard_map/pallas_call | solution.py:60
  64.9 2.7 %collective-permute-start.9 = (bf16[16,3072]{1,0:T(8,128)(2,1)S(1)}, bf16[16,3072]{1,0:T(8,128)(2,1)S(1)}, u32[]{:S(2)}, u32[]{:S(2)}) collective-permute-start(bf16[16,3072]{1,0:T(8,128)(2,1)S(1)} %get-tuple-element.26), channel_id=1, source_target_pairs={{0,1},{1,0},{2,3},{3,2},{4,5},{5,4},{6,7},{7,6},{8,9},{9,8},{10,11... | collective-permute-start | bytes 294920 | tf_op jit(solution)/shard_map/ppermute | solution.py:371
  67.6 0.9 %collective-permute-done.9 = bf16[16,3072]{1,0:T(8,128)(2,1)S(1)} collective-permute-done((bf16[16,3072]{1,0:T(8,128)(2,1)S(1)}, bf16[16,3072]{1,0:T(8,128)(2,1)S(1)}, u32[]{:S(2)}, u32[]{:S(2)}) %collective-permute-start.9) | collective-permute-done | bytes 98336 | tf_op jit(solution)/shard_map/ppermute | solution.py:371
  68.6 0.0 copy-done.3
  68.6 0.0 copy-done.4
  68.6 0.0 copy-done.5
  68.6 0.7 fusion.1
  (2 shorter events, 0.0 us)
Async XLA Ops:
  0.6 24.6 %copy-start = (bf16[1,256,3,1024]{3,1,2,0:T(8,128)(2,1)S(1)}, bf16[1,256,3,1024]{3,1,2,0:T(8,128)(2,1)}, u32[]{:S(2)}) copy-start(bf16[1,256,3,1024]{3,1,2,0:T(8,128)(2,1)} %param.12) | copy-start | bytes 4718596
  13.9 11.1 %collective-permute-start.4 = (bf16[8,32,128]{2,1,0:T(8,128)(2,1)S(1)}, bf16[8,32,128]{2,1,0:T(8,128)(2,1)S(1)}, u32[]{:S(2)}, u32[]{:S(2)}) collective-permute-start(bf16[8,32,128]{2,1,0:T(8,128)(2,1)S(1)} %slice.9), channel_id=1, source_target_pairs={{0,6},{2,4},{4,2},{6,0},{1,7},{3,5},{5,3},{7,1},{8,14},{10,12},{12... | collective-permute-start | bytes 196616 | tf_op jit(solution)/shard_map/ppermute | solution.py:338
  16.6 13.0 %collective-permute-start.5 = (bf16[8,64,128]{2,1,0:T(8,128)(2,1)S(1)}, bf16[8,64,128]{2,1,0:T(8,128)(2,1)S(1)}, u32[]{:S(2)}, u32[]{:S(2)}) collective-permute-start(bf16[8,64,128]{2,1,0:T(8,128)(2,1)S(1)} %slice.8), channel_id=1, source_target_pairs={{0,128},{64,192},{128,0},{192,64},{1,129},{65,193},{129,1},{193,65... | collective-permute-start | bytes 393224 | tf_op jit(solution)/shard_map/ppermute | solution.py:337
  22.7 12.4 %collective-permute-start.1 = (bf16[8,64,128]{2,1,0:T(8,128)(2,1)S(1)}, bf16[8,64,128]{2,1,0:T(8,128)(2,1)S(1)}, u32[]{:S(2)}, u32[]{:S(2)}) collective-permute-start(bf16[8,64,128]{2,1,0:T(8,128)(2,1)S(1)} %slice.8), channel_id=1, source_target_pairs={{0,64},{64,0},{128,192},{192,128},{1,65},{65,1},{129,193},{193,129... | collective-permute-start | bytes 393224 | tf_op jit(solution)/shard_map/ppermute | solution.py:337
  23.9 11.2 %collective-permute-start = (bf16[8,64,128]{2,1,0:T(8,128)(2,1)S(1)}, bf16[8,64,128]{2,1,0:T(8,128)(2,1)S(1)}, u32[]{:S(2)}, u32[]{:S(2)}) collective-permute-start(bf16[8,64,128]{2,1,0:T(8,128)(2,1)S(1)} %slice.8), channel_id=1, source_target_pairs={{0,192},{64,128},{128,64},{192,0},{1,193},{65,129},{129,65},{193,1... | collective-permute-start | bytes 393224 | tf_op jit(solution)/shard_map/ppermute | solution.py:337
  24.6 5.0 %collective-permute-start.3 = (bf16[8,32,128]{2,1,0:T(8,128)(2,1)S(1)}, bf16[8,32,128]{2,1,0:T(8,128)(2,1)S(1)}, u32[]{:S(2)}, u32[]{:S(2)}) collective-permute-start(bf16[8,32,128]{2,1,0:T(8,128)(2,1)S(1)} %slice.9), channel_id=1, source_target_pairs={{0,4},{2,6},{4,0},{6,2},{1,5},{3,7},{5,1},{7,3},{8,12},{10,14},{12... | collective-permute-start | bytes 196616 | tf_op jit(solution)/shard_map/ppermute | solution.py:338
  25.0 4.6 %collective-permute-start.2 = (bf16[8,32,128]{2,1,0:T(8,128)(2,1)S(1)}, bf16[8,32,128]{2,1,0:T(8,128)(2,1)S(1)}, u32[]{:S(2)}, u32[]{:S(2)}) collective-permute-start(bf16[8,32,128]{2,1,0:T(8,128)(2,1)S(1)} %slice.9), channel_id=1, source_target_pairs={{0,2},{2,0},{4,6},{6,4},{1,3},{3,1},{5,7},{7,5},{8,10},{10,8},{12,... | collective-permute-start | bytes 196616 | tf_op jit(solution)/shard_map/ppermute | solution.py:338
  37.2 4.7 %collective-permute-start.6 = (bf16[528,128]{1,0:T(8,128)(2,1)S(1)}, bf16[528,128]{1,0:T(8,128)(2,1)S(1)}, u32[]{:S(2)}, u32[]{:S(2)}) collective-permute-start(bf16[528,128]{1,0:T(8,128)(2,1)S(1)} %get-tuple-element.22), channel_id=1, source_target_pairs={{0,2},{2,0},{4,6},{6,4},{1,3},{3,1},{5,7},{7,5},{8,10},{10,8},{12,... | collective-permute-start | bytes 405512 | tf_op jit(solution)/shard_map/ppermute | solution.py:355
  37.3 7.2 %collective-permute-start.7 = (bf16[528,128]{1,0:T(8,128)(2,1)S(1)}, bf16[528,128]{1,0:T(8,128)(2,1)S(1)}, u32[]{:S(2)}, u32[]{:S(2)}) collective-permute-start(bf16[528,128]{1,0:T(8,128)(2,1)S(1)} %get-tuple-element.23), channel_id=1, source_target_pairs={{0,4},{2,6},{4,0},{6,2},{1,5},{3,7},{5,1},{7,3},{8,12},{10,14},{12... | collective-permute-start | bytes 405512 | tf_op jit(solution)/shard_map/ppermute | solution.py:355
  38.5 8.3 %collective-permute-start.8 = (bf16[528,128]{1,0:T(8,128)(2,1)S(1)}, bf16[528,128]{1,0:T(8,128)(2,1)S(1)}, u32[]{:S(2)}, u32[]{:S(2)}) collective-permute-start(bf16[528,128]{1,0:T(8,128)(2,1)S(1)} %get-tuple-element.24), channel_id=1, source_target_pairs={{0,6},{2,4},{4,2},{6,0},{1,7},{3,5},{5,3},{7,1},{8,14},{10,12},{12... | collective-permute-start | bytes 405512 | tf_op jit(solution)/shard_map/ppermute | solution.py:355
  48.3 12.5 %all-to-all-start.1 = ((bf16[8,288,128]{2,1,0:T(8,128)(2,1)}), bf16[8,288,128]{2,1,0:T(8,128)(2,1)S(1)}, u32[]{:S(2)}, u32[]{:S(2)}) async-start(bf16[8,288,128]{2,1,0:T(8,128)(2,1)} %shard_map.125), calls=%async_computation.1 | async-start | bytes 1179648 | tf_op jit(solution)/shard_map/all_to_all | solution.py:359
  55.1 2.7 %copy-start.1 = (bf16[1024,3072]{1,0:T(8,128)(2,1)}, bf16[1024,3072]{1,0:T(8,128)(2,1)S(1)}, u32[]{:S(2)}) copy-start(bf16[1024,3072]{1,0:T(8,128)(2,1)S(1)} %shard_map.126.w_ref) | copy-start | bytes 18874372
  60.8 2.8 %copy-start.2 = (bf16[1024,3072]{1,0:T(8,128)(2,1)S(1)}, bf16[1024,3072]{1,0:T(8,128)(2,1)}, u32[]{:S(2)}) copy-start(bf16[1024,3072]{1,0:T(8,128)(2,1)} %copy-done.1) | copy-start | bytes 18874372
  63.6 5.0 %copy-start.3 = (bf16[1,16,3072]{2,1,0:T(8,128)(2,1)S(1)}, bf16[1,16,3072]{2,1,0:T(8,128)(2,1)}, u32[]{:S(2)}) copy-start(bf16[1,16,3072]{2,1,0:T(8,128)(2,1)} %param.17) | copy-start | bytes 294916
  63.6 5.0 %copy-start.4 = (f32[3072]{0:T(1024)S(1)}, f32[3072]{0:T(1024)}, u32[]{:S(2)}) copy-start(f32[3072]{0:T(1024)} %param.19) | copy-start | bytes 36868
  63.6 5.0 %copy-start.5 = (f32[3072]{0:T(1024)S(1)}, f32[3072]{0:T(1024)}, u32[]{:S(2)}) copy-start(f32[3072]{0:T(1024)} %param.20) | copy-start | bytes 36868
  64.9 3.7 %collective-permute-start.9 = (bf16[16,3072]{1,0:T(8,128)(2,1)S(1)}, bf16[16,3072]{1,0:T(8,128)(2,1)S(1)}, u32[]{:S(2)}, u32[]{:S(2)}) collective-permute-start(bf16[16,3072]{1,0:T(8,128)(2,1)S(1)} %get-tuple-element.26), channel_id=1, source_target_pairs={{0,1},{1,0},{2,3},{3,2},{4,5},{5,4},{6,7},{7,6},{8,9},{9,8},{10,11... | collective-permute-start | bytes 294920 | tf_op jit(solution)/shard_map/ppermute | solution.py:371

commit v13 on v12

--- a/solution.py
+++ b/solution.py
@@ -204,39 +204,59 @@
         stat_ref[1, at, :] = jnp.broadcast_to(total, (256, 128))
 
 
-def late_body(
-    recv_ref, kv0_ref, kv1_ref, q1_ref, q2_ref, q3_ref, txt_ref, acc_ref, stat_ref,
-    m1_ref, m2_ref, m3_ref, keep_ref,
-):
-    keys = jnp.concatenate([r[:, 0:32, :].reshape(256, HD) for r in (kv0_ref, kv1_ref)], axis=0)
-    values = jnp.concatenate([r[:, 32:64, :].reshape(256, HD) for r in (kv0_ref, kv1_ref)], axis=0)
-    messages = (m1_ref, m2_ref, m3_ref)
-    for b in range(5):
-        q = query_block(b, recv_ref, (q1_ref, q2_ref, q3_ref), txt_ref)
-        at = slice(256 * b, 256 * b + 256)
-        scores = lax.dot_general(q, keys, (((1,), (1,)), ((), ())), preferred_element_type=f32)
-        before = stat_ref[0, at, 0:1]
-        peak = jnp.maximum(before, jnp.max(scores, axis=1, keepdims=True))
-        shrink = jnp.exp2((before - peak) * SCALE)
-        weights = jnp.exp2((scores - peak) * SCALE)
-        total = stat_ref[1, at, 0:1] * shrink + jnp.sum(weights, axis=1, keepdims=True)
-        out = acc_ref[at, :] * shrink + jnp.dot(
-            weights.astype(bf16), values, preferred_element_type=f32
-        )
-        out = out / total
-        lse = peak * SCALE + jnp.log2(total)
-        if b in (0, 4):
-            rows = slice(0, 256) if b == 0 else slice(256, 512)
-            keep_ref[0, rows, :] = out
-            keep_ref[1, rows, :] = jnp.broadcast_to(lse, (256, 128))
-        if b in (1, 2, 3):
-            messages[b - 1][0:256, :] = out.astype(bf16)
-            messages[b - 1][512:520, :] = stat_rows(lse)
-        if b == 4:
-            stats = stat_rows(lse)
-            for m in messages:
-                m[256:512, :] = out.astype(bf16)
-                m[520:528, :] = stats
+def late_keys(kv0_ref, kv1_ref):
+    both = (kv0_ref, kv1_ref)
+    keys = jnp.concatenate([r[:, 0:32, :].reshape(256, HD) for r in both], axis=0)
+    values = jnp.concatenate([r[:, 32:64, :].reshape(256, HD) for r in both], axis=0)
+    return keys, values
+
+
+def late_block(b, q, keys, values, acc_ref, stat_ref):
+    at = slice(256 * b, 256 * b + 256)
+    scores = lax.dot_general(q, keys, (((1,), (1,)), ((), ())), preferred_element_type=f32)
+    before = stat_ref[0, at, 0:1]
+    peak = jnp.maximum(before, jnp.max(scores, axis=1, keepdims=True))
+    shrink = jnp.exp2((before - peak) * SCALE)
+    weights = jnp.exp2((scores - peak) * SCALE)
+    total = stat_ref[1, at, 0:1] * shrink + jnp.sum(weights, axis=1, keepdims=True)
+    out = acc_ref[at, :] * shrink + jnp.dot(
+        weights.astype(bf16), values, preferred_element_type=f32
+    )
+    return out / total, peak * SCALE + jnp.log2(total)
+
+
+def late_first_body(
+    kv0_ref, kv1_ref, q2_ref, txt_ref, acc_ref, stat_ref, m2_ref, keep_ref
+):
+    keys, values = late_keys(kv0_ref, kv1_ref)
+    out, lse = late_block(4, txt_ref[0], keys, values, acc_ref, stat_ref)
+    keep_ref[0] = out
+    keep_ref[1] = jnp.broadcast_to(lse, (256, 128))
+    m2_ref[256:512, :] = out.astype(bf16)
+    m2_ref[520:528, :] = stat_rows(lse)
+    out, lse = late_block(2, q2_ref[...].reshape(256, HD), keys, values, acc_ref, stat_ref)
+    m2_ref[0:256, :] = out.astype(bf16)
+    m2_ref[512:520, :] = stat_rows(lse)
+
+
+def late_second_body(
+    kv0_ref, kv1_ref, q3_ref, q1_ref, acc_ref, stat_ref, m2_ref, m3_ref, m1_ref
+):
+    keys, values = late_keys(kv0_ref, kv1_ref)
+    for b, q_ref, m_ref in ((3, q3_ref, m3_ref), (1, q1_ref, m1_ref)):
+        out, lse = late_block(b, q_ref[...].reshape(256, HD), keys, values, acc_ref, stat_ref)
+        m_ref[0:256, :] = out.astype(bf16)
+        m_ref[256:512, :] = m2_ref[256:512, :]
+        m_ref[512:520, :] = stat_rows(lse)
+        m_ref[520:528, :] = m2_ref[520:528, :]
+
+
+def late_own_body(kv0_ref, kv1_ref, recv_ref, acc_ref, stat_ref, keep_ref):
+    keys, values = late_keys(kv0_ref, kv1_ref)
+    q = recv_ref[:, 0:32, :].reshape(256, HD)
+    out, lse = late_block(0, q, keys, values, acc_ref, stat_ref)
+    keep_ref[0] = out
+    keep_ref[1] = jnp.broadcast_to(lse, (256, 128))
 
 
 def weights_body(w_hbm, w_out, sems):
@@ -267,12 +287,13 @@
     return mixed / total
 
 
-def mix_body(len_ref, keep_ref, g1_ref, g2_ref, g3_ref, out_ref):
+def mix_body(len_ref, own_ref, keep_ref, g1_ref, g2_ref, g3_ref, out_ref):
     got = (g1_ref, g2_ref, g3_ref)
     for part in range(2):
         rows = slice(256 * part, 256 * part + 256)
-        outs = [keep_ref[0, rows, :]] + [g[rows, :].astype(f32) for g in got]
-        lses = [keep_ref[1, rows, 0:1]]
+        kept = (own_ref, keep_ref)[part]
+        outs = [kept[0]] + [g[rows, :].astype(f32) for g in got]
+        lses = [kept[1, :, 0:1]]
         lses += [stat_column(g[512 + 8 * part : 520 + 8 * part, :]) for g in got]
         mixed = blend(outs, lses)
         if part == 0:
@@ -336,25 +357,32 @@
     for s in (2, 3, 1):
         others[s] = lax.ppermute(kv, "zh", [(i, i ^ s) for i in range(4)])
     queries = [lax.ppermute(q, "y", [(i, i ^ s) for i in range(4)]) for s in (1, 2, 3)]
-    w_near = call(
-        weights_body, pltpu.VMEM(w_proj.shape, bf16), 1, hbm=(0,),
-        scratch=(pltpu.SemaphoreType.DMA((8,)),),
-    )(w_proj)
+
     acc, stat = call(
         early_body,
         [jax.ShapeDtypeStruct((1280, HD), f32), jax.ShapeDtypeStruct((2, 1280, 128), f32)],
         8, smem=(0, 1),
     )(j, txt_len, recv, others[2], *queries, txt)
-    *messages, keep = call(
-        late_body,
-        [jax.ShapeDtypeStruct((528, HD), bf16)] * 3 + [jax.ShapeDtypeStruct((2, 512, 128), f32)],
-        9,
-    )(recv, others[3], others[1], *queries, txt, acc, stat)
+    late = (others[3], others[1])
+    message = jax.ShapeDtypeStruct((528, HD), bf16)
+    kept = jax.ShapeDtypeStruct((2, 256, 128), f32)
     got = {}
-    for s in (2, 3, 1):
-        got[s] = lax.ppermute(messages[s - 1], "y", [(i, i ^ s) for i in range(4)])
-    back = call(mix_body, jax.ShapeDtypeStruct((8, 288, HD), bf16), 5, smem=(0,))(
-        txt_len, keep, got[1], got[2], got[3]
+
+    def pass_on(m, s):
+        got[s] = lax.ppermute(m, "y", [(i, i ^ s) for i in range(4)])
+
+    m2, keep = call(late_first_body, [message, kept], 6)(*late, queries[1], txt, acc, stat)
+    pass_on(m2, 2)
+    m3, m1 = call(late_second_body, [message] * 2, 7)(*late, queries[2], queries[0], acc, stat, m2)
+    pass_on(m3, 3)
+    pass_on(m1, 1)
+    own = call(late_own_body, kept, 5)(*late, recv, acc, stat)
+    w_near = call(
+        weights_body, pltpu.VMEM(w_proj.shape, bf16), 1, hbm=(0,),
+        scratch=(pltpu.SemaphoreType.DMA((8,)),),
+    )(w_proj)
+    back = call(mix_body, jax.ShapeDtypeStruct((8, 288, HD), bf16), 6, smem=(0,))(
+        txt_len, own, keep, got[1], got[2], got[3]
     )
     home = lax.all_to_all(back, HEAD, 0, 0, tiled=True)
     half = tokens // 2

time: 69.5 us -> 68.5 us (0.986)
  waiting for transfers between devices: 17.3 us -> 15.1 us
  starting transfers between devices: 21.3 us -> 22 us
    ppermute x3, waiting for transfers between devices: 5.6 us -> 3.61 us  [pass_on(): got[s] = lax.ppermute(m, 'y', [(i, i ^ s) for i in range(4)])]
    all_to_all x1, starting transfers between devices: 3.96 us -> 5.01 us  [shards(): home = lax.all_to_all(back, HEAD, 0, 0, tiled=True)]
    pallas_call x6 -> x8, Pallas kernels: 11.2 us -> 11.6 us  [run(): return kernel(*held)]
  transfers between devices with their start and end apart: 11 -> 11, of which waited for: 7 -> 6; matrix products, arithmetic and copies ran while one was open for 0% -> 0% of each run, Pallas kernels for 7% -> 8%
where the time goes in v13:
time: 68.5 us; the launch traced here: 68.2 us
  starting transfers between devices  22 us (32%)
  waiting for transfers between devices  15.1 us (22%)
  blocking collectives  11.9 us (17%)
  Pallas kernels  11.6 us (17%)
  local copies, waits for them, and re-layouts  5.53 us (8%)
  between operations  1.39 us (2%)
  other arithmetic  0.69 us (1%)
    all_to_all x1, blocking collectives, shards(): recv = lax.all_to_all(send, HEAD, 0, 0, tiled=True)  11.9 us
    pallas_call x8, Pallas kernels, run(): return kernel(*held)  11.6 us
    ppermute x3, starting transfers between devices, shards(): others[s] = lax.ppermute(kv, 'zh', [(i, i ^ s) for i in range(4)])  7.29 us
    unnamed x12, local copies, waits for them, and re-layouts  5.46 us
    all_to_all x1, starting transfers between devices, shards(): home = lax.all_to_all(back, HEAD, 0, 0, tiled=True)  5.01 us
    ppermute x3, waiting for transfers between devices, shards(): lax.ppermute(q, 'y', [(i, i ^ s) for i in range(4)])  4.27 us
    ppermute x3, waiting for transfers between devices, pass_on(): got[s] = lax.ppermute(m, 'y', [(i, i ^ s) for i in range(4)])  3.61 us
    ppermute x3, starting transfers between devices, shards(): lax.ppermute(q, 'y', [(i, i ^ s) for i in range(4)])  3.41 us
  transfers between devices with their start and end apart: 11, of which 6 were waited for; matrix products, arithmetic and copies ran while one was open for 0% of the time, Pallas kernels for 8%

profile of v13, /device:TPU:1, one launch (start us, length us, event | category | flops | bytes accessed | tf_op | source)
XLA Modules:
  0.0 68.2 jit_solution(15663494737389789471)
XLA Ops:
  0.6 0.0 copy-start
  0.7 1.3 %shard_map.122 = bf16[8,96,128]{2,1,0:T(8,128)(2,1)S(1)} custom-call(bf16[3,32,1024]{2,1,0:T(8,128)(2,1)} %bitcast.15, s32[1,32]{1,0:T(1,128)} %frame_hbm, s32[1,32]{1,0:T(1,128)} %row_hbm.1, s32[1,32]{1,0:T(1,128)} %col_hbm.1, f32[8,128]{1,0:T(8,128)} %constant.26.clone.rate_hbm), custom_call_target="tpu_custom_call" | custom-call | tf_op jit(solution)/shard_map/pallas_call | solution.py:60
  2.0 11.9 %all_to_all.10.recv_ref = bf16[8,96,128]{2,1,0:T(8,128)(2,1)S(1)} all-to-all(bf16[8,96,128]{2,1,0:T(8,128)(2,1)S(1)} %shard_map.122), channel_id=1, replica_groups=mesh['zh'=4,'zl'=2,'x'=4,'y'=4,'tp'=2] {'zl','x'}, dimensions={0} | all-to-all | bytes 393216 | tf_op jit(solution)/shard_map/all_to_all | solution.py:353
  13.9 2.7 %collective-permute-start.5 = (bf16[8,32,128]{2,1,0:T(8,128)(2,1)S(1)}, bf16[8,32,128]{2,1,0:T(8,128)(2,1)S(1)}, u32[]{:S(2)}, u32[]{:S(2)}) collective-permute-start(bf16[8,32,128]{2,1,0:T(8,128)(2,1)S(1)} %slice.9), channel_id=1, source_target_pairs={{0,6},{2,4},{4,2},{6,0},{1,7},{3,5},{5,3},{7,1},{8,14},{10,12},{12... | collective-permute-start | bytes 196616 | tf_op jit(solution)/shard_map/ppermute | solution.py:359
  16.6 6.1 %collective-permute-start.2 = (bf16[8,64,128]{2,1,0:T(8,128)(2,1)S(1)}, bf16[8,64,128]{2,1,0:T(8,128)(2,1)S(1)}, u32[]{:S(2)}, u32[]{:S(2)}) collective-permute-start(bf16[8,64,128]{2,1,0:T(8,128)(2,1)S(1)} %slice.8), channel_id=1, source_target_pairs={{0,128},{64,192},{128,0},{192,64},{1,129},{65,193},{129,1},{193,65... | collective-permute-start | bytes 393224 | tf_op jit(solution)/shard_map/ppermute | solution.py:358
  22.7 1.2 %collective-permute-start.1 = (bf16[8,64,128]{2,1,0:T(8,128)(2,1)S(1)}, bf16[8,64,128]{2,1,0:T(8,128)(2,1)S(1)}, u32[]{:S(2)}, u32[]{:S(2)}) collective-permute-start(bf16[8,64,128]{2,1,0:T(8,128)(2,1)S(1)} %slice.8), channel_id=1, source_target_pairs={{0,64},{64,0},{128,192},{192,128},{1,65},{65,1},{129,193},{193,129... | collective-permute-start | bytes 393224 | tf_op jit(solution)/shard_map/ppermute | solution.py:358
  23.9 0.0 collective-permute-start
  24.6 0.4 collective-permute-start.4
  25.0 0.0 collective-permute-done.5.q3_ref
  25.0 0.2 collective-permute-start.3
  25.3 0.0 copy-done
  25.3 0.1 dynamic-slice_bitcast_fusion.txt_ref
  25.3 4.3 %collective-permute-done.4.q2_ref = bf16[8,32,128]{2,1,0:T(8,128)(2,1)S(1)} collective-permute-done((bf16[8,32,128]{2,1,0:T(8,128)(2,1)S(1)}, bf16[8,32,128]{2,1,0:T(8,128)(2,1)S(1)}, u32[]{:S(2)}, u32[]{:S(2)}) %collective-permute-start.4) | collective-permute-done | bytes 65568 | tf_op jit(solution)/shard_map/ppermute | solution.py:359
  29.6 0.0 collective-permute-done.3.q1_ref
  29.6 0.0 collective-permute-done.2.kv_ref
  29.6 2.1 %shard_map.123 = (f32[1280,128]{1,0:T(8,128)S(1)}, f32[2,1280,128]{2,1,0:T(8,128)S(1)}) custom-call(s32[1]{0:T(128)} %bitcast.1.where_ref, s32[1]{0:T(128)S(6)} %copy.13.len_ref, bf16[8,96,128]{2,1,0:T(8,128)(2,1)S(1)} %all_to_all.10.recv_ref, bf16[8,64,128]{2,1,0:T(8,128)(2,1)S(1)} %collective-permute-done.2.kv_ref, ...), custom_call_target="tpu_custom_call" | custom-call | tf_op jit(solution)/shard_map/pallas_call | solution.py:60
  31.7 3.4 %collective-permute-done.1.kv1_ref = bf16[8,64,128]{2,1,0:T(8,128)(2,1)S(1)} collective-permute-done((bf16[8,64,128]{2,1,0:T(8,128)(2,1)S(1)}, bf16[8,64,128]{2,1,0:T(8,128)(2,1)S(1)}, u32[]{:S(2)}, u32[]{:S(2)}) %collective-permute-start.1) | collective-permute-done | bytes 131104 | tf_op jit(solution)/shard_map/ppermute | solution.py:358
  35.1 0.0 collective-permute-done.kv0_ref
  35.1 1.0 %shard_map.125 = (bf16[528,128]{1,0:T(8,128)(2,1)S(1)}, f32[2,256,128]{2,1,0:T(8,128)S(1)}) custom-call(bf16[8,64,128]{2,1,0:T(8,128)(2,1)S(1)} %collective-permute-done.kv0_ref, bf16[8,64,128]{2,1,0:T(8,128)(2,1)S(1)} %collective-permute-done.1.kv1_ref, bf16[8,32,128]{2,1,0:T(8,128)(2,1)S(1)} %collective-permute-done.4.q2_ref, ...), custom_call_target="tpu_custom_call" | custom-call | tf_op jit(solution)/shard_map/pallas_call | solution.py:60
  36.1 1.0 %shard_map.126 = (bf16[528,128]{1,0:T(8,128)(2,1)S(1)}, bf16[528,128]{1,0:T(8,128)(2,1)S(1)}) custom-call(bf16[8,64,128]{2,1,0:T(8,128)(2,1)S(1)} %collective-permute-done.kv0_ref, bf16[8,64,128]{2,1,0:T(8,128)(2,1)S(1)} %collective-permute-done.1.kv1_ref, bf16[8,32,128]{2,1,0:T(8,128)(2,1)S(1)} %collective-permute-done.5.q3_ref, ...), custom_call_target="tpu_custom_call" | custom-call | tf_op jit(solution)/shard_map/pallas_call | solution.py:60
  37.1 0.1 collective-permute-start.6
  37.2 0.6 collective-permute-start.8
  37.8 2.6 %collective-permute-start.7 = (bf16[528,128]{1,0:T(8,128)(2,1)S(1)}, bf16[528,128]{1,0:T(8,128)(2,1)S(1)}, u32[]{:S(2)}, u32[]{:S(2)}) collective-permute-start(bf16[528,128]{1,0:T(8,128)(2,1)S(1)} %get-tuple-element.22.m2_ref), channel_id=1, source_target_pairs={{0,4},{2,6},{4,0},{6,2},{1,5},{3,7},{5,1},{7,3},{8,12},{10,14},{12... | collective-permute-start | bytes 405512 | tf_op jit(solution)/shard_map/ppermute | solution.py:372
  40.4 0.6 shard_map.124.own_ref
  41.0 0.8 %collective-permute-done.6.g1_ref = bf16[528,128]{1,0:T(8,128)(2,1)S(1)} collective-permute-done((bf16[528,128]{1,0:T(8,128)(2,1)S(1)}, bf16[528,128]{1,0:T(8,128)(2,1)S(1)}, u32[]{:S(2)}, u32[]{:S(2)}) %collective-permute-start.6) | collective-permute-done | bytes 135200 | tf_op jit(solution)/shard_map/ppermute | solution.py:372
  41.8 2.8 %collective-permute-done.8.g3_ref = bf16[528,128]{1,0:T(8,128)(2,1)S(1)} collective-permute-done((bf16[528,128]{1,0:T(8,128)(2,1)S(1)}, bf16[528,128]{1,0:T(8,128)(2,1)S(1)}, u32[]{:S(2)}, u32[]{:S(2)}) %collective-permute-start.8) | collective-permute-done | bytes 135200 | tf_op jit(solution)/shard_map/ppermute | solution.py:372
  44.6 0.0 collective-permute-done.7.g2_ref
  44.6 1.5 %shard_map.127 = bf16[8,288,128]{2,1,0:T(8,128)(2,1)} custom-call(s32[1]{0:T(128)S(6)} %copy.13.len_ref, f32[2,256,128]{2,1,0:T(8,128)S(1)} %shard_map.124.own_ref, f32[2,256,128]{2,1,0:T(8,128)S(1)} %get-tuple-element.21.keep_ref, bf16[528,128]{1,0:T(8,128)(2,1)S(1)} %collective-permute-done.6.g1_ref, bf16[528,128]{1,0:T(8,128)(2,1)S(1)} %collective-permute-done.7.g2_ref, ...), custom_call_target="tpu_custom_call" | custom-call | tf_op jit(solution)/shard_map/pallas_call | solution.py:60
  46.1 5.0 %all-to-all-start.1 = ((bf16[8,288,128]{2,1,0:T(8,128)(2,1)}), bf16[8,288,128]{2,1,0:T(8,128)(2,1)S(1)}, u32[]{:S(2)}, u32[]{:S(2)}) async-start(bf16[8,288,128]{2,1,0:T(8,128)(2,1)} %shard_map.127), calls=%async_computation.1 | async-start | bytes 1179648 | tf_op jit(solution)/shard_map/all_to_all | solution.py:387
  51.2 2.9 %shard_map.128.w_ref = bf16[1024,3072]{1,0:T(8,128)(2,1)S(1)} custom-call(bf16[1024,3072]{1,0:T(8,128)(2,1)} %w_hbm.1), custom_call_target="tpu_custom_call" | custom-call | tf_op jit(solution)/shard_map/pallas_call | solution.py:60
  54.0 0.0 copy-start.1
  54.0 2.7 %copy-done.1 = bf16[1024,3072]{1,0:T(8,128)(2,1)} copy-done((bf16[1024,3072]{1,0:T(8,128)(2,1)}, bf16[1024,3072]{1,0:T(8,128)(2,1)S(1)}, u32[]{:S(2)}) %copy-start.1) | copy-done | bytes 6291480
  56.7 2.8 %all-to-all-done.1.recv_ref = bf16[8,288,128]{2,1,0:T(8,128)(2,1)S(1)} async-done(((bf16[8,288,128]{2,1,0:T(8,128)(2,1)}), bf16[8,288,128]{2,1,0:T(8,128)(2,1)S(1)}, u32[]{:S(2)}, u32[]{:S(2)}) %all-to-all-start.1) | async-done | bytes 589856 | tf_op jit(solution)/shard_map/all_to_all | solution.py:387
  59.5 0.0 copy-start.2
  59.5 2.8 %copy-done.2 = bf16[1024,3072]{1,0:T(8,128)(2,1)S(1)} copy-done((bf16[1024,3072]{1,0:T(8,128)(2,1)S(1)}, bf16[1024,3072]{1,0:T(8,128)(2,1)}, u32[]{:S(2)}) %copy-start.2) | copy-done | bytes 6291480
  62.3 0.0 copy-start.3
  62.3 0.0 copy-start.4
  62.3 0.0 copy-start.5
  62.3 1.3 %shard_map.129 = (f32[16,3072]{1,0:T(8,128)S(1)}, bf16[16,3072]{1,0:T(8,128)(2,1)S(1)}, bf16[256,1024]{1,0:T(8,128)(2,1)}) custom-call(s32[1]{0:T(128)} %bitcast.2.core_ref, bf16[8,288,128]{2,1,0:T(8,128)(2,1)S(1)} %all-to-all-done.1.recv_ref, bf16[1024,3072]{1,0:T(8,128)(2,1)S(1)} %copy-done.2), custom_call_target="tpu_custom_call" | custom-call | tf_op jit(solution)/shard_map/pallas_call | solution.py:60
  63.6 3.0 %collective-permute-start.9 = (bf16[16,3072]{1,0:T(8,128)(2,1)S(1)}, bf16[16,3072]{1,0:T(8,128)(2,1)S(1)}, u32[]{:S(2)}, u32[]{:S(2)}) collective-permute-start(bf16[16,3072]{1,0:T(8,128)(2,1)S(1)} %get-tuple-element.26), channel_id=1, source_target_pairs={{0,1},{1,0},{2,3},{3,2},{4,5},{5,4},{6,7},{7,6},{8,9},{9,8},{10,11... | collective-permute-start | bytes 294920 | tf_op jit(solution)/shard_map/ppermute | solution.py:399
  66.6 0.9 %collective-permute-done.9 = bf16[16,3072]{1,0:T(8,128)(2,1)S(1)} collective-permute-done((bf16[16,3072]{1,0:T(8,128)(2,1)S(1)}, bf16[16,3072]{1,0:T(8,128)(2,1)S(1)}, u32[]{:S(2)}, u32[]{:S(2)}) %collective-permute-start.9) | collective-permute-done | bytes 98336 | tf_op jit(solution)/shard_map/ppermute | solution.py:399
  67.5 0.0 copy-done.3
  67.5 0.0 copy-done.4
  67.5 0.0 copy-done.5
  67.5 0.7 %fusion.1 = bf16[1,16,3072]{2,1,0:T(8,128)(2,1)} fusion(f32[16,3072]{1,0:T(8,128)S(1)} %get-tuple-element.25, bf16[16,3072]{1,0:T(8,128)(2,1)S(1)} %collective-permute-done.9, bf16[1,16,3072]{2,1,0:T(8,128)(2,1)S(1)} %copy-done.3, f32[3072]{0:T(1024)S(1)} %copy-done.4, f32[3072]{0:T(1024)S(1)} %copy-done.5), kind=kLoop, calls=%fused_computation.3 | loop fusion | flops 344064 | bytes 516096 | tf_op jit(solution)/shard_map/broadcast_in_dim | solution.py:402
  (2 shorter events, 0.0 us)
Async XLA Ops:
  0.6 24.6 %copy-start = (bf16[1,256,3,1024]{3,1,2,0:T(8,128)(2,1)S(1)}, bf16[1,256,3,1024]{3,1,2,0:T(8,128)(2,1)}, u32[]{:S(2)}) copy-start(bf16[1,256,3,1024]{3,1,2,0:T(8,128)(2,1)} %param.12) | copy-start | bytes 4718596
  13.9 11.1 %collective-permute-start.5 = (bf16[8,32,128]{2,1,0:T(8,128)(2,1)S(1)}, bf16[8,32,128]{2,1,0:T(8,128)(2,1)S(1)}, u32[]{:S(2)}, u32[]{:S(2)}) collective-permute-start(bf16[8,32,128]{2,1,0:T(8,128)(2,1)S(1)} %slice.9), channel_id=1, source_target_pairs={{0,6},{2,4},{4,2},{6,0},{1,7},{3,5},{5,3},{7,1},{8,14},{10,12},{12... | collective-permute-start | bytes 196616 | tf_op jit(solution)/shard_map/ppermute | solution.py:359
  16.6 13.0 %collective-permute-start.2 = (bf16[8,64,128]{2,1,0:T(8,128)(2,1)S(1)}, bf16[8,64,128]{2,1,0:T(8,128)(2,1)S(1)}, u32[]{:S(2)}, u32[]{:S(2)}) collective-permute-start(bf16[8,64,128]{2,1,0:T(8,128)(2,1)S(1)} %slice.8), channel_id=1, source_target_pairs={{0,128},{64,192},{128,0},{192,64},{1,129},{65,193},{129,1},{193,65... | collective-permute-start | bytes 393224 | tf_op jit(solution)/shard_map/ppermute | solution.py:358
  22.7 12.4 %collective-permute-start.1 = (bf16[8,64,128]{2,1,0:T(8,128)(2,1)S(1)}, bf16[8,64,128]{2,1,0:T(8,128)(2,1)S(1)}, u32[]{:S(2)}, u32[]{:S(2)}) collective-permute-start(bf16[8,64,128]{2,1,0:T(8,128)(2,1)S(1)} %slice.8), channel_id=1, source_target_pairs={{0,64},{64,0},{128,192},{192,128},{1,65},{65,1},{129,193},{193,129... | collective-permute-start | bytes 393224 | tf_op jit(solution)/shard_map/ppermute | solution.py:358
  23.9 11.2 %collective-permute-start = (bf16[8,64,128]{2,1,0:T(8,128)(2,1)S(1)}, bf16[8,64,128]{2,1,0:T(8,128)(2,1)S(1)}, u32[]{:S(2)}, u32[]{:S(2)}) collective-permute-start(bf16[8,64,128]{2,1,0:T(8,128)(2,1)S(1)} %slice.8), channel_id=1, source_target_pairs={{0,192},{64,128},{128,64},{192,0},{1,193},{65,129},{129,65},{193,1... | collective-permute-start | bytes 393224 | tf_op jit(solution)/shard_map/ppermute | solution.py:358
  24.6 5.0 %collective-permute-start.4 = (bf16[8,32,128]{2,1,0:T(8,128)(2,1)S(1)}, bf16[8,32,128]{2,1,0:T(8,128)(2,1)S(1)}, u32[]{:S(2)}, u32[]{:S(2)}) collective-permute-start(bf16[8,32,128]{2,1,0:T(8,128)(2,1)S(1)} %slice.9), channel_id=1, source_target_pairs={{0,4},{2,6},{4,0},{6,2},{1,5},{3,7},{5,1},{7,3},{8,12},{10,14},{12... | collective-permute-start | bytes 196616 | tf_op jit(solution)/shard_map/ppermute | solution.py:359
  25.0 4.6 %collective-permute-start.3 = (bf16[8,32,128]{2,1,0:T(8,128)(2,1)S(1)}, bf16[8,32,128]{2,1,0:T(8,128)(2,1)S(1)}, u32[]{:S(2)}, u32[]{:S(2)}) collective-permute-start(bf16[8,32,128]{2,1,0:T(8,128)(2,1)S(1)} %slice.9), channel_id=1, source_target_pairs={{0,2},{2,0},{4,6},{6,4},{1,3},{3,1},{5,7},{7,5},{8,10},{10,8},{12,... | collective-permute-start | bytes 196616 | tf_op jit(solution)/shard_map/ppermute | solution.py:359
  37.1 4.7 %collective-permute-start.6 = (bf16[528,128]{1,0:T(8,128)(2,1)S(1)}, bf16[528,128]{1,0:T(8,128)(2,1)S(1)}, u32[]{:S(2)}, u32[]{:S(2)}) collective-permute-start(bf16[528,128]{1,0:T(8,128)(2,1)S(1)} %get-tuple-element.23), channel_id=1, source_target_pairs={{0,2},{2,0},{4,6},{6,4},{1,3},{3,1},{5,7},{7,5},{8,10},{10,8},{12,... | collective-permute-start | bytes 405512 | tf_op jit(solution)/shard_map/ppermute | solution.py:372
  37.2 7.4 %collective-permute-start.8 = (bf16[528,128]{1,0:T(8,128)(2,1)S(1)}, bf16[528,128]{1,0:T(8,128)(2,1)S(1)}, u32[]{:S(2)}, u32[]{:S(2)}) collective-permute-start(bf16[528,128]{1,0:T(8,128)(2,1)S(1)} %get-tuple-element.24), channel_id=1, source_target_pairs={{0,6},{2,4},{4,2},{6,0},{1,7},{3,5},{5,3},{7,1},{8,14},{10,12},{12... | collective-permute-start | bytes 405512 | tf_op jit(solution)/shard_map/ppermute | solution.py:372
  37.8 6.8 %collective-permute-start.7 = (bf16[528,128]{1,0:T(8,128)(2,1)S(1)}, bf16[528,128]{1,0:T(8,128)(2,1)S(1)}, u32[]{:S(2)}, u32[]{:S(2)}) collective-permute-start(bf16[528,128]{1,0:T(8,128)(2,1)S(1)} %get-tuple-element.22.m2_ref), channel_id=1, source_target_pairs={{0,4},{2,6},{4,0},{6,2},{1,5},{3,7},{5,1},{7,3},{8,12},{10,14},{12... | collective-permute-start | bytes 405512 | tf_op jit(solution)/shard_map/ppermute | solution.py:372
  46.1 13.4 %all-to-all-start.1 = ((bf16[8,288,128]{2,1,0:T(8,128)(2,1)}), bf16[8,288,128]{2,1,0:T(8,128)(2,1)S(1)}, u32[]{:S(2)}, u32[]{:S(2)}) async-start(bf16[8,288,128]{2,1,0:T(8,128)(2,1)} %shard_map.127), calls=%async_computation.1 | async-start | bytes 1179648 | tf_op jit(solution)/shard_map/all_to_all | solution.py:387
  54.0 2.7 %copy-start.1 = (bf16[1024,3072]{1,0:T(8,128)(2,1)}, bf16[1024,3072]{1,0:T(8,128)(2,1)S(1)}, u32[]{:S(2)}) copy-start(bf16[1024,3072]{1,0:T(8,128)(2,1)S(1)} %shard_map.128.w_ref) | copy-start | bytes 18874372
  59.5 2.8 %copy-start.2 = (bf16[1024,3072]{1,0:T(8,128)(2,1)S(1)}, bf16[1024,3072]{1,0:T(8,128)(2,1)}, u32[]{:S(2)}) copy-start(bf16[1024,3072]{1,0:T(8,128)(2,1)} %copy-done.1) | copy-start | bytes 18874372
  62.3 5.2 %copy-start.3 = (bf16[1,16,3072]{2,1,0:T(8,128)(2,1)S(1)}, bf16[1,16,3072]{2,1,0:T(8,128)(2,1)}, u32[]{:S(2)}) copy-start(bf16[1,16,3072]{2,1,0:T(8,128)(2,1)} %param.17) | copy-start | bytes 294916
  62.3 5.2 %copy-start.4 = (f32[3072]{0:T(1024)S(1)}, f32[3072]{0:T(1024)}, u32[]{:S(2)}) copy-start(f32[3072]{0:T(1024)} %param.19) | copy-start | bytes 36868
  62.3 5.2 %copy-start.5 = (f32[3072]{0:T(1024)S(1)}, f32[3072]{0:T(1024)}, u32[]{:S(2)}) copy-start(f32[3072]{0:T(1024)} %param.20) | copy-start | bytes 36868
  63.6 3.9 %collective-permute-start.9 = (bf16[16,3072]{1,0:T(8,128)(2,1)S(1)}, bf16[16,3072]{1,0:T(8,128)(2,1)S(1)}, u32[]{:S(2)}, u32[]{:S(2)}) collective-permute-start(bf16[16,3072]{1,0:T(8,128)(2,1)S(1)} %get-tuple-element.26), channel_id=1, source_target_pairs={{0,1},{1,0},{2,3},{3,2},{4,5},{5,4},{6,7},{7,6},{8,9},{9,8},{10,11... | collective-permute-start | bytes 294920 | tf_op jit(solution)/shard_map/ppermute | solution.py:399

commit v14 on v13

--- a/solution.py
+++ b/solution.py
@@ -160,16 +160,7 @@
     return jnp.concatenate(halves, axis=0)
 
 
-def query_block(b, recv_ref, q_refs, txt_ref):
-    if b == 4:
-        return txt_ref[0]
-    q = recv_ref[:, 0:32, :] if b == 0 else q_refs[b - 1][...]
-    return q.reshape(256, HD)
-
-
-def early_body(
-    where_ref, len_ref, recv_ref, kv_ref, q1_ref, q2_ref, q3_ref, txt_ref, acc_ref, stat_ref
-):
+def early_rows(where_ref, len_ref, recv_ref, kv_ref, txt_ref, blocks, acc_ref, stat_ref):
     j = where_ref[0]
     start = pl.multiple_of((j // 2) * 128, 128)
     keys = jnp.concatenate(
@@ -187,8 +178,7 @@
         axis=0,
     )
     live = live_mask(j, len_ref[0])
-    for b in range(5):
-        q = query_block(b, recv_ref, (q1_ref, q2_ref, q3_ref), txt_ref)
+    for slot, q in enumerate(blocks):
         scores = lax.dot_general(q, keys, (((1,), (1,)), ((), ())), preferred_element_type=f32)
         s_txt = jnp.where(live, scores[:, 512:], neg_large)
         peak = jnp.maximum(
@@ -198,10 +188,22 @@
         w_txt = jnp.exp2((s_txt - peak) * SCALE)
         total = jnp.sum(w_img, axis=1, keepdims=True) + jnp.sum(w_txt, axis=1, keepdims=True)
         weights = jnp.concatenate([w_img.astype(bf16), w_txt.astype(bf16)], axis=1)
-        at = slice(256 * b, 256 * b + 256)
+        at = slice(256 * slot, 256 * slot + 256)
         acc_ref[at, :] = jnp.dot(weights, values, preferred_element_type=f32)
         stat_ref[0, at, :] = jnp.broadcast_to(peak, (256, 128))
         stat_ref[1, at, :] = jnp.broadcast_to(total, (256, 128))
+
+
+def early_near_body(where_ref, len_ref, recv_ref, kv_ref, txt_ref, acc_ref, stat_ref):
+    blocks = (txt_ref[0], recv_ref[:, 0:32, :].reshape(256, HD))
+    early_rows(where_ref, len_ref, recv_ref, kv_ref, txt_ref, blocks, acc_ref, stat_ref)
+
+
+def early_far_body(
+    where_ref, len_ref, recv_ref, kv_ref, txt_ref, q1_ref, q2_ref, q3_ref, acc_ref, stat_ref
+):
+    blocks = [q[...].reshape(256, HD) for q in (q1_ref, q2_ref, q3_ref)]
+    early_rows(where_ref, len_ref, recv_ref, kv_ref, txt_ref, blocks, acc_ref, stat_ref)
 
 
 def late_keys(kv0_ref, kv1_ref):
@@ -211,8 +213,8 @@
     return keys, values
 
 
-def late_block(b, q, keys, values, acc_ref, stat_ref):
-    at = slice(256 * b, 256 * b + 256)
+def late_block(slot, q, keys, values, acc_ref, stat_ref):
+    at = slice(256 * slot, 256 * slot + 256)
     scores = lax.dot_general(q, keys, (((1,), (1,)), ((), ())), preferred_element_type=f32)
     before = stat_ref[0, at, 0:1]
     peak = jnp.maximum(before, jnp.max(scores, axis=1, keepdims=True))
@@ -226,15 +228,15 @@
 
 
 def late_first_body(
-    kv0_ref, kv1_ref, q2_ref, txt_ref, acc_ref, stat_ref, m2_ref, keep_ref
+    kv0_ref, kv1_ref, q2_ref, txt_ref, acc_ref, stat_ref, facc_ref, fstat_ref, m2_ref, keep_ref
 ):
     keys, values = late_keys(kv0_ref, kv1_ref)
-    out, lse = late_block(4, txt_ref[0], keys, values, acc_ref, stat_ref)
+    out, lse = late_block(0, txt_ref[0], keys, values, acc_ref, stat_ref)
     keep_ref[0] = out
     keep_ref[1] = jnp.broadcast_to(lse, (256, 128))
     m2_ref[256:512, :] = out.astype(bf16)
     m2_ref[520:528, :] = stat_rows(lse)
-    out, lse = late_block(2, q2_ref[...].reshape(256, HD), keys, values, acc_ref, stat_ref)
+    out, lse = late_block(1, q2_ref[...].reshape(256, HD), keys, values, facc_ref, fstat_ref)
     m2_ref[0:256, :] = out.astype(bf16)
     m2_ref[512:520, :] = stat_rows(lse)
 
@@ -243,8 +245,8 @@
     kv0_ref, kv1_ref, q3_ref, q1_ref, acc_ref, stat_ref, m2_ref, m3_ref, m1_ref
 ):
     keys, values = late_keys(kv0_ref, kv1_ref)
-    for b, q_ref, m_ref in ((3, q3_ref, m3_ref), (1, q1_ref, m1_ref)):
-        out, lse = late_block(b, q_ref[...].reshape(256, HD), keys, values, acc_ref, stat_ref)
+    for slot, q_ref, m_ref in ((2, q3_ref, m3_ref), (0, q1_ref, m1_ref)):
+        out, lse = late_block(slot, q_ref[...].reshape(256, HD), keys, values, acc_ref, stat_ref)
         m_ref[0:256, :] = out.astype(bf16)
         m_ref[256:512, :] = m2_ref[256:512, :]
         m_ref[512:520, :] = stat_rows(lse)
@@ -254,7 +256,7 @@
 def late_own_body(kv0_ref, kv1_ref, recv_ref, acc_ref, stat_ref, keep_ref):
     keys, values = late_keys(kv0_ref, kv1_ref)
     q = recv_ref[:, 0:32, :].reshape(256, HD)
-    out, lse = late_block(0, q, keys, values, acc_ref, stat_ref)
+    out, lse = late_block(1, q, keys, values, acc_ref, stat_ref)
     keep_ref[0] = out
     keep_ref[1] = jnp.broadcast_to(lse, (256, 128))
 
@@ -356,13 +358,21 @@
     others = {}
     for s in (2, 3, 1):
         others[s] = lax.ppermute(kv, "zh", [(i, i ^ s) for i in range(4)])
-    queries = [lax.ppermute(q, "y", [(i, i ^ s) for i in range(4)]) for s in (1, 2, 3)]
-
+    queries = {}
+    for s in (2, 3, 1):
+        queries[s] = lax.ppermute(q, "y", [(i, i ^ s) for i in range(4)])
+
+    here = (j, txt_len, recv, others[2], txt)
     acc, stat = call(
-        early_body,
-        [jax.ShapeDtypeStruct((1280, HD), f32), jax.ShapeDtypeStruct((2, 1280, 128), f32)],
+        early_near_body,
+        [jax.ShapeDtypeStruct((512, HD), f32), jax.ShapeDtypeStruct((2, 512, 128), f32)],
+        5, smem=(0, 1),
+    )(*here)
+    far = call(
+        early_far_body,
+        [jax.ShapeDtypeStruct((768, HD), f32), jax.ShapeDtypeStruct((2, 768, 128), f32)],
         8, smem=(0, 1),
-    )(j, txt_len, recv, others[2], *queries, txt)
+    )(*here, queries[1], queries[2], queries[3])
     late = (others[3], others[1])
     message = jax.ShapeDtypeStruct((528, HD), bf16)
     kept = jax.ShapeDtypeStruct((2, 256, 128), f32)
@@ -371,9 +381,9 @@
     def pass_on(m, s):
         got[s] = lax.ppermute(m, "y", [(i, i ^ s) for i in range(4)])
 
-    m2, keep = call(late_first_body, [message, kept], 6)(*late, queries[1], txt, acc, stat)
+    m2, keep = call(late_first_body, [message, kept], 8)(*late, queries[2], txt, acc, stat, *far)
     pass_on(m2, 2)
-    m3, m1 = call(late_second_body, [message] * 2, 7)(*late, queries[2], queries[0], acc, stat, m2)
+    m3, m1 = call(late_second_body, [message] * 2, 7)(*late, queries[3], queries[1], *far, m2)
     pass_on(m3, 3)
     pass_on(m1, 1)
     own = call(late_own_body, kept, 5)(*late, recv, acc, stat)

time: 68.5 us -> 67.2 us (0.981)
  waiting for transfers between devices: 15.1 us -> 11.3 us
  starting transfers between devices: 22 us -> 24.2 us
    ppermute x3, waiting for transfers between devices: 3.41 us -> 1.42 us  [shards(): others[s] = lax.ppermute(kv, 'zh', [(i, i ^ s) for i in range(4)])]
    ppermute x3, waiting for transfers between devices: 4.27 us -> 2.6 us  [shards(): queries[s] = lax.ppermute(q, 'y', [(i, i ^ s) for i in range(4)])]
    ppermute x1, starting transfers between devices: 2.96 us -> 4.37 us  [shards(): theirs = lax.ppermute(other, 'tp', [(0, 1), (1, 0)])]
    all_to_all x1, waiting for transfers between devices: 2.84 us -> 1.87 us  [shards(): home = lax.all_to_all(back, HEAD, 0, 0, tiled=True)]
    ppermute x3, waiting for transfers between devices: 3.61 us -> 4.46 us  [pass_on(): got[s] = lax.ppermute(m, 'y', [(i, i ^ s) for i in range(4)])]
    ppermute x3, starting transfers between devices: 3.41 us -> 4.1 us  [shards(): queries[s] = lax.ppermute(q, 'y', [(i, i ^ s) for i in range(4)])]
    pallas_call x8 -> x9, Pallas kernels: 11.6 us -> 11.9 us  [run(): return kernel(*held)]
  transfers between devices with their start and end apart: 11 -> 11, of which waited for: 6 -> 7; matrix products, arithmetic and copies ran while one was open for 0% -> 0% of each run, Pallas kernels for 8% -> 9%
where the time goes in v14:
time: 67.2 us; the launch traced here: 66.9 us
  starting transfers between devices  24.2 us (36%)
  Pallas kernels  11.9 us (18%)
  blocking collectives  11.9 us (18%)
  waiting for transfers between devices  11.3 us (17%)
  local copies, waits for them, and re-layouts  5.52 us (8%)
  between operations  1.41 us (2%)
  other arithmetic  0.69 us (1%)
    all_to_all x1, blocking collectives, shards(): recv = lax.all_to_all(send, HEAD, 0, 0, tiled=True)  11.9 us
    pallas_call x9, Pallas kernels, run(): return kernel(*held)  11.9 us
    ppermute x3, starting transfers between devices, shards(): others[s] = lax.ppermute(kv, 'zh', [(i, i ^ s) for i in range(4)])  7.29 us
    unnamed x12, local copies, waits for them, and re-layouts  5.45 us
    all_to_all x1, starting transfers between devices, shards(): home = lax.all_to_all(back, HEAD, 0, 0, tiled=True)  4.47 us
    ppermute x3, waiting for transfers between devices, pass_on(): got[s] = lax.ppermute(m, 'y', [(i, i ^ s) for i in range(4)])  4.46 us
    ppermute x1, starting transfers between devices, shards(): theirs = lax.ppermute(other, 'tp', [(0, 1), (1, 0)])  4.37 us
    ppermute x3, starting transfers between devices, shards(): queries[s] = lax.ppermute(q, 'y', [(i, i ^ s) for i in range(4)])  4.1 us
  transfers between devices with their start and end apart: 11, of which 7 were waited for; matrix products, arithmetic and copies ran while one was open for 0% of the time, Pallas kernels for 9%

profile of v14, /device:TPU:1, one launch (start us, length us, event | category | flops | bytes accessed | tf_op | source)
XLA Modules:
  0.0 66.9 jit_solution(1429536370479380647)
XLA Ops:
  0.6 0.0 copy-start
  0.7 1.3 %shard_map.122 = bf16[8,96,128]{2,1,0:T(8,128)(2,1)S(1)} custom-call(bf16[3,32,1024]{2,1,0:T(8,128)(2,1)} %bitcast.15, s32[1,32]{1,0:T(1,128)} %frame_hbm, s32[1,32]{1,0:T(1,128)} %row_hbm.1, s32[1,32]{1,0:T(1,128)} %col_hbm.1, f32[8,128]{1,0:T(8,128)} %constant.26.clone.rate_hbm), custom_call_target="tpu_custom_call" | custom-call | tf_op jit(solution)/shard_map/pallas_call | solution.py:60
  2.0 11.9 %all_to_all.10.recv_ref = bf16[8,96,128]{2,1,0:T(8,128)(2,1)S(1)} all-to-all(bf16[8,96,128]{2,1,0:T(8,128)(2,1)S(1)} %shard_map.122), channel_id=1, replica_groups=mesh['zh'=4,'zl'=2,'x'=4,'y'=4,'tp'=2] {'zl','x'}, dimensions={0} | all-to-all | bytes 393216 | tf_op jit(solution)/shard_map/all_to_all | solution.py:355
  13.9 6.1 %collective-permute-start.2 = (bf16[8,64,128]{2,1,0:T(8,128)(2,1)S(1)}, bf16[8,64,128]{2,1,0:T(8,128)(2,1)S(1)}, u32[]{:S(2)}, u32[]{:S(2)}) collective-permute-start(bf16[8,64,128]{2,1,0:T(8,128)(2,1)S(1)} %slice.8), channel_id=1, source_target_pairs={{0,128},{64,192},{128,0},{192,64},{1,129},{65,193},{129,1},{193,65... | collective-permute-start | bytes 393224 | tf_op jit(solution)/shard_map/ppermute | solution.py:360
  20.0 1.2 %collective-permute-start.1 = (bf16[8,64,128]{2,1,0:T(8,128)(2,1)S(1)}, bf16[8,64,128]{2,1,0:T(8,128)(2,1)S(1)}, u32[]{:S(2)}, u32[]{:S(2)}) collective-permute-start(bf16[8,64,128]{2,1,0:T(8,128)(2,1)S(1)} %slice.8), channel_id=1, source_target_pairs={{0,64},{64,0},{128,192},{192,128},{1,65},{65,1},{129,193},{193,129... | collective-permute-start | bytes 393224 | tf_op jit(solution)/shard_map/ppermute | solution.py:360
  21.2 0.0 collective-permute-start
  21.8 2.8 %collective-permute-start.5 = (bf16[8,32,128]{2,1,0:T(8,128)(2,1)S(1)}, bf16[8,32,128]{2,1,0:T(8,128)(2,1)S(1)}, u32[]{:S(2)}, u32[]{:S(2)}) collective-permute-start(bf16[8,32,128]{2,1,0:T(8,128)(2,1)S(1)} %slice.9), channel_id=1, source_target_pairs={{0,6},{2,4},{4,2},{6,0},{1,7},{3,5},{5,3},{7,1},{8,14},{10,12},{12... | collective-permute-start | bytes 196616 | tf_op jit(solution)/shard_map/ppermute | solution.py:363
  24.7 0.0 collective-permute-start.4
  24.7 0.0 collective-permute-done.2.kv_ref
  24.7 1.3 %collective-permute-start.3 = (bf16[8,32,128]{2,1,0:T(8,128)(2,1)S(1)}, bf16[8,32,128]{2,1,0:T(8,128)(2,1)S(1)}, u32[]{:S(2)}, u32[]{:S(2)}) collective-permute-start(bf16[8,32,128]{2,1,0:T(8,128)(2,1)S(1)} %slice.9), channel_id=1, source_target_pairs={{0,4},{2,6},{4,0},{6,2},{1,5},{3,7},{5,1},{7,3},{8,12},{10,14},{12... | collective-permute-start | bytes 196616 | tf_op jit(solution)/shard_map/ppermute | solution.py:363
  26.0 0.0 copy-done
  26.0 0.1 dynamic-slice_bitcast_fusion.txt_ref
  26.0 1.0 %shard_map.123 = (f32[512,128]{1,0:T(8,128)S(1)}, f32[2,512,128]{2,1,0:T(8,128)S(1)}) custom-call(s32[1]{0:T(128)} %bitcast.1.where_ref, s32[1]{0:T(128)S(6)} %copy.13.len_ref, bf16[8,96,128]{2,1,0:T(8,128)(2,1)S(1)} %all_to_all.10.recv_ref, bf16[8,64,128]{2,1,0:T(8,128)(2,1)S(1)} %collective-permute-done.2.kv_ref, ...), custom_call_target="tpu_custom_call" | custom-call | tf_op jit(solution)/shard_map/pallas_call | solution.py:60
  27.0 0.0 collective-permute-done.5.q3_ref
  27.0 0.8 %collective-permute-done.4.q1_ref = bf16[8,32,128]{2,1,0:T(8,128)(2,1)S(1)} collective-permute-done((bf16[8,32,128]{2,1,0:T(8,128)(2,1)S(1)}, bf16[8,32,128]{2,1,0:T(8,128)(2,1)S(1)}, u32[]{:S(2)}, u32[]{:S(2)}) %collective-permute-start.4) | collective-permute-done | bytes 65568 | tf_op jit(solution)/shard_map/ppermute | solution.py:363
  27.8 1.8 %collective-permute-done.3.q2_ref = bf16[8,32,128]{2,1,0:T(8,128)(2,1)S(1)} collective-permute-done((bf16[8,32,128]{2,1,0:T(8,128)(2,1)S(1)}, bf16[8,32,128]{2,1,0:T(8,128)(2,1)S(1)}, u32[]{:S(2)}, u32[]{:S(2)}) %collective-permute-start.3) | collective-permute-done | bytes 65568 | tf_op jit(solution)/shard_map/ppermute | solution.py:363
  29.6 1.3 %shard_map.125 = (f32[768,128]{1,0:T(8,128)S(1)}, f32[2,768,128]{2,1,0:T(8,128)S(1)}) custom-call(s32[1]{0:T(128)} %bitcast.1.where_ref, s32[1]{0:T(128)S(6)} %copy.13.len_ref, bf16[8,96,128]{2,1,0:T(8,128)(2,1)S(1)} %all_to_all.10.recv_ref, bf16[8,64,128]{2,1,0:T(8,128)(2,1)S(1)} %collective-permute-done.2.kv_ref, ...), custom_call_target="tpu_custom_call" | custom-call | tf_op jit(solution)/shard_map/pallas_call | solution.py:60
  30.9 1.4 %collective-permute-done.1.kv1_ref = bf16[8,64,128]{2,1,0:T(8,128)(2,1)S(1)} collective-permute-done((bf16[8,64,128]{2,1,0:T(8,128)(2,1)S(1)}, bf16[8,64,128]{2,1,0:T(8,128)(2,1)S(1)}, u32[]{:S(2)}, u32[]{:S(2)}) %collective-permute-start.1) | collective-permute-done | bytes 131104 | tf_op jit(solution)/shard_map/ppermute | solution.py:360
  32.3 0.0 collective-permute-done.kv0_ref
  32.3 1.0 %shard_map.126 = (bf16[528,128]{1,0:T(8,128)(2,1)S(1)}, f32[2,256,128]{2,1,0:T(8,128)S(1)}) custom-call(bf16[8,64,128]{2,1,0:T(8,128)(2,1)S(1)} %collective-permute-done.kv0_ref, bf16[8,64,128]{2,1,0:T(8,128)(2,1)S(1)} %collective-permute-done.1.kv1_ref, bf16[8,32,128]{2,1,0:T(8,128)(2,1)S(1)} %collective-permute-done.3.q2_ref, ...), custom_call_target="tpu_custom_call" | custom-call | tf_op jit(solution)/shard_map/pallas_call | solution.py:60
  33.3 1.0 %shard_map.127 = (bf16[528,128]{1,0:T(8,128)(2,1)S(1)}, bf16[528,128]{1,0:T(8,128)(2,1)S(1)}) custom-call(bf16[8,64,128]{2,1,0:T(8,128)(2,1)S(1)} %collective-permute-done.kv0_ref, bf16[8,64,128]{2,1,0:T(8,128)(2,1)S(1)} %collective-permute-done.1.kv1_ref, bf16[8,32,128]{2,1,0:T(8,128)(2,1)S(1)} %collective-permute-done.5.q3_ref, ...), custom_call_target="tpu_custom_call" | custom-call | tf_op jit(solution)/shard_map/pallas_call | solution.py:60
  34.3 1.4 %collective-permute-start.6 = (bf16[528,128]{1,0:T(8,128)(2,1)S(1)}, bf16[528,128]{1,0:T(8,128)(2,1)S(1)}, u32[]{:S(2)}, u32[]{:S(2)}) collective-permute-start(bf16[528,128]{1,0:T(8,128)(2,1)S(1)} %get-tuple-element.27), channel_id=1, source_target_pairs={{0,2},{2,0},{4,6},{6,4},{1,3},{3,1},{5,7},{7,5},{8,10},{10,8},{12,... | collective-permute-start | bytes 405512 | tf_op jit(solution)/shard_map/ppermute | solution.py:382
  35.7 1.9 %collective-permute-start.8 = (bf16[528,128]{1,0:T(8,128)(2,1)S(1)}, bf16[528,128]{1,0:T(8,128)(2,1)S(1)}, u32[]{:S(2)}, u32[]{:S(2)}) collective-permute-start(bf16[528,128]{1,0:T(8,128)(2,1)S(1)} %get-tuple-element.28), channel_id=1, source_target_pairs={{0,6},{2,4},{4,2},{6,0},{1,7},{3,5},{5,3},{7,1},{8,14},{10,12},{12... | collective-permute-start | bytes 405512 | tf_op jit(solution)/shard_map/ppermute | solution.py:382
  37.6 0.7 %collective-permute-start.7 = (bf16[528,128]{1,0:T(8,128)(2,1)S(1)}, bf16[528,128]{1,0:T(8,128)(2,1)S(1)}, u32[]{:S(2)}, u32[]{:S(2)}) collective-permute-start(bf16[528,128]{1,0:T(8,128)(2,1)S(1)} %get-tuple-element.26.m2_ref), channel_id=1, source_target_pairs={{0,4},{2,6},{4,0},{6,2},{1,5},{3,7},{5,1},{7,3},{8,12},{10,14},{12... | collective-permute-start | bytes 405512 | tf_op jit(solution)/shard_map/ppermute | solution.py:382
  38.3 0.6 shard_map.124.own_ref
  38.9 0.0 collective-permute-done.6.g1_ref
  38.9 1.9 %collective-permute-done.8.g3_ref = bf16[528,128]{1,0:T(8,128)(2,1)S(1)} collective-permute-done((bf16[528,128]{1,0:T(8,128)(2,1)S(1)}, bf16[528,128]{1,0:T(8,128)(2,1)S(1)}, u32[]{:S(2)}, u32[]{:S(2)}) %collective-permute-start.8) | collective-permute-done | bytes 135200 | tf_op jit(solution)/shard_map/ppermute | solution.py:382
  40.8 2.6 %collective-permute-done.7.g2_ref = bf16[528,128]{1,0:T(8,128)(2,1)S(1)} collective-permute-done((bf16[528,128]{1,0:T(8,128)(2,1)S(1)}, bf16[528,128]{1,0:T(8,128)(2,1)S(1)}, u32[]{:S(2)}, u32[]{:S(2)}) %collective-permute-start.7) | collective-permute-done | bytes 135200 | tf_op jit(solution)/shard_map/ppermute | solution.py:382
  43.4 1.5 %shard_map.128 = bf16[8,288,128]{2,1,0:T(8,128)(2,1)} custom-call(s32[1]{0:T(128)S(6)} %copy.13.len_ref, f32[2,256,128]{2,1,0:T(8,128)S(1)} %shard_map.124.own_ref, f32[2,256,128]{2,1,0:T(8,128)S(1)} %get-tuple-element.25.keep_ref, bf16[528,128]{1,0:T(8,128)(2,1)S(1)} %collective-permute-done.6.g1_ref, bf16[528,128]{1,0:T(8,128)(2,1)S(1)} %collective-permute-done.7.g2_ref, ...), custom_call_target="tpu_custom_call" | custom-call | tf_op jit(solution)/shard_map/pallas_call | solution.py:60
  44.9 4.5 %all-to-all-start.1 = ((bf16[8,288,128]{2,1,0:T(8,128)(2,1)}), bf16[8,288,128]{2,1,0:T(8,128)(2,1)S(1)}, u32[]{:S(2)}, u32[]{:S(2)}) async-start(bf16[8,288,128]{2,1,0:T(8,128)(2,1)} %shard_map.128), calls=%async_computation.1 | async-start | bytes 1179648 | tf_op jit(solution)/shard_map/all_to_all | solution.py:397
  49.4 2.9 %shard_map.129.w_ref = bf16[1024,3072]{1,0:T(8,128)(2,1)S(1)} custom-call(bf16[1024,3072]{1,0:T(8,128)(2,1)} %w_hbm.1), custom_call_target="tpu_custom_call" | custom-call | tf_op jit(solution)/shard_map/pallas_call | solution.py:60
  52.3 0.0 copy-start.1
  52.3 2.6 %copy-done.1 = bf16[1024,3072]{1,0:T(8,128)(2,1)} copy-done((bf16[1024,3072]{1,0:T(8,128)(2,1)}, bf16[1024,3072]{1,0:T(8,128)(2,1)S(1)}, u32[]{:S(2)}) %copy-start.1) | copy-done | bytes 6291480
  54.9 1.9 %all-to-all-done.1.recv_ref = bf16[8,288,128]{2,1,0:T(8,128)(2,1)S(1)} async-done(((bf16[8,288,128]{2,1,0:T(8,128)(2,1)}), bf16[8,288,128]{2,1,0:T(8,128)(2,1)S(1)}, u32[]{:S(2)}, u32[]{:S(2)}) %all-to-all-start.1) | async-done | bytes 589856 | tf_op jit(solution)/shard_map/all_to_all | solution.py:397
  56.8 0.0 copy-start.2
  56.8 2.8 %copy-done.2 = bf16[1024,3072]{1,0:T(8,128)(2,1)S(1)} copy-done((bf16[1024,3072]{1,0:T(8,128)(2,1)S(1)}, bf16[1024,3072]{1,0:T(8,128)(2,1)}, u32[]{:S(2)}) %copy-start.2) | copy-done | bytes 6291480
  59.6 0.0 copy-start.3
  59.6 0.0 copy-start.4
  59.6 0.0 copy-start.5
  59.6 1.3 %shard_map.130 = (f32[16,3072]{1,0:T(8,128)S(1)}, bf16[16,3072]{1,0:T(8,128)(2,1)S(1)}, bf16[256,1024]{1,0:T(8,128)(2,1)}) custom-call(s32[1]{0:T(128)} %bitcast.2.core_ref, bf16[8,288,128]{2,1,0:T(8,128)(2,1)S(1)} %all-to-all-done.1.recv_ref, bf16[1024,3072]{1,0:T(8,128)(2,1)S(1)} %copy-done.2), custom_call_target="tpu_custom_call" | custom-call | tf_op jit(solution)/shard_map/pallas_call | solution.py:60
  60.9 4.4 %collective-permute-start.9 = (bf16[16,3072]{1,0:T(8,128)(2,1)S(1)}, bf16[16,3072]{1,0:T(8,128)(2,1)S(1)}, u32[]{:S(2)}, u32[]{:S(2)}) collective-permute-start(bf16[16,3072]{1,0:T(8,128)(2,1)S(1)} %get-tuple-element.30), channel_id=1, source_target_pairs={{0,1},{1,0},{2,3},{3,2},{4,5},{5,4},{6,7},{7,6},{8,9},{9,8},{10,11... | collective-permute-start | bytes 294920 | tf_op jit(solution)/shard_map/ppermute | solution.py:409
  65.2 0.9 %collective-permute-done.9 = bf16[16,3072]{1,0:T(8,128)(2,1)S(1)} collective-permute-done((bf16[16,3072]{1,0:T(8,128)(2,1)S(1)}, bf16[16,3072]{1,0:T(8,128)(2,1)S(1)}, u32[]{:S(2)}, u32[]{:S(2)}) %collective-permute-start.9) | collective-permute-done | bytes 98336 | tf_op jit(solution)/shard_map/ppermute | solution.py:409
  66.2 0.0 copy-done.3
  66.2 0.0 copy-done.4
  66.2 0.0 copy-done.5
  66.2 0.7 %fusion.1 = bf16[1,16,3072]{2,1,0:T(8,128)(2,1)} fusion(f32[16,3072]{1,0:T(8,128)S(1)} %get-tuple-element.29, bf16[16,3072]{1,0:T(8,128)(2,1)S(1)} %collective-permute-done.9, bf16[1,16,3072]{2,1,0:T(8,128)(2,1)S(1)} %copy-done.3, f32[3072]{0:T(1024)S(1)} %copy-done.4, f32[3072]{0:T(1024)S(1)} %copy-done.5), kind=kLoop, calls=%fused_computation.3 | loop fusion | flops 344064 | bytes 516096 | tf_op jit(solution)/shard_map/broadcast_in_dim | solution.py:412
  (2 shorter events, 0.0 us)
Async XLA Ops:
  0.6 25.3 %copy-start = (bf16[1,256,3,1024]{3,1,2,0:T(8,128)(2,1)S(1)}, bf16[1,256,3,1024]{3,1,2,0:T(8,128)(2,1)}, u32[]{:S(2)}) copy-start(bf16[1,256,3,1024]{3,1,2,0:T(8,128)(2,1)} %param.12) | copy-start | bytes 4718596
  13.9 10.8 %collective-permute-start.2 = (bf16[8,64,128]{2,1,0:T(8,128)(2,1)S(1)}, bf16[8,64,128]{2,1,0:T(8,128)(2,1)S(1)}, u32[]{:S(2)}, u32[]{:S(2)}) collective-permute-start(bf16[8,64,128]{2,1,0:T(8,128)(2,1)S(1)} %slice.8), channel_id=1, source_target_pairs={{0,128},{64,192},{128,0},{192,64},{1,129},{65,193},{129,1},{193,65... | collective-permute-start | bytes 393224 | tf_op jit(solution)/shard_map/ppermute | solution.py:360
  20.0 12.4 %collective-permute-start.1 = (bf16[8,64,128]{2,1,0:T(8,128)(2,1)S(1)}, bf16[8,64,128]{2,1,0:T(8,128)(2,1)S(1)}, u32[]{:S(2)}, u32[]{:S(2)}) collective-permute-start(bf16[8,64,128]{2,1,0:T(8,128)(2,1)S(1)} %slice.8), channel_id=1, source_target_pairs={{0,64},{64,0},{128,192},{192,128},{1,65},{65,1},{129,193},{193,129... | collective-permute-start | bytes 393224 | tf_op jit(solution)/shard_map/ppermute | solution.py:360
  21.2 11.2 %collective-permute-start = (bf16[8,64,128]{2,1,0:T(8,128)(2,1)S(1)}, bf16[8,64,128]{2,1,0:T(8,128)(2,1)S(1)}, u32[]{:S(2)}, u32[]{:S(2)}) collective-permute-start(bf16[8,64,128]{2,1,0:T(8,128)(2,1)S(1)} %slice.8), channel_id=1, source_target_pairs={{0,192},{64,128},{128,64},{192,0},{1,193},{65,129},{129,65},{193,1... | collective-permute-start | bytes 393224 | tf_op jit(solution)/shard_map/ppermute | solution.py:360
  21.8 5.1 %collective-permute-start.5 = (bf16[8,32,128]{2,1,0:T(8,128)(2,1)S(1)}, bf16[8,32,128]{2,1,0:T(8,128)(2,1)S(1)}, u32[]{:S(2)}, u32[]{:S(2)}) collective-permute-start(bf16[8,32,128]{2,1,0:T(8,128)(2,1)S(1)} %slice.9), channel_id=1, source_target_pairs={{0,6},{2,4},{4,2},{6,0},{1,7},{3,5},{5,3},{7,1},{8,14},{10,12},{12... | collective-permute-start | bytes 196616 | tf_op jit(solution)/shard_map/ppermute | solution.py:363
  24.7 3.1 %collective-permute-start.4 = (bf16[8,32,128]{2,1,0:T(8,128)(2,1)S(1)}, bf16[8,32,128]{2,1,0:T(8,128)(2,1)S(1)}, u32[]{:S(2)}, u32[]{:S(2)}) collective-permute-start(bf16[8,32,128]{2,1,0:T(8,128)(2,1)S(1)} %slice.9), channel_id=1, source_target_pairs={{0,2},{2,0},{4,6},{6,4},{1,3},{3,1},{5,7},{7,5},{8,10},{10,8},{12,... | collective-permute-start | bytes 196616 | tf_op jit(solution)/shard_map/ppermute | solution.py:363
  24.7 4.9 %collective-permute-start.3 = (bf16[8,32,128]{2,1,0:T(8,128)(2,1)S(1)}, bf16[8,32,128]{2,1,0:T(8,128)(2,1)S(1)}, u32[]{:S(2)}, u32[]{:S(2)}) collective-permute-start(bf16[8,32,128]{2,1,0:T(8,128)(2,1)S(1)} %slice.9), channel_id=1, source_target_pairs={{0,4},{2,6},{4,0},{6,2},{1,5},{3,7},{5,1},{7,3},{8,12},{10,14},{12... | collective-permute-start | bytes 196616 | tf_op jit(solution)/shard_map/ppermute | solution.py:363
  34.3 4.6 %collective-permute-start.6 = (bf16[528,128]{1,0:T(8,128)(2,1)S(1)}, bf16[528,128]{1,0:T(8,128)(2,1)S(1)}, u32[]{:S(2)}, u32[]{:S(2)}) collective-permute-start(bf16[528,128]{1,0:T(8,128)(2,1)S(1)} %get-tuple-element.27), channel_id=1, source_target_pairs={{0,2},{2,0},{4,6},{6,4},{1,3},{3,1},{5,7},{7,5},{8,10},{10,8},{12,... | collective-permute-start | bytes 405512 | tf_op jit(solution)/shard_map/ppermute | solution.py:382
  35.7 5.1 %collective-permute-start.8 = (bf16[528,128]{1,0:T(8,128)(2,1)S(1)}, bf16[528,128]{1,0:T(8,128)(2,1)S(1)}, u32[]{:S(2)}, u32[]{:S(2)}) collective-permute-start(bf16[528,128]{1,0:T(8,128)(2,1)S(1)} %get-tuple-element.28), channel_id=1, source_target_pairs={{0,6},{2,4},{4,2},{6,0},{1,7},{3,5},{5,3},{7,1},{8,14},{10,12},{12... | collective-permute-start | bytes 405512 | tf_op jit(solution)/shard_map/ppermute | solution.py:382
  37.6 5.8 %collective-permute-start.7 = (bf16[528,128]{1,0:T(8,128)(2,1)S(1)}, bf16[528,128]{1,0:T(8,128)(2,1)S(1)}, u32[]{:S(2)}, u32[]{:S(2)}) collective-permute-start(bf16[528,128]{1,0:T(8,128)(2,1)S(1)} %get-tuple-element.26.m2_ref), channel_id=1, source_target_pairs={{0,4},{2,6},{4,0},{6,2},{1,5},{3,7},{5,1},{7,3},{8,12},{10,14},{12... | collective-permute-start | bytes 405512 | tf_op jit(solution)/shard_map/ppermute | solution.py:382
  44.9 11.9 %all-to-all-start.1 = ((bf16[8,288,128]{2,1,0:T(8,128)(2,1)}), bf16[8,288,128]{2,1,0:T(8,128)(2,1)S(1)}, u32[]{:S(2)}, u32[]{:S(2)}) async-start(bf16[8,288,128]{2,1,0:T(8,128)(2,1)} %shard_map.128), calls=%async_computation.1 | async-start | bytes 1179648 | tf_op jit(solution)/shard_map/all_to_all | solution.py:397
  52.3 2.7 %copy-start.1 = (bf16[1024,3072]{1,0:T(8,128)(2,1)}, bf16[1024,3072]{1,0:T(8,128)(2,1)S(1)}, u32[]{:S(2)}) copy-start(bf16[1024,3072]{1,0:T(8,128)(2,1)S(1)} %shard_map.129.w_ref) | copy-start | bytes 18874372
  56.8 2.8 %copy-start.2 = (bf16[1024,3072]{1,0:T(8,128)(2,1)S(1)}, bf16[1024,3072]{1,0:T(8,128)(2,1)}, u32[]{:S(2)}) copy-start(bf16[1024,3072]{1,0:T(8,128)(2,1)} %copy-done.1) | copy-start | bytes 18874372
  59.6 6.6 %copy-start.3 = (bf16[1,16,3072]{2,1,0:T(8,128)(2,1)S(1)}, bf16[1,16,3072]{2,1,0:T(8,128)(2,1)}, u32[]{:S(2)}) copy-start(bf16[1,16,3072]{2,1,0:T(8,128)(2,1)} %param.17) | copy-start | bytes 294916
  59.6 6.6 %copy-start.4 = (f32[3072]{0:T(1024)S(1)}, f32[3072]{0:T(1024)}, u32[]{:S(2)}) copy-start(f32[3072]{0:T(1024)} %param.19) | copy-start | bytes 36868
  59.6 6.6 %copy-start.5 = (f32[3072]{0:T(1024)S(1)}, f32[3072]{0:T(1024)}, u32[]{:S(2)}) copy-start(f32[3072]{0:T(1024)} %param.20) | copy-start | bytes 36868
  60.9 5.3 %collective-permute-start.9 = (bf16[16,3072]{1,0:T(8,128)(2,1)S(1)}, bf16[16,3072]{1,0:T(8,128)(2,1)S(1)}, u32[]{:S(2)}, u32[]{:S(2)}) collective-permute-start(bf16[16,3072]{1,0:T(8,128)(2,1)S(1)} %get-tuple-element.30), channel_id=1, source_target_pairs={{0,1},{1,0},{2,3},{3,2},{4,5},{5,4},{6,7},{7,6},{8,9},{9,8},{10,11... | collective-permute-start | bytes 294920 | tf_op jit(solution)/shard_map/ppermute | solution.py:409

commit v15 on v14

--- a/solution.py
+++ b/solution.py
@@ -11,8 +11,9 @@
 
 
 HD = 128
-SEQ = ("zh", "zl", "x", "y")
-HEAD = ("zl", "x")
+SEQ = ("zh", "zl", "xh", "xl", "yh", "yl")
+BLOCK = ("xh", "yh")
+HEAD = ("zl", "xl", "yl")
 rope_base = 256.0
 neg_large = -1e30
 LOG2E = 1.4426950408889634
@@ -332,8 +333,8 @@
     tokens = img_qkv.shape[1]
     width = img_qkv.shape[3]
     d_model = w_proj.shape[1]
-    j = lax.axis_index("y").astype(jnp.int32).reshape(1)
-    head = lax.axis_index("zl") * 4 + lax.axis_index("x")
+    j = lax.axis_index(BLOCK).astype(jnp.int32).reshape(1)
+    head = lax.axis_index(HEAD)
     core = lax.axis_index("tp").astype(jnp.int32).reshape(1)
     j, core, head, frame_index = lax.optimization_barrier((j, core, head, frame_index))
     qkv = img_qkv.reshape(tokens, 3, width).transpose(1, 0, 2)
@@ -360,7 +361,7 @@
         others[s] = lax.ppermute(kv, "zh", [(i, i ^ s) for i in range(4)])
     queries = {}
     for s in (2, 3, 1):
-        queries[s] = lax.ppermute(q, "y", [(i, i ^ s) for i in range(4)])
+        queries[s] = lax.ppermute(q, BLOCK, [(i, i ^ s) for i in range(4)])
 
     here = (j, txt_len, recv, others[2], txt)
     acc, stat = call(
@@ -379,7 +380,7 @@
     got = {}
 
     def pass_on(m, s):
-        got[s] = lax.ppermute(m, "y", [(i, i ^ s) for i in range(4)])
+        got[s] = lax.ppermute(m, BLOCK, [(i, i ^ s) for i in range(4)])
 
     m2, keep = call(late_first_body, [message, kept], 8)(*late, queries[2], txt, acc, stat, *far)
     pass_on(m2, 2)
@@ -414,7 +415,7 @@
 
 def solution(mesh):
     split = Mesh(
-        mesh.devices.reshape(4, 2, 4, 4, mesh.shape["tp"]), ("zh", "zl", "x", "y", "tp")
+        mesh.devices.reshape(4, 2, 2, 2, 2, 2, mesh.shape["tp"]), SEQ + ("tp",)
     )
     placed = (
         P(None, SEQ, None, "tp"),

time: 67.2 us -> 69.2 us (1.030)
  starting transfers between devices: 24.2 us -> 28.7 us
  waiting for transfers between devices: 11.3 us -> 9.76 us
  blocking collectives: 11.9 us -> 10.9 us
    ppermute x6, starting transfers between devices: 8.11 us -> 11.5 us  [the longest x3 5.74 us: shards(): queries[s] = lax.ppermute(q, BLOCK, [(i, i ^ s) for i in range(4)])]
    ppermute x1, starting transfers between devices: 4.37 us -> 6.4 us  [shards(): theirs = lax.ppermute(other, 'tp', [(0, 1), (1, 0)])]
    ppermute x3, waiting for transfers between devices: 1.42 us -> 0.01 us  [shards(): others[s] = lax.ppermute(kv, 'zh', [(i, i ^ s) for i in range(4)])]
    all_to_all x1, blocking collectives: 11.9 us -> 10.9 us  [shards(): recv = lax.all_to_all(send, HEAD, 0, 0, tiled=True)]
    all_to_all x1, starting transfers between devices: 4.47 us -> 3.54 us  [shards(): home = lax.all_to_all(back, HEAD, 0, 0, tiled=True)]
  transfers between devices with their start and end apart: 11 -> 11, of which waited for: 7 -> 6; matrix products, arithmetic and copies ran while one was open for 0% -> 0% of each run, Pallas kernels for 9% -> 8%
where the time goes in v15:
time: 69.2 us; the launch traced here: 68.9 us
  starting transfers between devices  28.7 us (41%)
  Pallas kernels  11.9 us (17%)
  blocking collectives  10.9 us (16%)
  waiting for transfers between devices  9.76 us (14%)
  local copies, waits for them, and re-layouts  5.52 us (8%)
  between operations  1.44 us (2%)
    pallas_call x9, Pallas kernels, run(): return kernel(*held)  11.9 us
    all_to_all x1, blocking collectives, shards(): recv = lax.all_to_all(send, HEAD, 0, 0, tiled=True)  10.9 us
    ppermute x3, starting transfers between devices, shards(): others[s] = lax.ppermute(kv, 'zh', [(i, i ^ s) for i in range(4)])  7.29 us
    ppermute x1, starting transfers between devices, shards(): theirs = lax.ppermute(other, 'tp', [(0, 1), (1, 0)])  6.4 us
    ppermute x3, starting transfers between devices, shards(): queries[s] = lax.ppermute(q, BLOCK, [(i, i ^ s) for i in range(4)])  5.74 us
    ppermute x3, starting transfers between devices, pass_on(): got[s] = lax.ppermute(m, BLOCK, [(i, i ^ s) for i in range(4)])  5.74 us
    unnamed x12, local copies, waits for them, and re-layouts  5.45 us
    ppermute x3, waiting for transfers between devices, pass_on(): got[s] = lax.ppermute(m, BLOCK, [(i, i ^ s) for i in range(4)])  3.9 us
  transfers between devices with their start and end apart: 11, of which 6 were waited for; matrix products, arithmetic and copies ran while one was open for 0% of the time, Pallas kernels for 8%

profile of v15, /device:TPU:1, one launch (start us, length us, event | category | flops | bytes accessed | tf_op | source)
XLA Modules:
  0.0 68.9 jit_solution(909333677303700630)
XLA Ops:
  0.6 0.0 copy-start
  0.7 1.3 %shard_map.122 = bf16[8,96,128]{2,1,0:T(8,128)(2,1)S(1)} custom-call(bf16[3,32,1024]{2,1,0:T(8,128)(2,1)} %bitcast.15, s32[1,32]{1,0:T(1,128)} %frame_hbm, s32[1,32]{1,0:T(1,128)} %row_hbm.1, s32[1,32]{1,0:T(1,128)} %col_hbm.1, f32[8,128]{1,0:T(8,128)} %constant.35.clone.rate_hbm), custom_call_target="tpu_custom_call" | custom-call | tf_op jit(solution)/shard_map/pallas_call | solution.py:61
  2.0 10.9 %all_to_all.10.recv_ref = bf16[8,96,128]{2,1,0:T(8,128)(2,1)S(1)} all-to-all(bf16[8,96,128]{2,1,0:T(8,128)(2,1)S(1)} %shard_map.122), channel_id=1, replica_groups=mesh['zh'=4,'zl'=2,'xh'=2,'xl'=2,'yh'=2,'yl'=2,'tp'=2] {'zl','xl','yl'}, dimensions={0} | all-to-all | bytes 393216 | tf_op jit(solution)/shard_map/all_to_all | solution.py:356
  13.0 6.1 %collective-permute-start.2 = (bf16[8,64,128]{2,1,0:T(8,128)(2,1)S(1)}, bf16[8,64,128]{2,1,0:T(8,128)(2,1)S(1)}, u32[]{:S(2)}, u32[]{:S(2)}) collective-permute-start(bf16[8,64,128]{2,1,0:T(8,128)(2,1)S(1)} %slice.8), channel_id=1, source_target_pairs={{0,128},{64,192},{128,0},{192,64},{1,129},{65,193},{129,1},{193,65... | collective-permute-start | bytes 393224 | tf_op jit(solution)/shard_map/ppermute | solution.py:361
  19.0 1.2 %collective-permute-start.1 = (bf16[8,64,128]{2,1,0:T(8,128)(2,1)S(1)}, bf16[8,64,128]{2,1,0:T(8,128)(2,1)S(1)}, u32[]{:S(2)}, u32[]{:S(2)}) collective-permute-start(bf16[8,64,128]{2,1,0:T(8,128)(2,1)S(1)} %slice.8), channel_id=1, source_target_pairs={{0,64},{64,0},{128,192},{192,128},{1,65},{65,1},{129,193},{193,129... | collective-permute-start | bytes 393224 | tf_op jit(solution)/shard_map/ppermute | solution.py:361
  20.2 0.0 collective-permute-start
  20.9 4.9 %collective-permute-start.5 = (bf16[8,32,128]{2,1,0:T(8,128)(2,1)S(1)}, bf16[8,32,128]{2,1,0:T(8,128)(2,1)S(1)}, u32[]{:S(2)}, u32[]{:S(2)}) collective-permute-start(bf16[8,32,128]{2,1,0:T(8,128)(2,1)S(1)} %slice.9), channel_id=1, source_target_pairs={{0,20},{4,16},{16,4},{20,0},{1,21},{5,17},{17,5},{21,1},{2,22},{6,... | collective-permute-start | bytes 196616 | tf_op jit(solution)/shard_map/ppermute | solution.py:364
  25.8 0.3 collective-permute-start.4
  26.1 0.0 collective-permute-done.2.kv_ref
  26.1 0.5 collective-permute-start.3
  26.7 0.0 copy-done
  26.7 0.1 dynamic-slice_bitcast_fusion.txt_ref
  26.7 1.0 %shard_map.123 = (f32[512,128]{1,0:T(8,128)S(1)}, f32[2,512,128]{2,1,0:T(8,128)S(1)}) custom-call(s32[1]{0:T(128)} %bitcast.1.where_ref, s32[1]{0:T(128)S(6)} %copy.13.len_ref, bf16[8,96,128]{2,1,0:T(8,128)(2,1)S(1)} %all_to_all.10.recv_ref, bf16[8,64,128]{2,1,0:T(8,128)(2,1)S(1)} %collective-permute-done.2.kv_ref, ...), custom_call_target="tpu_custom_call" | custom-call | tf_op jit(solution)/shard_map/pallas_call | solution.py:61
  27.7 0.3 collective-permute-done.5.q3_ref
  28.0 3.2 %collective-permute-done.4.q1_ref = bf16[8,32,128]{2,1,0:T(8,128)(2,1)S(1)} collective-permute-done((bf16[8,32,128]{2,1,0:T(8,128)(2,1)S(1)}, bf16[8,32,128]{2,1,0:T(8,128)(2,1)S(1)}, u32[]{:S(2)}, u32[]{:S(2)}) %collective-permute-start.4) | collective-permute-done | bytes 65568 | tf_op jit(solution)/shard_map/ppermute | solution.py:364
  31.2 0.2 collective-permute-done.3.q2_ref
  31.4 1.3 %shard_map.125 = (f32[768,128]{1,0:T(8,128)S(1)}, f32[2,768,128]{2,1,0:T(8,128)S(1)}) custom-call(s32[1]{0:T(128)} %bitcast.1.where_ref, s32[1]{0:T(128)S(6)} %copy.13.len_ref, bf16[8,96,128]{2,1,0:T(8,128)(2,1)S(1)} %all_to_all.10.recv_ref, bf16[8,64,128]{2,1,0:T(8,128)(2,1)S(1)} %collective-permute-done.2.kv_ref, ...), custom_call_target="tpu_custom_call" | custom-call | tf_op jit(solution)/shard_map/pallas_call | solution.py:61
  32.7 0.0 collective-permute-done.1.kv1_ref
  32.7 0.0 collective-permute-done.kv0_ref
  32.7 1.0 %shard_map.126 = (bf16[528,128]{1,0:T(8,128)(2,1)S(1)}, f32[2,256,128]{2,1,0:T(8,128)S(1)}) custom-call(bf16[8,64,128]{2,1,0:T(8,128)(2,1)S(1)} %collective-permute-done.kv0_ref, bf16[8,64,128]{2,1,0:T(8,128)(2,1)S(1)} %collective-permute-done.1.kv1_ref, bf16[8,32,128]{2,1,0:T(8,128)(2,1)S(1)} %collective-permute-done.3.q2_ref, ...), custom_call_target="tpu_custom_call" | custom-call | tf_op jit(solution)/shard_map/pallas_call | solution.py:61
  33.7 1.0 %shard_map.127 = (bf16[528,128]{1,0:T(8,128)(2,1)S(1)}, bf16[528,128]{1,0:T(8,128)(2,1)S(1)}) custom-call(bf16[8,64,128]{2,1,0:T(8,128)(2,1)S(1)} %collective-permute-done.kv0_ref, bf16[8,64,128]{2,1,0:T(8,128)(2,1)S(1)} %collective-permute-done.1.kv1_ref, bf16[8,32,128]{2,1,0:T(8,128)(2,1)S(1)} %collective-permute-done.5.q3_ref, ...), custom_call_target="tpu_custom_call" | custom-call | tf_op jit(solution)/shard_map/pallas_call | solution.py:61
  34.7 2.4 %collective-permute-start.6 = (bf16[528,128]{1,0:T(8,128)(2,1)S(1)}, bf16[528,128]{1,0:T(8,128)(2,1)S(1)}, u32[]{:S(2)}, u32[]{:S(2)}) collective-permute-start(bf16[528,128]{1,0:T(8,128)(2,1)S(1)} %get-tuple-element.27), channel_id=1, source_target_pairs={{0,4},{4,0},{16,20},{20,16},{1,5},{5,1},{17,21},{21,17},{2,6},{6,2... | collective-permute-start | bytes 405512 | tf_op jit(solution)/shard_map/ppermute | solution.py:383
  37.1 1.9 %collective-permute-start.8 = (bf16[528,128]{1,0:T(8,128)(2,1)S(1)}, bf16[528,128]{1,0:T(8,128)(2,1)S(1)}, u32[]{:S(2)}, u32[]{:S(2)}) collective-permute-start(bf16[528,128]{1,0:T(8,128)(2,1)S(1)} %get-tuple-element.28), channel_id=1, source_target_pairs={{0,20},{4,16},{16,4},{20,0},{1,21},{5,17},{17,5},{21,1},{2,22},{6,... | collective-permute-start | bytes 405512 | tf_op jit(solution)/shard_map/ppermute | solution.py:383
  39.0 1.5 %collective-permute-start.7 = (bf16[528,128]{1,0:T(8,128)(2,1)S(1)}, bf16[528,128]{1,0:T(8,128)(2,1)S(1)}, u32[]{:S(2)}, u32[]{:S(2)}) collective-permute-start(bf16[528,128]{1,0:T(8,128)(2,1)S(1)} %get-tuple-element.26.m2_ref), channel_id=1, source_target_pairs={{0,16},{4,20},{16,0},{20,4},{1,17},{5,21},{17,1},{21,5},{2,18},{6,... | collective-permute-start | bytes 405512 | tf_op jit(solution)/shard_map/ppermute | solution.py:383
  40.5 0.6 shard_map.124.own_ref
  41.1 0.0 collective-permute-done.6.g1_ref
  41.1 3.9 %collective-permute-done.8.g3_ref = bf16[528,128]{1,0:T(8,128)(2,1)S(1)} collective-permute-done((bf16[528,128]{1,0:T(8,128)(2,1)S(1)}, bf16[528,128]{1,0:T(8,128)(2,1)S(1)}, u32[]{:S(2)}, u32[]{:S(2)}) %collective-permute-start.8) | collective-permute-done | bytes 135200 | tf_op jit(solution)/shard_map/ppermute | solution.py:383
  45.0 0.0 collective-permute-done.7.g2_ref
  45.0 1.5 %shard_map.128 = bf16[8,288,128]{2,1,0:T(8,128)(2,1)} custom-call(s32[1]{0:T(128)S(6)} %copy.13.len_ref, f32[2,256,128]{2,1,0:T(8,128)S(1)} %shard_map.124.own_ref, f32[2,256,128]{2,1,0:T(8,128)S(1)} %get-tuple-element.25.keep_ref, bf16[528,128]{1,0:T(8,128)(2,1)S(1)} %collective-permute-done.6.g1_ref, bf16[528,128]{1,0:T(8,128)(2,1)S(1)} %collective-permute-done.7.g2_ref, ...), custom_call_target="tpu_custom_call" | custom-call | tf_op jit(solution)/shard_map/pallas_call | solution.py:61
  46.5 3.5 %all-to-all-start.1 = ((bf16[8,288,128]{2,1,0:T(8,128)(2,1)}), bf16[8,288,128]{2,1,0:T(8,128)(2,1)S(1)}, u32[]{:S(2)}, u32[]{:S(2)}) async-start(bf16[8,288,128]{2,1,0:T(8,128)(2,1)} %shard_map.128), calls=%async_computation.1 | async-start | bytes 1179648 | tf_op jit(solution)/shard_map/all_to_all | solution.py:398
  50.1 2.9 %shard_map.129.w_ref = bf16[1024,3072]{1,0:T(8,128)(2,1)S(1)} custom-call(bf16[1024,3072]{1,0:T(8,128)(2,1)} %w_hbm.1), custom_call_target="tpu_custom_call" | custom-call | tf_op jit(solution)/shard_map/pallas_call | solution.py:61
  52.9 0.0 copy-start.1
  53.0 2.6 %copy-done.1 = bf16[1024,3072]{1,0:T(8,128)(2,1)} copy-done((bf16[1024,3072]{1,0:T(8,128)(2,1)}, bf16[1024,3072]{1,0:T(8,128)(2,1)S(1)}, u32[]{:S(2)}) %copy-start.1) | copy-done | bytes 6291480
  55.6 1.2 %all-to-all-done.1.recv_ref = bf16[8,288,128]{2,1,0:T(8,128)(2,1)S(1)} async-done(((bf16[8,288,128]{2,1,0:T(8,128)(2,1)}), bf16[8,288,128]{2,1,0:T(8,128)(2,1)S(1)}, u32[]{:S(2)}, u32[]{:S(2)}) %all-to-all-start.1) | async-done | bytes 589856 | tf_op jit(solution)/shard_map/all_to_all | solution.py:398
  56.8 0.0 copy-start.2
  56.8 2.8 %copy-done.2 = bf16[1024,3072]{1,0:T(8,128)(2,1)S(1)} copy-done((bf16[1024,3072]{1,0:T(8,128)(2,1)S(1)}, bf16[1024,3072]{1,0:T(8,128)(2,1)}, u32[]{:S(2)}) %copy-start.2) | copy-done | bytes 6291480
  59.6 0.0 copy-start.3
  59.6 0.0 copy-start.4
  59.6 0.0 copy-start.5
  59.6 1.3 %shard_map.130 = (f32[16,3072]{1,0:T(8,128)S(1)}, bf16[16,3072]{1,0:T(8,128)(2,1)S(1)}, bf16[256,1024]{1,0:T(8,128)(2,1)}) custom-call(s32[1]{0:T(128)} %bitcast.2.core_ref, bf16[8,288,128]{2,1,0:T(8,128)(2,1)S(1)} %all-to-all-done.1.recv_ref, bf16[1024,3072]{1,0:T(8,128)(2,1)S(1)} %copy-done.2), custom_call_target="tpu_custom_call" | custom-call | tf_op jit(solution)/shard_map/pallas_call | solution.py:61
  60.9 6.4 %collective-permute-start.9 = (bf16[16,3072]{1,0:T(8,128)(2,1)S(1)}, bf16[16,3072]{1,0:T(8,128)(2,1)S(1)}, u32[]{:S(2)}, u32[]{:S(2)}) collective-permute-start(bf16[16,3072]{1,0:T(8,128)(2,1)S(1)} %get-tuple-element.30), channel_id=1, source_target_pairs={{0,1},{1,0},{2,3},{3,2},{4,5},{5,4},{6,7},{7,6},{8,9},{9,8},{10,11... | collective-permute-start | bytes 294920 | tf_op jit(solution)/shard_map/ppermute | solution.py:410
  67.3 0.9 %collective-permute-done.9 = bf16[16,3072]{1,0:T(8,128)(2,1)S(1)} collective-permute-done((bf16[16,3072]{1,0:T(8,128)(2,1)S(1)}, bf16[16,3072]{1,0:T(8,128)(2,1)S(1)}, u32[]{:S(2)}, u32[]{:S(2)}) %collective-permute-start.9) | collective-permute-done | bytes 98336 | tf_op jit(solution)/shard_map/ppermute | solution.py:410
  68.2 0.0 copy-done.3
  68.2 0.0 copy-done.4
  68.2 0.0 copy-done.5
  68.2 0.7 %fusion.1 = bf16[1,16,3072]{2,1,0:T(8,128)(2,1)} fusion(f32[16,3072]{1,0:T(8,128)S(1)} %get-tuple-element.29, bf16[16,3072]{1,0:T(8,128)(2,1)S(1)} %collective-permute-done.9, bf16[1,16,3072]{2,1,0:T(8,128)(2,1)S(1)} %copy-done.3, f32[3072]{0:T(1024)S(1)} %copy-done.4, f32[3072]{0:T(1024)S(1)} %copy-done.5), kind=kLoop, calls=%fused_computation.3 | loop fusion | flops 344064 | bytes 516096 | tf_op jit(solution)/shard_map/broadcast_in_dim | solution.py:413
  (2 shorter events, 0.0 us)
Async XLA Ops:
  0.6 26.0 %copy-start = (bf16[1,256,3,1024]{3,1,2,0:T(8,128)(2,1)S(1)}, bf16[1,256,3,1024]{3,1,2,0:T(8,128)(2,1)}, u32[]{:S(2)}) copy-start(bf16[1,256,3,1024]{3,1,2,0:T(8,128)(2,1)} %param.12) | copy-start | bytes 4718596
  13.0 13.2 %collective-permute-start.2 = (bf16[8,64,128]{2,1,0:T(8,128)(2,1)S(1)}, bf16[8,64,128]{2,1,0:T(8,128)(2,1)S(1)}, u32[]{:S(2)}, u32[]{:S(2)}) collective-permute-start(bf16[8,64,128]{2,1,0:T(8,128)(2,1)S(1)} %slice.8), channel_id=1, source_target_pairs={{0,128},{64,192},{128,0},{192,64},{1,129},{65,193},{129,1},{193,65... | collective-permute-start | bytes 393224 | tf_op jit(solution)/shard_map/ppermute | solution.py:361
  19.0 13.7 %collective-permute-start.1 = (bf16[8,64,128]{2,1,0:T(8,128)(2,1)S(1)}, bf16[8,64,128]{2,1,0:T(8,128)(2,1)S(1)}, u32[]{:S(2)}, u32[]{:S(2)}) collective-permute-start(bf16[8,64,128]{2,1,0:T(8,128)(2,1)S(1)} %slice.8), channel_id=1, source_target_pairs={{0,64},{64,0},{128,192},{192,128},{1,65},{65,1},{129,193},{193,129... | collective-permute-start | bytes 393224 | tf_op jit(solution)/shard_map/ppermute | solution.py:361
  20.2 12.5 %collective-permute-start = (bf16[8,64,128]{2,1,0:T(8,128)(2,1)S(1)}, bf16[8,64,128]{2,1,0:T(8,128)(2,1)S(1)}, u32[]{:S(2)}, u32[]{:S(2)}) collective-permute-start(bf16[8,64,128]{2,1,0:T(8,128)(2,1)S(1)} %slice.8), channel_id=1, source_target_pairs={{0,192},{64,128},{128,64},{192,0},{1,193},{65,129},{129,65},{193,1... | collective-permute-start | bytes 393224 | tf_op jit(solution)/shard_map/ppermute | solution.py:361
  20.9 7.1 %collective-permute-start.5 = (bf16[8,32,128]{2,1,0:T(8,128)(2,1)S(1)}, bf16[8,32,128]{2,1,0:T(8,128)(2,1)S(1)}, u32[]{:S(2)}, u32[]{:S(2)}) collective-permute-start(bf16[8,32,128]{2,1,0:T(8,128)(2,1)S(1)} %slice.9), channel_id=1, source_target_pairs={{0,20},{4,16},{16,4},{20,0},{1,21},{5,17},{17,5},{21,1},{2,22},{6,... | collective-permute-start | bytes 196616 | tf_op jit(solution)/shard_map/ppermute | solution.py:364
  25.8 5.4 %collective-permute-start.4 = (bf16[8,32,128]{2,1,0:T(8,128)(2,1)S(1)}, bf16[8,32,128]{2,1,0:T(8,128)(2,1)S(1)}, u32[]{:S(2)}, u32[]{:S(2)}) collective-permute-start(bf16[8,32,128]{2,1,0:T(8,128)(2,1)S(1)} %slice.9), channel_id=1, source_target_pairs={{0,4},{4,0},{16,20},{20,16},{1,5},{5,1},{17,21},{21,17},{2,6},{6,2... | collective-permute-start | bytes 196616 | tf_op jit(solution)/shard_map/ppermute | solution.py:364
  26.1 5.3 %collective-permute-start.3 = (bf16[8,32,128]{2,1,0:T(8,128)(2,1)S(1)}, bf16[8,32,128]{2,1,0:T(8,128)(2,1)S(1)}, u32[]{:S(2)}, u32[]{:S(2)}) collective-permute-start(bf16[8,32,128]{2,1,0:T(8,128)(2,1)S(1)} %slice.9), channel_id=1, source_target_pairs={{0,16},{4,20},{16,0},{20,4},{1,17},{5,21},{17,1},{21,5},{2,18},{6,... | collective-permute-start | bytes 196616 | tf_op jit(solution)/shard_map/ppermute | solution.py:364
  34.7 6.3 %collective-permute-start.6 = (bf16[528,128]{1,0:T(8,128)(2,1)S(1)}, bf16[528,128]{1,0:T(8,128)(2,1)S(1)}, u32[]{:S(2)}, u32[]{:S(2)}) collective-permute-start(bf16[528,128]{1,0:T(8,128)(2,1)S(1)} %get-tuple-element.27), channel_id=1, source_target_pairs={{0,4},{4,0},{16,20},{20,16},{1,5},{5,1},{17,21},{21,17},{2,6},{6,2... | collective-permute-start | bytes 405512 | tf_op jit(solution)/shard_map/ppermute | solution.py:383
  37.1 7.9 %collective-permute-start.8 = (bf16[528,128]{1,0:T(8,128)(2,1)S(1)}, bf16[528,128]{1,0:T(8,128)(2,1)S(1)}, u32[]{:S(2)}, u32[]{:S(2)}) collective-permute-start(bf16[528,128]{1,0:T(8,128)(2,1)S(1)} %get-tuple-element.28), channel_id=1, source_target_pairs={{0,20},{4,16},{16,4},{20,0},{1,21},{5,17},{17,5},{21,1},{2,22},{6,... | collective-permute-start | bytes 405512 | tf_op jit(solution)/shard_map/ppermute | solution.py:383
  39.0 6.0 %collective-permute-start.7 = (bf16[528,128]{1,0:T(8,128)(2,1)S(1)}, bf16[528,128]{1,0:T(8,128)(2,1)S(1)}, u32[]{:S(2)}, u32[]{:S(2)}) collective-permute-start(bf16[528,128]{1,0:T(8,128)(2,1)S(1)} %get-tuple-element.26.m2_ref), channel_id=1, source_target_pairs={{0,16},{4,20},{16,0},{20,4},{1,17},{5,21},{17,1},{21,5},{2,18},{6,... | collective-permute-start | bytes 405512 | tf_op jit(solution)/shard_map/ppermute | solution.py:383
  46.5 10.3 %all-to-all-start.1 = ((bf16[8,288,128]{2,1,0:T(8,128)(2,1)}), bf16[8,288,128]{2,1,0:T(8,128)(2,1)S(1)}, u32[]{:S(2)}, u32[]{:S(2)}) async-start(bf16[8,288,128]{2,1,0:T(8,128)(2,1)} %shard_map.128), calls=%async_computation.1 | async-start | bytes 1179648 | tf_op jit(solution)/shard_map/all_to_all | solution.py:398
  52.9 2.7 %copy-start.1 = (bf16[1024,3072]{1,0:T(8,128)(2,1)}, bf16[1024,3072]{1,0:T(8,128)(2,1)S(1)}, u32[]{:S(2)}) copy-start(bf16[1024,3072]{1,0:T(8,128)(2,1)S(1)} %shard_map.129.w_ref) | copy-start | bytes 18874372
  56.8 2.8 %copy-start.2 = (bf16[1024,3072]{1,0:T(8,128)(2,1)S(1)}, bf16[1024,3072]{1,0:T(8,128)(2,1)}, u32[]{:S(2)}) copy-start(bf16[1024,3072]{1,0:T(8,128)(2,1)} %copy-done.1) | copy-start | bytes 18874372
  59.6 8.6 %copy-start.3 = (bf16[1,16,3072]{2,1,0:T(8,128)(2,1)S(1)}, bf16[1,16,3072]{2,1,0:T(8,128)(2,1)}, u32[]{:S(2)}) copy-start(bf16[1,16,3072]{2,1,0:T(8,128)(2,1)} %param.17) | copy-start | bytes 294916
  59.6 8.6 %copy-start.4 = (f32[3072]{0:T(1024)S(1)}, f32[3072]{0:T(1024)}, u32[]{:S(2)}) copy-start(f32[3072]{0:T(1024)} %param.19) | copy-start | bytes 36868
  59.6 8.6 %copy-start.5 = (f32[3072]{0:T(1024)S(1)}, f32[3072]{0:T(1024)}, u32[]{:S(2)}) copy-start(f32[3072]{0:T(1024)} %param.20) | copy-start | bytes 36868
  60.9 7.3 %collective-permute-start.9 = (bf16[16,3072]{1,0:T(8,128)(2,1)S(1)}, bf16[16,3072]{1,0:T(8,128)(2,1)S(1)}, u32[]{:S(2)}, u32[]{:S(2)}) collective-permute-start(bf16[16,3072]{1,0:T(8,128)(2,1)S(1)} %get-tuple-element.30), channel_id=1, source_target_pairs={{0,1},{1,0},{2,3},{3,2},{4,5},{5,4},{6,7},{7,6},{8,9},{9,8},{10,11... | collective-permute-start | bytes 294920 | tf_op jit(solution)/shard_map/ppermute | solution.py:410
